TPU v7x, 32 devices: a whole 2x2x4 slice. The times are simulated.
32 devices in a mesh: ctx: 4 (over y, x), fsdp: 8 (over z, core).
Axes of the slice: x: 2, y: 2, z: 4, core: 2. Of those that a mesh axis runs over, the one named last changes fastest.
Arguments:
- layer_input: bfloat16 [1280, 4, 1536], P(('ctx', 'fsdp')), may hold values from -6 to 6
- block_order: int32 [2, 8], replicated, may hold values from 0 to 7, each once within a row
- first_gain: bfloat16 [1536], P('fsdp'), may hold values from 0.25 to 1.75
- w_qkv: bfloat16 [1536, 2048], P('fsdp'), may hold values from -0.15625 to 0.15625
- b_qkv: bfloat16 [2048], P('fsdp'), may hold values from -1.5 to 1.5
- w_o: bfloat16 [1536, 1536], P('fsdp'), may hold values from -1.25 to 1.25
- second_gain: bfloat16 [1536], P('fsdp'), may hold values from 0.25 to 1.75
- w_gate: bfloat16 [1536, 8960], P('fsdp'), may hold values from -0.15625 to 0.15625
- w_up: bfloat16 [1536, 8960], P('fsdp'), may hold values from -0.15625 to 0.15625
- w_down: bfloat16 [8960, 1536], P('fsdp'), may hold values from -0.0625 to 0.0625
- cotangent: bfloat16 [1280, 4, 1536], P(('ctx', 'fsdp')), may hold values from -6 to 6
Outputs:
- mixed: bfloat16 [1280, 4, 1536], P(('ctx', 'fsdp'))
- input_grad: float32 [1280, 4, 1536], P(('ctx', 'fsdp'))
- first_gain_grad: float32 [1536], P('fsdp')
- w_qkv_grad: float32 [1536, 2048], P('fsdp')
- b_qkv_grad: float32 [1792], P('fsdp')
- value_bias_grad: float32 [256], P('fsdp')
- w_o_grad: float32 [1536, 1536], P('fsdp')
- second_gain_grad: float32 [1536], P('fsdp')
- w_gate_grad: float32 [1536, 8960], P('fsdp')
- w_up_grad: float32 [1536, 8960], P('fsdp')
- w_down_grad: float32 [8960, 1536], P('fsdp')
Inputs may be any that keep to these rules, and one draw needn't show every extreme that they name: `block_order`: each row is a permutation.
All inputs are finite; a program needn't handle non-finite values.
Results may differ from a plain program's by a relative error of at most 0.02.
Values may be sent and summed in bfloat16 or wider, within the bound.
A program may use at most 576 MiB of HBM per device.

v0:
```python
import math

import jax
import jax.numpy as jnp
from jax import lax
from jax.sharding import PartitionSpec as P

D = 1536
H = 12
KVH = 2
HD = 128
FF = 8960
SEQS = 2
QKV = 2048
QK = 1792


EPS = 1e-06
THETA = 1000000.0
KEY_BLOCK = 256
NEG_FILL = -1e30
CONTRACT_LAST = (((1,), (1,)), ((), ()))
CONTRACT_FIRST = (((0,), (0,)), ((), ()))


def narrowed(values):
    return lax.optimization_barrier(values.astype(jnp.bfloat16)).astype(jnp.float32)


def block_positions(block_order, first_row, row_count, block_rows, ctx_size):
    row_index = first_row + jnp.arange(row_count, dtype=jnp.int32)
    slot_index = jnp.arange(2 * SEQS, dtype=jnp.int32)
    entries = (slot_index // SEQS)[None, :] * ctx_size + (row_index // block_rows)[:, None]
    tiled = jnp.tile(block_order, (2, 1))
    entry_ids = jnp.arange(2 * ctx_size, dtype=jnp.int32)
    picked = jnp.sum(
        jnp.where(entries[:, :, None] == entry_ids[None, None, :], tiled[None, :, :], 0), -1
    )
    return picked * block_rows + (row_index % block_rows)[:, None]


def pos_groups(positions):
    row_count = positions.shape[0]
    return positions.reshape(row_count, 2, SEQS).transpose(2, 0, 1).reshape(SEQS, row_count * 2)


def to_groups(tokens, row_count, group_size):
    shaped = tokens.reshape(row_count, 2, SEQS, KVH, group_size, HD)
    return shaped.transpose(2, 3, 4, 0, 1, 5).reshape(SEQS, KVH, group_size * row_count * 2, HD)


def from_groups(grouped, row_count, group_size):
    shaped = grouped.reshape(SEQS, KVH, group_size, row_count, 2, HD).transpose(3, 4, 0, 1, 2, 5)
    return shaped.reshape(row_count * 2 * SEQS, KVH * group_size * HD)


def rope_tables(positions):
    half_width = HD // 2
    frequency = THETA ** (-jnp.arange(half_width, dtype=jnp.float32) * 2.0 / HD)
    angles = positions.astype(jnp.float32)[:, None] * frequency[None, :]
    cosine_table = jnp.concatenate([jnp.cos(angles), jnp.cos(angles)], -1)[:, None, :]
    sine_table = jnp.concatenate([jnp.sin(angles), jnp.sin(angles)], -1)[:, None, :]
    return (cosine_table, sine_table)


def rotate(head_values, cosine_table, sine_table):
    half_width = HD // 2
    turned = jnp.concatenate([-head_values[..., half_width:], head_values[..., :half_width]], -1)
    return head_values * cosine_table + turned * sine_table


def rotate_back(grad_values, cosine_table, sine_table):
    half_width = HD // 2
    moved = grad_values * sine_table
    return grad_values * cosine_table + jnp.concatenate(
        [moved[..., half_width:], -moved[..., :half_width]], -1
    )


def normalize(values, gain):
    scale = lax.rsqrt(jnp.mean(values * values, -1, keepdims=True) + EPS)
    unit = values * scale
    return (unit, scale, unit * gain)


def norm_back(grad_out, unit, scale, gain):
    grad_unit = grad_out * gain
    inner = jnp.mean(grad_unit * unit, -1, keepdims=True)
    return (scale * (grad_unit - unit * inner), jnp.sum(grad_out * unit, 0))


def split_blocks(piece):
    row_count = piece.shape[0]
    size = math.gcd(row_count, KEY_BLOCK)
    stacked = piece.reshape(row_count // size, size, piece.shape[1], piece.shape[2])
    firsts = size * jnp.arange(row_count // size, dtype=jnp.int32)
    return (stacked, firsts)


def shards(
    layer_input,
    block_order,
    first_gain,
    w_qkv,
    b_qkv,
    w_o,
    second_gain,
    w_gate,
    w_up,
    w_down,
    cotangent,
):
    ctx_size = lax.axis_size("ctx")
    shard_count = lax.axis_size("fsdp")
    rows_here = layer_input.shape[0]
    slots = layer_input.shape[1]
    block_rows = rows_here * shard_count
    group_size = H // KVH
    kv_width = KVH * HD
    first_row = (lax.axis_index("ctx") * shard_count + lax.axis_index("fsdp")) * rows_here
    own_pos = block_positions(block_order, first_row, rows_here, block_rows, ctx_size)
    cosine_table, sine_table = rope_tables(own_pos.reshape(-1))
    query_scale = HD ** (-0.5)
    w_qkv_all, w_o_all, bias_all, gain_one, gain_two = (
        lax.all_gather(w_qkv, "fsdp", axis=0, tiled=True),
        lax.all_gather(w_o, "fsdp", axis=0, tiled=True),
        lax.all_gather(b_qkv, "fsdp", axis=0, tiled=True),
        lax.all_gather(first_gain, "fsdp", axis=0, tiled=True),
        lax.all_gather(second_gain, "fsdp", axis=0, tiled=True),
    )
    gain_one = gain_one.astype(jnp.float32)
    gain_two = gain_two.astype(jnp.float32)
    inputs = layer_input.reshape(-1, D).astype(jnp.float32)
    unit_one, scale_one, normed = normalize(inputs, gain_one)
    normed_one = normed.astype(jnp.bfloat16)
    projected = jnp.dot(
        normed_one, w_qkv_all, preferred_element_type=jnp.float32
    ) + bias_all.astype(jnp.float32)
    query_raw = projected[:, : H * HD].reshape(-1, H, HD)
    key_raw = projected[:, H * HD : H * HD + kv_width].reshape(-1, KVH, HD)
    value_raw = projected[:, H * HD + kv_width :]
    query_tokens = (
        (rotate(query_raw, cosine_table, sine_table) * query_scale)
        .astype(jnp.bfloat16)
        .reshape(-1, H * HD)
    )
    key_tokens = (
        rotate(key_raw, cosine_table, sine_table).astype(jnp.bfloat16).reshape(-1, kv_width)
    )
    own_kv = jnp.concatenate([key_tokens, value_raw.astype(jnp.bfloat16)], -1).reshape(
        rows_here, slots, 2 * kv_width
    )
    block_kv = lax.all_gather(own_kv, "fsdp", axis=0, tiled=True)
    queries = to_groups(query_tokens, rows_here, group_size)
    query_pos = jnp.tile(pos_groups(own_pos), (1, group_size))
    query_count = queries.shape[2]

    def piece_keys(key_rows, row_start):
        row_count = key_rows.shape[0]
        flat = key_rows.reshape(row_count * slots, 2 * kv_width)
        keys_grouped = to_groups(flat[:, :kv_width], row_count, 1)
        values_grouped = to_groups(flat[:, kv_width:], row_count, 1)
        key_pos = pos_groups(
            block_positions(block_order, row_start, row_count, block_rows, ctx_size)
        )
        visible = query_pos[:, None, :, None] >= key_pos[:, None, None, :]
        scores = jnp.einsum(
            "snmd,snkd->snmk", queries, keys_grouped, preferred_element_type=jnp.float32
        )
        return (keys_grouped, values_grouped, visible, scores)

    start_state = (
        jnp.full((SEQS, KVH, query_count), NEG_FILL, jnp.float32),
        jnp.zeros((SEQS, KVH, query_count), jnp.float32),
        jnp.zeros((SEQS, KVH, query_count, HD), jnp.float32),
    )
    state = start_state
    stacked, firsts = split_blocks(lax.all_gather(block_kv, "ctx", axis=0, tiled=True))

    def forward_one_block(carry, item):
        best, totals, accum = carry
        key_rows, row_start = item
        keys_grouped, values_grouped, visible, scores = piece_keys(key_rows, row_start)
        scores = jnp.where(visible, scores, NEG_FILL)
        fresh = jnp.maximum(best, jnp.max(scores, -1))
        weights = jnp.where(visible, jnp.exp(scores - fresh[..., None]), 0.0)
        decay = jnp.exp(best - fresh)
        totals = totals * decay + jnp.sum(weights, -1)
        accum = accum * decay[..., None] + jnp.einsum(
            "snmk,snkd->snmd",
            weights.astype(jnp.bfloat16),
            values_grouped,
            preferred_element_type=jnp.float32,
        )
        return ((fresh, totals, accum), None)

    state, unused = lax.scan(forward_one_block, state, (stacked, firsts))
    best, totals, accum = state
    attended_grouped = accum / totals[..., None]
    logsum = best + jnp.log(totals)
    attended_low = from_groups(attended_grouped, rows_here, group_size).astype(jnp.bfloat16)
    middle = inputs + jnp.dot(attended_low, w_o_all, preferred_element_type=jnp.float32)
    unit_two, scale_two, normed = normalize(middle, gain_two)
    normed_two = normed.astype(jnp.bfloat16)
    gate_all, up_all, down_all = (
        lax.all_gather(w_gate, "fsdp", axis=0, tiled=True),
        lax.all_gather(w_up, "fsdp", axis=0, tiled=True),
        lax.all_gather(w_down, "fsdp", axis=0, tiled=True),
    )
    gate_part = jnp.dot(normed_two, gate_all, preferred_element_type=jnp.float32)
    up_part = jnp.dot(normed_two, up_all, preferred_element_type=jnp.float32)
    activated = jax.nn.silu(gate_part)
    hidden = (activated * up_part).astype(jnp.bfloat16)
    mixed_out = middle + jnp.dot(hidden, down_all, preferred_element_type=jnp.float32)
    output = mixed_out.astype(jnp.bfloat16).reshape(rows_here, slots, D)
    gate_all, up_all, down_all = (
        lax.all_gather(w_gate, "fsdp", axis=0, tiled=True),
        lax.all_gather(w_up, "fsdp", axis=0, tiled=True),
        lax.all_gather(w_down, "fsdp", axis=0, tiled=True),
    )
    w_qkv_all, w_o_all = (
        lax.all_gather(w_qkv, "fsdp", axis=0, tiled=True),
        lax.all_gather(w_o, "fsdp", axis=0, tiled=True),
    )
    grad_branch_two = cotangent.reshape(-1, D)
    grad_hidden = lax.dot_general(
        grad_branch_two, down_all, CONTRACT_LAST, preferred_element_type=jnp.float32
    )
    sigmoid_gate = jax.nn.sigmoid(gate_part)
    grad_gate = grad_hidden * up_part * sigmoid_gate * (1.0 + gate_part * (1.0 - sigmoid_gate))
    grad_gate_up = jnp.concatenate([grad_gate, grad_hidden * activated], -1).astype(jnp.bfloat16)
    grad_normed_two = lax.dot_general(
        grad_gate_up[:, :FF], gate_all, CONTRACT_LAST, preferred_element_type=jnp.float32
    )
    grad_normed_two = grad_normed_two + lax.dot_general(
        grad_gate_up[:, FF:], up_all, CONTRACT_LAST, preferred_element_type=jnp.float32
    )
    grad_middle_norm, grad_gain_two = norm_back(grad_normed_two, unit_two, scale_two, gain_two)
    grad_middle = cotangent.reshape(-1, D).astype(jnp.float32) + grad_middle_norm
    grad_branch_one = grad_middle.astype(jnp.bfloat16)
    grad_attended = lax.dot_general(
        grad_branch_one, w_o_all, CONTRACT_LAST, preferred_element_type=jnp.float32
    ).astype(jnp.bfloat16)
    grad_out_grouped = to_groups(grad_attended, rows_here, group_size)
    delta = jnp.sum(grad_out_grouped.astype(jnp.float32) * attended_grouped, -1)
    back_state = (
        jnp.zeros((SEQS, KVH, query_count, HD), jnp.float32),
        jnp.zeros((ctx_size * block_rows, slots, 2 * kv_width), jnp.float32),
    )
    state = back_state
    stacked, firsts = split_blocks(lax.all_gather(block_kv, "ctx", axis=0, tiled=True))

    def backward_one_block(carry, item):
        grad_queries, grad_kv_full = carry
        key_rows, row_start = item
        row_count = key_rows.shape[0]
        keys_grouped, values_grouped, visible, scores = piece_keys(key_rows, row_start)
        probs = jnp.where(
            visible, jnp.exp(jnp.where(visible, scores, NEG_FILL) - logsum[..., None]), 0.0
        )
        grad_probs = jnp.einsum(
            "snmd,snkd->snmk", grad_out_grouped, values_grouped, preferred_element_type=jnp.float32
        )
        grad_scores = (probs * (grad_probs - delta[..., None])).astype(jnp.bfloat16)
        grad_queries = grad_queries + jnp.einsum(
            "snmk,snkd->snmd", grad_scores, keys_grouped, preferred_element_type=jnp.float32
        )
        grad_keys = jnp.einsum(
            "snmk,snmd->snkd", grad_scores, queries, preferred_element_type=jnp.float32
        )
        grad_values = jnp.einsum(
            "snmk,snmd->snkd",
            probs.astype(jnp.bfloat16),
            grad_out_grouped,
            preferred_element_type=jnp.float32,
        )
        block_terms = jnp.concatenate(
            [from_groups(grad_keys, row_count, 1), from_groups(grad_values, row_count, 1)], -1
        ).reshape(row_count, slots, 2 * kv_width)
        previous = lax.dynamic_slice_in_dim(grad_kv_full, row_start, row_count, 0)
        grad_kv_full = lax.dynamic_update_slice_in_dim(
            grad_kv_full, previous + block_terms, row_start, 0
        )
        return ((grad_queries, grad_kv_full), None)

    state, unused = lax.scan(backward_one_block, state, (stacked, firsts))
    grad_queries, grad_kv_full = state
    grad_kv = lax.psum_scatter(grad_kv_full, ("ctx", "fsdp"), scatter_dimension=0, tiled=True)
    grad_kv_low = narrowed(grad_kv).reshape(-1, 2 * kv_width)
    grad_query_tokens = from_groups(narrowed(grad_queries), rows_here, group_size) * query_scale
    grad_query_raw = rotate_back(
        grad_query_tokens.reshape(-1, H, HD), cosine_table, sine_table
    ).reshape(-1, H * HD)
    grad_key_raw = rotate_back(
        grad_kv_low[:, :kv_width].reshape(-1, KVH, HD), cosine_table, sine_table
    ).reshape(-1, kv_width)
    grad_projected = jnp.concatenate(
        [grad_query_raw, grad_key_raw, grad_kv_low[:, kv_width:]], -1
    ).astype(jnp.bfloat16)
    grad_bias = jnp.sum(grad_projected, 0, dtype=jnp.float32)
    grad_bias_qk = grad_bias[:QK]
    grad_bias_value = grad_bias[QK:]
    grad_normed_one = lax.dot_general(
        grad_projected, w_qkv_all, CONTRACT_LAST, preferred_element_type=jnp.float32
    )
    grad_input_norm, grad_gain_one = norm_back(grad_normed_one, unit_one, scale_one, gain_one)
    grad_input = (grad_middle + grad_input_norm).reshape(rows_here, slots, D)
    weight_rows = lax.psum_scatter(
        jnp.concatenate(
            [
                lax.dot_general(
                    normed_two, grad_gate_up, CONTRACT_FIRST, preferred_element_type=jnp.float32
                ),
                lax.dot_general(
                    normed_one, grad_projected, CONTRACT_FIRST, preferred_element_type=jnp.float32
                ),
                lax.dot_general(
                    attended_low,
                    grad_branch_one,
                    CONTRACT_FIRST,
                    preferred_element_type=jnp.float32,
                ),
            ],
            1,
        ).astype(jnp.bfloat16),
        "fsdp",
        scatter_dimension=0,
        tiled=True,
    ).astype(jnp.float32)
    down_rows = lax.psum_scatter(
        lax.dot_general(
            hidden, grad_branch_two, CONTRACT_FIRST, preferred_element_type=jnp.float32
        ).astype(jnp.bfloat16),
        "fsdp",
        scatter_dimension=0,
        tiled=True,
    ).astype(jnp.float32)
    gain_one_rows, gain_two_rows, bias_rows, value_bias_rows = (
        lax.psum_scatter(grad_gain_one, "fsdp", scatter_dimension=0, tiled=True),
        lax.psum_scatter(grad_gain_two, "fsdp", scatter_dimension=0, tiled=True),
        lax.psum_scatter(grad_bias_qk, "fsdp", scatter_dimension=0, tiled=True),
        lax.psum_scatter(grad_bias_value, "fsdp", scatter_dimension=0, tiled=True),
    )
    weight_rows, down_rows, gain_one_rows, gain_two_rows, bias_rows, value_bias_rows = (
        lax.psum(weight_rows.astype(jnp.bfloat16), "ctx").astype(jnp.float32),
        lax.psum(down_rows.astype(jnp.bfloat16), "ctx").astype(jnp.float32),
        lax.psum(gain_one_rows.astype(jnp.bfloat16), "ctx").astype(jnp.float32),
        lax.psum(gain_two_rows.astype(jnp.bfloat16), "ctx").astype(jnp.float32),
        lax.psum(bias_rows.astype(jnp.bfloat16), "ctx").astype(jnp.float32),
        lax.psum(value_bias_rows.astype(jnp.bfloat16), "ctx").astype(jnp.float32),
    )
    return (
        output,
        grad_input,
        gain_one_rows,
        weight_rows[:, 2 * FF : 2 * FF + QKV],
        bias_rows,
        value_bias_rows,
        weight_rows[:, 2 * FF + QKV :],
        gain_two_rows,
        weight_rows[:, :FF],
        weight_rows[:, FF : 2 * FF],
        down_rows,
    )


def solution(mesh):
    in_specs = (
        P(("ctx", "fsdp"), None, None),
        P(),
        P("fsdp"),
        P("fsdp", None),
        P("fsdp"),
        P("fsdp", None),
        P("fsdp"),
        P("fsdp", None),
        P("fsdp", None),
        P("fsdp", None),
        P(("ctx", "fsdp"), None, None),
    )
    out_specs = (
        P(("ctx", "fsdp"), None, None),
        P(("ctx", "fsdp"), None, None),
        P("fsdp"),
        P("fsdp", None),
        P("fsdp"),
        P("fsdp"),
        P("fsdp", None),
        P("fsdp"),
        P("fsdp", None),
        P("fsdp", None),
        P("fsdp", None),
    )
    return jax.shard_map(shards, mesh=mesh, in_specs=in_specs, out_specs=out_specs, check_vma=False)
```

profile of v0, /device:TPU:0, one launch (start us, length us, event | category | flops | bytes accessed | tf_op | source)
XLA Modules:
  0.0 2331.4 jit_solution(8139246037101609936)
XLA Ops:
  9.8 13.5 all-gather
  27.0 15.6 all-reduce.8
  46.4 31.2 %all-gather.9.cloned.1.call-done = bf16[1536,2048]{1,0:T(8,128)(2,1)} async-done(((bf16[192,2048]{1,0:T(8,128)(2,1)}), bf16[1536,2048]{1,0:T(8,128)(2,1)}) %all-gather.9.cloned.1.call-update) | async-done | bytes 6291472 | tf_op jit(solution)/shard_map/all_gather | solution.py:125
  84.0 22.2 all-gather.11.cloned.1.call-done
  125.8 43.1 %all-gather.13.cloned.1.call-done = bf16[1280,4,512]{2,1,0:T(4,128)(2,1)} async-done(((bf16[320,4,512]{2,1,0:T(4,128)(2,1)}), bf16[1280,4,512]{2,1,0:T(4,128)(2,1)}) %all-gather.13.cloned.1.call-update) | async-done | bytes 5242896 | tf_op jit(solution)/shard_map/all_gather | solution.py:178
  168.8 82.6 %while.34 = (s32[]{:T(128)}, f32[2,2,480]{2,1,0:T(2,128)S(1)}, f32[2,2,480]{2,1,0:T(2,128)S(1)}, f32[2,2,480,128]{3,2,1,0:T(8,128)}, s32[5]{0:T(128)S(1)}, /*ind...) while((s32[]{:T(128)}, f32[2,2,480]{2,1,0:T(2,128)S(1)}, ...), condition=%wide.region_6.7_spmd.clone, body=%wide.region_2.6_spmd.clone.sunk | while | flops 514415264 | bytes 27955316 | solution.py:197
  257.6 203.4 %all-gather.17.cloned.1.call-done = bf16[1536,8960]{1,0:T(8,128)(2,1)} async-done(((bf16[192,8960]{1,0:T(8,128)(2,1)}), bf16[1536,8960]{1,0:T(8,128)(2,1)}) %all-gather.17.cloned.1.call-update) | async-done | bytes 27525136 | tf_op jit(solution)/shard_map/all_gather | solution.py:206
  461.0 16.3 fusion.69
  477.3 222.6 %all-gather.19.cloned.1.call-done = bf16[1536,8960]{1,0:T(8,128)(2,1)} async-done(((bf16[192,8960]{1,0:T(8,128)(2,1)}), bf16[1536,8960]{1,0:T(8,128)(2,1)}) %all-gather.19.cloned.1.call-update) | async-done | bytes 27525136 | tf_op jit(solution)/shard_map/all_gather | solution.py:207
  699.9 16.4 fusion.70
  716.4 222.6 %all-gather.21.cloned.1.call-done = bf16[8960,1536]{1,0:T(8,128)(2,1)} async-done(((bf16[1120,1536]{1,0:T(8,128)(2,1)}), bf16[8960,1536]{1,0:T(8,128)(2,1)}) %all-gather.21.cloned.1.call-update) | async-done | bytes 27525136 | tf_op jit(solution)/shard_map/all_gather | solution.py:208
  939.0 19.8 multiply_convert_fusion
  958.8 14.9 convolution_convert_fusion.1
  973.8 17.0 fusion.71
  990.8 16.1 multiply_reduce_fusion
  1019.5 165.8 %while.35 = (s32[]{:T(128)}, f32[2,2,480,128]{3,2,1,0:T(8,128)}, f32[1280,4,512]{2,1,0:T(4,128)}, s32[5]{0:T(128)S(1)}, s32[2,8]{1,0:T(2,128)S(1)}, /*index=5*/b...) while((s32[]{:T(128)}, f32[2,2,480,128]{3,2,1,0:T(8,128)}, ...), condition=%wide.region_12.13_spmd.clone, body=%wide.region_10.12_spmd.clone.sunk | while | flops 1270183168 | bytes 55970532 | solution.py:286
  1188.1 176.6 %all-reduce.15 = bf16[1280,4,512]{2,1,0:T(4,128)(2,1)} all-reduce(f32[1280,4,512]{2,1,0:T(4,128)} %get-tuple-element.344), channel_id=2, replica_groups=mesh['ctx'=4,'fsdp'=8] {'ctx','fsdp'}, use_global_device_ids=true, to_apply=%region_13.14.clone | all-reduce | flops 2621440 | bytes 15728640
  1380.7 23.8 %convolution_convert_fusion = bf16[1536,17920]{1,0:T(8,128)(2,1)} fusion(bf16[160,1536]{1,0:T(8,128)(2,1)S(1)} %copy-done.10, bf16[160,8960]{1,0:T(8,128)(2,1)} %get-tuple-element.485, bf16[160,8960]{1,0:T(8,128)(2,1)} %get-tuple-element.486), kind=kOutput, calls=%fused_computation.72 | convolution fusion | flops 8847032320 | bytes 61276160 | tf_op jit(solution)/shard_map/dot_general | solution.py:311
  1404.5 44.2 %pad_maximum_fusion = bf16[1536,21504]{1,0:T(8,128)(2,1)} fusion(bf16[1536,1536]{1,0:T(8,128)(2,1)} %convolution_convert_fusion.3, bf16[1536,2048]{1,0:T(8,128)(2,1)} %convolution_convert_fusion.2, bf16[1536,17920]{1,0:T(8,128)(2,1)} %convolution_convert_fusion), kind=kLoop, calls=%fused_computation.73 | loop fusion | flops 198180864 | bytes 132120576 | tf_op jit(solution)/shard_map/concatenate | solution.py:309
  1448.8 629.6 %reduce-scatter.3.cloned.1.call-done = bf16[192,21504]{1,0:T(8,128)(2,1)} async-done(((bf16[1536,21504]{1,0:T(8,128)(2,1)}), bf16[192,21504]{1,0:T(8,128)(2,1)}) %reduce-scatter.3.cloned.1.call-update) | async-done | bytes 8257552 | tf_op jit(solution)/shard_map/reduce_scatter | solution.py:308
  2080.4 16.4 fusion.44
  2107.0 26.1 %all-reduce.7 = (bf16[1536]{0:T(1024)(128)(2,1)S(1)}, bf16[1792]{0:T(1024)(128)(2,1)S(1)}, bf16[256]{0:T(256)(128)(2,1)S(1)}, bf16[1536]{0:T(1024)(128)(2,1)S(1)}) all-reduce(f32[1536]{0:T(1024)S(1)} %get-tuple-element.419, f32[1792]{0:T(1024)S(1)} %bitcast.253, ...), channel_id=3, replica_groups=mesh['ctx'=4,'fsdp'=8] {'fsdp'}, use_global_device_ids=true, to_apply=%region_16.17.clone | all-reduce | flops 5120 | bytes 30720
  2133.4 10.3 all-reduce.9
  2145.9 160.7 %all-reduce.14.cloned.1.call-done = (bf16[192,21504]{1,0:T(8,128)(2,1)}, bf16[1120,1536]{1,0:T(8,128)(2,1)}) async-done(((bf16[192,21504]{1,0:T(8,128)(2,1)}, bf16[1120,1536]{1,0:T(8,128)(2,1)}), (bf16[192,21504]{1,0:T(8,128)(2,1)}, bf16[1120,1536]{1,0:T(8,128)(2,1)})) %all-reduce.14.cloned.1.call-update) | async-done | bytes 11698192 | tf_op jit(solution)/shard_map/psum | solution.py:345
  (512 shorter events, 339.2 us)
Async XLA Ops:
  7.2 70.4 %all-gather.9.cloned.1.call-start = ((), (), s32[]{:S(2)}) async-start(), calls=%async_computation.2 | async-start | bytes 7077888 | tf_op jit(solution)/shard_map/all_gather | solution.py:125
  7.9 98.2 %all-gather.11.cloned.1.call-start = ((), (), s32[]{:S(2)}) async-start(), calls=%async_computation.3 | async-start | bytes 1474560 | tf_op jit(solution)/shard_map/all_gather | solution.py:153
  9.1 72.6 %copy-start = (f32[160,1536]{1,0:T(8,128)}, f32[160,1536]{1,0:T(8,128)S(1)}, u32[]{:S(2)}) copy-start(f32[160,1536]{1,0:T(8,128)S(1)} %reshape.608) | copy-start | bytes 2949124
  42.6 39.1 %copy-start.29 = (f32[1536]{0:T(1024)}, f32[1536]{0:T(1024)S(1)}, u32[]{:S(2)}) copy-start(f32[1536]{0:T(1024)S(1)} %convert_element_type.151) | copy-start | bytes 18436
  44.1 33.6 %copy-start.32 = (f32[160]{0:T(256)}, f32[160]{0:T(256)S(1)}, u32[]{:S(2)}) copy-start(f32[160]{0:T(256)S(1)} %rsqrt.20) | copy-start | bytes 1924
  45.6 36.7 %copy-start.26 = (f32[160,128]{1,0:T(8,128)}, f32[160,128]{1,0:T(8,128)S(1)}, u32[]{:S(2)}) copy-start(f32[160,128]{1,0:T(8,128)S(1)} %pad_maximum_fusion.4) | copy-start | bytes 245764
  46.4 35.7 %copy-start.24 = (f32[160,128]{1,0:T(8,128)}, f32[160,128]{1,0:T(8,128)S(1)}, u32[]{:S(2)}) copy-start(f32[160,128]{1,0:T(8,128)S(1)} %get-tuple-element.501) | copy-start | bytes 245764
  81.7 25.7 %copy-start.13 = (f32[160,2048]{1,0:T(8,128)}, f32[160,2048]{1,0:T(8,128)S(1)}, u32[]{:S(2)}) copy-start(f32[160,2048]{1,0:T(8,128)S(1)} %convolution_add_fusion.4) | copy-start | bytes 3932164
  83.9 84.9 %all-gather.13.cloned.1.call-start = ((), (), s32[]{:S(2)}) async-start(), calls=%async_computation.4 | async-start | bytes 6553600 | tf_op jit(solution)/shard_map/all_gather | solution.py:178
  106.1 147.7 %all-gather.15.cloned.1.call-start = ((), (), s32[]{:S(2)}) async-start(), calls=%async_computation.5 | async-start | bytes 5308416 | tf_op jit(solution)/shard_map/all_gather | solution.py:126
  106.7 354.3 %all-gather.17.cloned.1.call-start = ((), (), s32[]{:S(2)}) async-start(), calls=%async_computation.6 | async-start | bytes 30965760 | tf_op jit(solution)/shard_map/all_gather | solution.py:206
  107.3 592.6 %all-gather.19.cloned.1.call-start = ((), (), s32[]{:S(2)}) async-start(), calls=%async_computation.7 | async-start | bytes 30965760 | tf_op jit(solution)/shard_map/all_gather | solution.py:207
  107.9 831.1 %all-gather.21.cloned.1.call-start = ((), (), s32[]{:S(2)}) async-start(), calls=%async_computation.8 | async-start | bytes 30965760 | tf_op jit(solution)/shard_map/all_gather | solution.py:208
  108.7 1340.1 %reduce-scatter.5.cloned.1.call-start = ((), (), s32[]{:S(2)}) async-start(), calls=%async_computation.10 | async-start | bytes 30965760 | tf_op jit(solution)/shard_map/reduce_scatter | solution.py:330
  116.5 7.4 copy-start.15
  122.1 46.8 %copy-start.31 = (s32[2,8]{1,0:T(2,128)S(1)}, s32[2,8]{1,0:T(2,128)}, u32[]{:S(2)}) copy-start(s32[2,8]{1,0:T(2,128)} %param.16) | copy-start | bytes 196
  257.4 749.5 %copy-start.7 = (f32[160,1536]{1,0:T(8,128)}, f32[160,1536]{1,0:T(8,128)S(1)}, u32[]{:S(2)}) copy-start(f32[160,1536]{1,0:T(8,128)S(1)} %get-tuple-element.513) | copy-start | bytes 2949124
  257.6 442.3 %copy-start.9 = (bf16[160,1536]{1,0:T(8,128)(2,1)}, bf16[160,1536]{1,0:T(8,128)(2,1)S(1)}, u32[]{:S(2)}) copy-start(bf16[160,1536]{1,0:T(8,128)(2,1)S(1)} %multiply_convert_fusion.3) | copy-start | bytes 1474564
  477.3 461.7 %copy-start.16 = (bf16[160,1536]{1,0:T(8,128)(2,1)S(1)}, bf16[160,1536]{1,0:T(8,128)(2,1)}, u32[]{:S(2)}) copy-start(bf16[160,1536]{1,0:T(8,128)(2,1)} %reshape.600) | copy-start | bytes 1474564
  973.7 1104.6 %reduce-scatter.3.cloned.1.call-start = ((), (), s32[]{:S(2)}) async-start(), calls=%async_computation.9 | async-start | bytes 74317824 | tf_op jit(solution)/shard_map/reduce_scatter | solution.py:308
  1008.2 5.8 copy-start.17
  1369.8 5.8 copy-start.23
  1448.7 857.9 %all-reduce.14.cloned.1.call-start = ((), (), s32[]{:S(2)}) async-start(), calls=%async_computation.11 | async-start | bytes 23396352 | tf_op jit(solution)/shard_map/psum | solution.py:345
  2311.2 9.2 copy-start.19
  (29 other events, 90.3 us)
Sparse Core Ops, SparseCore 0:
  9.6 67.9 all-gather.8
  84.0 22.0 all-gather.10
  108.0 60.8 all-gather.12
  170.3 51.1 all-gather.14
  223.1 237.9 all-gather.16
  462.5 237.3 all-gather.18
  701.6 237.3 all-gather.20
  973.9 267.4 reduce-scatter.4
  1448.8 629.5 reduce-scatter.2
  2082.0 224.5 all-reduce.13
where the time goes:
time: 2340 us; the launch traced here: 2330 us
  waiting for transfers between devices  1540 us (66%)
  matrix products  274 us (12%)
  blocking collectives  242 us (10%)
  local copies, waits for them, and re-layouts  128 us (5%)
  other arithmetic  118 us (5%)
    reduce_scatter x1, waiting for transfers between devices, shards(): lax.psum_scatter(jnp.concatenate([lax.dot_general(normed_two, grad_gate_u...  630 us
    all_gather x1, waiting for transfers between devices, shards(): lax.all_gather(w_down, 'fsdp', axis=0, tiled=True)  223 us
    all_gather x1, waiting for transfers between devices, shards(): lax.all_gather(w_up, 'fsdp', axis=0, tiled=True)  223 us
    unnamed x3, blocking collectives  218 us
    all_gather x1, waiting for transfers between devices, shards(): lax.all_gather(w_gate, 'fsdp', axis=0, tiled=True)  203 us
    psum x1, waiting for transfers between devices, shards(): lax.psum(weight_rows.astype(jnp.bfloat16), 'ctx').astype(jnp.float32)  161 us
  transfers between devices with their start and end apart: 10, of which 8 were waited for; matrix products, arithmetic and copies ran while one was open for 20% of the time, Pallas kernels for 0%

commit v1 on v0

v1 whole, which is shorter than its diff:
```python
import functools

import jax
import jax.numpy as jnp
from jax import lax
from jax.experimental import pallas as pl
from jax.experimental.pallas import tpu as pltpu
from jax.sharding import PartitionSpec as P

D = 1536
H = 12
KVH = 2
HD = 128
FF = 8960
SEQS = 2
QKV = 2048
QK = 1792


EPS = 1e-06
THETA = 1000000.0
NEG_FILL = -1e30
CONTRACT_LAST = (((1,), (1,)), ((), ()))
CONTRACT_FIRST = (((0,), (0,)), ((), ()))


def narrowed(values):
    return lax.optimization_barrier(values.astype(jnp.bfloat16)).astype(jnp.float32)


def block_positions(block_order, first_row, row_count, block_rows, ctx_size):
    row_index = first_row + jnp.arange(row_count, dtype=jnp.int32)
    slot_index = jnp.arange(2 * SEQS, dtype=jnp.int32)
    entries = (slot_index // SEQS)[None, :] * ctx_size + (row_index // block_rows)[:, None]
    tiled = jnp.tile(block_order, (2, 1))
    entry_ids = jnp.arange(2 * ctx_size, dtype=jnp.int32)
    picked = jnp.sum(
        jnp.where(entries[:, :, None] == entry_ids[None, None, :], tiled[None, :, :], 0), -1
    )
    return picked * block_rows + (row_index % block_rows)[:, None]


def to_groups(tokens, row_count):
    shaped = tokens.reshape(row_count, 2, SEQS, KVH, H // KVH, HD)
    return shaped.transpose(2, 1, 3, 4, 0, 5).reshape(SEQS, 2, KVH, H // KVH * row_count, HD)


def from_groups(grouped, row_count):
    shaped = grouped.reshape(SEQS, 2, KVH, H // KVH, row_count, HD).transpose(4, 1, 0, 2, 3, 5)
    return shaped.reshape(row_count * 2 * SEQS, H * HD)


def rope_tables(positions):
    half_width = HD // 2
    frequency = THETA ** (-jnp.arange(half_width, dtype=jnp.float32) * 2.0 / HD)
    angles = positions.astype(jnp.float32)[:, None] * frequency[None, :]
    cosine_table = jnp.concatenate([jnp.cos(angles), jnp.cos(angles)], -1)[:, None, :]
    sine_table = jnp.concatenate([jnp.sin(angles), jnp.sin(angles)], -1)[:, None, :]
    return (cosine_table, sine_table)


def rotate(head_values, cosine_table, sine_table):
    half_width = HD // 2
    turned = jnp.concatenate([-head_values[..., half_width:], head_values[..., :half_width]], -1)
    return head_values * cosine_table + turned * sine_table


def rotate_back(grad_values, cosine_table, sine_table):
    half_width = HD // 2
    moved = grad_values * sine_table
    return grad_values * cosine_table + jnp.concatenate(
        [moved[..., half_width:], -moved[..., :half_width]], -1
    )


def normalize(values, gain):
    scale = lax.rsqrt(jnp.mean(values * values, -1, keepdims=True) + EPS)
    unit = values * scale
    return (unit, scale, unit * gain)


def norm_back(grad_out, unit, scale, gain):
    grad_unit = grad_out * gain
    inner = jnp.mean(grad_unit * unit, -1, keepdims=True)
    return (scale * (grad_unit - unit * inner), jnp.sum(grad_out * unit, 0))


def attend_forward_kernel(ctx_size, block_rows, rows_here, scalars, q_ref, kv_ref, out_ref, stat_ref, best_ref, total_ref, accum_ref):
    seq = pl.program_id(0)
    blocks = 2 * ctx_size
    own_ctx = scalars[SEQS * blocks]
    own_shard = scalars[SEQS * blocks + 1]
    lanes = q_ref.shape[3]
    best_ref[...] = jnp.full(best_ref.shape, NEG_FILL, jnp.float32)
    total_ref[...] = jnp.zeros(total_ref.shape, jnp.float32)
    accum_ref[...] = jnp.zeros(accum_ref.shape, jnp.float32)

    def step(key_ctx, half_key, half):
        order_key = scalars[seq * blocks + half_key * ctx_size + key_ctx]
        order_query = scalars[seq * blocks + half * ctx_size + own_ctx]

        def work(masked):
            rows = pl.ds(pl.multiple_of(key_ctx * block_rows, block_rows), block_rows)
            keys = kv_ref[rows, half_key * 2 * HD : half_key * 2 * HD + HD]
            values = kv_ref[rows, half_key * 2 * HD + HD : half_key * 2 * HD + 2 * HD]
            scores = lax.dot_general(
                keys, q_ref[0, half, 0], CONTRACT_LAST, preferred_element_type=jnp.float32
            )
            if masked:
                row = lax.broadcasted_iota(jnp.int32, (block_rows, lanes), 0)
                lane = lax.broadcasted_iota(jnp.int32, (block_rows, lanes), 1)
                scores = jnp.where(
                    row <= own_shard * rows_here + lax.rem(lane, rows_here), scores, NEG_FILL
                )
            best = best_ref[half]
            fresh = jnp.maximum(best, jnp.max(scores, 0, keepdims=True))
            decay = jnp.exp(best - fresh)
            weights = jnp.exp(scores - fresh)
            total_ref[half] = total_ref[half] * decay + jnp.sum(weights, 0, keepdims=True)
            accum_ref[half] = accum_ref[half] * decay + lax.dot_general(
                values,
                weights.astype(jnp.bfloat16),
                CONTRACT_FIRST,
                preferred_element_type=jnp.float32,
            )
            best_ref[half] = fresh

        @pl.when(order_key < order_query)
        def full():
            work(False)

        @pl.when(order_key == order_query)
        def diagonal():
            work(True)

    @pl.loop(0, ctx_size)
    def sweep(key_ctx):
        for half_key in range(2):
            for half in range(2):
                step(key_ctx, half_key, half)

    for half in range(2):
        totals = total_ref[half]
        out_ref[0, half, 0] = (accum_ref[half] / totals).T
        stat_ref[0, half, 0] = best_ref[half] + jnp.log(totals)


def attend_forward(scalars, queries, all_kv, ctx_size, block_rows, rows_here):
    lanes = queries.shape[3]
    kernel = functools.partial(attend_forward_kernel, ctx_size, block_rows, rows_here)
    group = pl.BlockSpec((1, 2, 1, lanes, HD), lambda s, n, _: (s, 0, n, 0, 0))
    stat = pl.BlockSpec((1, 2, 1, 1, lanes), lambda s, n, _: (s, 0, n, 0, 0))
    return pl.pallas_call(
        kernel,
        grid_spec=pltpu.PrefetchScalarGridSpec(
            num_scalar_prefetch=1,
            grid=(SEQS, KVH),
            in_specs=[
                group,
                pl.BlockSpec((all_kv.shape[0], 4 * HD), lambda s, n, _: (0, s * KVH + n)),
            ],
            out_specs=[group, stat],
            scratch_shapes=[
                pltpu.VMEM((2, 1, lanes), jnp.float32),
                pltpu.VMEM((2, 1, lanes), jnp.float32),
                pltpu.VMEM((2, HD, lanes), jnp.float32),
            ],
        ),
        out_shape=(
            jax.ShapeDtypeStruct(queries.shape, jnp.float32),
            jax.ShapeDtypeStruct((SEQS, 2, KVH, 1, lanes), jnp.float32),
        ),
        compiler_params=pltpu.CompilerParams(vmem_limit_bytes=56 * 2**20),
        name="attend_forward",
    )(scalars, queries, all_kv)


def attend_backward_kernel(ctx_size, block_rows, rows_here, scalars, q_ref, go_ref, att_ref, stat_ref, kv_ref, gq_ref, gkv_ref, delta_ref, gq_acc, gk_acc, gv_acc):
    seq = pl.program_id(0)
    blocks = 2 * ctx_size
    own_ctx = scalars[SEQS * blocks]
    own_shard = scalars[SEQS * blocks + 1]
    lanes = q_ref.shape[3]
    gq_acc[...] = jnp.zeros(gq_acc.shape, jnp.float32)
    for half in range(2):
        product = go_ref[0, half, 0].astype(jnp.float32) * att_ref[0, half, 0]
        delta_ref[half] = jnp.sum(product.T, 0, keepdims=True)

    def step(key_ctx, half_key, half):
        order_key = scalars[seq * blocks + half_key * ctx_size + key_ctx]
        order_query = scalars[seq * blocks + half * ctx_size + own_ctx]

        def work(masked):
            rows = pl.ds(pl.multiple_of(key_ctx * block_rows, block_rows), block_rows)
            keys = kv_ref[rows, half_key * 2 * HD : half_key * 2 * HD + HD]
            values = kv_ref[rows, half_key * 2 * HD + HD : half_key * 2 * HD + 2 * HD]
            queries = q_ref[0, half, 0]
            grad_out = go_ref[0, half, 0]
            scores = lax.dot_general(
                keys, queries, CONTRACT_LAST, preferred_element_type=jnp.float32
            )
            probs = jnp.exp(scores - stat_ref[0, half, 0])
            if masked:
                row = lax.broadcasted_iota(jnp.int32, (block_rows, lanes), 0)
                lane = lax.broadcasted_iota(jnp.int32, (block_rows, lanes), 1)
                probs = jnp.where(
                    row <= own_shard * rows_here + lax.rem(lane, rows_here), probs, 0.0
                )
            grad_probs = lax.dot_general(
                values, grad_out, CONTRACT_LAST, preferred_element_type=jnp.float32
            )
            grad_scores = (probs * (grad_probs - delta_ref[half])).astype(jnp.bfloat16)
            gv_acc[...] += jnp.dot(
                probs.astype(jnp.bfloat16), grad_out, preferred_element_type=jnp.float32
            )
            gk_acc[...] += jnp.dot(grad_scores, queries, preferred_element_type=jnp.float32)
            gq_acc[half] += lax.dot_general(
                keys, grad_scores, CONTRACT_FIRST, preferred_element_type=jnp.float32
            )

        @pl.when(order_key < order_query)
        def full():
            work(False)

        @pl.when(order_key == order_query)
        def diagonal():
            work(True)

    @pl.loop(0, ctx_size)
    def sweep(key_ctx):
        rows = pl.ds(pl.multiple_of(key_ctx * block_rows, block_rows), block_rows)
        for half_key in range(2):
            gk_acc[...] = jnp.zeros(gk_acc.shape, jnp.float32)
            gv_acc[...] = jnp.zeros(gv_acc.shape, jnp.float32)
            for half in range(2):
                step(key_ctx, half_key, half)
            at = half_key * 2 * HD
            gkv_ref[rows, at : at + HD] = gk_acc[...].astype(jnp.bfloat16)
            gkv_ref[rows, at + HD : at + 2 * HD] = gv_acc[...].astype(jnp.bfloat16)

    for half in range(2):
        gq_ref[0, half, 0] = gq_acc[half].T


def attend_backward(scalars, queries, grad_out, attended, stats, all_kv, ctx_size, block_rows, rows_here):
    lanes = queries.shape[3]
    kernel = functools.partial(attend_backward_kernel, ctx_size, block_rows, rows_here)
    group = pl.BlockSpec((1, 2, 1, lanes, HD), lambda s, n, _: (s, 0, n, 0, 0))
    stat = pl.BlockSpec((1, 2, 1, 1, lanes), lambda s, n, _: (s, 0, n, 0, 0))
    full = pl.BlockSpec((all_kv.shape[0], 4 * HD), lambda s, n, _: (0, s * KVH + n))
    return pl.pallas_call(
        kernel,
        grid_spec=pltpu.PrefetchScalarGridSpec(
            num_scalar_prefetch=1,
            grid=(SEQS, KVH),
            in_specs=[group, group, group, stat, full],
            out_specs=[group, full],
            scratch_shapes=[
                pltpu.VMEM((2, 1, lanes), jnp.float32),
                pltpu.VMEM((2, HD, lanes), jnp.float32),
                pltpu.VMEM((block_rows, HD), jnp.float32),
                pltpu.VMEM((block_rows, HD), jnp.float32),
            ],
        ),
        out_shape=(
            jax.ShapeDtypeStruct(queries.shape, jnp.float32),
            jax.ShapeDtypeStruct(all_kv.shape, jnp.bfloat16),
        ),
        compiler_params=pltpu.CompilerParams(vmem_limit_bytes=56 * 2**20),
        name="attend_backward",
    )(scalars, queries, grad_out, attended, stats, all_kv)


def column_terms_to_rows(terms):
    ctx_size = lax.axis_size("ctx")
    shard_count = lax.axis_size("fsdp")
    cut = D // (ctx_size * shard_count)
    columns = terms.shape[1]
    stacked = terms.reshape(shard_count, ctx_size, cut, columns).transpose(1, 0, 2, 3)
    summed = lax.psum_scatter(stacked, "ctx", scatter_dimension=0, tiled=True)
    summed = summed.reshape(shard_count * cut, columns)
    rows = lax.all_to_all(summed, "fsdp", 0, 1, tiled=True)
    return lax.all_gather(rows, "ctx", axis=0, tiled=True).astype(jnp.float32)


def shards(
    layer_input,
    block_order,
    first_gain,
    w_qkv,
    b_qkv,
    w_o,
    second_gain,
    w_gate,
    w_up,
    w_down,
    cotangent,
):
    ctx_size = lax.axis_size("ctx")
    shard_count = lax.axis_size("fsdp")
    rows_here = layer_input.shape[0]
    slots = layer_input.shape[1]
    block_rows = rows_here * shard_count
    kv_width = KVH * HD
    first_row = (lax.axis_index("ctx") * shard_count + lax.axis_index("fsdp")) * rows_here
    own_pos = block_positions(block_order, first_row, rows_here, block_rows, ctx_size)
    cosine_table, sine_table = rope_tables(own_pos.reshape(-1))
    query_scale = HD ** (-0.5)
    w_qkv_all, w_o_all, bias_all, gain_one, gain_two = (
        lax.all_gather(w_qkv, "fsdp", axis=0, tiled=True),
        lax.all_gather(w_o, "fsdp", axis=0, tiled=True),
        lax.all_gather(b_qkv, "fsdp", axis=0, tiled=True),
        lax.all_gather(first_gain, "fsdp", axis=0, tiled=True),
        lax.all_gather(second_gain, "fsdp", axis=0, tiled=True),
    )
    gate_cols = lax.all_to_all(w_gate, "fsdp", 1, 0, tiled=True)
    up_cols = lax.all_to_all(w_up, "fsdp", 1, 0, tiled=True)
    cotangent_all = lax.all_gather(cotangent.reshape(-1, D), "fsdp", axis=0, tiled=True)
    gain_one = gain_one.astype(jnp.float32)
    gain_two = gain_two.astype(jnp.float32)
    inputs = layer_input.reshape(-1, D).astype(jnp.float32)
    unit_one, scale_one, normed = normalize(inputs, gain_one)
    normed_one = normed.astype(jnp.bfloat16)
    projected = jnp.dot(
        normed_one, w_qkv_all, preferred_element_type=jnp.float32
    ) + bias_all.astype(jnp.float32)
    query_raw = projected[:, : H * HD].reshape(-1, H, HD)
    key_raw = projected[:, H * HD : H * HD + kv_width].reshape(-1, KVH, HD)
    value_raw = projected[:, H * HD + kv_width :]
    query_tokens = (
        (rotate(query_raw, cosine_table, sine_table) * query_scale)
        .astype(jnp.bfloat16)
        .reshape(-1, H * HD)
    )
    key_tokens = (
        rotate(key_raw, cosine_table, sine_table).astype(jnp.bfloat16).reshape(-1, kv_width)
    )
    own_kv = jnp.stack([key_tokens, value_raw.astype(jnp.bfloat16)], 1)
    own_kv = own_kv.reshape(rows_here, 2, SEQS, 2, KVH, HD).transpose(0, 2, 4, 1, 3, 5)
    own_kv = own_kv.reshape(rows_here, SEQS * KVH * 4 * HD)
    all_kv = lax.all_gather(own_kv, ("ctx", "fsdp"), axis=0, tiled=True)
    queries = to_groups(query_tokens, rows_here)
    scalars = jnp.concatenate(
        [
            block_order.reshape(-1),
            jnp.stack([lax.axis_index("ctx"), lax.axis_index("fsdp")]).astype(jnp.int32),
        ]
    )
    attended_grouped, stats = attend_forward(
        scalars, queries, all_kv, ctx_size, block_rows, rows_here
    )
    attended_low = from_groups(attended_grouped, rows_here).astype(jnp.bfloat16)
    middle = inputs + jnp.dot(attended_low, w_o_all, preferred_element_type=jnp.float32)
    unit_two, scale_two, normed = normalize(middle, gain_two)
    normed_two = normed.astype(jnp.bfloat16)
    tokens_all = lax.all_gather(normed_two, "fsdp", axis=0, tiled=True)
    gate_part = jnp.dot(tokens_all, gate_cols, preferred_element_type=jnp.float32)
    up_part = jnp.dot(tokens_all, up_cols, preferred_element_type=jnp.float32)
    sigmoid_gate = jax.nn.sigmoid(gate_part)
    activated = gate_part * sigmoid_gate
    hidden = (activated * up_part).astype(jnp.bfloat16)
    grad_hidden = lax.dot_general(
        cotangent_all, w_down, CONTRACT_LAST, preferred_element_type=jnp.float32
    )
    grad_gate = (
        grad_hidden * up_part * sigmoid_gate * (1.0 + gate_part * (1.0 - sigmoid_gate))
    ).astype(jnp.bfloat16)
    grad_up = (grad_hidden * activated).astype(jnp.bfloat16)
    grad_tokens = lax.dot_general(
        grad_gate, gate_cols, CONTRACT_LAST, preferred_element_type=jnp.float32
    ) + lax.dot_general(grad_up, up_cols, CONTRACT_LAST, preferred_element_type=jnp.float32)
    grad_normed_two = lax.psum_scatter(
        grad_tokens.astype(jnp.bfloat16), "fsdp", scatter_dimension=0, tiled=True
    ).astype(jnp.float32)
    mixed_terms = jnp.dot(hidden, w_down, preferred_element_type=jnp.float32)
    mixed_out = middle + lax.psum_scatter(
        mixed_terms.astype(jnp.bfloat16), "fsdp", scatter_dimension=0, tiled=True
    ).astype(jnp.float32)
    output = mixed_out.astype(jnp.bfloat16).reshape(rows_here, slots, D)
    down_terms = lax.dot_general(
        hidden, cotangent_all, CONTRACT_FIRST, preferred_element_type=jnp.float32
    ).astype(jnp.bfloat16)
    gate_terms = lax.dot_general(
        tokens_all, grad_gate, CONTRACT_FIRST, preferred_element_type=jnp.float32
    ).astype(jnp.bfloat16)
    up_terms = lax.dot_general(
        tokens_all, grad_up, CONTRACT_FIRST, preferred_element_type=jnp.float32
    ).astype(jnp.bfloat16)
    down_rows = lax.psum(down_terms, "ctx").astype(jnp.float32)
    gate_rows = column_terms_to_rows(gate_terms)
    up_rows = column_terms_to_rows(up_terms)
    grad_middle_norm, grad_gain_two = norm_back(grad_normed_two, unit_two, scale_two, gain_two)
    grad_middle = cotangent.reshape(-1, D).astype(jnp.float32) + grad_middle_norm
    grad_branch_one = grad_middle.astype(jnp.bfloat16)
    grad_attended = lax.dot_general(
        grad_branch_one, w_o_all, CONTRACT_LAST, preferred_element_type=jnp.float32
    ).astype(jnp.bfloat16)
    grad_queries, grad_kv_full = attend_backward(
        scalars,
        queries,
        to_groups(grad_attended, rows_here),
        attended_grouped,
        stats,
        all_kv,
        ctx_size,
        block_rows,
        rows_here,
    )
    grad_kv = lax.psum_scatter(
        grad_kv_full, ("ctx", "fsdp"), scatter_dimension=0, tiled=True
    ).astype(jnp.float32)
    grad_kv_low = narrowed(grad_kv).reshape(rows_here, SEQS, KVH, 2, 2, HD)
    grad_kv_low = grad_kv_low.transpose(0, 3, 1, 4, 2, 5).reshape(-1, 2 * kv_width)
    grad_query_tokens = from_groups(narrowed(grad_queries), rows_here) * query_scale
    grad_query_raw = rotate_back(
        grad_query_tokens.reshape(-1, H, HD), cosine_table, sine_table
    ).reshape(-1, H * HD)
    grad_key_raw = rotate_back(
        grad_kv_low[:, :kv_width].reshape(-1, KVH, HD), cosine_table, sine_table
    ).reshape(-1, kv_width)
    grad_projected = jnp.concatenate(
        [grad_query_raw, grad_key_raw, grad_kv_low[:, kv_width:]], -1
    ).astype(jnp.bfloat16)
    grad_bias = jnp.sum(grad_projected, 0, dtype=jnp.float32)
    grad_bias_qk = grad_bias[:QK]
    grad_bias_value = grad_bias[QK:]
    grad_normed_one = lax.dot_general(
        grad_projected, w_qkv_all, CONTRACT_LAST, preferred_element_type=jnp.float32
    )
    grad_input_norm, grad_gain_one = norm_back(grad_normed_one, unit_one, scale_one, gain_one)
    grad_input = (grad_middle + grad_input_norm).reshape(rows_here, slots, D)
    qkv_rows = lax.psum_scatter(
        lax.dot_general(
            normed_one, grad_projected, CONTRACT_FIRST, preferred_element_type=jnp.float32
        ).astype(jnp.bfloat16),
        "fsdp",
        scatter_dimension=0,
        tiled=True,
    )
    o_rows = lax.psum_scatter(
        lax.dot_general(
            attended_low, grad_branch_one, CONTRACT_FIRST, preferred_element_type=jnp.float32
        ).astype(jnp.bfloat16),
        "fsdp",
        scatter_dimension=0,
        tiled=True,
    )
    qkv_rows = lax.psum(qkv_rows, "ctx").astype(jnp.float32)
    o_rows = lax.psum(o_rows, "ctx").astype(jnp.float32)
    gain_one_rows, gain_two_rows, bias_rows, value_bias_rows = (
        lax.psum_scatter(grad_gain_one, "fsdp", scatter_dimension=0, tiled=True),
        lax.psum_scatter(grad_gain_two, "fsdp", scatter_dimension=0, tiled=True),
        lax.psum_scatter(grad_bias_qk, "fsdp", scatter_dimension=0, tiled=True),
        lax.psum_scatter(grad_bias_value, "fsdp", scatter_dimension=0, tiled=True),
    )
    gain_one_rows, gain_two_rows, bias_rows, value_bias_rows = (
        lax.psum(gain_one_rows, "ctx"),
        lax.psum(gain_two_rows, "ctx"),
        lax.psum(bias_rows, "ctx"),
        lax.psum(value_bias_rows, "ctx"),
    )
    return (
        output,
        grad_input,
        gain_one_rows,
        qkv_rows,
        bias_rows,
        value_bias_rows,
        o_rows,
        gain_two_rows,
        gate_rows,
        up_rows,
        down_rows,
    )


def solution(mesh):
    in_specs = (
        P(("ctx", "fsdp"), None, None),
        P(),
        P("fsdp"),
        P("fsdp", None),
        P("fsdp"),
        P("fsdp", None),
        P("fsdp"),
        P("fsdp", None),
        P("fsdp", None),
        P("fsdp", None),
        P(("ctx", "fsdp"), None, None),
    )
    out_specs = (
        P(("ctx", "fsdp"), None, None),
        P(("ctx", "fsdp"), None, None),
        P("fsdp"),
        P("fsdp", None),
        P("fsdp"),
        P("fsdp"),
        P("fsdp", None),
        P("fsdp"),
        P("fsdp", None),
        P("fsdp", None),
        P("fsdp", None),
    )
    return jax.shard_map(shards, mesh=mesh, in_specs=in_specs, out_specs=out_specs, check_vma=False)
```

time: 2340 us -> 1280 us (0.55)
  waiting for transfers between devices: 1540 us -> 825 us
  matrix products: 274 us -> 114 us
  blocking collectives: 242 us -> 118 us
  other arithmetic: 118 us -> 42 us
  Pallas kernels: 0 us -> 35.1 us
    all_gather x5, waiting for transfers between devices: 714 us -> 38.6 us  [the longest x1 38.6 us: shards(): all_kv = lax.all_gather(own_kv, ('ctx', 'fsdp'), axis=0, tiled=True)]
    reduce_scatter x2 -> x5, waiting for transfers between devices: 630 us -> 308 us  [the longest x1 146 us: shards(): lax.psum_scatter(grad_kv_full, ('ctx', 'fsdp'), scatter_dimension=0, tile...]
    all_to_all x0 -> x2, waiting for transfers between devices: none -> 186 us  [the longest x1 99.1 us: shards(): up_cols = lax.all_to_all(w_up, 'fsdp', 1, 0, tiled=True)]
    unnamed x3 -> x2, blocking collectives: 218 us -> 45.9 us
    dot_general x43 -> x9, matrix products: 248 us -> 88 us  [the longest x1 11.6 us: shards(): lax.dot_general(cotangent_all, w_down, CONTRACT_LAST, preferred_element_t...]
    psum x1, waiting for transfers between devices: 161 us -> 231 us  [shards(): qkv_rows = lax.psum(qkv_rows, 'ctx').astype(jnp.float32)]
    all_to_all x0 -> x2, blocking collectives: none -> 53.1 us  [column_terms_to_rows(): rows = lax.all_to_all(summed, 'fsdp', 0, 1, tiled=True)]
    concatenate x2, other arithmetic: 44.9 us -> 1.69 us  [the longest x1 1.11 us: rotate(): jnp.concatenate([-head_values[..., half_width:], head_values[..., :half_w...]
  transfers between devices with their start and end apart: 10 -> 15, of which waited for: 8 -> 11; matrix products, arithmetic and copies ran while one was open for 20% -> 13% of each run, Pallas kernels for 0% -> 1%
where the time goes in v1:
time: 1280 us; the launch traced here: 1270 us
  waiting for transfers between devices  825 us (64%)
  blocking collectives  118 us (9%)
  matrix products  114 us (9%)
  local copies, waits for them, and re-layouts  108 us (8%)
  other arithmetic  42 us (3%)
  Pallas kernels  35.1 us (3%)
  between operations  17.2 us (1%)
    psum x1, waiting for transfers between devices, shards(): qkv_rows = lax.psum(qkv_rows, 'ctx').astype(jnp.float32)  231 us
    reduce_scatter x1, waiting for transfers between devices, shards(): lax.psum_scatter(grad_kv_full, ('ctx', 'fsdp'), scatter_dimension=0, tile...  146 us
    all_to_all x1, waiting for transfers between devices, shards(): up_cols = lax.all_to_all(w_up, 'fsdp', 1, 0, tiled=True)  99.1 us
    all_to_all x1, waiting for transfers between devices, shards(): gate_cols = lax.all_to_all(w_gate, 'fsdp', 1, 0, tiled=True)  87.3 us
    reduce_scatter x1, waiting for transfers between devices, shards(): lax.psum_scatter(lax.dot_general(normed_one, grad_projected, CONTRACT_FIR...  71 us
    all_to_all x2, blocking collectives, column_terms_to_rows(): rows = lax.all_to_all(summed, 'fsdp', 0, 1, tiled=True)  53.1 us
    reduce_scatter x1, waiting for transfers between devices, shards(): lax.psum_scatter(mixed_terms.astype(jnp.bfloat16), 'fsdp', scatter_dimens...  47.1 us
    unnamed x2, blocking collectives  45.9 us
  transfers between devices with their start and end apart: 15, of which 11 were waited for; matrix products, arithmetic and copies ran while one was open for 13% of the time, Pallas kernels for 1%

profile of v1, /device:TPU:0, one launch (start us, length us, event | category | flops | bytes accessed | tf_op | source)
XLA Modules:
  0.0 1271.4 jit_solution(656694817850277560)
XLA Ops:
  11.8 19.2 %all-reduce.10 = (bf16[1536]{0:T(1024)(128)(2,1)S(1)}, bf16[1536]{0:T(1024)(128)(2,1)S(1)}) all-reduce(bf16[1536]{0:T(1024)(128)(2,1)S(1)} %dynamic-update-slice, bf16[1536]{0:T(1024)(128)(2,1)S(1)} %dynamic-update-slice.1), channel_id=1, replica_groups=mesh['ctx'=4,'fsdp'=8] {'fsdp'}, use_global_device_ids=true, to_apply=%add | all-reduce | flops 3072 | bytes 12288
  47.5 29.9 %all-gather.9.cloned.1.call-done = bf16[1536,2048]{1,0:T(8,128)(2,1)} async-done(((bf16[192,2048]{1,0:T(8,128)(2,1)}), bf16[1536,2048]{1,0:T(8,128)(2,1)}) %all-gather.9.cloned.1.call-update) | async-done | bytes 6291472 | tf_op jit(solution)/shard_map/all_gather | solution.py:310
  124.0 38.6 %all-gather.11.cloned.1.call-done.kv_ref = bf16[1280,2048]{1,0:T(8,128)(2,1)} async-done(((bf16[40,2048]{1,0:T(8,128)(2,1)}), bf16[1280,2048]{1,0:T(8,128)(2,1)}) %all-gather.11.cloned.1.call-update) | async-done | bytes 5242896 | tf_op jit(solution)/shard_map/all_gather | solution.py:341
  162.6 16.8 %attend_forward.1 = (f32[2,2,2,240,128]{4,3,2,1,0:T(8,128)}, f32[2,2,2,1,240]{4,3,2,1,0:T(1,128)}) custom-call(s32[18]{0:T(128)} %pad_add_fusion.scalars, bf16[2,2,2,240,128]{4,3,2,1,0:T(8,128)(2,1)} %bitcast.112, bf16[1280,2048]{1,0:T(8,128)(2,1)} %all-gather.11.cloned.1.call-done.kv_ref), custom_call_target="tpu_custom_call" | custom-call | tf_op jit(solution)/shard_map/attend_forward/pallas_call | solution.py:153
  184.1 30.0 %all-gather.13.cloned.1.call-done = bf16[1536,1536]{1,0:T(8,128)(2,1)} async-done(((bf16[192,1536]{1,0:T(8,128)(2,1)}), bf16[1536,1536]{1,0:T(8,128)(2,1)}) %all-gather.13.cloned.1.call-update) | async-done | bytes 4718608 | tf_op jit(solution)/shard_map/all_gather | solution.py:311
  250.7 87.3 %all-to-all-done = bf16[192,8,1120]{2,0,1:T(8,128)(2,1)} async-done(((bf16[192,8,1120]{2,0,1:T(8,128)(2,1)}), bf16[192,8,1120]{2,0,1:T(8,128)(2,1)}, u32[]{:S(2)}, u32[]{:S(2)}) %all-to-all-start) | async-done | bytes 3440672 | tf_op jit(solution)/shard_map/all_to_all | solution.py:316
  345.0 10.4 fusion.27
  355.4 99.1 %all-to-all-done.1 = bf16[192,8,1120]{2,0,1:T(8,128)(2,1)} async-done(((bf16[192,8,1120]{2,0,1:T(8,128)(2,1)}), bf16[192,8,1120]{2,0,1:T(8,128)(2,1)}, u32[]{:S(2)}, u32[]{:S(2)}) %all-to-all-start.1) | async-done | bytes 3440672 | tf_op jit(solution)/shard_map/all_to_all | solution.py:317
  454.5 10.4 fusion.28
  464.9 11.6 multiply_convert_fusion
  476.5 9.4 fusion.29
  503.9 37.4 %reduce-scatter.14.cloned.1.call-done = bf16[160,1536]{1,0:T(8,128)(2,1)} async-done(((bf16[1280,1536]{1,0:T(8,128)(2,1)}), bf16[160,1536]{1,0:T(8,128)(2,1)}) %reduce-scatter.14.cloned.1.call-update) | async-done | bytes 491536 | tf_op jit(solution)/shard_map/reduce_scatter | solution.py:372
  542.7 47.1 %reduce-scatter.12.cloned.1.call-done = bf16[160,1536]{1,0:T(8,128)(2,1)} async-done(((bf16[1280,1536]{1,0:T(8,128)(2,1)}), bf16[160,1536]{1,0:T(8,128)(2,1)}) %reduce-scatter.12.cloned.1.call-update) | async-done | bytes 491536 | tf_op jit(solution)/shard_map/reduce_scatter | solution.py:376
  597.8 18.3 %attend_backward.1 = (f32[2,2,2,240,128]{4,3,2,1,0:T(8,128)}, bf16[1280,2048]{1,0:T(8,128)(2,1)}) custom-call(s32[18]{0:T(128)} %pad_add_fusion.scalars, bf16[2,2,2,240,128]{4,3,2,1,0:T(8,128)(2,1)} %bitcast.113, bf16[2,2,2,240,128]{4,3,2,1,0:T(8,128)(2,1)} %bitcast.123, f32[2,2,2,240,128]{4,3,2,1,0:T(8,128)} %get-tuple-element.15.att_ref, ...), custom_call_target="tpu_custom_call" | custom-call | tf_op jit(solution)/shard_map/attend_backward/pallas_call | solution.py:251
  627.7 145.8 %reduce-scatter.16.cloned.1.call-done = bf16[40,2048]{1,0:T(8,128)(2,1)} async-done(((bf16[1280,2048]{1,0:T(8,128)(2,1)}), bf16[40,2048]{1,0:T(8,128)(2,1)}) %reduce-scatter.16.cloned.1.call-update) | async-done | bytes 163856 | tf_op jit(solution)/shard_map/reduce_scatter | solution.py:409
  781.6 9.4 convolution_convert_fusion.2
  796.6 9.6 convolution_convert_fusion.1
  811.9 9.5 convolution_convert_fusion.3
  828.4 71.0 %reduce-scatter.18.cloned.1.call-done = bf16[192,2048]{1,0:T(8,128)(2,1)} async-done(((bf16[1536,2048]{1,0:T(8,128)(2,1)}), bf16[192,2048]{1,0:T(8,128)(2,1)}) %reduce-scatter.18.cloned.1.call-update) | async-done | bytes 786448 | tf_op jit(solution)/shard_map/reduce_scatter | solution.py:432
  900.6 230.5 %all-reduce.14.cloned.1.call-done = (bf16[192,2048]{1,0:T(8,128)(2,1)}, bf16[192,1536]{1,0:T(8,128)(2,1)}, bf16[4,8,48,1120]{3,2,0,1:T(8,128)(2,1)}, bf16[4,8,48,1120]{3,2,0,1:T(8,128)(2,1)}, bf16[1120,1536]{1,0:T(8,128)(2,1)}) async-done(((bf16[192,2048]{1,0:T(8,128)(2,1)}, bf16[192,1536]{1,0:T(8,128)(2,1)}, bf16[4,8,48,1120]{3,2,0,1:T(8,128)(2,1)}, bf16[4,8,48,1120]{3,2,0,1:T(8,128)(2,1)}, ...) | async-done | bytes 11698192 | tf_op jit(solution)/shard_map/psum | solution.py:448
  1133.0 27.5 %all_to_all.76 = bf16[8,48,1120]{2,1,0:T(8,128)(2,1)S(1)} all-to-all(bf16[8,48,1120]{2,1,0:T(8,128)(2,1)S(1)} %dynamic-slice_bitcast_fusion.1), channel_id=1, replica_groups=mesh['ctx'=4,'fsdp'=8] {'fsdp'}, dimensions={0} | all-to-all | bytes 1720320 | tf_op jit(solution)/shard_map/all_to_all | solution.py:282
  1166.1 25.6 %all_to_all.77 = bf16[8,48,1120]{2,1,0:T(8,128)(2,1)S(1)} all-to-all(bf16[8,48,1120]{2,1,0:T(8,128)(2,1)S(1)} %dynamic-slice_bitcast_fusion), channel_id=1, replica_groups=mesh['ctx'=4,'fsdp'=8] {'fsdp'}, dimensions={0} | all-to-all | bytes 1720320 | tf_op jit(solution)/shard_map/all_to_all | solution.py:282
  1205.4 26.7 %all-reduce.8 = (f32[1536]{0:T(1024)S(1)}, f32[1792]{0:T(1024)S(1)}, f32[256]{0:T(256)S(1)}, f32[1536]{0:T(1024)S(1)}) all-reduce(f32[1536]{0:T(1024)S(1)} %get-tuple-element.19, f32[1792]{0:T(1024)S(1)} %bitcast.129, f32[256]{0:T(256)S(1)} %slice.80, f32[1536]{0:T(1024)S(1)} %get-tuple-element.21), channel_id=5, replica_groups=mesh['ctx'=4,'fsdp'=8] {'fsdp'}, use_global_device_ids=true, to_apply=%region_9.10.clone | all-reduce | flops 5120 | bytes 40960
  1235.1 10.3 all-reduce.9
  (201 shorter events, 223.0 us)
Async XLA Ops:
  7.2 457.7 %copy-start = (bf16[1120,1536]{1,0:T(8,128)(2,1)S(1)}, bf16[1120,1536]{1,0:T(8,128)(2,1)}, u32[]{:S(2)}) copy-start(bf16[1120,1536]{1,0:T(8,128)(2,1)} %param.20) | copy-start | bytes 10321924
  7.2 70.2 %all-gather.9.cloned.1.call-start = ((), (), s32[]{:S(2)}) async-start(), calls=%async_computation.9 | async-start | bytes 7077888 | tf_op jit(solution)/shard_map/all_gather | solution.py:310
  7.9 154.7 %all-gather.11.cloned.1.call-start = ((), (), s32[]{:S(2)}) async-start(), calls=%async_computation.10 | async-start | bytes 5406720 | tf_op jit(solution)/shard_map/all_gather | solution.py:341
  45.2 36.5 %copy-start.15 = (f32[64]{0:T(128)}, f32[64]{0:T(128)S(1)}, u32[]{:S(2)}) copy-start(f32[64]{0:T(128)S(1)} %multiply_power_fusion) | copy-start | bytes 772
  82.8 16.7 %copy-start.17 = (s32[2,8]{1,0:T(2,128)S(1)}, s32[2,8]{1,0:T(2,128)}, u32[]{:S(2)}) copy-start(s32[2,8]{1,0:T(2,128)} %param.12) | copy-start | bytes 196
  98.4 115.7 %all-gather.13.cloned.1.call-start = ((), (), s32[]{:S(2)}) async-start(), calls=%async_computation.11 | async-start | bytes 5308416 | tf_op jit(solution)/shard_map/all_gather | solution.py:311
  99.2 245.9 %all-gather.15.cloned.1.call-start = ((), (), s32[]{:S(2)}) async-start(), calls=%async_computation.12 | async-start | bytes 4423680 | tf_op jit(solution)/shard_map/all_gather | solution.py:356
  233.0 105.0 %all-to-all-start = ((bf16[192,8,1120]{2,0,1:T(8,128)(2,1)}), bf16[192,8,1120]{2,0,1:T(8,128)(2,1)}, u32[]{:S(2)}, u32[]{:S(2)}) async-start(bf16[192,8,1120]{2,0,1:T(8,128)(2,1)} %copy.137), calls=%async_computation | async-start | bytes 7077888 | tf_op jit(solution)/shard_map/all_to_all | solution.py:316
  337.9 116.6 %all-to-all-start.1 = ((bf16[192,8,1120]{2,0,1:T(8,128)(2,1)}), bf16[192,8,1120]{2,0,1:T(8,128)(2,1)}, u32[]{:S(2)}, u32[]{:S(2)}) async-start(bf16[192,8,1120]{2,0,1:T(8,128)(2,1)} %copy.138), calls=%async_computation.1 | async-start | bytes 7077888 | tf_op jit(solution)/shard_map/all_to_all | solution.py:317
  343.0 121.9 %all-gather.17.cloned.1.call-start = ((), (), s32[]{:S(2)}) async-start(), calls=%async_computation.14 | async-start | bytes 4423680 | tf_op jit(solution)/shard_map/all_gather | solution.py:318
  345.0 196.3 %reduce-scatter.14.cloned.1.call-start = ((), (), s32[]{:S(2)}) async-start(), calls=%async_computation.15 | async-start | bytes 4423680 | tf_op jit(solution)/shard_map/reduce_scatter | solution.py:372
  476.5 9.4 copy-start.19
  494.8 95.0 %reduce-scatter.12.cloned.1.call-start = ((), (), s32[]{:S(2)}) async-start(), calls=%async_computation.13 | async-start | bytes 4423680 | tf_op jit(solution)/shard_map/reduce_scatter | solution.py:376
  503.8 37.5 %copy-start.4 = (f32[160,1536]{1,0:T(8,128)S(1)}, f32[160,1536]{1,0:T(8,128)}, u32[]{:S(2)}) copy-start(f32[160,1536]{1,0:T(8,128)} %copy-done.3) | copy-start | bytes 2949124
  503.8 86.0 %copy-start.9 = (bf16[160,1536]{1,0:T(8,128)(2,1)S(1)}, bf16[160,1536]{1,0:T(8,128)(2,1)}, u32[]{:S(2)}) copy-start(bf16[160,1536]{1,0:T(8,128)(2,1)} %reshape.384) | copy-start | bytes 1474564
  503.8 269.6 %reduce-scatter.16.cloned.1.call-start = ((), (), s32[]{:S(2)}) async-start(), calls=%async_computation.16 | async-start | bytes 5406720 | tf_op jit(solution)/shard_map/reduce_scatter | solution.py:409
  616.2 212.2 %reduce-scatter.20.cloned.1.call-start = ((), (), s32[]{:S(2)}) async-start(), calls=%async_computation.18 | async-start | bytes 5308416 | tf_op jit(solution)/shard_map/reduce_scatter | solution.py:440
  620.8 278.6 %reduce-scatter.18.cloned.1.call-start = ((), (), s32[]{:S(2)}) async-start(), calls=%async_computation.17 | async-start | bytes 7077888 | tf_op jit(solution)/shard_map/reduce_scatter | solution.py:432
  626.2 150.2 %copy-start.2 = (f32[160,1536]{1,0:T(8,128)S(1)}, f32[160,1536]{1,0:T(8,128)}, u32[]{:S(2)}) copy-start(f32[160,1536]{1,0:T(8,128)} %reshape.395) | copy-start | bytes 2949124
  627.7 148.8 %copy-start.8 = (bf16[160,1536]{1,0:T(8,128)(2,1)S(1)}, bf16[160,1536]{1,0:T(8,128)(2,1)}, u32[]{:S(2)}) copy-start(bf16[160,1536]{1,0:T(8,128)(2,1)} %fusion.12) | copy-start | bytes 1474564
  781.1 350.1 %all-reduce.14.cloned.1.call-start = ((), (), s32[]{:S(2)}) async-start(), calls=%async_computation.21 | async-start | bytes 23789568 | tf_op jit(solution)/shard_map/psum | solution.py:448
  899.4 354.5 %all-gather.19.cloned.1.call-start = ((), (), s32[]{:S(2)}) async-start(), calls=%async_computation.19 | async-start | bytes 4300800 | tf_op jit(solution)/shard_map/all_gather | solution.py:283
  1164.2 95.2 %all-gather.21.cloned.1.call-start = ((), (), s32[]{:S(2)}) async-start(), calls=%async_computation.20 | async-start | bytes 4300800 | tf_op jit(solution)/shard_map/all_gather | solution.py:283
  1253.9 10.8 copy-start.1
  (12 other events, 38.2 us)
Sparse Core Ops, SparseCore 0:
  9.6 67.6 all-gather.8
  98.6 63.9 all-gather.10
  164.2 49.8 all-gather.12
  220.0 63.6 all-gather.14
  345.1 94.9 all-gather.16
  494.9 46.2 reduce-scatter.13
  544.2 45.5 reduce-scatter.11
  616.3 157.1 reduce-scatter.15
  776.4 52.0 reduce-scatter.19
  831.1 68.1 reduce-scatter.17
  904.3 226.8 all-reduce.13
  1164.3 44.5 all-gather.18
  1210.8 46.4 all-gather.20

commit v2 on v1

--- a/solution.py
+++ b/solution.py
@@ -20,6 +20,7 @@
 EPS = 1e-06
 THETA = 1000000.0
 NEG_FILL = -1e30
+MESH_ID = pl.DeviceIdType.MESH
 CONTRACT_LAST = (((1,), (1,)), ((), ()))
 CONTRACT_FIRST = (((0,), (0,)), ((), ()))
 
@@ -271,17 +272,353 @@
     )(scalars, queries, grad_out, attended, stats, all_kv)
 
 
-def column_terms_to_rows(terms):
-    ctx_size = lax.axis_size("ctx")
-    shard_count = lax.axis_size("fsdp")
-    cut = D // (ctx_size * shard_count)
-    columns = terms.shape[1]
-    stacked = terms.reshape(shard_count, ctx_size, cut, columns).transpose(1, 0, 2, 3)
-    summed = lax.psum_scatter(stacked, "ctx", scatter_dimension=0, tiled=True)
-    summed = summed.reshape(shard_count * cut, columns)
-    rows = lax.all_to_all(summed, "fsdp", 0, 1, tiled=True)
-    return lax.all_gather(rows, "ctx", axis=0, tiled=True).astype(jnp.float32)
-
+def peers_of(ctx_size):
+    return ctx_size == 4, range(1, ctx_size)
+
+
+def ctx_target(position, way, square, ctx_size):
+    return position ^ way if square else lax.rem(position + way, ctx_size)
+
+
+def ctx_source(position, way, square, ctx_size):
+    return position ^ way if square else lax.rem(position + ctx_size - way, ctx_size)
+
+
+def greet(ctx_size, pair_count, with_ctx):
+    ctx = lax.axis_index("ctx")
+    shard = lax.axis_index("fsdp")
+    pair, core = shard // 2, shard % 2
+    barrier = pltpu.get_barrier_semaphore()
+    count = 0
+    for step in range(1, pair_count):
+        there = lax.rem(pair + step, pair_count) * 2 + core
+        pl.semaphore_signal(barrier, inc=1, device_id=(ctx, there), device_id_type=MESH_ID)
+        count += 1
+    if with_ctx:
+        for way in range(1, ctx_size):
+            there = lax.rem(ctx + way, ctx_size)
+            pl.semaphore_signal(barrier, inc=1, device_id=(there, shard), device_id_type=MESH_ID)
+            count += 1
+    pl.semaphore_signal(barrier, inc=1, device_id=(ctx, pair * 2 + 1 - core), device_id_type=MESH_ID)
+    pl.semaphore_wait(barrier, count + 1)
+    return ctx, pair, core
+
+
+def gather_kernel(arity, ctx_size, pair_count, slot, *refs):
+    sources, outs = refs[:arity], refs[arity : 2 * arity]
+    pair_send, pair_recv, ctx_send, ctx_recv, core_send, core_recv, local_sem = refs[2 * arity :]
+    square, ways = peers_of(ctx_size)
+    ctx, pair, core = greet(ctx_size, pair_count, True)
+    started = []
+
+    def send(item, source, place, target, sems, at):
+        copy = pltpu.make_async_remote_copy(
+            src_ref=source,
+            dst_ref=outs[item].at[place],
+            send_sem=sems[0].at[at],
+            recv_sem=sems[1].at[at],
+            device_id=target,
+            device_id_type=MESH_ID,
+        )
+        copy.start()
+        started.append(copy)
+
+    def arrive(item, place, sems, at):
+        pltpu.make_async_remote_copy(
+            src_ref=outs[item].at[place],
+            dst_ref=outs[item].at[place],
+            send_sem=sems[0].at[at],
+            recv_sem=sems[1].at[at],
+            device_id=(ctx, pair * 2 + core),
+            device_id_type=MESH_ID,
+        ).wait_recv()
+
+    pair_sems, ctx_sems, core_sems = (pair_send, pair_recv), (ctx_send, ctx_recv), (core_send, core_recv)
+    home = slot(ctx, pair * 2 + core)
+    locals_ = []
+    for item in range(arity):
+        copy = pltpu.make_async_copy(sources[item], outs[item].at[home], local_sem.at[item])
+        copy.start()
+        locals_.append(copy)
+
+    def origin(step):
+        return lax.rem(pair + pair_count - step, pair_count)
+
+    def to_core(item, source, from_ctx, way, step):
+        send(
+            item,
+            source,
+            slot(from_ctx, origin(step) * 2 + core),
+            (ctx, pair * 2 + 1 - core),
+            core_sems,
+            (way, step, item),
+        )
+
+    def spread(step):
+        for item in range(arity):
+            place = slot(ctx, origin(step) * 2 + core)
+            if step == 0:
+                source = sources[item]
+            else:
+                arrive(item, place, pair_sems, (step - 1, item))
+                source = outs[item].at[place]
+            for way in ways:
+                if square and way == 3:
+                    continue
+                there = ctx_target(ctx, way, square, ctx_size)
+                send(item, source, place, (there, pair * 2 + core), ctx_sems, (way - 1, step, item))
+            to_core(item, source, ctx, 0, step)
+
+    def collect(step):
+        for way in ways:
+            if square and way == 3:
+                continue
+            for item in range(arity):
+                come = ctx_source(ctx, way, square, ctx_size)
+                place = slot(come, origin(step) * 2 + core)
+                arrive(item, place, ctx_sems, (way - 1, step, item))
+                source = outs[item].at[place]
+                if square and (step % 2 == 0) == (way == 1):
+                    send(
+                        item,
+                        source,
+                        place,
+                        (ctx ^ (3 - way), pair * 2 + core),
+                        ctx_sems,
+                        (2, step, item),
+                    )
+                to_core(item, source, come, way, step)
+
+    def collect_far(step):
+        for item in range(arity):
+            place = slot(ctx ^ 3, origin(step) * 2 + core)
+            arrive(item, place, ctx_sems, (2, step, item))
+            to_core(item, outs[item].at[place], ctx ^ 3, 3, step)
+
+    for item in range(arity):
+        for step in range(1, pair_count):
+            there = lax.rem(pair + step, pair_count) * 2 + core
+            send(item, sources[item], home, (ctx, there), pair_sems, (step - 1, item))
+    for step in range(pair_count + 2):
+        if step < pair_count:
+            spread(step)
+        if 1 <= step <= pair_count:
+            collect(step - 1)
+        if square and step >= 2:
+            collect_far(step - 2)
+    for step in range(pair_count):
+        for way in range(ctx_size):
+            come = ctx_source(ctx, way, square, ctx_size) if way else ctx
+            for item in range(arity):
+                arrive(item, slot(come, origin(step) * 2 + 1 - core), core_sems, (way, step, item))
+    for copy in locals_:
+        copy.wait()
+    for copy in started:
+        copy.wait_send()
+
+
+def gather(pieces, slot, collective_id, name):
+    ctx_size, shard_count = lax.axis_size("ctx"), lax.axis_size("fsdp")
+    pair_count = shard_count // 2
+    arity = len(pieces)
+    dma = pltpu.SemaphoreType.DMA
+    moved = sum(piece.size for piece in pieces) * 2
+    return pl.pallas_call(
+        functools.partial(gather_kernel, arity, ctx_size, pair_count, slot),
+        in_specs=[pl.BlockSpec(memory_space=pltpu.VMEM)] * arity,
+        out_specs=[pl.BlockSpec(memory_space=pl.ANY)] * arity,
+        out_shape=[
+            jax.ShapeDtypeStruct((ctx_size * shard_count,) + piece.shape, piece.dtype) for piece in pieces
+        ],
+        scratch_shapes=[dma((pair_count - 1, arity))] * 2
+        + [dma((ctx_size - 1, pair_count, arity))] * 2
+        + [dma((ctx_size, pair_count, arity))] * 2
+        + [dma((arity,))],
+        compiler_params=pltpu.CompilerParams(collective_id=collective_id, has_side_effects=True),
+        cost_estimate=pl.CostEstimate(
+            flops=0, bytes_accessed=moved * ctx_size * shard_count * 4, transcendentals=0
+        ),
+        name=name,
+    )(*pieces)
+
+
+def scatter_kernel(arity, ctx_size, pair_count, slot, spread_ctx, *refs):
+    sources, outs, refs = refs[:arity], refs[arity : 2 * arity], refs[2 * arity :]
+    halves, relays, asides, ends, finals = (refs[i * arity : (i + 1) * arity] for i in range(5))
+    sems = refs[5 * arity :]
+    core_sems, relay_sems, ctx_sems, pair_sems, last_sems = (sems[2 * i : 2 * i + 2] for i in range(5))
+    square, ways = peers_of(ctx_size)
+    ctx, pair, core = greet(ctx_size, pair_count, True)
+    order = list(range(1, pair_count)) + [0]
+    started = []
+
+    def send(source, target, device, pair_of_sems, at):
+        copy = pltpu.make_async_remote_copy(
+            src_ref=source,
+            dst_ref=target,
+            send_sem=pair_of_sems[0].at[at],
+            recv_sem=pair_of_sems[1].at[at],
+            device_id=device,
+            device_id_type=MESH_ID,
+        )
+        copy.start()
+        started.append(copy)
+
+    def arrive(target, pair_of_sems, at):
+        pltpu.make_async_remote_copy(
+            src_ref=target,
+            dst_ref=target,
+            send_sem=pair_of_sems[0].at[at],
+            recv_sem=pair_of_sems[1].at[at],
+            device_id=(ctx, pair * 2 + core),
+            device_id_type=MESH_ID,
+        ).wait_recv()
+
+    def toward(step):
+        return lax.rem(pair + step, pair_count)
+
+    def target_ctx(way):
+        return ctx_target(ctx, way, square, ctx_size) if way else ctx
+
+    def f32(value):
+        return value.astype(jnp.float32)
+
+    far_first = [3, 1, 2, 0] if square else list(ways) + [0]
+    for step in order:
+        for way in far_first:
+            for item in range(arity):
+                send(
+                    sources[item].at[slot(target_ctx(way), toward(step) * 2 + 1 - core)],
+                    halves[item].at[way, step],
+                    (ctx, pair * 2 + 1 - core),
+                    core_sems,
+                    (way, step, item),
+                )
+
+    def fold_core(step):
+        for way in far_first:
+            for item in range(arity):
+                half = halves[item].at[way, step]
+                arrive(half, core_sems, (way, step, item))
+                mine = sources[item][slot(target_ctx(way), toward(step) * 2 + core)]
+                half[...] = (f32(mine) + f32(half[...])).astype(half.dtype)
+                if square and way == 3:
+                    there = ctx ^ (1 if step % 2 == 0 else 2)
+                    send(
+                        half,
+                        relays[item].at[step],
+                        (there, pair * 2 + core),
+                        relay_sems,
+                        (step, item),
+                    )
+
+    def fold_relay(step):
+        for item in range(arity):
+            if square:
+                relay = relays[item].at[step]
+                arrive(relay, relay_sems, (step, item))
+                half = halves[item].at[2 if step % 2 == 0 else 1, step]
+                half[...] = (f32(half[...]) + f32(relay[...])).astype(half.dtype)
+            for way in ways:
+                if square and way == 3:
+                    continue
+                send(
+                    halves[item].at[way, step],
+                    asides[item].at[way - 1, step],
+                    (target_ctx(way), pair * 2 + core),
+                    ctx_sems,
+                    (way - 1, step, item),
+                )
+
+    def fold_ctx(step):
+        for item in range(arity):
+            half = halves[item].at[0, step]
+            total = f32(half[...])
+            for way in ways:
+                if square and way == 3:
+                    continue
+                aside = asides[item].at[way - 1, step]
+                arrive(aside, ctx_sems, (way - 1, step, item))
+                total = total + f32(aside[...])
+            if step:
+                half[...] = total.astype(half.dtype)
+                send(
+                    half,
+                    ends[item].at[step - 1],
+                    (ctx, toward(step) * 2 + core),
+                    pair_sems,
+                    (step - 1, item),
+                )
+            else:
+                for other in range(1, pair_count):
+                    end = ends[item].at[other - 1]
+                    arrive(end, pair_sems, (other - 1, item))
+                    total = total + f32(end[...])
+                if spread_ctx:
+                    finals[item][...] = total.astype(finals[item].dtype)
+                else:
+                    outs[item][...] = total.astype(outs[item].dtype)
+
+    for turn in range(pair_count + 2):
+        if turn < pair_count:
+            fold_core(order[turn])
+        if 1 <= turn <= pair_count:
+            fold_relay(order[turn - 1])
+        if turn >= 2:
+            fold_ctx(order[turn - 2])
+    if spread_ctx:
+        for item in range(arity):
+            for way in ways:
+                send(
+                    finals[item],
+                    outs[item].at[ctx],
+                    (target_ctx(way), pair * 2 + core),
+                    last_sems,
+                    (way - 1, item),
+                )
+            outs[item][ctx] = finals[item][...]
+        for item in range(arity):
+            for way in ways:
+                arrive(outs[item].at[ctx_source(ctx, way, square, ctx_size)], last_sems, (way - 1, item))
+    for copy in started:
+        copy.wait_send()
+
+
+def scatter(terms, slot, collective_id, name, spread_ctx=False, out_dtype=None):
+    ctx_size, shard_count = lax.axis_size("ctx"), lax.axis_size("fsdp")
+    pair_count = shard_count // 2
+    arity = len(terms)
+    dma = pltpu.SemaphoreType.DMA
+    lead = (ctx_size,) if spread_ctx else ()
+    asides = 2 if ctx_size == 4 else ctx_size - 1
+
+    def room(*extent):
+        return [pltpu.VMEM(extent + term.shape[1:], term.dtype) for term in terms]
+
+    moved = sum(term.size * term.dtype.itemsize for term in terms)
+    return pl.pallas_call(
+        functools.partial(scatter_kernel, arity, ctx_size, pair_count, slot, spread_ctx),
+        in_specs=[pl.BlockSpec(memory_space=pltpu.VMEM)] * arity,
+        out_specs=[pl.BlockSpec(memory_space=pltpu.VMEM)] * arity,
+        out_shape=[
+            jax.ShapeDtypeStruct(lead + term.shape[1:], out_dtype or term.dtype) for term in terms
+        ],
+        scratch_shapes=room(ctx_size, pair_count)
+        + room(pair_count)
+        + room(asides, pair_count)
+        + room(pair_count - 1)
+        + room()
+        + [dma((ctx_size, pair_count, arity))] * 2
+        + [dma((pair_count, arity))] * 2
+        + [dma((ctx_size - 1, pair_count, arity))] * 2
+        + [dma((pair_count - 1, arity))] * 2
+        + [dma((ctx_size - 1, arity))] * 2,
+        compiler_params=pltpu.CompilerParams(
+            collective_id=collective_id, has_side_effects=True, vmem_limit_bytes=60 * 2**20
+        ),
+        cost_estimate=pl.CostEstimate(flops=0, bytes_accessed=moved * 16, transcendentals=0),
+        name=name,
+    )(*terms)
 
 def shards(
     layer_input,
@@ -298,32 +635,70 @@
 ):
     ctx_size = lax.axis_size("ctx")
     shard_count = lax.axis_size("fsdp")
+    own_ctx = lax.axis_index("ctx")
+    own_shard = lax.axis_index("fsdp")
     rows_here = layer_input.shape[0]
     slots = layer_input.shape[1]
     block_rows = rows_here * shard_count
     kv_width = KVH * HD
-    first_row = (lax.axis_index("ctx") * shard_count + lax.axis_index("fsdp")) * rows_here
+    cut = D // (ctx_size * shard_count)
+    columns = FF // shard_count
+    first_row = (own_ctx * shard_count + own_shard) * rows_here
     own_pos = block_positions(block_order, first_row, rows_here, block_rows, ctx_size)
     cosine_table, sine_table = rope_tables(own_pos.reshape(-1))
     query_scale = HD ** (-0.5)
-    w_qkv_all, w_o_all, bias_all, gain_one, gain_two = (
-        lax.all_gather(w_qkv, "fsdp", axis=0, tiled=True),
-        lax.all_gather(w_o, "fsdp", axis=0, tiled=True),
-        lax.all_gather(b_qkv, "fsdp", axis=0, tiled=True),
-        lax.all_gather(first_gain, "fsdp", axis=0, tiled=True),
-        lax.all_gather(second_gain, "fsdp", axis=0, tiled=True),
-    )
-    gate_cols = lax.all_to_all(w_gate, "fsdp", 1, 0, tiled=True)
-    up_cols = lax.all_to_all(w_up, "fsdp", 1, 0, tiled=True)
+
+    def by_rows(ctx, shard):
+        return shard * ctx_size + ctx
+
+    def by_tokens(ctx, shard):
+        return ctx * shard_count + shard
+
+    def own_cut(weight):
+        return lax.dynamic_slice_in_dim(weight, own_ctx * cut, cut, 0)
+
+    def mix_features(values):
+        shaped = values.reshape(-1, shard_count, ctx_size, cut)
+        return shaped.transpose(0, 2, 1, 3).reshape(-1, D)
+
+    def unmix_features(values):
+        shaped = values.reshape(-1, ctx_size, shard_count, cut)
+        return shaped.transpose(0, 2, 1, 3).reshape(-1, D)
+
+    small = jnp.concatenate([b_qkv, first_gain, second_gain]).reshape(ctx_size, -1)
+    small_width = small.shape[1]
+    small = lax.dynamic_slice_in_dim(small, own_ctx, 1, 0)
+    small = jnp.pad(small, ((0, 0), (0, 16 * HD - small_width))).reshape(16, HD)
+    w_qkv_all, w_o_all, small_all = gather(
+        [own_cut(w_qkv), own_cut(w_o), small], by_rows, 1, "gather_weights"
+    )
+    w_qkv_all = w_qkv_all.reshape(D, QKV)
+    w_o_all = w_o_all.reshape(D, D)
+    small_all = small_all.reshape(shard_count, ctx_size, -1)[:, :, :small_width]
+    small_all = small_all.reshape(shard_count, -1).astype(jnp.float32)
+    bias_width = QKV // shard_count
+    gain_width = D // shard_count
+    bias_all = small_all[:, :bias_width].reshape(-1)
+    gain_one = small_all[:, bias_width : bias_width + gain_width].reshape(-1)
+    gain_two = small_all[:, bias_width + gain_width :].reshape(-1)
+
+    gate_up_cut = jnp.concatenate(
+        [
+            own_cut(w_gate).reshape(cut, shard_count, columns),
+            own_cut(w_up).reshape(cut, shard_count, columns),
+        ],
+        2,
+    ).transpose(1, 0, 2)
+    gate_up_cut = lax.all_to_all(gate_up_cut, "fsdp", 0, 0, tiled=True)
+    gate_up_cols = lax.all_gather(
+        gate_up_cut.reshape(shard_count * cut, 2 * columns), "ctx", axis=0, tiled=True
+    )
     cotangent_all = lax.all_gather(cotangent.reshape(-1, D), "fsdp", axis=0, tiled=True)
-    gain_one = gain_one.astype(jnp.float32)
-    gain_two = gain_two.astype(jnp.float32)
+
     inputs = layer_input.reshape(-1, D).astype(jnp.float32)
     unit_one, scale_one, normed = normalize(inputs, gain_one)
     normed_one = normed.astype(jnp.bfloat16)
-    projected = jnp.dot(
-        normed_one, w_qkv_all, preferred_element_type=jnp.float32
-    ) + bias_all.astype(jnp.float32)
+    projected = jnp.dot(normed_one, w_qkv_all, preferred_element_type=jnp.float32) + bias_all
     query_raw = projected[:, : H * HD].reshape(-1, H, HD)
     key_raw = projected[:, H * HD : H * HD + kv_width].reshape(-1, KVH, HD)
     value_raw = projected[:, H * HD + kv_width :]
@@ -338,13 +713,11 @@
     own_kv = jnp.stack([key_tokens, value_raw.astype(jnp.bfloat16)], 1)
     own_kv = own_kv.reshape(rows_here, 2, SEQS, 2, KVH, HD).transpose(0, 2, 4, 1, 3, 5)
     own_kv = own_kv.reshape(rows_here, SEQS * KVH * 4 * HD)
-    all_kv = lax.all_gather(own_kv, ("ctx", "fsdp"), axis=0, tiled=True)
+    (all_kv,) = gather([own_kv], by_tokens, 2, "gather_keys")
+    all_kv = all_kv.reshape(-1, SEQS * KVH * 4 * HD)
     queries = to_groups(query_tokens, rows_here)
     scalars = jnp.concatenate(
-        [
-            block_order.reshape(-1),
-            jnp.stack([lax.axis_index("ctx"), lax.axis_index("fsdp")]).astype(jnp.int32),
-        ]
+        [block_order.reshape(-1), jnp.stack([own_ctx, own_shard]).astype(jnp.int32)]
     )
     attended_grouped, stats = attend_forward(
         scalars, queries, all_kv, ctx_size, block_rows, rows_here
@@ -352,48 +725,55 @@
     attended_low = from_groups(attended_grouped, rows_here).astype(jnp.bfloat16)
     middle = inputs + jnp.dot(attended_low, w_o_all, preferred_element_type=jnp.float32)
     unit_two, scale_two, normed = normalize(middle, gain_two)
-    normed_two = normed.astype(jnp.bfloat16)
+    normed_two = mix_features(normed.astype(jnp.bfloat16))
+
     tokens_all = lax.all_gather(normed_two, "fsdp", axis=0, tiled=True)
-    gate_part = jnp.dot(tokens_all, gate_cols, preferred_element_type=jnp.float32)
-    up_part = jnp.dot(tokens_all, up_cols, preferred_element_type=jnp.float32)
+    gate_up_part = jnp.dot(tokens_all, gate_up_cols, preferred_element_type=jnp.float32)
+    gate_part, up_part = gate_up_part[:, :columns], gate_up_part[:, columns:]
     sigmoid_gate = jax.nn.sigmoid(gate_part)
     activated = gate_part * sigmoid_gate
     hidden = (activated * up_part).astype(jnp.bfloat16)
     grad_hidden = lax.dot_general(
         cotangent_all, w_down, CONTRACT_LAST, preferred_element_type=jnp.float32
     )
-    grad_gate = (
-        grad_hidden * up_part * sigmoid_gate * (1.0 + gate_part * (1.0 - sigmoid_gate))
-    ).astype(jnp.bfloat16)
-    grad_up = (grad_hidden * activated).astype(jnp.bfloat16)
+    grad_gate = grad_hidden * up_part * sigmoid_gate * (1.0 + gate_part * (1.0 - sigmoid_gate))
+    grad_gate_up = jnp.concatenate([grad_gate, grad_hidden * activated], -1).astype(jnp.bfloat16)
     grad_tokens = lax.dot_general(
-        grad_gate, gate_cols, CONTRACT_LAST, preferred_element_type=jnp.float32
-    ) + lax.dot_general(grad_up, up_cols, CONTRACT_LAST, preferred_element_type=jnp.float32)
+        grad_gate_up, gate_up_cols, CONTRACT_LAST, preferred_element_type=jnp.float32
+    )
     grad_normed_two = lax.psum_scatter(
         grad_tokens.astype(jnp.bfloat16), "fsdp", scatter_dimension=0, tiled=True
-    ).astype(jnp.float32)
-    mixed_terms = jnp.dot(hidden, w_down, preferred_element_type=jnp.float32)
-    mixed_out = middle + lax.psum_scatter(
-        mixed_terms.astype(jnp.bfloat16), "fsdp", scatter_dimension=0, tiled=True
-    ).astype(jnp.float32)
-    output = mixed_out.astype(jnp.bfloat16).reshape(rows_here, slots, D)
+    )
     down_terms = lax.dot_general(
         hidden, cotangent_all, CONTRACT_FIRST, preferred_element_type=jnp.float32
     ).astype(jnp.bfloat16)
-    gate_terms = lax.dot_general(
-        tokens_all, grad_gate, CONTRACT_FIRST, preferred_element_type=jnp.float32
+    gate_up_terms = lax.dot_general(
+        tokens_all, grad_gate_up, CONTRACT_FIRST, preferred_element_type=jnp.float32
     ).astype(jnp.bfloat16)
-    up_terms = lax.dot_general(
-        tokens_all, grad_up, CONTRACT_FIRST, preferred_element_type=jnp.float32
-    ).astype(jnp.bfloat16)
-    down_rows = lax.psum(down_terms, "ctx").astype(jnp.float32)
-    gate_rows = column_terms_to_rows(gate_terms)
-    up_rows = column_terms_to_rows(up_terms)
+    mixed_terms = jnp.dot(hidden, w_down, preferred_element_type=jnp.float32).astype(jnp.bfloat16)
+    down_rows = lax.psum(down_terms, "ctx")
+    gate_up_rows = lax.psum_scatter(gate_up_terms, "ctx", scatter_dimension=0, tiled=True)
+    gate_up_rows = lax.all_to_all(
+        gate_up_rows.reshape(shard_count, cut, 2 * columns), "fsdp", 0, 0, tiled=True
+    )
+    gate_up_rows = lax.all_gather(gate_up_rows, "ctx", axis=0, tiled=False)
+    mixed_out = middle + lax.psum_scatter(
+        mixed_terms, "fsdp", scatter_dimension=0, tiled=True
+    ).astype(jnp.float32)
+    output = mixed_out.astype(jnp.bfloat16).reshape(rows_here, slots, D)
+
+    grad_normed_two, down_terms, gate_up_terms, mixed_terms = lax.optimization_barrier(
+        (grad_normed_two, down_terms, gate_up_terms, mixed_terms)
+    )
+    grad_normed_two = unmix_features(grad_normed_two.astype(jnp.float32))
     grad_middle_norm, grad_gain_two = norm_back(grad_normed_two, unit_two, scale_two, gain_two)
     grad_middle = cotangent.reshape(-1, D).astype(jnp.float32) + grad_middle_norm
     grad_branch_one = grad_middle.astype(jnp.bfloat16)
     grad_attended = lax.dot_general(
         grad_branch_one, w_o_all, CONTRACT_LAST, preferred_element_type=jnp.float32
+    ).astype(jnp.bfloat16)
+    o_terms = lax.dot_general(
+        attended_low, grad_branch_one, CONTRACT_FIRST, preferred_element_type=jnp.float32
     ).astype(jnp.bfloat16)
     grad_queries, grad_kv_full = attend_backward(
         scalars,
@@ -406,9 +786,13 @@
         block_rows,
         rows_here,
     )
-    grad_kv = lax.psum_scatter(
-        grad_kv_full, ("ctx", "fsdp"), scatter_dimension=0, tiled=True
-    ).astype(jnp.float32)
+    (grad_kv,) = scatter(
+        [grad_kv_full.reshape(-1, rows_here, SEQS * KVH * 4 * HD)],
+        by_tokens,
+        3,
+        "scatter_keys",
+        out_dtype=jnp.float32,
+    )
     grad_kv_low = narrowed(grad_kv).reshape(rows_here, SEQS, KVH, 2, 2, HD)
     grad_kv_low = grad_kv_low.transpose(0, 3, 1, 4, 2, 5).reshape(-1, 2 * kv_width)
     grad_query_tokens = from_groups(narrowed(grad_queries), rows_here) * query_scale
@@ -422,55 +806,54 @@
         [grad_query_raw, grad_key_raw, grad_kv_low[:, kv_width:]], -1
     ).astype(jnp.bfloat16)
     grad_bias = jnp.sum(grad_projected, 0, dtype=jnp.float32)
-    grad_bias_qk = grad_bias[:QK]
-    grad_bias_value = grad_bias[QK:]
     grad_normed_one = lax.dot_general(
         grad_projected, w_qkv_all, CONTRACT_LAST, preferred_element_type=jnp.float32
     )
     grad_input_norm, grad_gain_one = norm_back(grad_normed_one, unit_one, scale_one, gain_one)
     grad_input = (grad_middle + grad_input_norm).reshape(rows_here, slots, D)
-    qkv_rows = lax.psum_scatter(
-        lax.dot_general(
-            normed_one, grad_projected, CONTRACT_FIRST, preferred_element_type=jnp.float32
-        ).astype(jnp.bfloat16),
-        "fsdp",
-        scatter_dimension=0,
-        tiled=True,
-    )
-    o_rows = lax.psum_scatter(
-        lax.dot_general(
-            attended_low, grad_branch_one, CONTRACT_FIRST, preferred_element_type=jnp.float32
-        ).astype(jnp.bfloat16),
-        "fsdp",
-        scatter_dimension=0,
-        tiled=True,
-    )
-    qkv_rows = lax.psum(qkv_rows, "ctx").astype(jnp.float32)
-    o_rows = lax.psum(o_rows, "ctx").astype(jnp.float32)
-    gain_one_rows, gain_two_rows, bias_rows, value_bias_rows = (
-        lax.psum_scatter(grad_gain_one, "fsdp", scatter_dimension=0, tiled=True),
-        lax.psum_scatter(grad_gain_two, "fsdp", scatter_dimension=0, tiled=True),
-        lax.psum_scatter(grad_bias_qk, "fsdp", scatter_dimension=0, tiled=True),
-        lax.psum_scatter(grad_bias_value, "fsdp", scatter_dimension=0, tiled=True),
-    )
-    gain_one_rows, gain_two_rows, bias_rows, value_bias_rows = (
-        lax.psum(gain_one_rows, "ctx"),
-        lax.psum(gain_two_rows, "ctx"),
-        lax.psum(bias_rows, "ctx"),
-        lax.psum(value_bias_rows, "ctx"),
-    )
+    qkv_terms = lax.dot_general(
+        normed_one, grad_projected, CONTRACT_FIRST, preferred_element_type=jnp.float32
+    ).astype(jnp.bfloat16)
+    small_terms = jnp.concatenate(
+        [
+            part.reshape(shard_count, -1)
+            for part in (grad_gain_one, grad_gain_two, grad_bias[:QK], grad_bias[QK:])
+        ],
+        1,
+    )
+    small_terms = small_terms.reshape(ctx_size * shard_count, small_width)
+    small_terms = jnp.pad(small_terms, ((0, 0), (0, 8 * HD - small_width)))
+    qkv_rows, o_rows, small_rows = scatter(
+        [
+            qkv_terms.reshape(-1, cut, QKV),
+            o_terms.reshape(-1, cut, D),
+            small_terms.reshape(-1, 8, HD),
+        ],
+        by_rows,
+        4,
+        "scatter_weights",
+        spread_ctx=True,
+    )
+    small_rows = small_rows.reshape(ctx_size, -1)[:, :small_width].reshape(-1)
+    bias_start = 2 * gain_width
+    value_start = bias_start + QK // shard_count
+
+    def own_rows(part):
+        shaped = part.transpose(0, 2, 1, 3)
+        return shaped.reshape(ctx_size * cut, FF).astype(jnp.float32)
+
     return (
         output,
         grad_input,
-        gain_one_rows,
-        qkv_rows,
-        bias_rows,
-        value_bias_rows,
-        o_rows,
-        gain_two_rows,
-        gate_rows,
-        up_rows,
-        down_rows,
+        small_rows[:gain_width],
+        qkv_rows.reshape(-1, QKV).astype(jnp.float32),
+        small_rows[bias_start:value_start],
+        small_rows[value_start:],
+        o_rows.reshape(-1, D).astype(jnp.float32),
+        small_rows[gain_width:bias_start],
+        own_rows(gate_up_rows[:, :, :, :columns]),
+        own_rows(gate_up_rows[:, :, :, columns:]),
+        down_rows.astype(jnp.float32),
     )
 
 

time: 1280 us -> 983 us (0.77)
  waiting for transfers between devices: 825 us -> 186 us
  Pallas kernels: 35.1 us -> 315 us
  local copies, waits for them, and re-layouts: 108 us -> 147 us
  blocking collectives: 118 us -> 152 us
  other arithmetic: 42 us -> 59.5 us
    pallas_call x0 -> x4, Pallas kernels: none -> 276 us  [the longest x2 167 us: scatter(): pl.pallas_call(functools.partial(scatter_kernel, arity, ctx_size, pair_co...]
    psum x1, waiting for transfers between devices: 231 us -> 0.01 us  [shards(): down_rows = lax.psum(down_terms, 'ctx')]
    reduce_scatter x4 -> x2, waiting for transfers between devices: 271 us -> 77.6 us  [the longest x1 77.5 us: shards(): lax.psum_scatter(gate_up_terms, 'ctx', scatter_dimension=0, tiled=True)]
    all_to_all x2 -> x0, waiting for transfers between devices: 186 us -> none  [the longest x1 99.1 us: shards(): up_cols = lax.all_to_all(w_up, 'fsdp', 1, 0, tiled=True)]
    all_to_all x2, blocking collectives: 53.1 us -> 152 us  [the longest x1 79 us: shards(): gate_up_cut = lax.all_to_all(gate_up_cut, 'fsdp', 0, 0, tiled=True)]
    unnamed x2 -> x0, blocking collectives: 45.9 us -> none
    all_to_all x10 -> x0, local copies, waits for them, and re-layouts: 37.4 us -> none  [the longest x2 13.2 us: shards(): up_cols = lax.all_to_all(w_up, 'fsdp', 1, 0, tiled=True)]
    reduce_scatter x1, waiting for transfers between devices: 37.4 us -> 3.3 us  [shards(): lax.psum_scatter(grad_tokens.astype(jnp.bfloat16), 'fsdp', scatter_dimens...]
  transfers between devices with their start and end apart: 15 -> 8, of which waited for: 11 -> 4; matrix products, arithmetic and copies ran while one was open for 13% -> 17% of each run, Pallas kernels for 1% -> 19%
where the time goes in v2:
time: 983 us; the launch traced here: 978 us
  Pallas kernels  315 us (32%)
  waiting for transfers between devices  186 us (19%)
  blocking collectives  152 us (15%)
  local copies, waits for them, and re-layouts  147 us (15%)
  matrix products  104 us (11%)
  other arithmetic  59.5 us (6%)
  between operations  14.8 us (2%)
    pallas_call x2, Pallas kernels, scatter(): pl.pallas_call(functools.partial(scatter_kernel, arity, ctx_size, pair_co...  167 us
    pallas_call x2, Pallas kernels, gather(): pl.pallas_call(functools.partial(gather_kernel, arity, ctx_size, pair_cou...  109 us
    all_to_all x1, blocking collectives, shards(): gate_up_cut = lax.all_to_all(gate_up_cut, 'fsdp', 0, 0, tiled=True)  79 us
    reduce_scatter x1, waiting for transfers between devices, shards(): lax.psum_scatter(gate_up_terms, 'ctx', scatter_dimension=0, tiled=True)  77.5 us
    all_gather x1, waiting for transfers between devices, shards(): lax.all_gather(gate_up_cut.reshape(shard_count * cut, 2 * columns), 'ctx'...  73.4 us
    all_to_all x1, blocking collectives, shards(): lax.all_to_all(gate_up_rows.reshape(shard_count, cut, 2 * columns), 'fsdp...  72.7 us
    all_gather x1, waiting for transfers between devices, shards(): lax.all_gather(cotangent.reshape(-1, D), 'fsdp', axis=0, tiled=True)  31.7 us
    convert_element_type x4, local copies, waits for them, and re-layouts, own_rows(): return shaped.reshape(ctx_size * cut, FF).astype(jnp.float32)  28.9 us
  transfers between devices with their start and end apart: 8, of which 4 were waited for; matrix products, arithmetic and copies ran while one was open for 17% of the time, Pallas kernels for 19%

profile of v2, /device:TPU:0, one launch (start us, length us, event | category | flops | bytes accessed | tf_op | source)
XLA Modules:
  0.0 978.0 jit_solution(3478215289691625507)
XLA Ops:
  12.1 66.6 %gather_weights.1 = (bf16[32,48,2048]{2,1,0:T(8,128)(2,1)}, bf16[32,48,1536]{2,1,0:T(8,128)(2,1)}, bf16[32,16,128]{2,1,0:T(8,128)(2,1)}) custom-call(bf16[48,2048]{1,0:T(8,128)(2,1)} %constant_dynamic-slice_fusion.4.refs_0_, bf16[48,1536]{1,0:T(8,128)(2,1)} %constant_dynamic-slice_fusion.3.refs_1_, bf16[16,128]{1,0:T(8,128)(2,1)} %bitcast.149), custom_call_target="tpu_custom_call" | custom-call | bytes 44564480 | tf_op jit(solution)/shard_map/gather_weights/pallas_call | solution.py:426
  120.6 42.1 %gather_keys.1 = bf16[32,40,2048]{2,1,0:T(8,128)(2,1)} custom-call(bf16[40,2048]{1,0:T(8,128)(2,1)} %reshape.479.refs_0_), custom_call_target="tpu_custom_call" | custom-call | bytes 20971520 | tf_op jit(solution)/shard_map/gather_keys/pallas_call | solution.py:426
  180.1 18.8 %attend_forward.1 = (f32[2,2,2,240,128]{4,3,2,1,0:T(8,128)}, f32[2,2,2,1,240]{4,3,2,1,0:T(1,128)}) custom-call(s32[18]{0:T(128)} %pad_add_fusion.scalars, bf16[2,2,2,240,128]{4,3,2,1,0:T(8,128)(2,1)} %bitcast.127, bf16[1280,2048]{1,0:T(8,128)(2,1)} %bitcast.113), custom_call_target="tpu_custom_call" | custom-call | tf_op jit(solution)/shard_map/attend_forward/pallas_call | solution.py:154
  229.2 79.0 %all_to_all.10 = bf16[8,48,2240]{2,1,0:T(8,128)(2,1)} all-to-all(bf16[8,48,2240]{2,1,0:T(8,128)(2,1)S(1)} %copy.160), channel_id=1, replica_groups=mesh['ctx'=4,'fsdp'=8] {'fsdp'}, dimensions={0} | all-to-all | bytes 3440640 | tf_op jit(solution)/shard_map/all_to_all | solution.py:692
  310.2 73.4 %all-gather.8.cloned.1.call-done = bf16[1536,2240]{1,0:T(8,128)(2,1)} async-done(((bf16[384,2240]{1,0:T(8,128)(2,1)}), bf16[1536,2240]{1,0:T(8,128)(2,1)}) %all-gather.8.cloned.1.call-update) | async-done | bytes 6881296 | tf_op jit(solution)/shard_map/all_gather | solution.py:693
  383.7 15.3 %fusion.25 = f32[1280,2240]{0,1:T(8,128)} fusion(bf16[1280,1536]{1,0:T(8,128)(2,1)} %all-gather.6.cloned.1.call-done, bf16[1536,2240]{1,0:T(8,128)(2,1)} %all-gather.8.cloned.1.call-done), kind=kOutput, calls=%fused_computation.118 | convolution fusion | flops 8808038400 | bytes 22282240 | tf_op jit(solution)/shard_map/dot_general | solution.py:731
  398.9 31.7 %all-gather.10.cloned.1.call-done = bf16[1280,1536]{1,0:T(8,128)(2,1)} async-done(((bf16[160,1536]{1,0:T(8,128)(2,1)}), bf16[1280,1536]{1,0:T(8,128)(2,1)}) %all-gather.10.cloned.1.call-update) | async-done | bytes 3932176 | tf_op jit(solution)/shard_map/all_gather | solution.py:696
  430.6 12.1 %multiply_convert_fusion.1 = (bf16[1280,1120]{0,1:T(8,128)(2,1)S(1)}, bf16[1280,1120]{0,1:T(8,128)(2,1)}, bf16[1280,1120]{0,1:T(8,128)(2,1)}) fusion(f32[1280,2240]{0,1:T(8,128)} %fusion.25, bf16[1280,1536]{1,0:T(8,128)(2,1)} %all-gather.10.cloned.1.call-done, bf16[1120,1536]{1,0:T(8,128)(2,1)S(1)} %copy-done), kind=kOutput, calls=%fused_computation.10 | convolution fusion | flops 4425523200 | bytes 27443200 | tf_op jit(solution)/shard_map/dot_general | solution.py:736
  444.2 12.3 %convolution_convert_fusion.5 = bf16[1280,1536]{1,0:T(8,128)(2,1)} fusion(bf16[1536,2240]{1,0:T(8,128)(2,1)S(1)} %copy-done.18, bf16[1280,1120]{0,1:T(8,128)(2,1)} %get-tuple-element.38, bf16[1280,1120]{0,1:T(8,128)(2,1)S(1)} %get-tuple-element.37), kind=kOutput, calls=%fused_computation.5 | convolution fusion | flops 8821473280 | bytes 16547840 | tf_op jit(solution)/shard_map/dot_general | solution.py:741
  456.6 14.5 %convolution_convert_fusion = bf16[1536,2240]{0,1:T(8,128)(2,1)} fusion(bf16[1280,1536]{1,0:T(8,128)(2,1)} %all-gather.6.cloned.1.call-done, bf16[1280,1120]{0,1:T(8,128)(2,1)} %get-tuple-element.38, bf16[1280,1120]{0,1:T(8,128)(2,1)} %copy-done.19), kind=kOutput, calls=%fused_computation | convolution fusion | flops 8822947840 | bytes 16547840 | tf_op jit(solution)/shard_map/dot_general | solution.py:750
  471.2 10.2 %copy.175 = bf16[1536,2240]{1,0:T(8,128)(2,1)} copy(bf16[1536,2240]{0,1:T(8,128)(2,1)} %convolution_convert_fusion) | data formatting | bytes 13762560
  481.5 8.7 convolution_convert_fusion.1
  490.3 9.4 convolution_convert_fusion.3
  503.1 77.5 %reduce-scatter.10.cloned.1.call-done = bf16[384,2240]{1,0:T(8,128)(2,1)} async-done(((bf16[1536,2240]{1,0:T(8,128)(2,1)}), bf16[384,2240]{1,0:T(8,128)(2,1)}) %reduce-scatter.10.cloned.1.call-update) | async-done | bytes 1720336 | tf_op jit(solution)/shard_map/reduce_scatter | solution.py:755
  580.7 72.7 %all_to_all.11 = bf16[8,48,2240]{2,1,0:T(8,128)(2,1)} all-to-all(bf16[8,48,2240]{2,1,0:T(8,128)(2,1)} %bitcast.140), channel_id=1, replica_groups=mesh['ctx'=4,'fsdp'=8] {'fsdp'}, dimensions={0} | all-to-all | bytes 3440640 | tf_op jit(solution)/shard_map/all_to_all | solution.py:756
  678.8 20.3 %attend_backward.1 = (f32[2,2,2,240,128]{4,3,2,1,0:T(8,128)}, bf16[1280,2048]{1,0:T(8,128)(2,1)}) custom-call(s32[18]{0:T(128)} %pad_add_fusion.scalars, bf16[2,2,2,240,128]{4,3,2,1,0:T(8,128)(2,1)} %bitcast.128, bf16[2,2,2,240,128]{4,3,2,1,0:T(8,128)(2,1)} %bitcast.138, f32[2,2,2,240,128]{4,3,2,1,0:T(8,128)} %get-tuple-element.24.att_ref, ...), custom_call_target="tpu_custom_call" | custom-call | tf_op jit(solution)/shard_map/attend_backward/pallas_call | solution.py:252
  706.3 53.4 %scatter_keys.1 = f32[40,2048]{1,0:T(8,128)} custom-call(bf16[32,40,2048]{2,1,0:T(8,128)(2,1)} %bitcast.126), custom_call_target="tpu_custom_call" | custom-call | bytes 83886080 | tf_op jit(solution)/shard_map/scatter_keys/pallas_call | solution.py:599
  777.8 8.0 multiply_reduce_fusion.1
  799.9 113.8 %scatter_weights.1 = (bf16[4,48,2048]{2,1,0:T(8,128)(2,1)}, bf16[4,48,1536]{2,1,0:T(8,128)(2,1)}, f32[4,8,128]{2,1,0:T(8,128)}) custom-call(bf16[32,48,2048]{2,1,0:T(8,128)(2,1)} %bitcast.115, bf16[32,48,1536]{2,1,0:T(8,128)(2,1)} %bitcast.116, f32[32,8,128]{2,1,0:T(8,128)} %bitcast.145), custom_call_target="tpu_custom_call" | custom-call | bytes 178257920 | tf_op jit(solution)/shard_map/scatter_weights/pallas_call | solution.py:599
  928.3 5.8 convert_element_type.202
  934.1 7.9 convert_bitcast_fusion
  947.1 7.9 reshape.518
  955.0 8.0 copy.173
  963.0 7.9 reshape.519
  (197 shorter events, 185.7 us)
Async XLA Ops:
  7.2 423.4 %copy-start = (bf16[1120,1536]{1,0:T(8,128)(2,1)S(1)}, bf16[1120,1536]{1,0:T(8,128)(2,1)}, u32[]{:S(2)}) copy-start(bf16[1120,1536]{1,0:T(8,128)(2,1)} %param.20) | copy-start | bytes 10321924
  7.2 303.0 %all-gather.6.cloned.1.call-start = ((), (), s32[]{:S(2)}) async-start(), calls=%async_computation.5 | async-start | bytes 4423680 | tf_op jit(solution)/shard_map/all_gather | solution.py:730
  96.5 14.5 %copy-start.14 = (f32[64]{0:T(128)}, f32[64]{0:T(128)S(1)}, u32[]{:S(2)}) copy-start(f32[64]{0:T(128)S(1)} %multiply_power_fusion) | copy-start | bytes 772
  100.2 9.7 copy-start.16
  173.6 4.2 copy-start.3
  173.6 4.2 copy-start.11
  203.6 4.7 copy-start.12
  216.9 166.7 %all-gather.8.cloned.1.call-start = ((), (), s32[]{:S(2)}) async-start(), calls=%async_computation.6 | async-start | bytes 8847360 | tf_op jit(solution)/shard_map/all_gather | solution.py:693
  308.2 122.4 %all-gather.10.cloned.1.call-start = ((), (), s32[]{:S(2)}) async-start(), calls=%async_computation.8 | async-start | bytes 4423680 | tf_op jit(solution)/shard_map/all_gather | solution.py:696
  310.2 192.9 %reduce-scatter.8.cloned.1.call-start = ((), (), s32[]{:S(2)}) async-start(), calls=%async_computation.9 | async-start | bytes 4423680 | tf_op jit(solution)/shard_map/reduce_scatter | solution.py:744
  430.6 13.6 %copy-start.18 = (bf16[1536,2240]{1,0:T(8,128)(2,1)S(1)}, bf16[1536,2240]{1,0:T(8,128)(2,1)}, u32[]{:S(2)}) copy-start(bf16[1536,2240]{1,0:T(8,128)(2,1)} %all-gather.8.cloned.1.call-done) | copy-start | bytes 20643844
  456.6 124.1 %reduce-scatter.10.cloned.1.call-start = ((), (), s32[]{:S(2)}) async-start(), calls=%async_computation.12 | async-start | bytes 8847360 | tf_op jit(solution)/shard_map/reduce_scatter | solution.py:755
  481.4 184.0 %reduce-scatter.6.cloned.1.call-start = ((), (), s32[]{:S(2)}) async-start(), calls=%async_computation.7 | async-start | bytes 4423680 | tf_op jit(solution)/shard_map/reduce_scatter | solution.py:760
  490.2 438.1 %all-reduce.4.cloned.1.call-start = ((), (), s32[]{:S(2)}) async-start(), calls=%async_computation.10 | async-start | bytes 6881280 | tf_op jit(solution)/shard_map/psum | solution.py:754
  499.7 153.8 %copy-start.13 = (f32[40,4]{0,1:T(4,128)S(1)}, f32[40,4]{0,1:T(4,128)}, u32[]{:S(2)}) copy-start(f32[40,4]{0,1:T(4,128)} %get-tuple-element.62) | copy-start | bytes 1924
  503.1 150.7 %copy-start.15 = (f32[64]{0:T(128)S(1)}, f32[64]{0:T(128)}, u32[]{:S(2)}) copy-start(f32[64]{0:T(128)} %copy-done.14) | copy-start | bytes 772
  503.1 431.1 %all-gather.12.cloned.1.call-start = ((), (), s32[]{:S(2)}) async-start(), calls=%async_computation.11 | async-start | bytes 8847360 | tf_op jit(solution)/shard_map/all_gather | solution.py:759
  771.0 3.9 copy-start.10
  773.1 2.5 copy-start.8
  773.1 1.8 copy-start.7
  790.2 5.1 copy-start.1
  790.2 5.1 copy-start.6
  790.2 5.1 copy-start.9
  799.9 115.7 %copy-start.17 = (f32[160]{0:T(256)S(1)}, f32[160]{0:T(256)}, u32[]{:S(2)}) copy-start(f32[160]{0:T(256)} %get-tuple-element.34) | copy-start | bytes 1924
  (4 other events, 4.4 us)
Sparse Core Ops, SparseCore 0:
  217.0 89.5 all-gather.5
  308.4 75.1 all-gather.7
  385.9 44.6 all-gather.9
  456.7 46.2 reduce-scatter.7
  505.9 74.6 reduce-scatter.9
  583.4 78.3 reduce-scatter.5
  665.5 105.7 all-reduce.3
  773.1 114.1 all-gather.11

commit v3 on v2

--- a/solution.py
+++ b/solution.py
@@ -284,34 +284,122 @@
     return position ^ way if square else lax.rem(position + ctx_size - way, ctx_size)
 
 
-def greet(ctx_size, pair_count, with_ctx):
+def greet(ctx_size, pair_count, with_ctx, all_shards):
     ctx = lax.axis_index("ctx")
     shard = lax.axis_index("fsdp")
     pair, core = shard // 2, shard % 2
     barrier = pltpu.get_barrier_semaphore()
-    count = 0
+    shard_count = 2 * pair_count
+    partners = [(ctx, pair * 2 + 1 - core)]
     for step in range(1, pair_count):
-        there = lax.rem(pair + step, pair_count) * 2 + core
-        pl.semaphore_signal(barrier, inc=1, device_id=(ctx, there), device_id_type=MESH_ID)
-        count += 1
+        there = lax.rem(pair + step, pair_count) * 2
+        partners.append((ctx, there + core))
+        if all_shards:
+            partners.append((ctx, there + 1 - core))
     if with_ctx:
         for way in range(1, ctx_size):
-            there = lax.rem(ctx + way, ctx_size)
-            pl.semaphore_signal(barrier, inc=1, device_id=(there, shard), device_id_type=MESH_ID)
-            count += 1
-    pl.semaphore_signal(barrier, inc=1, device_id=(ctx, pair * 2 + 1 - core), device_id_type=MESH_ID)
-    pl.semaphore_wait(barrier, count + 1)
+            partners.append((lax.rem(ctx + way, ctx_size), shard))
+    for partner in partners:
+        pl.semaphore_signal(barrier, inc=1, device_id=partner, device_id_type=MESH_ID)
+    pl.semaphore_wait(barrier, len(partners))
     return ctx, pair, core
 
 
-def gather_kernel(arity, ctx_size, pair_count, slot, *refs):
-    sources, outs = refs[:arity], refs[arity : 2 * arity]
-    pair_send, pair_recv, ctx_send, ctx_recv, core_send, core_recv, local_sem = refs[2 * arity :]
+class Exchange:
+    def __init__(self, source, out, sems, own_sem, pair_count):
+        self.source, self.out, self.sems, self.own_sem = source, out, sems, own_sem
+        self.shard_count = 2 * pair_count
+
+    def start(self):
+        ctx, shard = lax.axis_index("ctx"), lax.axis_index("fsdp")
+        self.own = pltpu.make_async_copy(self.source.at[shard], self.out.at[shard], self.own_sem)
+        self.own.start()
+        self.copies = []
+        for step in range(1, self.shard_count):
+            there = lax.rem(shard + step, self.shard_count)
+            copy = pltpu.make_async_remote_copy(
+                src_ref=self.source.at[there],
+                dst_ref=self.out.at[shard],
+                send_sem=self.sems[0].at[step - 1],
+                recv_sem=self.sems[1].at[step - 1],
+                device_id=(ctx, there),
+                device_id_type=MESH_ID,
+            )
+            copy.start()
+            self.copies.append(copy)
+
+    def finish(self):
+        ctx, shard = lax.axis_index("ctx"), lax.axis_index("fsdp")
+        for step in range(1, self.shard_count):
+            come = lax.rem(shard + self.shard_count - step, self.shard_count)
+            pltpu.make_async_remote_copy(
+                src_ref=self.out.at[come],
+                dst_ref=self.out.at[come],
+                send_sem=self.sems[0].at[step - 1],
+                recv_sem=self.sems[1].at[step - 1],
+                device_id=(ctx, shard),
+                device_id_type=MESH_ID,
+            ).wait_recv()
+        self.own.wait()
+        for copy in self.copies:
+            copy.wait_send()
+
+
+def exchange_kernel(pair_count, source, out, send_sem, recv_sem, own_sem):
+    greet(1, pair_count, False, True)
+    flow = Exchange(source, out, (send_sem, recv_sem), own_sem, pair_count)
+    flow.start()
+    flow.finish()
+
+
+def exchange(pieces, collective_id, name):
+    shard_count = lax.axis_size("fsdp")
+    dma = pltpu.SemaphoreType.DMA
+    return pl.pallas_call(
+        functools.partial(exchange_kernel, shard_count // 2),
+        in_specs=[pl.BlockSpec(memory_space=pltpu.VMEM)],
+        out_specs=pl.BlockSpec(memory_space=pl.ANY),
+        out_shape=jax.ShapeDtypeStruct(pieces.shape, pieces.dtype),
+        scratch_shapes=[dma((shard_count - 1,))] * 2 + [dma],
+        compiler_params=pltpu.CompilerParams(collective_id=collective_id, has_side_effects=True),
+        cost_estimate=pl.CostEstimate(
+            flops=0, bytes_accessed=pieces.size * 64, transcendentals=0
+        ),
+        name=name,
+    )(pieces)
+
+
+def gather_kernel(arity, ctx_size, pair_count, slots, swaps, *refs):
+    sources, refs = refs[:arity], refs[arity:]
+    swap_sources, refs = refs[:swaps], refs[swaps:]
+    outs, refs = refs[:arity], refs[arity:]
+    swap_outs, refs = refs[:swaps], refs[swaps:]
+    pair_sems, ctx_sems, core_sems = refs[0:2], refs[2:4], refs[4:6]
+    local_sem = refs[6]
     square, ways = peers_of(ctx_size)
-    ctx, pair, core = greet(ctx_size, pair_count, True)
+    near = [way for way in ways if not (square and way == 3)]
+    ctx, pair, core = greet(ctx_size, pair_count, True, swaps > 0)
+    homes = [place(ctx, pair * 2 + core) for place in slots]
     started = []
-
-    def send(item, source, place, target, sems, at):
+    steps = [(0, 1)] + [(far, way) for far in range(1, pair_count) for way in (1, -1)]
+
+    def present(step):
+        far, way = steps[step]
+        if far == 0:
+            return None
+        return pair >= far if way == 1 else pair + far < pair_count
+
+    def origin(step):
+        far, way = steps[step]
+        return pair - far * way
+
+    def when(condition, work):
+        if condition is None:
+            work()
+        else:
+            pl.when(condition)(work)
+
+    def send(item, source, place, target, sems, at, condition):
         copy = pltpu.make_async_remote_copy(
             src_ref=source,
             dst_ref=outs[item].at[place],
@@ -321,7 +409,17 @@
             device_id_type=MESH_ID,
         )
         copy.start()
-        started.append(copy)
+        started.append((condition, item, sems, at))
+
+    def sent(item, sems, at):
+        pltpu.make_async_remote_copy(
+            src_ref=outs[item].at[0],
+            dst_ref=outs[item].at[0],
+            send_sem=sems[0].at[at],
+            recv_sem=sems[1].at[at],
+            device_id=(ctx, pair * 2 + core),
+            device_id_type=MESH_ID,
+        ).wait_send()
 
     def arrive(item, place, sems, at):
         pltpu.make_async_remote_copy(
@@ -333,52 +431,71 @@
             device_id_type=MESH_ID,
         ).wait_recv()
 
-    pair_sems, ctx_sems, core_sems = (pair_send, pair_recv), (ctx_send, ctx_recv), (core_send, core_recv)
-    home = slot(ctx, pair * 2 + core)
-    locals_ = []
-    for item in range(arity):
-        copy = pltpu.make_async_copy(sources[item], outs[item].at[home], local_sem.at[item])
-        copy.start()
-        locals_.append(copy)
-
-    def origin(step):
-        return lax.rem(pair + pair_count - step, pair_count)
+    def pass_on(step, item, source, place):
+        far, way = steps[step]
+        for side in (1, -1) if far == 0 else (way,):
+
+            def further(side=side):
+                return pair + 1 < pair_count if side == 1 else pair >= 1
+
+            def both(further=further):
+                return further() if far == 0 else jnp.logical_and(further(), present(step))
+
+            def work(side=side, both=both):
+                send(
+                    item,
+                    source,
+                    place,
+                    (ctx, (pair + side) * 2 + core),
+                    pair_sems,
+                    ((side + 1) // 2, far, item),
+                    both,
+                )
+
+            if far + 1 < pair_count:
+                pl.when(further())(work)
 
     def to_core(item, source, from_ctx, way, step):
         send(
             item,
             source,
-            slot(from_ctx, origin(step) * 2 + core),
+            slots[item](from_ctx, origin(step) * 2 + core),
             (ctx, pair * 2 + 1 - core),
             core_sems,
             (way, step, item),
+            functools.partial(present, step),
         )
 
     def spread(step):
         for item in range(arity):
-            place = slot(ctx, origin(step) * 2 + core)
-            if step == 0:
-                source = sources[item]
-            else:
-                arrive(item, place, pair_sems, (step - 1, item))
+            place = slots[item](ctx, origin(step) * 2 + core)
+            source = sources[item]
+            if step:
+                far, way = steps[step]
+                arrive(item, place, pair_sems, ((way + 1) // 2, far - 1, item))
                 source = outs[item].at[place]
-            for way in ways:
-                if square and way == 3:
-                    continue
+            pass_on(step, item, source, place)
+            for way in near:
                 there = ctx_target(ctx, way, square, ctx_size)
-                send(item, source, place, (there, pair * 2 + core), ctx_sems, (way - 1, step, item))
+                send(
+                    item,
+                    source,
+                    place,
+                    (there, pair * 2 + core),
+                    ctx_sems,
+                    (way - 1, step, item),
+                    functools.partial(present, step),
+                )
             to_core(item, source, ctx, 0, step)
 
     def collect(step):
-        for way in ways:
-            if square and way == 3:
-                continue
+        for way in near:
             for item in range(arity):
                 come = ctx_source(ctx, way, square, ctx_size)
-                place = slot(come, origin(step) * 2 + core)
+                place = slots[item](come, origin(step) * 2 + core)
                 arrive(item, place, ctx_sems, (way - 1, step, item))
                 source = outs[item].at[place]
-                if square and (step % 2 == 0) == (way == 1):
+                if square and (steps[step][0] % 2 == 0) == (way == 1):
                     send(
                         item,
                         source,
@@ -386,60 +503,85 @@
                         (ctx ^ (3 - way), pair * 2 + core),
                         ctx_sems,
                         (2, step, item),
+                        functools.partial(present, step),
                     )
                 to_core(item, source, come, way, step)
 
     def collect_far(step):
         for item in range(arity):
-            place = slot(ctx ^ 3, origin(step) * 2 + core)
+            place = slots[item](ctx ^ 3, origin(step) * 2 + core)
             arrive(item, place, ctx_sems, (2, step, item))
             to_core(item, outs[item].at[place], ctx ^ 3, 3, step)
 
+    locals_ = []
     for item in range(arity):
-        for step in range(1, pair_count):
-            there = lax.rem(pair + step, pair_count) * 2 + core
-            send(item, sources[item], home, (ctx, there), pair_sems, (step - 1, item))
-    for step in range(pair_count + 2):
-        if step < pair_count:
-            spread(step)
-        if 1 <= step <= pair_count:
-            collect(step - 1)
-        if square and step >= 2:
-            collect_far(step - 2)
-    for step in range(pair_count):
+        copy = pltpu.make_async_copy(sources[item], outs[item].at[homes[item]], local_sem.at[item])
+        copy.start()
+        locals_.append(copy)
+    when(None, lambda: spread(0))
+    flows = []
+    count = len(steps)
+    for turn in range(1, count + 4):
+        if turn < count:
+            when(present(turn), functools.partial(spread, turn))
+        if turn == count:
+            for item in range(swaps):
+                flow = Exchange(
+                    swap_sources[item],
+                    swap_outs[item],
+                    refs[7 + 3 * item : 9 + 3 * item],
+                    refs[9 + 3 * item],
+                    pair_count,
+                )
+                flow.start()
+                flows.append(flow)
+        if 0 <= turn - 2 < count:
+            when(present(turn - 2), functools.partial(collect, turn - 2))
+        if square and 0 <= turn - 4 < count:
+            when(present(turn - 4), functools.partial(collect_far, turn - 4))
+
+    def from_core(step):
         for way in range(ctx_size):
             come = ctx_source(ctx, way, square, ctx_size) if way else ctx
             for item in range(arity):
-                arrive(item, slot(come, origin(step) * 2 + 1 - core), core_sems, (way, step, item))
+                arrive(item, slots[item](come, origin(step) * 2 + 1 - core), core_sems, (way, step, item))
+
+    for step in range(count):
+        when(present(step), functools.partial(from_core, step))
+    for flow in flows:
+        flow.finish()
     for copy in locals_:
         copy.wait()
-    for copy in started:
-        copy.wait_send()
-
-
-def gather(pieces, slot, collective_id, name):
+    for condition, *which in started:
+        when(condition(), functools.partial(sent, *which))
+
+
+def gather(pieces, slots, collective_id, name, swaps=()):
     ctx_size, shard_count = lax.axis_size("ctx"), lax.axis_size("fsdp")
     pair_count = shard_count // 2
     arity = len(pieces)
     dma = pltpu.SemaphoreType.DMA
     moved = sum(piece.size for piece in pieces) * 2
+    steps = 2 * pair_count - 1
     return pl.pallas_call(
-        functools.partial(gather_kernel, arity, ctx_size, pair_count, slot),
-        in_specs=[pl.BlockSpec(memory_space=pltpu.VMEM)] * arity,
-        out_specs=[pl.BlockSpec(memory_space=pl.ANY)] * arity,
+        functools.partial(gather_kernel, arity, ctx_size, pair_count, slots, len(swaps)),
+        in_specs=[pl.BlockSpec(memory_space=pltpu.VMEM)] * (arity + len(swaps)),
+        out_specs=[pl.BlockSpec(memory_space=pl.ANY)] * (arity + len(swaps)),
         out_shape=[
             jax.ShapeDtypeStruct((ctx_size * shard_count,) + piece.shape, piece.dtype) for piece in pieces
-        ],
-        scratch_shapes=[dma((pair_count - 1, arity))] * 2
-        + [dma((ctx_size - 1, pair_count, arity))] * 2
-        + [dma((ctx_size, pair_count, arity))] * 2
-        + [dma((arity,))],
+        ]
+        + [jax.ShapeDtypeStruct(swap.shape, swap.dtype) for swap in swaps],
+        scratch_shapes=[dma((2, pair_count - 1, arity))] * 2
+        + [dma((ctx_size - 1, steps, arity))] * 2
+        + [dma((ctx_size, steps, arity))] * 2
+        + [dma((arity,))]
+        + [dma((shard_count - 1,)), dma((shard_count - 1,)), dma] * len(swaps),
         compiler_params=pltpu.CompilerParams(collective_id=collective_id, has_side_effects=True),
         cost_estimate=pl.CostEstimate(
             flops=0, bytes_accessed=moved * ctx_size * shard_count * 4, transcendentals=0
         ),
         name=name,
-    )(*pieces)
+    )(*pieces, *swaps)
 
 
 def scatter_kernel(arity, ctx_size, pair_count, slot, spread_ctx, *refs):
@@ -448,7 +590,7 @@
     sems = refs[5 * arity :]
     core_sems, relay_sems, ctx_sems, pair_sems, last_sems = (sems[2 * i : 2 * i + 2] for i in range(5))
     square, ways = peers_of(ctx_size)
-    ctx, pair, core = greet(ctx_size, pair_count, True)
+    ctx, pair, core = greet(ctx_size, pair_count, True, False)
     order = list(range(1, pair_count)) + [0]
     started = []
 
@@ -620,6 +762,47 @@
         name=name,
     )(*terms)
 
+def pack_kernel(columns, gate_ref, up_ref, out_ref):
+    width = out_ref.shape[2] // 2
+    cut = out_ref.shape[1]
+    for there in range(out_ref.shape[0]):
+        for side, ref in enumerate((gate_ref, up_ref)):
+            at = side * width
+            out_ref[there, :, at + width - HD : at + width] = jnp.zeros((cut, HD), out_ref.dtype)
+            out_ref[there, :, at : at + columns] = ref[:, there * columns : (there + 1) * columns]
+
+
+def pack(gate, up, shard_count, columns, width):
+    return pl.pallas_call(
+        functools.partial(pack_kernel, columns),
+        in_specs=[pl.BlockSpec(memory_space=pltpu.VMEM)] * 2,
+        out_specs=pl.BlockSpec(memory_space=pltpu.VMEM),
+        out_shape=jax.ShapeDtypeStruct((shard_count, gate.shape[0], 2 * width), gate.dtype),
+        name="pack",
+    )(gate, up)
+
+
+def unpack_kernel(columns, in_ref, gate_ref, up_ref):
+    width = in_ref.shape[3] // 2
+    for there in range(in_ref.shape[1]):
+        for side, ref in enumerate((gate_ref, up_ref)):
+            part = in_ref[0, there, :, side * width : side * width + columns]
+            ref[0, :, there * columns : (there + 1) * columns] = part.astype(jnp.float32)
+
+
+def unpack(rows, columns):
+    ctx_size, shard_count, cut, _ = rows.shape
+    out = jax.ShapeDtypeStruct((ctx_size, cut, shard_count * columns), jnp.float32)
+    return pl.pallas_call(
+        functools.partial(unpack_kernel, columns),
+        grid=(ctx_size,),
+        in_specs=[pl.BlockSpec((1,) + rows.shape[1:], lambda c: (c, 0, 0, 0))],
+        out_specs=[pl.BlockSpec((1, cut, shard_count * columns), lambda c: (c, 0, 0))] * 2,
+        out_shape=[out, out],
+        name="unpack",
+    )(rows)
+
+
 def shards(
     layer_input,
     block_order,
@@ -669,11 +852,15 @@
     small_width = small.shape[1]
     small = lax.dynamic_slice_in_dim(small, own_ctx, 1, 0)
     small = jnp.pad(small, ((0, 0), (0, 16 * HD - small_width))).reshape(16, HD)
-    w_qkv_all, w_o_all, small_all = gather(
-        [own_cut(w_qkv), own_cut(w_o), small], by_rows, 1, "gather_weights"
+    width = -(-columns // HD) * HD
+    w_qkv_all, small_all, gate_up_cut = gather(
+        [own_cut(w_qkv), small],
+        [by_rows, by_rows],
+        1,
+        "gather_weights",
+        swaps=[pack(own_cut(w_gate), own_cut(w_up), shard_count, columns, width)],
     )
     w_qkv_all = w_qkv_all.reshape(D, QKV)
-    w_o_all = w_o_all.reshape(D, D)
     small_all = small_all.reshape(shard_count, ctx_size, -1)[:, :, :small_width]
     small_all = small_all.reshape(shard_count, -1).astype(jnp.float32)
     bias_width = QKV // shard_count
@@ -682,17 +869,10 @@
     gain_one = small_all[:, bias_width : bias_width + gain_width].reshape(-1)
     gain_two = small_all[:, bias_width + gain_width :].reshape(-1)
 
-    gate_up_cut = jnp.concatenate(
-        [
-            own_cut(w_gate).reshape(cut, shard_count, columns),
-            own_cut(w_up).reshape(cut, shard_count, columns),
-        ],
-        2,
-    ).transpose(1, 0, 2)
-    gate_up_cut = lax.all_to_all(gate_up_cut, "fsdp", 0, 0, tiled=True)
     gate_up_cols = lax.all_gather(
-        gate_up_cut.reshape(shard_count * cut, 2 * columns), "ctx", axis=0, tiled=True
-    )
+        gate_up_cut.reshape(shard_count * cut, 2 * width), "ctx", axis=0, tiled=True
+    )
+    down_padded = jnp.pad(w_down, ((0, width - columns), (0, 0)))
     cotangent_all = lax.all_gather(cotangent.reshape(-1, D), "fsdp", axis=0, tiled=True)
 
     inputs = layer_input.reshape(-1, D).astype(jnp.float32)
@@ -713,7 +893,8 @@
     own_kv = jnp.stack([key_tokens, value_raw.astype(jnp.bfloat16)], 1)
     own_kv = own_kv.reshape(rows_here, 2, SEQS, 2, KVH, HD).transpose(0, 2, 4, 1, 3, 5)
     own_kv = own_kv.reshape(rows_here, SEQS * KVH * 4 * HD)
-    (all_kv,) = gather([own_kv], by_tokens, 2, "gather_keys")
+    all_kv, w_o_all = gather([own_kv, own_cut(w_o)], [by_tokens, by_rows], 2, "gather_keys")
+    w_o_all = w_o_all.reshape(D, D)
     all_kv = all_kv.reshape(-1, SEQS * KVH * 4 * HD)
     queries = to_groups(query_tokens, rows_here)
     scalars = jnp.concatenate(
@@ -729,12 +910,12 @@
 
     tokens_all = lax.all_gather(normed_two, "fsdp", axis=0, tiled=True)
     gate_up_part = jnp.dot(tokens_all, gate_up_cols, preferred_element_type=jnp.float32)
-    gate_part, up_part = gate_up_part[:, :columns], gate_up_part[:, columns:]
+    gate_part, up_part = gate_up_part[:, :width], gate_up_part[:, width:]
     sigmoid_gate = jax.nn.sigmoid(gate_part)
     activated = gate_part * sigmoid_gate
     hidden = (activated * up_part).astype(jnp.bfloat16)
     grad_hidden = lax.dot_general(
-        cotangent_all, w_down, CONTRACT_LAST, preferred_element_type=jnp.float32
+        cotangent_all, down_padded, CONTRACT_LAST, preferred_element_type=jnp.float32
     )
     grad_gate = grad_hidden * up_part * sigmoid_gate * (1.0 + gate_part * (1.0 - sigmoid_gate))
     grad_gate_up = jnp.concatenate([grad_gate, grad_hidden * activated], -1).astype(jnp.bfloat16)
@@ -750,17 +931,14 @@
     gate_up_terms = lax.dot_general(
         tokens_all, grad_gate_up, CONTRACT_FIRST, preferred_element_type=jnp.float32
     ).astype(jnp.bfloat16)
-    mixed_terms = jnp.dot(hidden, w_down, preferred_element_type=jnp.float32).astype(jnp.bfloat16)
+    mixed_terms = jnp.dot(hidden, down_padded, preferred_element_type=jnp.float32).astype(jnp.bfloat16)
     down_rows = lax.psum(down_terms, "ctx")
     gate_up_rows = lax.psum_scatter(gate_up_terms, "ctx", scatter_dimension=0, tiled=True)
-    gate_up_rows = lax.all_to_all(
-        gate_up_rows.reshape(shard_count, cut, 2 * columns), "fsdp", 0, 0, tiled=True
-    )
+    gate_up_rows = exchange(
+        gate_up_rows.reshape(shard_count, cut, 2 * width), 5, "exchange_rows"
+    )
+    gate_up_rows, down_rows = lax.optimization_barrier((gate_up_rows, down_rows))
     gate_up_rows = lax.all_gather(gate_up_rows, "ctx", axis=0, tiled=False)
-    mixed_out = middle + lax.psum_scatter(
-        mixed_terms, "fsdp", scatter_dimension=0, tiled=True
-    ).astype(jnp.float32)
-    output = mixed_out.astype(jnp.bfloat16).reshape(rows_here, slots, D)
 
     grad_normed_two, down_terms, gate_up_terms, mixed_terms = lax.optimization_barrier(
         (grad_normed_two, down_terms, gate_up_terms, mixed_terms)
@@ -793,6 +971,11 @@
         "scatter_keys",
         out_dtype=jnp.float32,
     )
+    grad_kv, mixed_terms = lax.optimization_barrier((grad_kv, mixed_terms))
+    mixed_out = middle + lax.psum_scatter(
+        mixed_terms, "fsdp", scatter_dimension=0, tiled=True
+    ).astype(jnp.float32)
+    output = mixed_out.astype(jnp.bfloat16).reshape(rows_here, slots, D)
     grad_kv_low = narrowed(grad_kv).reshape(rows_here, SEQS, KVH, 2, 2, HD)
     grad_kv_low = grad_kv_low.transpose(0, 3, 1, 4, 2, 5).reshape(-1, 2 * kv_width)
     grad_query_tokens = from_groups(narrowed(grad_queries), rows_here) * query_scale
@@ -838,10 +1021,7 @@
     bias_start = 2 * gain_width
     value_start = bias_start + QK // shard_count
 
-    def own_rows(part):
-        shaped = part.transpose(0, 2, 1, 3)
-        return shaped.reshape(ctx_size * cut, FF).astype(jnp.float32)
-
+    gate_rows, up_rows = unpack(gate_up_rows, columns)
     return (
         output,
         grad_input,
@@ -851,9 +1031,9 @@
         small_rows[value_start:],
         o_rows.reshape(-1, D).astype(jnp.float32),
         small_rows[gain_width:bias_start],
-        own_rows(gate_up_rows[:, :, :, :columns]),
-        own_rows(gate_up_rows[:, :, :, columns:]),
-        down_rows.astype(jnp.float32),
+        gate_rows.reshape(-1, FF),
+        up_rows.reshape(-1, FF),
+        down_rows[:columns].astype(jnp.float32),
     )
 
 

time: 983 us -> 854 us (0.87)
  blocking collectives: 152 us -> 0 us
  Pallas kernels: 315 us -> 404 us
  local copies, waits for them, and re-layouts: 147 us -> 63.3 us
  waiting for transfers between devices: 186 us -> 226 us
  other arithmetic: 59.5 us -> 34.6 us
    all_to_all x2 -> x0, blocking collectives: 152 us -> none  [the longest x1 79 us: shards(): gate_up_cut = lax.all_to_all(gate_up_cut, 'fsdp', 0, 0, tiled=True)]
    reduce_scatter x1, waiting for transfers between devices: 77.5 us -> 0.02 us  [shards(): lax.psum_scatter(gate_up_terms, 'ctx', scatter_dimension=0, tiled=True)]
    psum x1, waiting for transfers between devices: 0.01 us -> 60.8 us  [shards(): down_rows = lax.psum(down_terms, 'ctx')]
    pallas_call x0 -> x3, Pallas kernels: none -> 46.1 us  [the longest x1 34.1 us: exchange(): pl.pallas_call(functools.partial(exchange_kernel, shard_count // 2), in_s...]
    all_gather x1, waiting for transfers between devices: 0.02 us -> 43.1 us  [shards(): tokens_all = lax.all_gather(normed_two, 'fsdp', axis=0, tiled=True)]
    convert_element_type x4 -> x0, local copies, waits for them, and re-layouts: 28.9 us -> none  [own_rows(): return shaped.reshape(ctx_size * cut, FF).astype(jnp.float32)]
    pallas_call x2, Pallas kernels: 109 us -> 125 us  [gather(): pl.pallas_call(functools.partial(gather_kernel, arity, ctx_size, pair_cou...]
    unnamed x48 -> x51, local copies, waits for them, and re-layouts: 20.2 us -> 8.91 us
  transfers between devices with their start and end apart: 8 -> 8, of which waited for: 4 -> 5; matrix products, arithmetic and copies ran while one was open for 17% -> 16% of each run, Pallas kernels for 19% -> 28%
where the time goes in v3:
time: 854 us; the launch traced here: 843 us
  Pallas kernels  404 us (47%)
  waiting for transfers between devices  226 us (26%)
  matrix products  100 us (12%)
  local copies, waits for them, and re-layouts  63.3 us (7%)
  other arithmetic  34.6 us (4%)
  between operations  15.2 us (2%)
    pallas_call x2, Pallas kernels, scatter(): pl.pallas_call(functools.partial(scatter_kernel, arity, ctx_size, pair_co...  177 us
    pallas_call x2, Pallas kernels, gather(): pl.pallas_call(functools.partial(gather_kernel, arity, ctx_size, pair_cou...  125 us
    all_gather x1, waiting for transfers between devices, shards(): lax.all_gather(gate_up_cut.reshape(shard_count * cut, 2 * width), 'ctx',...  77.3 us
    psum x1, waiting for transfers between devices, shards(): down_rows = lax.psum(down_terms, 'ctx')  60.8 us
    all_gather x1, waiting for transfers between devices, shards(): tokens_all = lax.all_gather(normed_two, 'fsdp', axis=0, tiled=True)  43.1 us
    pallas_call x1, Pallas kernels, exchange(): pl.pallas_call(functools.partial(exchange_kernel, shard_count // 2), in_s...  34.1 us
    all_gather x1, waiting for transfers between devices, shards(): lax.all_gather(cotangent.reshape(-1, D), 'fsdp', axis=0, tiled=True)  31.1 us
    pallas_call x1, Pallas kernels, attend_backward(): pl.pallas_call(kernel, grid_spec=pltpu.PrefetchScalarGridSpec(num_scalar_...  28.3 us
  transfers between devices with their start and end apart: 8, of which 5 were waited for; matrix products, arithmetic and copies ran while one was open for 16% of the time, Pallas kernels for 28%

profile of v3, /device:TPU:0, one launch (start us, length us, event | category | flops | bytes accessed | tf_op | source)
XLA Modules:
  0.0 843.0 jit_solution(1757248349565241356)
XLA Ops:
  15.3 58.7 %gather_weights.1 = (bf16[32,48,2048]{2,1,0:T(8,128)(2,1)}, bf16[32,16,128]{2,1,0:T(8,128)(2,1)}, bf16[8,48,2304]{2,1,0:T(8,128)(2,1)}) custom-call(bf16[48,2048]{1,0:T(8,128)(2,1)} %constant_dynamic-slice_fusion.4.refs_0_, bf16[16,128]{1,0:T(8,128)(2,1)} %bitcast.140, bf16[8,48,2304]{2,1,0:T(8,128)(2,1)} %pack.1.refs_2_), custom_call_target="tpu_custom_call" | custom-call | bytes 25690112 | tf_op jit(solution)/shard_map/gather_weights/pallas_call | solution.py:566
  76.0 4.0 convolution_add_fusion.1
  96.2 66.5 %gather_keys.1 = (bf16[32,40,2048]{2,1,0:T(8,128)(2,1)}, bf16[32,48,1536]{2,1,0:T(8,128)(2,1)}) custom-call(bf16[40,2048]{1,0:T(8,128)(2,1)} %reshape.473.refs_0_, bf16[48,1536]{1,0:T(8,128)(2,1)} %constant_dynamic-slice_fusion.refs_1_), custom_call_target="tpu_custom_call" | custom-call | bytes 39845888 | tf_op jit(solution)/shard_map/gather_keys/pallas_call | solution.py:566
  163.2 26.9 %attend_forward.1 = (f32[2,2,2,240,128]{4,3,2,1,0:T(8,128)}, f32[2,2,2,1,240]{4,3,2,1,0:T(1,128)}) custom-call(s32[18]{0:T(128)} %pad_add_fusion.scalars, bf16[2,2,2,240,128]{4,3,2,1,0:T(8,128)(2,1)} %bitcast.117, bf16[1280,2048]{1,0:T(8,128)(2,1)} %bitcast.108), custom_call_target="tpu_custom_call" | custom-call | tf_op jit(solution)/shard_map/attend_forward/pallas_call | solution.py:154
  202.8 43.1 %all-gather.8.cloned.1.call-done = bf16[1280,1536]{1,0:T(8,128)(2,1)} async-done(((bf16[160,1536]{1,0:T(8,128)(2,1)}), bf16[1280,1536]{1,0:T(8,128)(2,1)}) %all-gather.8.cloned.1.call-update) | async-done | bytes 3932176 | tf_op jit(solution)/shard_map/all_gather | solution.py:911
  245.8 77.3 %all-gather.10.cloned.1.call-done = bf16[1536,2304]{1,0:T(8,128)(2,1)} async-done(((bf16[384,2304]{1,0:T(8,128)(2,1)}), bf16[1536,2304]{1,0:T(8,128)(2,1)}) %all-gather.10.cloned.1.call-update) | async-done | bytes 7077904 | tf_op jit(solution)/shard_map/all_gather | solution.py:872
  323.1 15.3 %fusion.29 = f32[1280,2304]{0,1:T(8,128)} fusion(bf16[1280,1536]{1,0:T(8,128)(2,1)} %all-gather.8.cloned.1.call-done, bf16[1536,2304]{1,0:T(8,128)(2,1)} %all-gather.10.cloned.1.call-done), kind=kOutput, calls=%fused_computation.121 | convolution fusion | flops 9059696640 | bytes 22806528 | tf_op jit(solution)/shard_map/dot_general | solution.py:912
  338.4 31.1 %all-gather.6.cloned.1.call-done = bf16[1280,1536]{1,0:T(8,128)(2,1)} async-done(((bf16[160,1536]{1,0:T(8,128)(2,1)}), bf16[1280,1536]{1,0:T(8,128)(2,1)}) %all-gather.6.cloned.1.call-update) | async-done | bytes 3932176 | tf_op jit(solution)/shard_map/all_gather | solution.py:876
  369.5 12.3 %multiply_convert_fusion.2 = (bf16[1280,1152]{0,1:T(8,128)(2,1)S(1)}, bf16[1280,1152]{0,1:T(8,128)(2,1)S(1)}, bf16[1280,1152]{0,1:T(8,128)(2,1)}) fusion(f32[1280,2304]{0,1:T(8,128)} %fusion.29, bf16[1280,1536]{1,0:T(8,128)(2,1)} %all-gather.6.cloned.1.call-done, bf16[1120,1536]{1,0:T(8,128)(2,1)} %param.20), kind=kOutput, calls=%fused_computation.10 | convolution fusion | flops 4551966720 | bytes 28016640 | tf_op jit(solution)/shard_map/dot_general | solution.py:917
  384.4 11.4 %convolution_convert_fusion.5 = bf16[1280,1536]{1,0:T(8,128)(2,1)} fusion(bf16[1536,2304]{1,0:T(8,128)(2,1)S(1)} %copy-done.19, bf16[1280,1152]{0,1:T(8,128)(2,1)S(1)} %get-tuple-element.56, bf16[1280,1152]{0,1:T(8,128)(2,1)S(1)} %get-tuple-element.55), kind=kOutput, calls=%fused_computation.6 | convolution fusion | flops 9073459200 | bytes 16908288 | tf_op jit(solution)/shard_map/dot_general | solution.py:922
  395.9 14.7 %convolution_convert_fusion = bf16[1536,2304]{1,0:T(8,128)(2,1)} fusion(bf16[1280,1536]{1,0:T(8,128)(2,1)} %all-gather.8.cloned.1.call-done, bf16[1280,1152]{0,1:T(8,128)(2,1)} %copy-done.21, bf16[1280,1152]{0,1:T(8,128)(2,1)} %copy-done.20), kind=kOutput, calls=%fused_computation | convolution fusion | flops 9075032064 | bytes 16908288 | tf_op jit(solution)/shard_map/dot_general | solution.py:931
  410.7 9.4 %convolution_convert_fusion.1 = bf16[1280,1536]{1,0:T(8,128)(2,1)} fusion(bf16[1280,1152]{0,1:T(8,128)(2,1)} %get-tuple-element.57, bf16[1120,1536]{1,0:T(8,128)(2,1)} %param.20), kind=kOutput, calls=%fused_computation.2 | convolution fusion | flops 4531814400 | bytes 10321920 | tf_op jit(solution)/shard_map/dot_general | solution.py:934
  420.1 9.6 %convolution_convert_fusion.3 = bf16[1152,1536]{1,0:T(8,128)(2,1)} fusion(bf16[1280,1152]{0,1:T(8,128)(2,1)} %get-tuple-element.57, bf16[1280,1536]{1,0:T(8,128)(2,1)} %all-gather.6.cloned.1.call-done), kind=kOutput, calls=%fused_computation.4 | convolution fusion | flops 4531617792 | bytes 10420224 | tf_op jit(solution)/shard_map/dot_general | solution.py:928
  429.7 12.6 %reduce-scatter.4.cloned.1.call-done = bf16[160,1536]{1,0:T(8,128)(2,1)} async-done(((bf16[1280,1536]{1,0:T(8,128)(2,1)}), bf16[160,1536]{1,0:T(8,128)(2,1)}) %reduce-scatter.4.cloned.1.call-update) | async-done | bytes 491536 | tf_op jit(solution)/shard_map/reduce_scatter | solution.py:925
  452.2 4.8 convolution_convert_fusion.6
  461.7 28.3 %attend_backward.1 = (f32[2,2,2,240,128]{4,3,2,1,0:T(8,128)}, bf16[1280,2048]{1,0:T(8,128)(2,1)}) custom-call(s32[18]{0:T(128)} %pad_add_fusion.scalars, bf16[2,2,2,240,128]{4,3,2,1,0:T(8,128)(2,1)} %bitcast.118, bf16[2,2,2,240,128]{4,3,2,1,0:T(8,128)(2,1)} %bitcast.128, f32[2,2,2,240,128]{4,3,2,1,0:T(8,128)} %get-tuple-element.34.att_ref, ...), custom_call_target="tpu_custom_call" | custom-call | tf_op jit(solution)/shard_map/attend_backward/pallas_call | solution.py:252
  490.1 49.8 %scatter_keys.1 = f32[40,2048]{1,0:T(8,128)} custom-call(bf16[32,40,2048]{2,1,0:T(8,128)(2,1)} %bitcast.116), custom_call_target="tpu_custom_call" | custom-call | bytes 83886080 | tf_op jit(solution)/shard_map/scatter_keys/pallas_call | solution.py:741
  540.0 34.1 %exchange_rows.1 = bf16[8,48,2304]{2,1,0:T(8,128)(2,1)} custom-call(bf16[8,48,2304]{2,1,0:T(8,128)(2,1)} %bitcast.131), custom_call_target="tpu_custom_call" | custom-call | bytes 56623104 | tf_op jit(solution)/shard_map/exchange_rows/pallas_call | solution.py:358
  574.1 60.8 %all-reduce.5.cloned.1.call-done = bf16[1152,1536]{1,0:T(8,128)(2,1)} async-done(((bf16[1152,1536]{1,0:T(8,128)(2,1)}), bf16[1152,1536]{1,0:T(8,128)(2,1)}) %all-reduce.5.cloned.1.call-update) | async-done | bytes 3538960 | tf_op jit(solution)/shard_map/psum | solution.py:935
  662.4 6.9 multiply_reduce_fusion.1
  677.2 4.6 convolution_convert_fusion.2
  681.8 127.6 %scatter_weights.1 = (bf16[4,48,2048]{2,1,0:T(8,128)(2,1)}, bf16[4,48,1536]{2,1,0:T(8,128)(2,1)}, f32[4,8,128]{2,1,0:T(8,128)}) custom-call(bf16[32,48,2048]{2,1,0:T(8,128)(2,1)} %bitcast.104, bf16[32,48,1536]{2,1,0:T(8,128)(2,1)} %bitcast.105, f32[32,8,128]{2,1,0:T(8,128)} %bitcast.136), custom_call_target="tpu_custom_call" | custom-call | bytes 178257920 | tf_op jit(solution)/shard_map/scatter_weights/pallas_call | solution.py:741
  821.0 3.8 slice_convert_fusion
  826.8 8.9 %unpack.1 = (f32[4,48,8960]{2,1,0:T(8,128)}, f32[4,48,8960]{2,1,0:T(8,128)}) custom-call(bf16[4,8,48,2304]{3,2,1,0:T(8,128)(2,1)} %bitcast.112), custom_call_target="tpu_custom_call" | custom-call | tf_op jit(solution)/shard_map/unpack/pallas_call | solution.py:796
  (193 shorter events, 105.3 us)
Async XLA Ops:
  7.2 238.7 %all-gather.8.cloned.1.call-start = ((), (), s32[]{:S(2)}) async-start(), calls=%async_computation.4 | async-start | bytes 4423680 | tf_op jit(solution)/shard_map/all_gather | solution.py:911
  12.2 63.0 %copy-start.4 = (bf16[40,4,1536]{2,1,0:T(4,128)(2,1)S(1)}, bf16[40,4,1536]{2,1,0:T(4,128)(2,1)}, u32[]{:S(2)}) copy-start(bf16[40,4,1536]{2,1,0:T(4,128)(2,1)} %param.11) | copy-start | bytes 1474564
  80.2 2.4 copy-start.15
  80.4 1.9 copy-start.17
  91.6 2.9 copy-start.3
  198.7 3.0 copy-start.13
  201.0 122.2 %all-gather.10.cloned.1.call-start = ((), (), s32[]{:S(2)}) async-start(), calls=%async_computation.5 | async-start | bytes 8847360 | tf_op jit(solution)/shard_map/all_gather | solution.py:872
  201.7 167.8 %all-gather.6.cloned.1.call-start = ((), (), s32[]{:S(2)}) async-start(), calls=%async_computation.3 | async-start | bytes 4423680 | tf_op jit(solution)/shard_map/all_gather | solution.py:876
  202.7 239.6 %reduce-scatter.4.cloned.1.call-start = ((), (), s32[]{:S(2)}) async-start(), calls=%async_computation.6 | async-start | bytes 4423680 | tf_op jit(solution)/shard_map/reduce_scatter | solution.py:925
  369.5 14.9 %copy-start.19 = (bf16[1536,2304]{1,0:T(8,128)(2,1)S(1)}, bf16[1536,2304]{1,0:T(8,128)(2,1)}, u32[]{:S(2)}) copy-start(bf16[1536,2304]{1,0:T(8,128)(2,1)} %all-gather.10.cloned.1.call-done) | copy-start | bytes 21233668
  381.8 2.6 copy-start.21
  395.8 144.1 %reduce-scatter.8.cloned.1.call-start = ((), (), s32[]{:S(2)}) async-start(), calls=%async_computation.8 | async-start | bytes 8847360 | tf_op jit(solution)/shard_map/reduce_scatter | solution.py:936
  410.7 224.3 %all-reduce.5.cloned.1.call-start = ((), (), s32[]{:S(2)}) async-start(), calls=%async_computation.9 | async-start | bytes 7077888 | tf_op jit(solution)/shard_map/psum | solution.py:935
  442.3 382.5 %reduce-scatter.6.cloned.1.call-start = ((), (), s32[]{:S(2)}) async-start(), calls=%async_computation.7 | async-start | bytes 4423680 | tf_op jit(solution)/shard_map/reduce_scatter | solution.py:975
  539.9 95.4 %copy-start.16 = (f32[64]{0:T(128)S(1)}, f32[64]{0:T(128)}, u32[]{:S(2)}) copy-start(f32[64]{0:T(128)} %copy-done.15) | copy-start | bytes 772
  539.9 286.9 %all-gather.12.cloned.1.call-start = ((), (), s32[]{:S(2)}) async-start(), calls=%async_computation.10 | async-start | bytes 8847360 | tf_op jit(solution)/shard_map/all_gather | solution.py:941
  655.5 3.9 copy-start.11
  657.7 2.5 copy-start.9
  673.6 3.6 copy-start.6
  673.6 3.6 copy-start.10
  681.8 129.6 %copy-start.18 = (f32[160]{0:T(256)S(1)}, f32[160]{0:T(256)}, u32[]{:S(2)}) copy-start(f32[160]{0:T(256)} %get-tuple-element.52) | copy-start | bytes 1924
  813.9 5.9 copy-start.12
  816.4 4.6 copy-start.8
  826.8 8.9 %copy-start.1 = (bf16[192,2048]{1,0:T(8,128)(2,1)S(1)}, bf16[192,2048]{1,0:T(8,128)(2,1)}, u32[]{:S(2)}) copy-start(bf16[192,2048]{1,0:T(8,128)(2,1)} %param.14) | copy-start | bytes 2359300
  (6 other events, 7.8 us)
Sparse Core Ops, SparseCore 0:
  201.1 44.6 all-gather.7
  247.7 75.3 all-gather.9
  324.8 44.6 all-gather.5
  396.0 46.3 reduce-scatter.3
  445.2 93.2 reduce-scatter.7
  542.2 92.7 all-reduce.4
  637.8 47.4 reduce-scatter.5
  687.1 124.5 all-gather.11

commit v4 on v3

--- a/solution.py
+++ b/solution.py
@@ -369,16 +369,16 @@
     )(pieces)
 
 
-def gather_kernel(arity, ctx_size, pair_count, slots, swaps, *refs):
+def gather_kernel(arity, ctx_size, pair_count, slots, swaps, with_ctx, *refs):
     sources, refs = refs[:arity], refs[arity:]
     swap_sources, refs = refs[:swaps], refs[swaps:]
     outs, refs = refs[:arity], refs[arity:]
     swap_outs, refs = refs[:swaps], refs[swaps:]
     pair_sems, ctx_sems, core_sems = refs[0:2], refs[2:4], refs[4:6]
     local_sem = refs[6]
-    square, ways = peers_of(ctx_size)
+    square, ways = peers_of(ctx_size) if with_ctx else (False, ())
     near = [way for way in ways if not (square and way == 3)]
-    ctx, pair, core = greet(ctx_size, pair_count, True, swaps > 0)
+    ctx, pair, core = greet(ctx_size, pair_count, with_ctx, swaps > 0)
     homes = [place(ctx, pair * 2 + core) for place in slots]
     started = []
     steps = [(0, 1)] + [(far, way) for far in range(1, pair_count) for way in (1, -1)]
@@ -541,7 +541,7 @@
             when(present(turn - 4), functools.partial(collect_far, turn - 4))
 
     def from_core(step):
-        for way in range(ctx_size):
+        for way in (0, *ways):
             come = ctx_source(ctx, way, square, ctx_size) if way else ctx
             for item in range(arity):
                 arrive(item, slots[item](come, origin(step) * 2 + 1 - core), core_sems, (way, step, item))
@@ -556,7 +556,7 @@
         when(condition(), functools.partial(sent, *which))
 
 
-def gather(pieces, slots, collective_id, name, swaps=()):
+def gather(pieces, slots, collective_id, name, swaps=(), with_ctx=True):
     ctx_size, shard_count = lax.axis_size("ctx"), lax.axis_size("fsdp")
     pair_count = shard_count // 2
     arity = len(pieces)
@@ -564,11 +564,14 @@
     moved = sum(piece.size for piece in pieces) * 2
     steps = 2 * pair_count - 1
     return pl.pallas_call(
-        functools.partial(gather_kernel, arity, ctx_size, pair_count, slots, len(swaps)),
+        functools.partial(gather_kernel, arity, ctx_size, pair_count, slots, len(swaps), with_ctx),
         in_specs=[pl.BlockSpec(memory_space=pltpu.VMEM)] * (arity + len(swaps)),
         out_specs=[pl.BlockSpec(memory_space=pl.ANY)] * (arity + len(swaps)),
         out_shape=[
-            jax.ShapeDtypeStruct((ctx_size * shard_count,) + piece.shape, piece.dtype) for piece in pieces
+            jax.ShapeDtypeStruct(
+                ((ctx_size if with_ctx else 1) * shard_count,) + piece.shape, piece.dtype
+            )
+            for piece in pieces
         ]
         + [jax.ShapeDtypeStruct(swap.shape, swap.dtype) for swap in swaps],
         scratch_shapes=[dma((2, pair_count - 1, arity))] * 2
@@ -584,15 +587,135 @@
     )(*pieces, *swaps)
 
 
-def scatter_kernel(arity, ctx_size, pair_count, slot, spread_ctx, *refs):
-    sources, outs, refs = refs[:arity], refs[arity : 2 * arity], refs[2 * arity :]
+class LineScatter:
+    def __init__(self, source, out, half, above, below, sems, where, pair_count):
+        self.source, self.out, self.half, self.rooms = source, out, half, {1: above, -1: below}
+        self.core_sems, self.line_sems = sems[0:2], {1: sems[2:4], -1: sems[4:6]}
+        self.ctx, self.pair, self.core = where
+        self.count = pair_count
+        self.order = []
+        for turn in range(pair_count - 1):
+            self.order += [(pair_count - 1 - turn, 1), (turn, -1)]
+
+    def copy(self, source, target, device, sems, at):
+        return pltpu.make_async_remote_copy(
+            src_ref=source,
+            dst_ref=target,
+            send_sem=sems[0].at[at],
+            recv_sem=sems[1].at[at],
+            device_id=device,
+            device_id_type=MESH_ID,
+        )
+
+    def here(self):
+        return (self.ctx, self.pair * 2 + self.core)
+
+    def core_copy(self, pair):
+        return self.copy(
+            self.source.at[pair * 2 + 1 - self.core],
+            self.half.at[pair],
+            (self.ctx, self.pair * 2 + 1 - self.core),
+            self.core_sems,
+            pair,
+        )
+
+    def line_copy(self, pair, way):
+        return self.copy(
+            self.half.at[pair],
+            self.rooms[way].at[pair],
+            (self.ctx, (self.pair + way) * 2 + self.core),
+            self.line_sems[way],
+            pair,
+        )
+
+    def line_room(self, pair, way):
+        room = self.rooms[way].at[pair]
+        return self.copy(room, room, self.here(), self.line_sems[way], pair)
+
+    def add(self, pair, value):
+        half = self.half.at[pair]
+        half[...] = (half[...].astype(jnp.float32) + value.astype(jnp.float32)).astype(half.dtype)
+
+    def beyond(self, pair, way):
+        return pair > self.pair if way == 1 else pair < self.pair
+
+    def behind(self, way):
+        return self.pair > 0 if way == 1 else self.pair < self.count - 1
+
+    def start(self):
+        done = []
+        for pair, _ in self.order:
+            if pair not in done:
+                done.append(pair)
+                self.core_copy(pair).start()
+        self.folds = done
+
+    def fold(self):
+        for pair in self.folds:
+            self.copy(
+                self.half.at[pair], self.half.at[pair], self.here(), self.core_sems, pair
+            ).wait_recv()
+            self.add(pair, self.source[pair * 2 + self.core])
+
+    def advance(self, turn):
+        pair, way = self.order[turn]
+
+        @pl.when(self.beyond(pair, way))
+        def pass_on():
+            @pl.when(self.behind(way))
+            def join():
+                self.line_room(pair, way).wait_recv()
+                self.add(pair, self.rooms[way][pair])
+
+            self.line_copy(pair, way).start()
+
+    def finish(self):
+        for pair in range(self.count):
+
+            @pl.when(self.pair == pair)
+            def close(pair=pair):
+                self.out[...] = self.half[pair].astype(jnp.float32)
+                for way in (1, -1):
+
+                    @pl.when(self.behind(way))
+                    def join(way=way):
+                        self.line_room(pair, way).wait_recv()
+                        self.out[...] += self.rooms[way][pair].astype(jnp.float32)
+
+        for pair in range(self.count):
+            self.core_copy(pair).wait_send()
+        for pair, way in self.order:
+
+            @pl.when(self.beyond(pair, way))
+            def sent(pair=pair, way=way):
+                self.line_copy(pair, way).wait_send()
+
+
+def scatter_kernel(arity, ctx_size, pair_count, slot, spread_ctx, lines, *refs):
+    sources, refs = refs[:arity], refs[arity:]
+    line_sources, refs = refs[:lines], refs[lines:]
+    outs, refs = refs[:arity], refs[arity:]
+    line_outs, refs = refs[:lines], refs[lines:]
     halves, relays, asides, ends, finals = (refs[i * arity : (i + 1) * arity] for i in range(5))
-    sems = refs[5 * arity :]
+    sems = refs[5 * arity : 5 * arity + 10]
     core_sems, relay_sems, ctx_sems, pair_sems, last_sems = (sems[2 * i : 2 * i + 2] for i in range(5))
     square, ways = peers_of(ctx_size)
     ctx, pair, core = greet(ctx_size, pair_count, True, False)
     order = list(range(1, pair_count)) + [0]
     started = []
+    flows = []
+    for item in range(lines):
+        at = 5 * arity + 10 + 9 * item
+        flows.append(
+            LineScatter(
+                line_sources[item],
+                line_outs[item],
+                *refs[at : at + 3],
+                refs[at + 3 : at + 9],
+                (ctx, pair, core),
+                pair_count,
+            )
+        )
 
     def send(source, target, device, pair_of_sems, at):
         copy = pltpu.make_async_remote_copy(
@@ -701,13 +824,24 @@
                 else:
                     outs[item][...] = total.astype(outs[item].dtype)
 
+    for flow in flows:
+        flow.start()
+    turns = 2 * (pair_count - 1)
     for turn in range(pair_count + 2):
         if turn < pair_count:
             fold_core(order[turn])
         if 1 <= turn <= pair_count:
             fold_relay(order[turn - 1])
+        for flow in flows:
+            if turn == pair_count - 1:
+                flow.fold()
+                for part in range(2):
+                    flow.advance(part)
         if turn >= 2:
             fold_ctx(order[turn - 2])
+    for flow in flows:
+        for part in range(2, turns):
+            flow.advance(part)
     if spread_ctx:
         for item in range(arity):
             for way in ways:
@@ -722,11 +856,13 @@
         for item in range(arity):
             for way in ways:
                 arrive(outs[item].at[ctx_source(ctx, way, square, ctx_size)], last_sems, (way - 1, item))
+    for flow in flows:
+        flow.finish()
     for copy in started:
         copy.wait_send()
 
 
-def scatter(terms, slot, collective_id, name, spread_ctx=False, out_dtype=None):
+def scatter(terms, slot, collective_id, name, spread_ctx=False, out_dtype=None, lines=()):
     ctx_size, shard_count = lax.axis_size("ctx"), lax.axis_size("fsdp")
     pair_count = shard_count // 2
     arity = len(terms)
@@ -739,12 +875,13 @@
 
     moved = sum(term.size * term.dtype.itemsize for term in terms)
     return pl.pallas_call(
-        functools.partial(scatter_kernel, arity, ctx_size, pair_count, slot, spread_ctx),
-        in_specs=[pl.BlockSpec(memory_space=pltpu.VMEM)] * arity,
-        out_specs=[pl.BlockSpec(memory_space=pltpu.VMEM)] * arity,
+        functools.partial(scatter_kernel, arity, ctx_size, pair_count, slot, spread_ctx, len(lines)),
+        in_specs=[pl.BlockSpec(memory_space=pltpu.VMEM)] * (arity + len(lines)),
+        out_specs=[pl.BlockSpec(memory_space=pltpu.VMEM)] * (arity + len(lines)),
         out_shape=[
             jax.ShapeDtypeStruct(lead + term.shape[1:], out_dtype or term.dtype) for term in terms
-        ],
+        ]
+        + [jax.ShapeDtypeStruct(line.shape[1:], jnp.float32) for line in lines],
         scratch_shapes=room(ctx_size, pair_count)
         + room(pair_count)
         + room(asides, pair_count)
@@ -754,13 +891,19 @@
         + [dma((pair_count, arity))] * 2
         + [dma((ctx_size - 1, pair_count, arity))] * 2
         + [dma((pair_count - 1, arity))] * 2
-        + [dma((ctx_size - 1, arity))] * 2,
+        + [dma((ctx_size - 1, arity))] * 2
+        + [
+            scratch
+            for line in lines
+            for scratch in [pltpu.VMEM((pair_count,) + line.shape[1:], line.dtype)] * 3
+            + [dma((pair_count,))] * 6
+        ],
         compiler_params=pltpu.CompilerParams(
             collective_id=collective_id, has_side_effects=True, vmem_limit_bytes=60 * 2**20
         ),
         cost_estimate=pl.CostEstimate(flops=0, bytes_accessed=moved * 16, transcendentals=0),
         name=name,
-    )(*terms)
+    )(*terms, *lines)
 
 def pack_kernel(columns, gate_ref, up_ref, out_ref):
     width = out_ref.shape[2] // 2
@@ -908,7 +1051,10 @@
     unit_two, scale_two, normed = normalize(middle, gain_two)
     normed_two = mix_features(normed.astype(jnp.bfloat16))
 
-    tokens_all = lax.all_gather(normed_two, "fsdp", axis=0, tiled=True)
+    (tokens_all,) = gather(
+        [normed_two], [lambda ctx, shard: shard], 6, "gather_tokens", with_ctx=False
+    )
+    tokens_all = tokens_all.reshape(-1, D)
     gate_up_part = jnp.dot(tokens_all, gate_up_cols, preferred_element_type=jnp.float32)
     gate_part, up_part = gate_up_part[:, :width], gate_up_part[:, width:]
     sigmoid_gate = jax.nn.sigmoid(gate_part)
@@ -937,7 +1083,6 @@
     gate_up_rows = exchange(
         gate_up_rows.reshape(shard_count, cut, 2 * width), 5, "exchange_rows"
     )
-    gate_up_rows, down_rows = lax.optimization_barrier((gate_up_rows, down_rows))
     gate_up_rows = lax.all_gather(gate_up_rows, "ctx", axis=0, tiled=False)
 
     grad_normed_two, down_terms, gate_up_terms, mixed_terms = lax.optimization_barrier(
@@ -971,11 +1116,6 @@
         "scatter_keys",
         out_dtype=jnp.float32,
     )
-    grad_kv, mixed_terms = lax.optimization_barrier((grad_kv, mixed_terms))
-    mixed_out = middle + lax.psum_scatter(
-        mixed_terms, "fsdp", scatter_dimension=0, tiled=True
-    ).astype(jnp.float32)
-    output = mixed_out.astype(jnp.bfloat16).reshape(rows_here, slots, D)
     grad_kv_low = narrowed(grad_kv).reshape(rows_here, SEQS, KVH, 2, 2, HD)
     grad_kv_low = grad_kv_low.transpose(0, 3, 1, 4, 2, 5).reshape(-1, 2 * kv_width)
     grad_query_tokens = from_groups(narrowed(grad_queries), rows_here) * query_scale
@@ -1006,7 +1146,7 @@
     )
     small_terms = small_terms.reshape(ctx_size * shard_count, small_width)
     small_terms = jnp.pad(small_terms, ((0, 0), (0, 8 * HD - small_width)))
-    qkv_rows, o_rows, small_rows = scatter(
+    qkv_rows, o_rows, small_rows, mixed_rows = scatter(
         [
             qkv_terms.reshape(-1, cut, QKV),
             o_terms.reshape(-1, cut, D),
@@ -1016,7 +1156,10 @@
         4,
         "scatter_weights",
         spread_ctx=True,
-    )
+        lines=[mixed_terms.reshape(shard_count, -1, D)],
+    )
+    mixed_out = middle + mixed_rows
+    output = mixed_out.astype(jnp.bfloat16).reshape(rows_here, slots, D)
     small_rows = small_rows.reshape(ctx_size, -1)[:, :small_width].reshape(-1)
     bias_start = 2 * gain_width
     value_start = bias_start + QK // shard_count

time: 854 us -> 823 us (0.964)
  waiting for transfers between devices: 226 us -> 103 us
  Pallas kernels: 404 us -> 502 us
    pallas_call x2 -> x3, Pallas kernels: 125 us -> 205 us  [gather(): pl.pallas_call(functools.partial(gather_kernel, arity, ctx_size, pair_cou...]
    reduce_scatter x1, waiting for transfers between devices: 0.02 us -> 77.3 us  [shards(): lax.psum_scatter(gate_up_terms, 'ctx', scatter_dimension=0, tiled=True)]
    all_gather x1, waiting for transfers between devices: 77.3 us -> 0.02 us  [shards(): lax.all_gather(gate_up_cut.reshape(shard_count * cut, 2 * width), 'ctx',...]
    psum x1, waiting for transfers between devices: 60.8 us -> 0.01 us  [shards(): down_rows = lax.psum(down_terms, 'ctx')]
    all_gather x1 -> x0, waiting for transfers between devices: 43.1 us -> none  [shards(): tokens_all = lax.all_gather(normed_two, 'fsdp', axis=0, tiled=True)]
    pallas_call x2, Pallas kernels: 177 us -> 210 us  [scatter(): pl.pallas_call(functools.partial(scatter_kernel, arity, ctx_size, pair_co...]
    all_gather x1, waiting for transfers between devices: 31.1 us -> 0.01 us  [shards(): lax.all_gather(cotangent.reshape(-1, D), 'fsdp', axis=0, tiled=True)]
    reduce_scatter x1, waiting for transfers between devices: 12.6 us -> 25.1 us  [shards(): lax.psum_scatter(grad_tokens.astype(jnp.bfloat16), 'fsdp', scatter_dimens...]
  transfers between devices with their start and end apart: 8 -> 6, of which waited for: 5 -> 2; matrix products, arithmetic and copies ran while one was open for 16% -> 19% of each run, Pallas kernels for 28% -> 53%
where the time goes in v4:
time: 823 us; the launch traced here: 810 us
  Pallas kernels  502 us (61%)
  waiting for transfers between devices  103 us (13%)
  matrix products  99.1 us (12%)
  local copies, waits for them, and re-layouts  58.1 us (7%)
  other arithmetic  32.7 us (4%)
  between operations  15.2 us (2%)
    pallas_call x2, Pallas kernels, scatter(): pl.pallas_call(functools.partial(scatter_kernel, arity, ctx_size, pair_co...  210 us
    pallas_call x3, Pallas kernels, gather(): pl.pallas_call(functools.partial(gather_kernel, arity, ctx_size, pair_cou...  205 us
    reduce_scatter x1, waiting for transfers between devices, shards(): lax.psum_scatter(gate_up_terms, 'ctx', scatter_dimension=0, tiled=True)  77.3 us
    pallas_call x1, Pallas kernels, exchange(): pl.pallas_call(functools.partial(exchange_kernel, shard_count // 2), in_s...  33.9 us
    reduce_scatter x1, waiting for transfers between devices, shards(): lax.psum_scatter(grad_tokens.astype(jnp.bfloat16), 'fsdp', scatter_dimens...  25.1 us
    pallas_call x1, Pallas kernels, attend_backward(): pl.pallas_call(kernel, grid_spec=pltpu.PrefetchScalarGridSpec(num_scalar_...  21.4 us
    pallas_call x1, Pallas kernels, attend_forward(): pl.pallas_call(kernel, grid_spec=pltpu.PrefetchScalarGridSpec(num_scalar_...  19.9 us
  transfers between devices with their start and end apart: 6, of which 2 were waited for; matrix products, arithmetic and copies ran while one was open for 19% of the time, Pallas kernels for 53%

profile of v4, /device:TPU:0, one launch (start us, length us, event | category | flops | bytes accessed | tf_op | source)
XLA Modules:
  0.0 810.3 jit_solution(8382516993531888111)
XLA Ops:
  15.3 58.7 %gather_weights.1 = (bf16[32,48,2048]{2,1,0:T(8,128)(2,1)}, bf16[32,16,128]{2,1,0:T(8,128)(2,1)}, bf16[8,48,2304]{2,1,0:T(8,128)(2,1)}) custom-call(bf16[48,2048]{1,0:T(8,128)(2,1)} %constant_dynamic-slice_fusion.4.refs_0_, bf16[16,128]{1,0:T(8,128)(2,1)} %bitcast.145, bf16[8,48,2304]{2,1,0:T(8,128)(2,1)} %pack.1.refs_2_), custom_call_target="tpu_custom_call" | custom-call | bytes 25690112 | tf_op jit(solution)/shard_map/gather_weights/pallas_call | solution.py:566
  77.1 4.0 convolution_add_fusion.1
  110.0 100.7 %gather_keys.1 = (bf16[32,40,2048]{2,1,0:T(8,128)(2,1)}, bf16[32,48,1536]{2,1,0:T(8,128)(2,1)}) custom-call(bf16[40,2048]{1,0:T(8,128)(2,1)} %reshape.479.refs_0_, bf16[48,1536]{1,0:T(8,128)(2,1)} %constant_dynamic-slice_fusion.refs_1_), custom_call_target="tpu_custom_call" | custom-call | bytes 39845888 | tf_op jit(solution)/shard_map/gather_keys/pallas_call | solution.py:566
  211.3 19.9 %attend_forward.1 = (f32[2,2,2,240,128]{4,3,2,1,0:T(8,128)}, f32[2,2,2,1,240]{4,3,2,1,0:T(1,128)}) custom-call(s32[18]{0:T(128)} %pad_add_fusion.scalars, bf16[2,2,2,240,128]{4,3,2,1,0:T(8,128)(2,1)} %bitcast.119, bf16[1280,2048]{1,0:T(8,128)(2,1)} %bitcast.110), custom_call_target="tpu_custom_call" | custom-call | tf_op jit(solution)/shard_map/attend_forward/pallas_call | solution.py:154
  233.3 3.4 multiply_reduce_fusion.4
  242.1 45.3 %gather_tokens.1 = bf16[8,160,1536]{2,1,0:T(8,128)(2,1)} custom-call(bf16[160,1536]{1,0:T(8,128)(2,1)} %copy.128.refs_0_), custom_call_target="tpu_custom_call" | custom-call | bytes 62914560 | tf_op jit(solution)/shard_map/gather_tokens/pallas_call | solution.py:566
  287.5 15.3 %fusion.29 = f32[1280,2304]{0,1:T(8,128)} fusion(bf16[1280,1536]{1,0:T(8,128)(2,1)} %bitcast.125, bf16[1536,2304]{1,0:T(8,128)(2,1)} %all-gather.7.cloned.1.call-done), kind=kOutput, calls=%fused_computation.121 | convolution fusion | flops 9059696640 | bytes 22806528 | tf_op jit(solution)/shard_map/dot_general | solution.py:1058
  302.8 13.2 %multiply_convert_fusion.2 = (bf16[1280,1152]{0,1:T(8,128)(2,1)S(1)}, bf16[1280,1152]{0,1:T(8,128)(2,1)}, bf16[1280,1152]{0,1:T(8,128)(2,1)}) fusion(f32[1280,2304]{0,1:T(8,128)} %fusion.29, bf16[1280,1536]{1,0:T(8,128)(2,1)} %all-gather.5.cloned.1.call-done, bf16[1120,1536]{1,0:T(8,128)(2,1)} %param.20), kind=kOutput, calls=%fused_computation.10 | convolution fusion | flops 4551966720 | bytes 28016640 | tf_op jit(solution)/shard_map/dot_general | solution.py:1063
  317.7 12.3 %convolution_convert_fusion.5 = bf16[1280,1536]{1,0:T(8,128)(2,1)} fusion(bf16[1536,2304]{1,0:T(8,128)(2,1)S(1)} %copy-done.17, bf16[1280,1152]{0,1:T(8,128)(2,1)} %get-tuple-element.50, bf16[1280,1152]{0,1:T(8,128)(2,1)S(1)} %get-tuple-element.49), kind=kOutput, calls=%fused_computation.6 | convolution fusion | flops 9073459200 | bytes 16908288 | tf_op jit(solution)/shard_map/dot_general | solution.py:1068
  330.0 14.9 %convolution_convert_fusion = bf16[1536,2304]{1,0:T(8,128)(2,1)} fusion(bf16[1280,1536]{1,0:T(8,128)(2,1)} %bitcast.126, bf16[1280,1152]{0,1:T(8,128)(2,1)} %get-tuple-element.50, bf16[1280,1152]{0,1:T(8,128)(2,1)} %copy-done.20), kind=kOutput, calls=%fused_computation | convolution fusion | flops 9075032064 | bytes 16908288 | tf_op jit(solution)/shard_map/dot_general | solution.py:1077
  345.0 9.4 %convolution_convert_fusion.1 = bf16[1280,1536]{1,0:T(8,128)(2,1)} fusion(bf16[1280,1152]{0,1:T(8,128)(2,1)} %get-tuple-element.51, bf16[1120,1536]{1,0:T(8,128)(2,1)} %param.20), kind=kOutput, calls=%fused_computation.2 | convolution fusion | flops 4531814400 | bytes 10321920 | tf_op jit(solution)/shard_map/dot_general | solution.py:1080
  354.4 6.3 convolution_convert_fusion.3
  360.7 25.1 %reduce-scatter.3.cloned.1.call-done = bf16[160,1536]{1,0:T(8,128)(2,1)} async-done(((bf16[1280,1536]{1,0:T(8,128)(2,1)}), bf16[160,1536]{1,0:T(8,128)(2,1)}) %reduce-scatter.3.cloned.1.call-update) | async-done | bytes 491536 | tf_op jit(solution)/shard_map/reduce_scatter | solution.py:1071
  386.0 77.3 %reduce-scatter.5.cloned.1.call-done = bf16[384,2304]{1,0:T(8,128)(2,1)} async-done(((bf16[1536,2304]{1,0:T(8,128)(2,1)}), bf16[384,2304]{1,0:T(8,128)(2,1)}) %reduce-scatter.5.cloned.1.call-update) | async-done | bytes 1769488 | tf_op jit(solution)/shard_map/reduce_scatter | solution.py:1082
  463.3 33.9 %exchange_rows.1 = bf16[8,48,2304]{2,1,0:T(8,128)(2,1)} custom-call(bf16[8,48,2304]{2,1,0:T(8,128)(2,1)} %bitcast.136), custom_call_target="tpu_custom_call" | custom-call | bytes 56623104 | tf_op jit(solution)/shard_map/exchange_rows/pallas_call | solution.py:358
  509.9 4.9 convolution_convert_fusion.6
  517.5 21.4 %attend_backward.1 = (f32[2,2,2,240,128]{4,3,2,1,0:T(8,128)}, bf16[1280,2048]{1,0:T(8,128)(2,1)}) custom-call(s32[18]{0:T(128)} %pad_add_fusion.scalars, bf16[2,2,2,240,128]{4,3,2,1,0:T(8,128)(2,1)} %bitcast.120, bf16[2,2,2,240,128]{4,3,2,1,0:T(8,128)(2,1)} %bitcast.133, f32[2,2,2,240,128]{4,3,2,1,0:T(8,128)} %get-tuple-element.31.att_ref, ...), custom_call_target="tpu_custom_call" | custom-call | tf_op jit(solution)/shard_map/attend_backward/pallas_call | solution.py:252
  538.9 70.6 %scatter_keys.1 = f32[40,2048]{1,0:T(8,128)} custom-call(bf16[32,40,2048]{2,1,0:T(8,128)(2,1)} %bitcast.118), custom_call_target="tpu_custom_call" | custom-call | bytes 83886080 | tf_op jit(solution)/shard_map/scatter_keys/pallas_call | solution.py:877
  621.8 6.0 multiply_reduce_fusion
  628.8 4.8 convolution_convert_fusion.4
  633.6 4.6 convolution_convert_fusion.2
  638.2 139.6 %scatter_weights.1 = (bf16[4,48,2048]{2,1,0:T(8,128)(2,1)}, bf16[4,48,1536]{2,1,0:T(8,128)(2,1)}, f32[4,8,128]{2,1,0:T(8,128)}, f32[160,1536]{1,0:T(8,128)}) custom-call(bf16[32,48,2048]{2,1,0:T(8,128)(2,1)} %bitcast.106, bf16[32,48,1536]{2,1,0:T(8,128)(2,1)} %bitcast.107, f32[32,8,128]{2,1,0:T(8,128)} %bitcast.141, bf16[8,160,1536]{2,1,0:T(8,128)(2,1)} %bitcast.123), custom_call_target="tpu_custom_call" | custom-call | bytes 178257920 | tf_op jit(solution)/shard_map/scatter_weights/pallas_call | solution.py:877
  788.2 5.8 slice_convert_fusion
  794.1 8.9 %unpack.1 = (f32[4,48,8960]{2,1,0:T(8,128)}, f32[4,48,8960]{2,1,0:T(8,128)}) custom-call(bf16[4,8,48,2304]{3,2,1,0:T(8,128)(2,1)} %bitcast.114), custom_call_target="tpu_custom_call" | custom-call | tf_op jit(solution)/shard_map/unpack/pallas_call | solution.py:939
  (186 shorter events, 88.7 us)
Async XLA Ops:
  7.2 1.6 copy-start
  7.2 280.3 %all-gather.7.cloned.1.call-start = ((), (), s32[]{:S(2)}) async-start(), calls=%async_computation.3 | async-start | bytes 8847360 | tf_op jit(solution)/shard_map/all_gather | solution.py:1015
  12.2 61.9 %copy-start.11 = (bf16[40,4,1536]{2,1,0:T(4,128)(2,1)S(1)}, bf16[40,4,1536]{2,1,0:T(4,128)(2,1)}, u32[]{:S(2)}) copy-start(bf16[40,4,1536]{2,1,0:T(4,128)(2,1)} %param.21) | copy-start | bytes 1474564
  15.3 61.0 %copy-start.6 = (bf16[40,4,1536]{2,1,0:T(4,128)(2,1)S(1)}, bf16[40,4,1536]{2,1,0:T(4,128)(2,1)}, u32[]{:S(2)}) copy-start(bf16[40,4,1536]{2,1,0:T(4,128)(2,1)} %param.11) | copy-start | bytes 1474564
  74.1 228.7 %all-gather.5.cloned.1.call-start = ((), (), s32[]{:S(2)}) async-start(), calls=%async_computation.2 | async-start | bytes 4423680 | tf_op jit(solution)/shard_map/all_gather | solution.py:1019
  75.1 310.6 %reduce-scatter.3.cloned.1.call-start = ((), (), s32[]{:S(2)}) async-start(), calls=%async_computation.4 | async-start | bytes 4423680 | tf_op jit(solution)/shard_map/reduce_scatter | solution.py:1071
  76.7 4.5 copy-start.14
  82.2 7.6 copy-start.16
  91.4 2.0 copy-start.4
  94.7 7.6 copy-start.3
  302.8 14.8 %copy-start.17 = (bf16[1536,2304]{1,0:T(8,128)(2,1)S(1)}, bf16[1536,2304]{1,0:T(8,128)(2,1)}, u32[]{:S(2)}) copy-start(bf16[1536,2304]{1,0:T(8,128)(2,1)} %all-gather.7.cloned.1.call-done) | copy-start | bytes 21233668
  316.1 1.6 copy-start.20
  330.0 133.3 %reduce-scatter.5.cloned.1.call-start = ((), (), s32[]{:S(2)}) async-start(), calls=%async_computation.5 | async-start | bytes 8847360 | tf_op jit(solution)/shard_map/reduce_scatter | solution.py:1082
  344.9 443.3 %all-reduce.5.cloned.1.call-start = ((), (), s32[]{:S(2)}) async-start(), calls=%async_computation.6 | async-start | bytes 7077888 | tf_op jit(solution)/shard_map/psum | solution.py:1081
  345.0 9.4 %copy-start.18 = (bf16[1280,1536]{1,0:T(8,128)(2,1)S(1)}, bf16[1280,1536]{1,0:T(8,128)(2,1)}, u32[]{:S(2)}) copy-start(bf16[1280,1536]{1,0:T(8,128)(2,1)} %all-gather.5.cloned.1.call-done) | copy-start | bytes 11796484
  345.0 9.4 %copy-start.19 = (bf16[1280,1152]{0,1:T(8,128)(2,1)S(1)}, bf16[1280,1152]{0,1:T(8,128)(2,1)}, u32[]{:S(2)}) copy-start(bf16[1280,1152]{0,1:T(8,128)(2,1)} %get-tuple-element.51) | copy-start | bytes 8847364
  385.7 111.6 %copy-start.15 = (f32[40,4]{1,0:T(8,128)S(1)}, f32[40,4]{1,0:T(8,128)}, u32[]{:S(2)}) copy-start(f32[40,4]{1,0:T(8,128)} %copy-done.14) | copy-start | bytes 1924
  385.7 113.1 %copy-start.12 = (bf16[160,1536]{1,0:T(8,128)(2,1)S(1)}, bf16[160,1536]{1,0:T(8,128)(2,1)}, u32[]{:S(2)}) copy-start(bf16[160,1536]{1,0:T(8,128)(2,1)} %reduce-scatter.3.cloned.1.call-done) | copy-start | bytes 1474564
  385.8 408.3 %all-gather.9.cloned.1.call-start = ((), (), s32[]{:S(2)}) async-start(), calls=%async_computation.7 | async-start | bytes 8847360 | tf_op jit(solution)/shard_map/all_gather | solution.py:1086
  500.3 7.1 copy-start.7
  617.1 2.5 copy-start.13
  781.0 4.6 copy-start.9
  782.0 5.1 copy-start.10
  794.1 8.9 %copy-start.1 = (bf16[192,2048]{1,0:T(8,128)(2,1)S(1)}, bf16[192,2048]{1,0:T(8,128)(2,1)}, u32[]{:S(2)}) copy-start(bf16[192,2048]{1,0:T(8,128)(2,1)} %param.14) | copy-start | bytes 2359300
  (3 other events, 3.2 us)
Sparse Core Ops, SparseCore 0:
  74.2 128.0 all-gather.6
  204.0 47.5 all-gather.4
  330.1 55.5 reduce-scatter.2
  388.6 74.6 reduce-scatter.4
  466.4 95.4 all-reduce.4
  563.5 94.3 all-gather.8

commit v5 on v4

--- a/solution.py
+++ b/solution.py
@@ -289,7 +289,6 @@
     shard = lax.axis_index("fsdp")
     pair, core = shard // 2, shard % 2
     barrier = pltpu.get_barrier_semaphore()
-    shard_count = 2 * pair_count
     partners = [(ctx, pair * 2 + 1 - core)]
     for step in range(1, pair_count):
         there = lax.rem(pair + step, pair_count) * 2
@@ -352,7 +351,7 @@
     flow.finish()
 
 
-def exchange(pieces, collective_id, name):
+def exchange(pieces, collective_id):
     shard_count = lax.axis_size("fsdp")
     dma = pltpu.SemaphoreType.DMA
     return pl.pallas_call(
@@ -365,7 +364,6 @@
         cost_estimate=pl.CostEstimate(
             flops=0, bytes_accessed=pieces.size * 64, transcendentals=0
         ),
-        name=name,
     )(pieces)
 
 
@@ -556,7 +554,7 @@
         when(condition(), functools.partial(sent, *which))
 
 
-def gather(pieces, slots, collective_id, name, swaps=(), with_ctx=True):
+def gather(pieces, slots, collective_id, swaps=(), with_ctx=True):
     ctx_size, shard_count = lax.axis_size("ctx"), lax.axis_size("fsdp")
     pair_count = shard_count // 2
     arity = len(pieces)
@@ -583,13 +581,14 @@
         cost_estimate=pl.CostEstimate(
             flops=0, bytes_accessed=moved * ctx_size * shard_count * 4, transcendentals=0
         ),
-        name=name,
     )(*pieces, *swaps)
 
 
 class LineScatter:
-    def __init__(self, source, out, half, above, below, sems, where, pair_count):
+    def __init__(self, source, out, half, above, below, sems, where, counts, last):
+        pair_count, self.ctx_size = counts
         self.source, self.out, self.half, self.rooms = source, out, half, {1: above, -1: below}
+        self.last = last
         self.core_sems, self.line_sems = sems[0:2], {1: sems[2:4], -1: sems[4:6]}
         self.ctx, self.pair, self.core = where
         self.count = pair_count
@@ -669,6 +668,35 @@
 
             self.line_copy(pair, way).start()
 
+    def over_ctx(self, terms, room, landing, *sems):
+        shard = self.pair * 2 + self.core
+        copies = []
+
+        def send(source, target, way, sems):
+            there = lax.rem(self.ctx + way, self.ctx_size)
+            copies.append(self.copy(source(there), target, (there, shard), sems, way - 1))
+            copies[-1].start()
+
+        def arrive(target, way, sems):
+            self.copy(target, target, self.here(), sems, way - 1).wait_recv()
+
+        terms[...] = self.out[...].astype(terms.dtype)
+        for way in range(1, self.ctx_size):
+            send(lambda there: terms.at[there], room.at[way - 1], way, sems[0:2])
+        total = self.out[self.ctx]
+        for way in range(1, self.ctx_size):
+            arrive(room.at[way - 1], way, sems[0:2])
+            total = total + room[way - 1].astype(jnp.float32)
+        landing[self.ctx] = total.astype(landing.dtype)
+        for way in range(1, self.ctx_size):
+            send(lambda there: landing.at[self.ctx], landing.at[self.ctx], way, sems[2:4])
+        for way in range(1, self.ctx_size):
+            come = lax.rem(self.ctx + self.ctx_size - way, self.ctx_size)
+            arrive(landing.at[come], way, sems[2:4])
+        self.out[...] = landing[...].astype(jnp.float32)
+        for copy in copies:
+            copy.wait_send()
+
     def finish(self):
         for pair in range(self.count):
 
@@ -682,6 +710,8 @@
                         self.line_room(pair, way).wait_recv()
                         self.out[...] += self.rooms[way][pair].astype(jnp.float32)
 
+        if self.last:
+            self.over_ctx(*self.last)
         for pair in range(self.count):
             self.core_copy(pair).wait_send()
         for pair, way in self.order:
@@ -705,7 +735,8 @@
     started = []
     flows = []
     for item in range(lines):
-        at = 5 * arity + 10 + 9 * item
+        at = 5 * arity + 10 + 16 * item
+        spread = len(line_sources[item].shape) == 4
         flows.append(
             LineScatter(
                 line_sources[item],
@@ -713,7 +744,8 @@
                 *refs[at : at + 3],
                 refs[at + 3 : at + 9],
                 (ctx, pair, core),
-                pair_count,
+                (pair_count, ctx_size),
+                refs[at + 9 : at + 16] if spread else (),
             )
         )
 
@@ -862,7 +894,7 @@
         copy.wait_send()
 
 
-def scatter(terms, slot, collective_id, name, spread_ctx=False, out_dtype=None, lines=()):
+def scatter(terms, slot, collective_id, spread_ctx=False, out_dtype=None, lines=()):
     ctx_size, shard_count = lax.axis_size("ctx"), lax.axis_size("fsdp")
     pair_count = shard_count // 2
     arity = len(terms)
@@ -872,6 +904,13 @@
 
     def room(*extent):
         return [pltpu.VMEM(extent + term.shape[1:], term.dtype) for term in terms]
+
+    def line_room(line):
+        if len(line.shape) == 3:
+            return [pltpu.VMEM((8, HD), line.dtype)] * 3 + [dma((1,))] * 4
+        cut = line.shape[2:]
+        rooms = [pltpu.VMEM((count,) + cut, line.dtype) for count in (ctx_size, ctx_size - 1, ctx_size)]
+        return rooms + [dma((ctx_size - 1,))] * 4
 
     moved = sum(term.size * term.dtype.itemsize for term in terms)
     return pl.pallas_call(
@@ -897,13 +936,14 @@
             for line in lines
             for scratch in [pltpu.VMEM((pair_count,) + line.shape[1:], line.dtype)] * 3
             + [dma((pair_count,))] * 6
+            + line_room(line)
         ],
         compiler_params=pltpu.CompilerParams(
-            collective_id=collective_id, has_side_effects=True, vmem_limit_bytes=60 * 2**20
+            collective_id=collective_id, has_side_effects=True, vmem_limit_bytes=63 * 2**20
         ),
         cost_estimate=pl.CostEstimate(flops=0, bytes_accessed=moved * 16, transcendentals=0),
-        name=name,
     )(*terms, *lines)
+
 
 def pack_kernel(columns, gate_ref, up_ref, out_ref):
     width = out_ref.shape[2] // 2
@@ -996,14 +1036,14 @@
     small = lax.dynamic_slice_in_dim(small, own_ctx, 1, 0)
     small = jnp.pad(small, ((0, 0), (0, 16 * HD - small_width))).reshape(16, HD)
     width = -(-columns // HD) * HD
-    w_qkv_all, small_all, gate_up_cut = gather(
-        [own_cut(w_qkv), small],
-        [by_rows, by_rows],
+    w_qkv_all, w_o_all, small_all, gate_up_cut = gather(
+        [own_cut(w_qkv), own_cut(w_o), small],
+        [by_rows, by_rows, by_rows],
         1,
-        "gather_weights",
         swaps=[pack(own_cut(w_gate), own_cut(w_up), shard_count, columns, width)],
     )
     w_qkv_all = w_qkv_all.reshape(D, QKV)
+    w_o_all = w_o_all.reshape(D, D)
     small_all = small_all.reshape(shard_count, ctx_size, -1)[:, :, :small_width]
     small_all = small_all.reshape(shard_count, -1).astype(jnp.float32)
     bias_width = QKV // shard_count
@@ -1036,8 +1076,7 @@
     own_kv = jnp.stack([key_tokens, value_raw.astype(jnp.bfloat16)], 1)
     own_kv = own_kv.reshape(rows_here, 2, SEQS, 2, KVH, HD).transpose(0, 2, 4, 1, 3, 5)
     own_kv = own_kv.reshape(rows_here, SEQS * KVH * 4 * HD)
-    all_kv, w_o_all = gather([own_kv, own_cut(w_o)], [by_tokens, by_rows], 2, "gather_keys")
-    w_o_all = w_o_all.reshape(D, D)
+    (all_kv,) = gather([own_kv], [by_tokens], 2)
     all_kv = all_kv.reshape(-1, SEQS * KVH * 4 * HD)
     queries = to_groups(query_tokens, rows_here)
     scalars = jnp.concatenate(
@@ -1051,9 +1090,7 @@
     unit_two, scale_two, normed = normalize(middle, gain_two)
     normed_two = mix_features(normed.astype(jnp.bfloat16))
 
-    (tokens_all,) = gather(
-        [normed_two], [lambda ctx, shard: shard], 6, "gather_tokens", with_ctx=False
-    )
+    (tokens_all,) = gather([normed_two], [lambda ctx, shard: shard], 6, with_ctx=False)
     tokens_all = tokens_all.reshape(-1, D)
     gate_up_part = jnp.dot(tokens_all, gate_up_cols, preferred_element_type=jnp.float32)
     gate_part, up_part = gate_up_part[:, :width], gate_up_part[:, width:]
@@ -1080,11 +1117,6 @@
     mixed_terms = jnp.dot(hidden, down_padded, preferred_element_type=jnp.float32).astype(jnp.bfloat16)
     down_rows = lax.psum(down_terms, "ctx")
     gate_up_rows = lax.psum_scatter(gate_up_terms, "ctx", scatter_dimension=0, tiled=True)
-    gate_up_rows = exchange(
-        gate_up_rows.reshape(shard_count, cut, 2 * width), 5, "exchange_rows"
-    )
-    gate_up_rows = lax.all_gather(gate_up_rows, "ctx", axis=0, tiled=False)
-
     grad_normed_two, down_terms, gate_up_terms, mixed_terms = lax.optimization_barrier(
         (grad_normed_two, down_terms, gate_up_terms, mixed_terms)
     )
@@ -1109,13 +1141,18 @@
         block_rows,
         rows_here,
     )
-    (grad_kv,) = scatter(
+    grad_kv, mixed_rows = scatter(
         [grad_kv_full.reshape(-1, rows_here, SEQS * KVH * 4 * HD)],
         by_tokens,
         3,
-        "scatter_keys",
         out_dtype=jnp.float32,
-    )
+        lines=[mixed_terms.reshape(shard_count, -1, D)],
+    )
+    gate_up_rows, grad_kv = lax.optimization_barrier((gate_up_rows, grad_kv))
+    gate_up_rows = exchange(gate_up_rows.reshape(shard_count, cut, 2 * width), 5)
+    gate_up_rows = lax.all_gather(gate_up_rows, "ctx", axis=0, tiled=False)
+    mixed_out = middle + mixed_rows
+    output = mixed_out.astype(jnp.bfloat16).reshape(rows_here, slots, D)
     grad_kv_low = narrowed(grad_kv).reshape(rows_here, SEQS, KVH, 2, 2, HD)
     grad_kv_low = grad_kv_low.transpose(0, 3, 1, 4, 2, 5).reshape(-1, 2 * kv_width)
     grad_query_tokens = from_groups(narrowed(grad_queries), rows_here) * query_scale
@@ -1146,20 +1183,16 @@
     )
     small_terms = small_terms.reshape(ctx_size * shard_count, small_width)
     small_terms = jnp.pad(small_terms, ((0, 0), (0, 8 * HD - small_width)))
-    qkv_rows, o_rows, small_rows, mixed_rows = scatter(
+    qkv_rows, small_rows, o_rows = scatter(
         [
             qkv_terms.reshape(-1, cut, QKV),
-            o_terms.reshape(-1, cut, D),
             small_terms.reshape(-1, 8, HD),
         ],
         by_rows,
         4,
-        "scatter_weights",
         spread_ctx=True,
-        lines=[mixed_terms.reshape(shard_count, -1, D)],
-    )
-    mixed_out = middle + mixed_rows
-    output = mixed_out.astype(jnp.bfloat16).reshape(rows_here, slots, D)
+        lines=[o_terms.reshape(shard_count, ctx_size, cut, D)],
+    )
     small_rows = small_rows.reshape(ctx_size, -1)[:, :small_width].reshape(-1)
     bias_start = 2 * gain_width
     value_start = bias_start + QK // shard_count
@@ -1172,7 +1205,7 @@
         qkv_rows.reshape(-1, QKV).astype(jnp.float32),
         small_rows[bias_start:value_start],
         small_rows[value_start:],
-        o_rows.reshape(-1, D).astype(jnp.float32),
+        o_rows.reshape(-1, D),
         small_rows[gain_width:bias_start],
         gate_rows.reshape(-1, FF),
         up_rows.reshape(-1, FF),

time: 823 us -> 778 us (0.945)
  the two profiles are of different devices: /device:TPU:0 before, /device:TPU:14 now
where the time goes in v5:
time: 778 us; the launch traced here: 771 us
  Pallas kernels  565 us (73%)
  matrix products  97.9 us (13%)
  local copies, waits for them, and re-layouts  41.5 us (5%)
  other arithmetic  26 us (3%)
  waiting for transfers between devices  25.6 us (3%)
  between operations  15.4 us (2%)
    pallas_call x2, Pallas kernels, scatter(): pl.pallas_call(functools.partial(scatter_kernel, arity, ctx_size, pair_co...  276 us
    pallas_call x3, Pallas kernels, gather(): pl.pallas_call(functools.partial(gather_kernel, arity, ctx_size, pair_cou...  201 us
    pallas_call x1, Pallas kernels, exchange(): pl.pallas_call(functools.partial(exchange_kernel, shard_count // 2), in_s...  42.7 us
    reduce_scatter x1, waiting for transfers between devices, shards(): lax.psum_scatter(grad_tokens.astype(jnp.bfloat16), 'fsdp', scatter_dimens...  25.5 us
    pallas_call x1, Pallas kernels, attend_backward(): pl.pallas_call(kernel, grid_spec=pltpu.PrefetchScalarGridSpec(num_scalar_...  17.4 us
    pallas_call x1, Pallas kernels, attend_forward(): pl.pallas_call(kernel, grid_spec=pltpu.PrefetchScalarGridSpec(num_scalar_...  15.8 us
    dot_general x1, matrix products, shards(): jnp.dot(tokens_all, gate_up_cols, preferred_element_type=jnp.float32)  15.6 us
  transfers between devices with their start and end apart: 6, of which 1 were waited for; matrix products, arithmetic and copies ran while one was open for 17% of the time, Pallas kernels for 60%

profile of v5, /device:TPU:14, one launch (start us, length us, event | category | flops | bytes accessed | tf_op | source)
XLA Modules:
  0.0 771.4 jit_solution(6272424829587992189)
XLA Ops:
  14.8 3.1 pack.1.refs_3_
  17.9 87.3 %shard_map.194 = (bf16[32,48,2048]{2,1,0:T(8,128)(2,1)}, bf16[32,48,1536]{2,1,0:T(8,128)(2,1)}, bf16[32,16,128]{2,1,0:T(8,128)(2,1)}, bf16[8,48,2304]{2,1,0:T(8,128)(2,1)}) custom-call(bf16[48,2048]{1,0:T(8,128)(2,1)} %constant_dynamic-slice_fusion.4.refs_0_, bf16[48,1536]{1,0:T(8,128)(2,1)} %constant_dynamic-slice_fusion.3.refs_1_, ...), custom_call_target="tpu_custom_call" | custom-call | bytes 44564480 | tf_op jit(solution)/shard_map/pallas_call | solution.py:564
  109.1 4.0 convolution_add_fusion.1
  119.7 44.0 %shard_map.195 = bf16[32,40,2048]{2,1,0:T(8,128)(2,1)} custom-call(bf16[40,2048]{1,0:T(8,128)(2,1)} %reshape.479.refs_0_), custom_call_target="tpu_custom_call" | custom-call | bytes 20971520 | tf_op jit(solution)/shard_map/pallas_call | solution.py:564
  173.9 15.8 %attend_forward.1 = (f32[2,2,2,240,128]{4,3,2,1,0:T(8,128)}, f32[2,2,2,1,240]{4,3,2,1,0:T(1,128)}) custom-call(s32[18]{0:T(128)} %pad_add_fusion.scalars, bf16[2,2,2,240,128]{4,3,2,1,0:T(8,128)(2,1)} %bitcast.117, bf16[1280,2048]{1,0:T(8,128)(2,1)} %bitcast.104), custom_call_target="tpu_custom_call" | custom-call | tf_op jit(solution)/shard_map/attend_forward/pallas_call | solution.py:154
  191.8 3.5 multiply_reduce_fusion.4
  196.8 69.9 %shard_map.196 = bf16[8,160,1536]{2,1,0:T(8,128)(2,1)} custom-call(bf16[160,1536]{1,0:T(8,128)(2,1)} %copy.128.refs_0_), custom_call_target="tpu_custom_call" | custom-call | bytes 62914560 | tf_op jit(solution)/shard_map/pallas_call | solution.py:564
  266.8 15.6 %fusion.29 = f32[1280,2304]{0,1:T(8,128)} fusion(bf16[1280,1536]{1,0:T(8,128)(2,1)} %bitcast.123, bf16[1536,2304]{1,0:T(8,128)(2,1)} %all-gather.7.cloned.1.call-done), kind=kOutput, calls=%fused_computation.120 | convolution fusion | flops 9059696640 | bytes 22806528 | tf_op jit(solution)/shard_map/dot_general | solution.py:1095
  282.4 12.3 %multiply_convert_fusion.2 = (bf16[1280,1152]{0,1:T(8,128)(2,1)S(1)}, bf16[1280,1152]{0,1:T(8,128)(2,1)S(1)}, bf16[1280,1152]{0,1:T(8,128)(2,1)}) fusion(f32[1280,2304]{0,1:T(8,128)} %fusion.29, bf16[1280,1536]{1,0:T(8,128)(2,1)} %all-gather.5.cloned.1.call-done, bf16[1120,1536]{1,0:T(8,128)(2,1)} %param.20), kind=kOutput, calls=%fused_computation.10 | convolution fusion | flops 4551966720 | bytes 28016640 | tf_op jit(solution)/shard_map/dot_general | solution.py:1100
  297.3 11.5 %convolution_convert_fusion.5 = bf16[1280,1536]{1,0:T(8,128)(2,1)} fusion(bf16[1536,2304]{1,0:T(8,128)(2,1)S(1)} %copy-done.27, bf16[1280,1152]{0,1:T(8,128)(2,1)S(1)} %get-tuple-element.54, bf16[1280,1152]{0,1:T(8,128)(2,1)S(1)} %get-tuple-element.53), kind=kOutput, calls=%fused_computation.6 | convolution fusion | flops 9073459200 | bytes 16908288 | tf_op jit(solution)/shard_map/dot_general | solution.py:1105
  308.8 14.7 %convolution_convert_fusion = bf16[1536,2304]{1,0:T(8,128)(2,1)} fusion(bf16[1280,1536]{1,0:T(8,128)(2,1)} %bitcast.124, bf16[1280,1152]{0,1:T(8,128)(2,1)} %copy-done.31, bf16[1280,1152]{0,1:T(8,128)(2,1)} %copy-done.30), kind=kOutput, calls=%fused_computation | convolution fusion | flops 9075032064 | bytes 16908288 | tf_op jit(solution)/shard_map/dot_general | solution.py:1114
  323.7 9.5 %convolution_convert_fusion.1 = bf16[1280,1536]{1,0:T(8,128)(2,1)} fusion(bf16[1280,1152]{0,1:T(8,128)(2,1)} %get-tuple-element.55, bf16[1120,1536]{1,0:T(8,128)(2,1)} %param.20), kind=kOutput, calls=%fused_computation.2 | convolution fusion | flops 4531814400 | bytes 10321920 | tf_op jit(solution)/shard_map/dot_general | solution.py:1117
  333.2 6.2 convolution_convert_fusion.3
  339.4 25.5 %reduce-scatter.3.cloned.1.call-done = bf16[160,1536]{1,0:T(8,128)(2,1)} async-done(((bf16[1280,1536]{1,0:T(8,128)(2,1)}), bf16[160,1536]{1,0:T(8,128)(2,1)}) %reduce-scatter.3.cloned.1.call-update) | async-done | bytes 491536 | tf_op jit(solution)/shard_map/reduce_scatter | solution.py:1108
  371.5 4.3 convolution_convert_fusion.6
  377.4 17.4 %attend_backward.1 = (f32[2,2,2,240,128]{4,3,2,1,0:T(8,128)}, bf16[1280,2048]{1,0:T(8,128)(2,1)}) custom-call(s32[18]{0:T(128)} %pad_add_fusion.scalars, bf16[2,2,2,240,128]{4,3,2,1,0:T(8,128)(2,1)} %bitcast.118, bf16[2,2,2,240,128]{4,3,2,1,0:T(8,128)(2,1)} %bitcast.131, f32[2,2,2,240,128]{4,3,2,1,0:T(8,128)} %get-tuple-element.32.att_ref, ...), custom_call_target="tpu_custom_call" | custom-call | tf_op jit(solution)/shard_map/attend_backward/pallas_call | solution.py:252
  394.8 127.6 %shard_map.197 = (f32[40,2048]{1,0:T(8,128)}, f32[160,1536]{1,0:T(8,128)}) custom-call(bf16[32,40,2048]{2,1,0:T(8,128)(2,1)} %bitcast.116, bf16[8,160,1536]{2,1,0:T(8,128)(2,1)} %bitcast.122), custom_call_target="tpu_custom_call" | custom-call | bytes 83886080 | tf_op jit(solution)/shard_map/pallas_call | solution.py:916
  522.5 42.7 %shard_map.199 = bf16[8,48,2304]{2,1,0:T(8,128)(2,1)} custom-call(bf16[8,48,2304]{2,1,0:T(8,128)(2,1)} %bitcast.134), custom_call_target="tpu_custom_call" | custom-call | bytes 56623104 | tf_op jit(solution)/shard_map/pallas_call | solution.py:357
  573.1 5.0 convolution_convert_fusion.4
  578.9 5.9 slice_convert_fusion
  586.2 6.6 multiply_reduce_fusion.1
  593.8 4.6 convolution_convert_fusion.2
  598.4 148.0 %shard_map.198 = (bf16[4,48,2048]{2,1,0:T(8,128)(2,1)}, f32[4,8,128]{2,1,0:T(8,128)}, f32[4,48,1536]{2,1,0:T(8,128)}) custom-call(bf16[32,48,2048]{2,1,0:T(8,128)(2,1)} %bitcast.106, f32[32,8,128]{2,1,0:T(8,128)} %bitcast.140, bf16[8,4,48,1536]{3,2,1,0:T(8,128)(2,1)} %bitcast.107), custom_call_target="tpu_custom_call" | custom-call | bytes 102760448 | tf_op jit(solution)/shard_map/pallas_call | solution.py:916
  754.2 8.9 %unpack.1 = (f32[4,48,8960]{2,1,0:T(8,128)}, f32[4,48,8960]{2,1,0:T(8,128)}) custom-call(bf16[4,8,48,2304]{3,2,1,0:T(8,128)(2,1)} %bitcast.112), custom_call_target="tpu_custom_call" | custom-call | tf_op jit(solution)/shard_map/unpack/pallas_call | solution.py:979
  (208 shorter events, 62.1 us)
Async XLA Ops:
  7.2 259.6 %all-gather.7.cloned.1.call-start = ((), (), s32[]{:S(2)}) async-start(), calls=%async_computation.3 | async-start | bytes 8847360 | tf_op jit(solution)/shard_map/all_gather | solution.py:1055
  14.8 90.5 %copy-start.13 = (bf16[40,4,1536]{2,1,0:T(4,128)(2,1)S(1)}, bf16[40,4,1536]{2,1,0:T(4,128)(2,1)}, u32[]{:S(2)}) copy-start(bf16[40,4,1536]{2,1,0:T(4,128)(2,1)} %param.21) | copy-start | bytes 1474564
  17.9 89.6 %copy-start.8 = (bf16[40,4,1536]{2,1,0:T(4,128)(2,1)S(1)}, bf16[40,4,1536]{2,1,0:T(4,128)(2,1)}, u32[]{:S(2)}) copy-start(bf16[40,4,1536]{2,1,0:T(4,128)(2,1)} %param.11) | copy-start | bytes 1474564
  105.2 177.1 %all-gather.5.cloned.1.call-start = ((), (), s32[]{:S(2)}) async-start(), calls=%async_computation.2 | async-start | bytes 4423680 | tf_op jit(solution)/shard_map/all_gather | solution.py:1059
  106.2 258.7 %reduce-scatter.3.cloned.1.call-start = ((), (), s32[]{:S(2)}) async-start(), calls=%async_computation.4 | async-start | bytes 4423680 | tf_op jit(solution)/shard_map/reduce_scatter | solution.py:1108
  115.0 76.8 %copy-start.2 = (f32[160,1536]{1,0:T(8,128)}, f32[160,1536]{1,0:T(8,128)S(1)}, u32[]{:S(2)}) copy-start(f32[160,1536]{1,0:T(8,128)S(1)} %reshape.515) | copy-start | bytes 2949124
  165.6 5.0 copy-start.7
  282.4 14.9 %copy-start.27 = (bf16[1536,2304]{1,0:T(8,128)(2,1)S(1)}, bf16[1536,2304]{1,0:T(8,128)(2,1)}, u32[]{:S(2)}) copy-start(bf16[1536,2304]{1,0:T(8,128)(2,1)} %all-gather.7.cloned.1.call-done) | copy-start | bytes 21233668
  308.8 213.7 %reduce-scatter.5.cloned.1.call-start = ((), (), s32[]{:S(2)}) async-start(), calls=%async_computation.5 | async-start | bytes 8847360 | tf_op jit(solution)/shard_map/reduce_scatter | solution.py:1119
  323.6 255.3 %all-reduce.5.cloned.1.call-start = ((), (), s32[]{:S(2)}) async-start(), calls=%async_computation.6 | async-start | bytes 7077888 | tf_op jit(solution)/shard_map/psum | solution.py:1118
  323.6 9.6 %copy-start.28 = (bf16[1280,1536]{1,0:T(8,128)(2,1)S(1)}, bf16[1280,1536]{1,0:T(8,128)(2,1)}, u32[]{:S(2)}) copy-start(bf16[1280,1536]{1,0:T(8,128)(2,1)} %all-gather.5.cloned.1.call-done) | copy-start | bytes 11796484
  323.7 9.5 %copy-start.29 = (bf16[1280,1152]{0,1:T(8,128)(2,1)S(1)}, bf16[1280,1152]{0,1:T(8,128)(2,1)}, u32[]{:S(2)}) copy-start(bf16[1280,1152]{0,1:T(8,128)(2,1)} %get-tuple-element.55) | copy-start | bytes 8847364
  364.9 389.3 %all-gather.9.cloned.1.call-start = ((), (), s32[]{:S(2)}) async-start(), calls=%async_computation.7 | async-start | bytes 8847360 | tf_op jit(solution)/shard_map/all_gather | solution.py:1153
  366.2 4.0 copy-start.9
  522.4 42.8 %copy-start.20 = (f32[40,4]{1,0:T(8,128)S(1)}, f32[40,4]{1,0:T(8,128)}, u32[]{:S(2)}) copy-start(f32[40,4]{1,0:T(8,128)} %copy-done.19) | copy-start | bytes 1924
  522.4 42.9 %copy-start.23 = (f32[40,4]{0,1:T(4,128)S(1)}, f32[40,4]{0,1:T(4,128)}, u32[]{:S(2)}) copy-start(f32[40,4]{0,1:T(4,128)} %get-tuple-element.74) | copy-start | bytes 1924
  522.4 43.1 %copy-start.25 = (f32[64]{0:T(128)S(1)}, f32[64]{0:T(128)}, u32[]{:S(2)}) copy-start(f32[64]{0:T(128)} %copy-done.24) | copy-start | bytes 772
  522.4 44.3 %copy-start.11 = (f32[2,2,2,240,128]{4,3,2,1,0:T(8,128)S(1)}, f32[2,2,2,240,128]{4,3,2,1,0:T(8,128)}, u32[]{:S(2)}) copy-start(f32[2,2,2,240,128]{4,3,2,1,0:T(8,128)} %get-tuple-element.40) | copy-start | bytes 2949124
  565.3 28.5 %copy-start.22 = (f32[160]{0:T(256)}, f32[160]{0:T(256)S(1)}, u32[]{:S(2)}) copy-start(f32[160]{0:T(256)S(1)} %rsqrt.22) | copy-start | bytes 1924
  578.8 5.9 copy-start.15
  578.9 6.4 copy-start.16
  746.4 6.4 copy-start.12
  754.2 10.0 %copy-start.1 = (bf16[192,2048]{1,0:T(8,128)(2,1)S(1)}, bf16[192,2048]{1,0:T(8,128)(2,1)}, u32[]{:S(2)}) copy-start(bf16[192,2048]{1,0:T(8,128)(2,1)} %param.14) | copy-start | bytes 2359300
  754.2 8.9 %copy-start.10 = (f32[4,48,1536]{2,1,0:T(8,128)S(1)}, f32[4,48,1536]{2,1,0:T(8,128)}, u32[]{:S(2)}) copy-start(f32[4,48,1536]{2,1,0:T(8,128)} %get-tuple-element.45) | copy-start | bytes 3538948
  (14 other events, 24.2 us)
Sparse Core Ops, SparseCore 0:
  105.4 92.1 all-gather.6
  199.8 55.3 all-gather.4
  308.9 55.9 reduce-scatter.2
  367.8 89.2 reduce-scatter.4
  460.1 98.6 all-reduce.4
  565.3 98.6 all-gather.8

commit v6 on v5

--- a/solution.py
+++ b/solution.py
@@ -367,16 +367,17 @@
     )(pieces)
 
 
-def gather_kernel(arity, ctx_size, pair_count, slots, swaps, with_ctx, *refs):
+def gather_kernel(arity, ctx_size, pair_count, slots, swaps, wide, *refs):
     sources, refs = refs[:arity], refs[arity:]
     swap_sources, refs = refs[:swaps], refs[swaps:]
     outs, refs = refs[:arity], refs[arity:]
     swap_outs, refs = refs[:swaps], refs[swaps:]
     pair_sems, ctx_sems, core_sems = refs[0:2], refs[2:4], refs[4:6]
     local_sem = refs[6]
-    square, ways = peers_of(ctx_size) if with_ctx else (False, ())
+    square, ways = peers_of(ctx_size) if wide else (False, ())
+    narrow = [item for item in range(arity) if item not in wide]
     near = [way for way in ways if not (square and way == 3)]
-    ctx, pair, core = greet(ctx_size, pair_count, with_ctx, swaps > 0)
+    ctx, pair, core = greet(ctx_size, pair_count, len(wide) > 0, swaps > 0)
     homes = [place(ctx, pair * 2 + core) for place in slots]
     started = []
     steps = [(0, 1)] + [(far, way) for far in range(1, pair_count) for way in (1, -1)]
@@ -464,8 +465,8 @@
             functools.partial(present, step),
         )
 
-    def spread(step):
-        for item in range(arity):
+    def spread(step, items):
+        for item in items:
             place = slots[item](ctx, origin(step) * 2 + core)
             source = sources[item]
             if step:
@@ -473,7 +474,7 @@
                 arrive(item, place, pair_sems, ((way + 1) // 2, far - 1, item))
                 source = outs[item].at[place]
             pass_on(step, item, source, place)
-            for way in near:
+            for way in near if item in wide else ():
                 there = ctx_target(ctx, way, square, ctx_size)
                 send(
                     item,
@@ -488,7 +489,7 @@
 
     def collect(step):
         for way in near:
-            for item in range(arity):
+            for item in wide:
                 come = ctx_source(ctx, way, square, ctx_size)
                 place = slots[item](come, origin(step) * 2 + core)
                 arrive(item, place, ctx_sems, (way - 1, step, item))
@@ -506,7 +507,7 @@
                 to_core(item, source, come, way, step)
 
     def collect_far(step):
-        for item in range(arity):
+        for item in wide:
             place = slots[item](ctx ^ 3, origin(step) * 2 + core)
             arrive(item, place, ctx_sems, (2, step, item))
             to_core(item, outs[item].at[place], ctx ^ 3, 3, step)
@@ -516,13 +517,14 @@
         copy = pltpu.make_async_copy(sources[item], outs[item].at[homes[item]], local_sem.at[item])
         copy.start()
         locals_.append(copy)
-    when(None, lambda: spread(0))
+    spread(0, wide)
     flows = []
     count = len(steps)
     for turn in range(1, count + 4):
         if turn < count:
-            when(present(turn), functools.partial(spread, turn))
+            when(present(turn), functools.partial(spread, turn, wide))
         if turn == count:
+            spread(0, narrow)
             for item in range(swaps):
                 flow = Exchange(
                     swap_sources[item],
@@ -538,10 +540,13 @@
         if square and 0 <= turn - 4 < count:
             when(present(turn - 4), functools.partial(collect_far, turn - 4))
 
+    for turn in range(1, count):
+        when(present(turn), functools.partial(spread, turn, narrow))
+
     def from_core(step):
         for way in (0, *ways):
             come = ctx_source(ctx, way, square, ctx_size) if way else ctx
-            for item in range(arity):
+            for item in wide if way else range(arity):
                 arrive(item, slots[item](come, origin(step) * 2 + 1 - core), core_sems, (way, step, item))
 
     for step in range(count):
@@ -554,22 +559,23 @@
         when(condition(), functools.partial(sent, *which))
 
 
-def gather(pieces, slots, collective_id, swaps=(), with_ctx=True):
+def gather(pieces, slots, collective_id, swaps=(), wide=None):
     ctx_size, shard_count = lax.axis_size("ctx"), lax.axis_size("fsdp")
     pair_count = shard_count // 2
     arity = len(pieces)
+    wide = range(arity) if wide is None else wide
     dma = pltpu.SemaphoreType.DMA
     moved = sum(piece.size for piece in pieces) * 2
     steps = 2 * pair_count - 1
     return pl.pallas_call(
-        functools.partial(gather_kernel, arity, ctx_size, pair_count, slots, len(swaps), with_ctx),
+        functools.partial(gather_kernel, arity, ctx_size, pair_count, slots, len(swaps), wide),
         in_specs=[pl.BlockSpec(memory_space=pltpu.VMEM)] * (arity + len(swaps)),
         out_specs=[pl.BlockSpec(memory_space=pl.ANY)] * (arity + len(swaps)),
         out_shape=[
             jax.ShapeDtypeStruct(
-                ((ctx_size if with_ctx else 1) * shard_count,) + piece.shape, piece.dtype
+                ((ctx_size if item in wide else 1) * shard_count,) + piece.shape, piece.dtype
             )
-            for piece in pieces
+            for item, piece in enumerate(pieces)
         ]
         + [jax.ShapeDtypeStruct(swap.shape, swap.dtype) for swap in swaps],
         scratch_shapes=[dma((2, pair_count - 1, arity))] * 2
@@ -585,16 +591,13 @@
 
 
 class LineScatter:
-    def __init__(self, source, out, half, above, below, sems, where, counts, last):
-        pair_count, self.ctx_size = counts
-        self.source, self.out, self.half, self.rooms = source, out, half, {1: above, -1: below}
+    def __init__(self, source, out, half, room, sems, where, counts, last):
+        self.count, self.ctx_size = counts
+        self.source, self.out, self.half, self.room = source, out, half, room
         self.last = last
-        self.core_sems, self.line_sems = sems[0:2], {1: sems[2:4], -1: sems[4:6]}
+        self.core_sems, self.pair_sems = sems[0:2], sems[2:4]
         self.ctx, self.pair, self.core = where
-        self.count = pair_count
-        self.order = []
-        for turn in range(pair_count - 1):
-            self.order += [(pair_count - 1 - turn, 1), (turn, -1)]
+        self.order = [*range(1, self.count), 0]
 
     def copy(self, source, target, device, sems, at):
         return pltpu.make_async_remote_copy(
@@ -609,64 +612,42 @@
     def here(self):
         return (self.ctx, self.pair * 2 + self.core)
 
-    def core_copy(self, pair):
-        return self.copy(
-            self.source.at[pair * 2 + 1 - self.core],
-            self.half.at[pair],
-            (self.ctx, self.pair * 2 + 1 - self.core),
-            self.core_sems,
-            pair,
+    def toward(self, step):
+        return lax.rem(self.pair + step, self.count)
+
+    def start(self):
+        self.copies = []
+        for step in self.order:
+            self.copies.append(
+                self.copy(
+                    self.source.at[self.toward(step) * 2 + 1 - self.core],
+                    self.half.at[step],
+                    (self.ctx, self.pair * 2 + 1 - self.core),
+                    self.core_sems,
+                    step,
+                )
+            )
+            self.copies[-1].start()
+
+    def fold(self, step):
+        half = self.half.at[step]
+        self.copy(half, half, self.here(), self.core_sems, step).wait_recv()
+        mine = self.source[self.toward(step) * 2 + self.core].astype(jnp.float32)
+        total = mine + half[...].astype(jnp.float32)
+        if step == 0:
+            self.out[...] = total
+            return
+        half[...] = total.astype(half.dtype)
+        self.copies.append(
+            self.copy(
+                half,
+                self.room.at[step - 1],
+                (self.ctx, self.toward(step) * 2 + self.core),
+                self.pair_sems,
+                step - 1,
+            )
         )
-
-    def line_copy(self, pair, way):
-        return self.copy(
-            self.half.at[pair],
-            self.rooms[way].at[pair],
-            (self.ctx, (self.pair + way) * 2 + self.core),
-            self.line_sems[way],
-            pair,
-        )
-
-    def line_room(self, pair, way):
-        room = self.rooms[way].at[pair]
-        return self.copy(room, room, self.here(), self.line_sems[way], pair)
-
-    def add(self, pair, value):
-        half = self.half.at[pair]
-        half[...] = (half[...].astype(jnp.float32) + value.astype(jnp.float32)).astype(half.dtype)
-
-    def beyond(self, pair, way):
-        return pair > self.pair if way == 1 else pair < self.pair
-
-    def behind(self, way):
-        return self.pair > 0 if way == 1 else self.pair < self.count - 1
-
-    def start(self):
-        done = []
-        for pair, _ in self.order:
-            if pair not in done:
-                done.append(pair)
-                self.core_copy(pair).start()
-        self.folds = done
-
-    def fold(self):
-        for pair in self.folds:
-            self.copy(
-                self.half.at[pair], self.half.at[pair], self.here(), self.core_sems, pair
-            ).wait_recv()
-            self.add(pair, self.source[pair * 2 + self.core])
-
-    def advance(self, turn):
-        pair, way = self.order[turn]
-
-        @pl.when(self.beyond(pair, way))
-        def pass_on():
-            @pl.when(self.behind(way))
-            def join():
-                self.line_room(pair, way).wait_recv()
-                self.add(pair, self.rooms[way][pair])
-
-            self.line_copy(pair, way).start()
+        self.copies[-1].start()
 
     def over_ctx(self, terms, room, landing, *sems):
         shard = self.pair * 2 + self.core
@@ -698,27 +679,14 @@
             copy.wait_send()
 
     def finish(self):
-        for pair in range(self.count):
-
-            @pl.when(self.pair == pair)
-            def close(pair=pair):
-                self.out[...] = self.half[pair].astype(jnp.float32)
-                for way in (1, -1):
-
-                    @pl.when(self.behind(way))
-                    def join(way=way):
-                        self.line_room(pair, way).wait_recv()
-                        self.out[...] += self.rooms[way][pair].astype(jnp.float32)
-
+        for step in range(1, self.count):
+            room = self.room.at[step - 1]
+            self.copy(room, room, self.here(), self.pair_sems, step - 1).wait_recv()
+            self.out[...] += room[...].astype(jnp.float32)
         if self.last:
             self.over_ctx(*self.last)
-        for pair in range(self.count):
-            self.core_copy(pair).wait_send()
-        for pair, way in self.order:
-
-            @pl.when(self.beyond(pair, way))
-            def sent(pair=pair, way=way):
-                self.line_copy(pair, way).wait_send()
+        for copy in self.copies:
+            copy.wait_send()
 
 
 def scatter_kernel(arity, ctx_size, pair_count, slot, spread_ctx, lines, *refs):
@@ -735,17 +703,17 @@
     started = []
     flows = []
     for item in range(lines):
-        at = 5 * arity + 10 + 16 * item
+        at = 5 * arity + 10 + 13 * item
         spread = len(line_sources[item].shape) == 4
         flows.append(
             LineScatter(
                 line_sources[item],
                 line_outs[item],
-                *refs[at : at + 3],
-                refs[at + 3 : at + 9],
+                *refs[at : at + 2],
+                refs[at + 2 : at + 6],
                 (ctx, pair, core),
                 (pair_count, ctx_size),
-                refs[at + 9 : at + 16] if spread else (),
+                refs[at + 6 : at + 13] if spread else (),
             )
         )
 
@@ -858,22 +826,15 @@
 
     for flow in flows:
         flow.start()
-    turns = 2 * (pair_count - 1)
     for turn in range(pair_count + 2):
         if turn < pair_count:
             fold_core(order[turn])
         if 1 <= turn <= pair_count:
             fold_relay(order[turn - 1])
-        for flow in flows:
-            if turn == pair_count - 1:
-                flow.fold()
-                for part in range(2):
-                    flow.advance(part)
+            for flow in flows:
+                flow.fold(order[turn - 1])
         if turn >= 2:
             fold_ctx(order[turn - 2])
-    for flow in flows:
-        for part in range(2, turns):
-            flow.advance(part)
     if spread_ctx:
         for item in range(arity):
             for way in ways:
@@ -934,8 +895,11 @@
         + [
             scratch
             for line in lines
-            for scratch in [pltpu.VMEM((pair_count,) + line.shape[1:], line.dtype)] * 3
-            + [dma((pair_count,))] * 6
+            for scratch in [
+                pltpu.VMEM((pair_count,) + line.shape[1:], line.dtype),
+                pltpu.VMEM((pair_count - 1,) + line.shape[1:], line.dtype),
+            ]
+            + [dma((pair_count,))] * 4
             + line_room(line)
         ],
         compiler_params=pltpu.CompilerParams(
@@ -1056,7 +1020,6 @@
         gate_up_cut.reshape(shard_count * cut, 2 * width), "ctx", axis=0, tiled=True
     )
     down_padded = jnp.pad(w_down, ((0, width - columns), (0, 0)))
-    cotangent_all = lax.all_gather(cotangent.reshape(-1, D), "fsdp", axis=0, tiled=True)
 
     inputs = layer_input.reshape(-1, D).astype(jnp.float32)
     unit_one, scale_one, normed = normalize(inputs, gain_one)
@@ -1076,7 +1039,10 @@
     own_kv = jnp.stack([key_tokens, value_raw.astype(jnp.bfloat16)], 1)
     own_kv = own_kv.reshape(rows_here, 2, SEQS, 2, KVH, HD).transpose(0, 2, 4, 1, 3, 5)
     own_kv = own_kv.reshape(rows_here, SEQS * KVH * 4 * HD)
-    (all_kv,) = gather([own_kv], [by_tokens], 2)
+    all_kv, cotangent_all = gather(
+        [own_kv, cotangent.reshape(-1, D)], [by_tokens, lambda ctx, shard: shard], 2, wide=(0,)
+    )
+    cotangent_all = cotangent_all.reshape(-1, D)
     all_kv = all_kv.reshape(-1, SEQS * KVH * 4 * HD)
     queries = to_groups(query_tokens, rows_here)
     scalars = jnp.concatenate(
@@ -1090,7 +1056,7 @@
     unit_two, scale_two, normed = normalize(middle, gain_two)
     normed_two = mix_features(normed.astype(jnp.bfloat16))
 
-    (tokens_all,) = gather([normed_two], [lambda ctx, shard: shard], 6, with_ctx=False)
+    (tokens_all,) = gather([normed_two], [lambda ctx, shard: shard], 6, wide=())
     tokens_all = tokens_all.reshape(-1, D)
     gate_up_part = jnp.dot(tokens_all, gate_up_cols, preferred_element_type=jnp.float32)
     gate_part, up_part = gate_up_part[:, :width], gate_up_part[:, width:]

time: 778 us -> 733 us (0.942)
  the two profiles are of different devices: /device:TPU:14 before, /device:TPU:0 now
where the time goes in v6:
time: 733 us; the launch traced here: 724 us
  Pallas kernels  497 us (68%)
  matrix products  102 us (14%)
  waiting for transfers between devices  43.7 us (6%)
  local copies, waits for them, and re-layouts  40 us (5%)
  other arithmetic  26.1 us (4%)
  between operations  15.1 us (2%)
    pallas_call x3, Pallas kernels, gather(): pl.pallas_call(functools.partial(gather_kernel, arity, ctx_size, pair_cou...  213 us
    pallas_call x2, Pallas kernels, scatter(): pl.pallas_call(functools.partial(scatter_kernel, arity, ctx_size, pair_co...  179 us
    pallas_call x1, Pallas kernels, exchange(): pl.pallas_call(functools.partial(exchange_kernel, shard_count // 2), in_s...  35.5 us
    psum x1, waiting for transfers between devices, shards(): down_rows = lax.psum(down_terms, 'ctx')  30.9 us
    pallas_call x1, Pallas kernels, attend_backward(): pl.pallas_call(kernel, grid_spec=pltpu.PrefetchScalarGridSpec(num_scalar_...  29.1 us
    pallas_call x1, Pallas kernels, attend_forward(): pl.pallas_call(kernel, grid_spec=pltpu.PrefetchScalarGridSpec(num_scalar_...  27.9 us
    dot_general x1, matrix products, shards(): jnp.dot(tokens_all, gate_up_cols, preferred_element_type=jnp.float32)  15.7 us
    dot_general x1, matrix products, shards(): lax.dot_general(tokens_all, grad_gate_up, CONTRACT_FIRST, preferred_eleme...  15.1 us
  transfers between devices with their start and end apart: 5, of which 2 were waited for; matrix products, arithmetic and copies ran while one was open for 16% of the time, Pallas kernels for 57%

profile of v6, /device:TPU:0, one launch (start us, length us, event | category | flops | bytes accessed | tf_op | source)
XLA Modules:
  0.0 723.7 jit_solution(12636842720672457013)
XLA Ops:
  17.9 73.7 %shard_map.194 = (bf16[32,48,2048]{2,1,0:T(8,128)(2,1)}, bf16[32,48,1536]{2,1,0:T(8,128)(2,1)}, bf16[32,16,128]{2,1,0:T(8,128)(2,1)}, bf16[8,48,2304]{2,1,0:T(8,128)(2,1)}) custom-call(bf16[48,2048]{1,0:T(8,128)(2,1)} %constant_dynamic-slice_fusion.4.refs_0_, bf16[48,1536]{1,0:T(8,128)(2,1)} %constant_dynamic-slice_fusion.3.refs_1_, ...), custom_call_target="tpu_custom_call" | custom-call | bytes 44564480 | tf_op jit(solution)/shard_map/pallas_call | solution.py:570
  94.6 4.0 convolution_add_fusion.1
  116.7 97.1 %shard_map.195 = (bf16[32,40,2048]{2,1,0:T(8,128)(2,1)}, bf16[8,160,1536]{2,1,0:T(8,128)(2,1)}) custom-call(bf16[40,2048]{1,0:T(8,128)(2,1)} %reshape.482.refs_0_, bf16[160,1536]{1,0:T(8,128)(2,1)} %reshape.483.refs_1_), custom_call_target="tpu_custom_call" | custom-call | bytes 83886080 | tf_op jit(solution)/shard_map/pallas_call | solution.py:570
  214.4 27.9 %attend_forward.1 = (f32[2,2,2,240,128]{4,3,2,1,0:T(8,128)}, f32[2,2,2,1,240]{4,3,2,1,0:T(1,128)}) custom-call(s32[18]{0:T(128)} %pad_add_fusion.scalars, bf16[2,2,2,240,128]{4,3,2,1,0:T(8,128)(2,1)} %bitcast.116, bf16[1280,2048]{1,0:T(8,128)(2,1)} %bitcast.107), custom_call_target="tpu_custom_call" | custom-call | tf_op jit(solution)/shard_map/attend_forward/pallas_call | solution.py:154
  244.3 3.5 multiply_reduce_fusion.4
  249.4 42.4 %shard_map.196 = bf16[8,160,1536]{2,1,0:T(8,128)(2,1)} custom-call(bf16[160,1536]{1,0:T(8,128)(2,1)} %copy.128.refs_0_), custom_call_target="tpu_custom_call" | custom-call | bytes 62914560 | tf_op jit(solution)/shard_map/pallas_call | solution.py:570
  291.9 15.7 %fusion.30 = f32[1280,2304]{0,1:T(8,128)} fusion(bf16[1280,1536]{1,0:T(8,128)(2,1)} %bitcast.122, bf16[1536,2304]{1,0:T(8,128)(2,1)} %all-gather.4.cloned.1.call-done), kind=kOutput, calls=%fused_computation.120 | convolution fusion | flops 9059696640 | bytes 22806528 | tf_op jit(solution)/shard_map/dot_general | solution.py:1061
  307.6 11.8 %multiply_convert_fusion.2 = (bf16[1280,1152]{0,1:T(8,128)(2,1)}, bf16[1280,1152]{0,1:T(8,128)(2,1)}, bf16[1280,1152]{0,1:T(8,128)(2,1)}) fusion(f32[1280,2304]{0,1:T(8,128)} %fusion.30, bf16[1280,1536]{1,0:T(8,128)(2,1)S(1)} %bitcast.151, bf16[1120,1536]{1,0:T(8,128)(2,1)S(1)} %copy-done.28), kind=kOutput, calls=%fused_computation.9 | convolution fusion | flops 4551966720 | bytes 28016640 | tf_op jit(solution)/shard_map/dot_general | solution.py:1066
  319.4 13.2 %convolution_convert_fusion.5 = bf16[1280,1536]{1,0:T(8,128)(2,1)} fusion(bf16[1536,2304]{1,0:T(8,128)(2,1)S(1)} %bitcast.148, bf16[1280,1152]{0,1:T(8,128)(2,1)} %get-tuple-element.58, bf16[1280,1152]{0,1:T(8,128)(2,1)} %get-tuple-element.57), kind=kOutput, calls=%fused_computation.5 | convolution fusion | flops 9073459200 | bytes 16908288 | tf_op jit(solution)/shard_map/dot_general | solution.py:1071
  332.7 15.1 %convolution_convert_fusion = bf16[1536,2304]{1,0:T(8,128)(2,1)} fusion(bf16[1280,1536]{1,0:T(8,128)(2,1)} %bitcast.123, bf16[1280,1152]{0,1:T(8,128)(2,1)} %get-tuple-element.58, bf16[1280,1152]{0,1:T(8,128)(2,1)} %get-tuple-element.57), kind=kOutput, calls=%fused_computation | convolution fusion | flops 9075032064 | bytes 16908288 | tf_op jit(solution)/shard_map/dot_general | solution.py:1080
  347.9 9.6 %convolution_convert_fusion.1 = bf16[1280,1536]{1,0:T(8,128)(2,1)} fusion(bf16[1280,1152]{0,1:T(8,128)(2,1)} %get-tuple-element.59, bf16[1120,1536]{1,0:T(8,128)(2,1)} %param.20), kind=kOutput, calls=%fused_computation.1 | convolution fusion | flops 4531814400 | bytes 10321920 | tf_op jit(solution)/shard_map/dot_general | solution.py:1083
  357.5 6.2 convolution_convert_fusion.3
  363.7 12.7 %reduce-scatter.3.cloned.1.call-done = bf16[160,1536]{1,0:T(8,128)(2,1)} async-done(((bf16[1280,1536]{1,0:T(8,128)(2,1)}), bf16[160,1536]{1,0:T(8,128)(2,1)}) %reduce-scatter.3.cloned.1.call-update) | async-done | bytes 491536 | tf_op jit(solution)/shard_map/reduce_scatter | solution.py:1074
  383.0 5.5 convolution_convert_fusion.6
  390.2 29.1 %attend_backward.1 = (f32[2,2,2,240,128]{4,3,2,1,0:T(8,128)}, bf16[1280,2048]{1,0:T(8,128)(2,1)}) custom-call(s32[18]{0:T(128)} %pad_add_fusion.scalars, bf16[2,2,2,240,128]{4,3,2,1,0:T(8,128)(2,1)} %bitcast.117, bf16[2,2,2,240,128]{4,3,2,1,0:T(8,128)(2,1)} %bitcast.130, f32[2,2,2,240,128]{4,3,2,1,0:T(8,128)} %get-tuple-element.35.att_ref, ...), custom_call_target="tpu_custom_call" | custom-call | tf_op jit(solution)/shard_map/attend_backward/pallas_call | solution.py:252
  419.3 67.1 %shard_map.197 = (f32[40,2048]{1,0:T(8,128)}, f32[160,1536]{1,0:T(8,128)}) custom-call(bf16[32,40,2048]{2,1,0:T(8,128)(2,1)} %bitcast.115, bf16[8,160,1536]{2,1,0:T(8,128)(2,1)} %bitcast.121), custom_call_target="tpu_custom_call" | custom-call | bytes 83886080 | tf_op jit(solution)/shard_map/pallas_call | solution.py:877
  486.5 35.5 %shard_map.199 = bf16[8,48,2304]{2,1,0:T(8,128)(2,1)} custom-call(bf16[8,48,2304]{2,1,0:T(8,128)(2,1)} %bitcast.133), custom_call_target="tpu_custom_call" | custom-call | bytes 56623104 | tf_op jit(solution)/shard_map/pallas_call | solution.py:357
  530.0 4.8 convolution_convert_fusion.4
  535.6 30.9 %all-reduce.5.cloned.1.call-done = bf16[1152,1536]{1,0:T(8,128)(2,1)} async-done(((bf16[1152,1536]{1,0:T(8,128)(2,1)}), bf16[1152,1536]{1,0:T(8,128)(2,1)}) %all-reduce.5.cloned.1.call-update) | async-done | bytes 3538960 | tf_op jit(solution)/shard_map/psum | solution.py:1084
  566.5 5.8 slice_convert_fusion
  573.8 7.6 %multiply_reduce_fusion.1 = (f32[1536]{0:T(1024)S(1)}, f32[160]{0:T(256)}, f32[160,1536]{1,0:T(8,128)}) fusion(f32[160,1536]{1,0:T(8,128)S(1)} %copy-done.3, f32[160]{0:T(256)S(1)} %rsqrt.22, f32[1536]{0:T(1024)S(1)} %copy-done.17, bf16[1536,2048]{1,0:T(8,128)(2,1)} %bitcast.106, bf16[160,256]{1,0:T(8,128)(2,1)S(1)} %get-tuple-element.67, ...), kind=kOutput, calls=%fused_computation.31 | convolution fusion | flops 1010071936 | bytes 8926464 | tf_op jit(solution)/shard_map/dot_general | solution.py:1135
  582.3 4.9 convolution_convert_fusion.2
  587.2 111.9 %shard_map.198 = (bf16[4,48,2048]{2,1,0:T(8,128)(2,1)}, f32[4,8,128]{2,1,0:T(8,128)}, f32[4,48,1536]{2,1,0:T(8,128)}) custom-call(bf16[32,48,2048]{2,1,0:T(8,128)(2,1)} %bitcast.103, f32[32,8,128]{2,1,0:T(8,128)} %bitcast.139, bf16[8,4,48,1536]{3,2,1,0:T(8,128)(2,1)} %bitcast.104), custom_call_target="tpu_custom_call" | custom-call | bytes 102760448 | tf_op jit(solution)/shard_map/pallas_call | solution.py:877
  706.8 8.9 %unpack.1 = (f32[4,48,8960]{2,1,0:T(8,128)}, f32[4,48,8960]{2,1,0:T(8,128)}) custom-call(bf16[4,8,48,2304]{3,2,1,0:T(8,128)(2,1)} %bitcast.111), custom_call_target="tpu_custom_call" | custom-call | tf_op jit(solution)/shard_map/unpack/pallas_call | solution.py:943
  (206 shorter events, 63.7 us)
Async XLA Ops:
  7.2 284.6 %all-gather.4.cloned.1.call-start = ((), (), s32[]{:S(2)}) async-start(), calls=%async_computation.2 | async-start | bytes 8847360 | tf_op jit(solution)/shard_map/all_gather | solution.py:1019
  14.8 78.1 %copy-start.8 = (bf16[40,4,1536]{2,1,0:T(4,128)(2,1)S(1)}, bf16[40,4,1536]{2,1,0:T(4,128)(2,1)}, u32[]{:S(2)}) copy-start(bf16[40,4,1536]{2,1,0:T(4,128)(2,1)} %param.11) | copy-start | bytes 1474564
  91.7 284.8 %reduce-scatter.3.cloned.1.call-start = ((), (), s32[]{:S(2)}) async-start(), calls=%async_computation.3 | async-start | bytes 4423680 | tf_op jit(solution)/shard_map/reduce_scatter | solution.py:1074
  100.5 143.8 %copy-start.2 = (f32[160,1536]{1,0:T(8,128)}, f32[160,1536]{1,0:T(8,128)S(1)}, u32[]{:S(2)}) copy-start(f32[160,1536]{1,0:T(8,128)S(1)} %reshape.519) | copy-start | bytes 2949124
  109.0 5.0 copy-start.7
  291.8 15.8 %copy-start.26 = (bf16[8,160,1536]{2,1,0:T(8,128)(2,1)S(1)}, bf16[8,160,1536]{2,1,0:T(8,128)(2,1)}, u32[]{:S(2)}) copy-start(bf16[8,160,1536]{2,1,0:T(8,128)(2,1)} %get-tuple-element.37) | copy-start | bytes 11796484
  291.8 15.8 %copy-start.28 = (bf16[1120,1536]{1,0:T(8,128)(2,1)S(1)}, bf16[1120,1536]{1,0:T(8,128)(2,1)}, u32[]{:S(2)}) copy-start(bf16[1120,1536]{1,0:T(8,128)(2,1)} %param.20) | copy-start | bytes 10321924
  291.9 27.6 %slice-start = ((s8[7077888]{0:T(1024)(128)(4,1)}), s8[4194304]{0:T(1024)(128)(4,1)S(1)}, s32[]{:S(2)}) async-start(s8[7077888]{0:T(1024)(128)(4,1)} %bitcast.147), calls=%async_computation.7 | async-start | bytes 8388608
  307.6 11.8 %slice-start.1 = ((s8[7077888]{0:T(1024)(128)(4,1)}), s8[2883584]{0:T(1024)(128)(4,1)S(1)}, s32[]{:S(2)}) async-start(s8[7077888]{0:T(1024)(128)(4,1)} %bitcast.147), calls=%async_computation.8 | async-start | bytes 5767168
  332.7 153.8 %reduce-scatter.5.cloned.1.call-start = ((), (), s32[]{:S(2)}) async-start(), calls=%async_computation.4 | async-start | bytes 8847360 | tf_op jit(solution)/shard_map/reduce_scatter | solution.py:1085
  347.9 218.6 %all-reduce.5.cloned.1.call-start = ((), (), s32[]{:S(2)}) async-start(), calls=%async_computation.5 | async-start | bytes 7077888 | tf_op jit(solution)/shard_map/psum | solution.py:1084
  347.9 9.6 %copy-start.27 = (bf16[8,160,1536]{2,1,0:T(8,128)(2,1)S(1)}, bf16[8,160,1536]{2,1,0:T(8,128)(2,1)}, u32[]{:S(2)}) copy-start(bf16[8,160,1536]{2,1,0:T(8,128)(2,1)} %get-tuple-element.37) | copy-start | bytes 11796484
  347.9 9.6 %copy-start.29 = (bf16[1280,1152]{0,1:T(8,128)(2,1)S(1)}, bf16[1280,1152]{0,1:T(8,128)(2,1)}, u32[]{:S(2)}) copy-start(bf16[1280,1152]{0,1:T(8,128)(2,1)} %get-tuple-element.59) | copy-start | bytes 8847364
  376.5 330.3 %all-gather.6.cloned.1.call-start = ((), (), s32[]{:S(2)}) async-start(), calls=%async_computation.6 | async-start | bytes 8847360 | tf_op jit(solution)/shard_map/all_gather | solution.py:1119
  486.4 35.6 %copy-start.19 = (f32[40,4]{1,0:T(8,128)S(1)}, f32[40,4]{1,0:T(8,128)}, u32[]{:S(2)}) copy-start(f32[40,4]{1,0:T(8,128)} %copy-done.18) | copy-start | bytes 1924
  486.4 35.7 %copy-start.22 = (f32[40,4]{0,1:T(4,128)S(1)}, f32[40,4]{0,1:T(4,128)}, u32[]{:S(2)}) copy-start(f32[40,4]{0,1:T(4,128)} %get-tuple-element.78) | copy-start | bytes 1924
  486.4 35.9 %copy-start.24 = (f32[64]{0:T(128)S(1)}, f32[64]{0:T(128)}, u32[]{:S(2)}) copy-start(f32[64]{0:T(128)} %copy-done.23) | copy-start | bytes 772
  486.4 37.1 %copy-start.11 = (f32[2,2,2,240,128]{4,3,2,1,0:T(8,128)S(1)}, f32[2,2,2,240,128]{4,3,2,1,0:T(8,128)}, u32[]{:S(2)}) copy-start(f32[2,2,2,240,128]{4,3,2,1,0:T(8,128)} %get-tuple-element.44) | copy-start | bytes 2949124
  522.1 60.2 %copy-start.21 = (f32[160]{0:T(256)}, f32[160]{0:T(256)S(1)}, u32[]{:S(2)}) copy-start(f32[160]{0:T(256)S(1)} %rsqrt.22) | copy-start | bytes 1924
  535.5 36.8 %copy-start.14 = (f32[40,2048]{1,0:T(8,128)S(1)}, f32[40,2048]{1,0:T(8,128)}, u32[]{:S(2)}) copy-start(f32[40,2048]{1,0:T(8,128)} %get-tuple-element.46) | copy-start | bytes 983044
  535.5 37.3 %copy-start.15 = (f32[160,128]{1,0:T(8,128)S(1)}, f32[160,128]{1,0:T(8,128)}, u32[]{:S(2)}) copy-start(f32[160,128]{1,0:T(8,128)} %get-tuple-element.71) | copy-start | bytes 245764
  699.0 6.4 copy-start.12
  706.8 10.0 %copy-start.1 = (bf16[192,2048]{1,0:T(8,128)(2,1)S(1)}, bf16[192,2048]{1,0:T(8,128)(2,1)}, u32[]{:S(2)}) copy-start(bf16[192,2048]{1,0:T(8,128)(2,1)} %param.14) | copy-start | bytes 2359300
  706.8 8.9 %copy-start.10 = (f32[4,48,1536]{2,1,0:T(8,128)S(1)}, f32[4,48,1536]{2,1,0:T(8,128)}, u32[]{:S(2)}) copy-start(f32[4,48,1536]{2,1,0:T(8,128)} %get-tuple-element.49) | copy-start | bytes 3538948
  (13 other events, 24.0 us)
Sparse Core Ops, SparseCore 0:
  91.8 109.7 all-gather.3
  332.8 43.5 reduce-scatter.2
  379.5 91.5 reduce-scatter.4
  474.1 92.3 all-reduce.4
  568.2 97.0 all-gather.5

commit v7 on v6

--- a/solution.py
+++ b/solution.py
@@ -909,6 +909,36 @@
     )(*terms, *lines)
 
 
+def line_sum_kernel(pair_count, source, out, half, room, *sems):
+    where = greet(1, pair_count, False, False)
+    flow = LineScatter(source, out, half, room, sems, where, (pair_count, 1), ())
+    flow.start()
+    for step in flow.order:
+        flow.fold(step)
+    flow.finish()
+
+
+def line_sum(terms, collective_id):
+    pair_count = lax.axis_size("fsdp") // 2
+    extent = terms.shape[1:]
+    dma = pltpu.SemaphoreType.DMA((pair_count,))
+    return pl.pallas_call(
+        functools.partial(line_sum_kernel, pair_count),
+        in_specs=[pl.BlockSpec(memory_space=pltpu.VMEM)],
+        out_specs=pl.BlockSpec(memory_space=pltpu.VMEM),
+        out_shape=jax.ShapeDtypeStruct(extent, jnp.float32),
+        scratch_shapes=[
+            pltpu.VMEM((pair_count,) + extent, terms.dtype),
+            pltpu.VMEM((pair_count - 1,) + extent, terms.dtype),
+        ]
+        + [dma] * 4,
+        compiler_params=pltpu.CompilerParams(
+            collective_id=collective_id, has_side_effects=True, vmem_limit_bytes=63 * 2**20
+        ),
+        cost_estimate=pl.CostEstimate(flops=0, bytes_accessed=terms.size * 16, transcendentals=0),
+    )(terms)
+
+
 def pack_kernel(columns, gate_ref, up_ref, out_ref):
     width = out_ref.shape[2] // 2
     cut = out_ref.shape[1]
@@ -1000,12 +1030,10 @@
     small = lax.dynamic_slice_in_dim(small, own_ctx, 1, 0)
     small = jnp.pad(small, ((0, 0), (0, 16 * HD - small_width))).reshape(16, HD)
     width = -(-columns // HD) * HD
-    w_qkv_all, w_o_all, small_all, gate_up_cut = gather(
-        [own_cut(w_qkv), own_cut(w_o), small],
-        [by_rows, by_rows, by_rows],
-        1,
-        swaps=[pack(own_cut(w_gate), own_cut(w_up), shard_count, columns, width)],
-    )
+    w_qkv_all, w_o_all, small_all = gather(
+        [own_cut(w_qkv), own_cut(w_o), small], [by_rows, by_rows, by_rows], 1
+    )
+    cotangent_all = lax.all_gather(cotangent.reshape(-1, D), "fsdp", axis=0, tiled=True)
     w_qkv_all = w_qkv_all.reshape(D, QKV)
     w_o_all = w_o_all.reshape(D, D)
     small_all = small_all.reshape(shard_count, ctx_size, -1)[:, :, :small_width]
@@ -1016,9 +1044,6 @@
     gain_one = small_all[:, bias_width : bias_width + gain_width].reshape(-1)
     gain_two = small_all[:, bias_width + gain_width :].reshape(-1)
 
-    gate_up_cols = lax.all_gather(
-        gate_up_cut.reshape(shard_count * cut, 2 * width), "ctx", axis=0, tiled=True
-    )
     down_padded = jnp.pad(w_down, ((0, width - columns), (0, 0)))
 
     inputs = layer_input.reshape(-1, D).astype(jnp.float32)
@@ -1039,10 +1064,15 @@
     own_kv = jnp.stack([key_tokens, value_raw.astype(jnp.bfloat16)], 1)
     own_kv = own_kv.reshape(rows_here, 2, SEQS, 2, KVH, HD).transpose(0, 2, 4, 1, 3, 5)
     own_kv = own_kv.reshape(rows_here, SEQS * KVH * 4 * HD)
-    all_kv, cotangent_all = gather(
-        [own_kv, cotangent.reshape(-1, D)], [by_tokens, lambda ctx, shard: shard], 2, wide=(0,)
-    )
-    cotangent_all = cotangent_all.reshape(-1, D)
+    all_kv, gate_up_cut = gather(
+        [own_kv],
+        [by_tokens],
+        2,
+        swaps=[pack(own_cut(w_gate), own_cut(w_up), shard_count, columns, width)],
+    )
+    gate_up_cols = lax.all_gather(
+        gate_up_cut.reshape(shard_count * cut, 2 * width), "ctx", axis=0, tiled=True
+    )
     all_kv = all_kv.reshape(-1, SEQS * KVH * 4 * HD)
     queries = to_groups(query_tokens, rows_here)
     scalars = jnp.concatenate(
@@ -1068,25 +1098,26 @@
     )
     grad_gate = grad_hidden * up_part * sigmoid_gate * (1.0 + gate_part * (1.0 - sigmoid_gate))
     grad_gate_up = jnp.concatenate([grad_gate, grad_hidden * activated], -1).astype(jnp.bfloat16)
-    grad_tokens = lax.dot_general(
-        grad_gate_up, gate_up_cols, CONTRACT_LAST, preferred_element_type=jnp.float32
-    )
-    grad_normed_two = lax.psum_scatter(
-        grad_tokens.astype(jnp.bfloat16), "fsdp", scatter_dimension=0, tiled=True
-    )
     down_terms = lax.dot_general(
         hidden, cotangent_all, CONTRACT_FIRST, preferred_element_type=jnp.float32
     ).astype(jnp.bfloat16)
+    down_rows = lax.psum(down_terms, "ctx")
+    grad_gate_up, hidden, down_terms = lax.optimization_barrier(
+        (grad_gate_up, hidden, down_terms)
+    )
     gate_up_terms = lax.dot_general(
         tokens_all, grad_gate_up, CONTRACT_FIRST, preferred_element_type=jnp.float32
     ).astype(jnp.bfloat16)
+    gate_up_rows = lax.psum_scatter(gate_up_terms, "ctx", scatter_dimension=0, tiled=True)
+    grad_gate_up, hidden, gate_up_terms = lax.optimization_barrier(
+        (grad_gate_up, hidden, gate_up_terms)
+    )
+    grad_tokens = lax.dot_general(
+        grad_gate_up, gate_up_cols, CONTRACT_LAST, preferred_element_type=jnp.float32
+    ).astype(jnp.bfloat16)
+    grad_normed_two = line_sum(grad_tokens.reshape(shard_count, -1, D), 7)
     mixed_terms = jnp.dot(hidden, down_padded, preferred_element_type=jnp.float32).astype(jnp.bfloat16)
-    down_rows = lax.psum(down_terms, "ctx")
-    gate_up_rows = lax.psum_scatter(gate_up_terms, "ctx", scatter_dimension=0, tiled=True)
-    grad_normed_two, down_terms, gate_up_terms, mixed_terms = lax.optimization_barrier(
-        (grad_normed_two, down_terms, gate_up_terms, mixed_terms)
-    )
-    grad_normed_two = unmix_features(grad_normed_two.astype(jnp.float32))
+    grad_normed_two = unmix_features(grad_normed_two)
     grad_middle_norm, grad_gain_two = norm_back(grad_normed_two, unit_two, scale_two, gain_two)
     grad_middle = cotangent.reshape(-1, D).astype(jnp.float32) + grad_middle_norm
     grad_branch_one = grad_middle.astype(jnp.bfloat16)
@@ -1149,15 +1180,17 @@
     )
     small_terms = small_terms.reshape(ctx_size * shard_count, small_width)
     small_terms = jnp.pad(small_terms, ((0, 0), (0, 8 * HD - small_width)))
-    qkv_rows, small_rows, o_rows = scatter(
+    small_rows, qkv_rows, o_rows = scatter(
         [
-            qkv_terms.reshape(-1, cut, QKV),
             small_terms.reshape(-1, 8, HD),
         ],
         by_rows,
         4,
         spread_ctx=True,
-        lines=[o_terms.reshape(shard_count, ctx_size, cut, D)],
+        lines=[
+            qkv_terms.reshape(shard_count, ctx_size, cut, QKV),
+            o_terms.reshape(shard_count, ctx_size, cut, D),
+        ],
     )
     small_rows = small_rows.reshape(ctx_size, -1)[:, :small_width].reshape(-1)
     bias_start = 2 * gain_width
@@ -1168,7 +1201,7 @@
         output,
         grad_input,
         small_rows[:gain_width],
-        qkv_rows.reshape(-1, QKV).astype(jnp.float32),
+        qkv_rows.reshape(-1, QKV),
         small_rows[bias_start:value_start],
         small_rows[value_start:],
         o_rows.reshape(-1, D),

time: 733 us -> 788 us (1.075)
  Pallas kernels: 497 us -> 575 us
  waiting for transfers between devices: 43.7 us -> 17.1 us
    pallas_call x2, Pallas kernels: 179 us -> 263 us  [scatter(): pl.pallas_call(functools.partial(scatter_kernel, arity, ctx_size, pair_co...]
    pallas_call x3, Pallas kernels: 213 us -> 167 us  [gather(): pl.pallas_call(functools.partial(gather_kernel, arity, ctx_size, pair_cou...]
    pallas_call x0 -> x1, Pallas kernels: none -> 41.6 us  [line_sum(): pl.pallas_call(functools.partial(line_sum_kernel, pair_count), in_specs=[...]
    psum x1, waiting for transfers between devices: 30.9 us -> 0.02 us  [shards(): down_rows = lax.psum(down_terms, 'ctx')]
    all_gather x0 -> x1, waiting for transfers between devices: none -> 16.5 us  [shards(): lax.all_gather(cotangent.reshape(-1, D), 'fsdp', axis=0, tiled=True)]
    reduce_scatter x1 -> x0, waiting for transfers between devices: 12.7 us -> none  [shards(): lax.psum_scatter(grad_tokens.astype(jnp.bfloat16), 'fsdp', scatter_dimens...]
  transfers between devices with their start and end apart: 5 -> 5, of which waited for: 2 -> 1; matrix products, arithmetic and copies ran while one was open for 16% -> 14% of each run, Pallas kernels for 57% -> 58%
where the time goes in v7:
time: 788 us; the launch traced here: 780 us
  Pallas kernels  575 us (73%)
  matrix products  97.9 us (12%)
  local copies, waits for them, and re-layouts  44 us (6%)
  other arithmetic  30.4 us (4%)
  waiting for transfers between devices  17.1 us (2%)
  between operations  15.1 us (2%)
    pallas_call x2, Pallas kernels, scatter(): pl.pallas_call(functools.partial(scatter_kernel, arity, ctx_size, pair_co...  263 us
    pallas_call x3, Pallas kernels, gather(): pl.pallas_call(functools.partial(gather_kernel, arity, ctx_size, pair_cou...  167 us
    pallas_call x1, Pallas kernels, line_sum(): pl.pallas_call(functools.partial(line_sum_kernel, pair_count), in_specs=[...  41.6 us
    pallas_call x1, Pallas kernels, exchange(): pl.pallas_call(functools.partial(exchange_kernel, shard_count // 2), in_s...  35 us
    pallas_call x1, Pallas kernels, attend_backward(): pl.pallas_call(kernel, grid_spec=pltpu.PrefetchScalarGridSpec(num_scalar_...  29.3 us
    pallas_call x1, Pallas kernels, attend_forward(): pl.pallas_call(kernel, grid_spec=pltpu.PrefetchScalarGridSpec(num_scalar_...  27.9 us
    all_gather x1, waiting for transfers between devices, shards(): lax.all_gather(cotangent.reshape(-1, D), 'fsdp', axis=0, tiled=True)  16.5 us
  transfers between devices with their start and end apart: 5, of which 1 were waited for; matrix products, arithmetic and copies ran while one was open for 14% of the time, Pallas kernels for 58%

profile of v7, /device:TPU:0, one launch (start us, length us, event | category | flops | bytes accessed | tf_op | source)
XLA Modules:
  0.0 780.2 jit_solution(2574849404107067613)
XLA Ops:
  12.1 57.7 %shard_map.194 = (bf16[32,48,2048]{2,1,0:T(8,128)(2,1)}, bf16[32,48,1536]{2,1,0:T(8,128)(2,1)}, bf16[32,16,128]{2,1,0:T(8,128)(2,1)}) custom-call(bf16[48,2048]{1,0:T(8,128)(2,1)} %constant_dynamic-slice_fusion.4.refs_0_, bf16[48,1536]{1,0:T(8,128)(2,1)} %constant_dynamic-slice_fusion.3.refs_1_, bf16[16,128]{1,0:T(8,128)(2,1)} %bitcast.147), custom_call_target="tpu_custom_call" | custom-call | bytes 44564480 | tf_op jit(solution)/shard_map/pallas_call | solution.py:570
  74.4 4.0 convolution_add_fusion.1
  88.9 51.3 %shard_map.195 = (bf16[32,40,2048]{2,1,0:T(8,128)(2,1)}, bf16[8,48,2304]{2,1,0:T(8,128)(2,1)}) custom-call(bf16[40,2048]{1,0:T(8,128)(2,1)} %reshape.478.refs_0_, bf16[8,48,2304]{2,1,0:T(8,128)(2,1)} %pack.1.refs_1_), custom_call_target="tpu_custom_call" | custom-call | bytes 20971520 | tf_op jit(solution)/shard_map/pallas_call | solution.py:570
  154.8 27.9 %attend_forward.1 = (f32[2,2,2,240,128]{4,3,2,1,0:T(8,128)}, f32[2,2,2,1,240]{4,3,2,1,0:T(1,128)}) custom-call(s32[18]{0:T(128)} %pad_add_fusion.scalars, bf16[2,2,2,240,128]{4,3,2,1,0:T(8,128)(2,1)} %bitcast.118, bf16[1280,2048]{1,0:T(8,128)(2,1)} %bitcast.109), custom_call_target="tpu_custom_call" | custom-call | tf_op jit(solution)/shard_map/attend_forward/pallas_call | solution.py:154
  184.7 3.5 multiply_reduce_fusion.4
  189.8 58.0 %shard_map.196 = bf16[8,160,1536]{2,1,0:T(8,128)(2,1)} custom-call(bf16[160,1536]{1,0:T(8,128)(2,1)} %copy.128.refs_0_), custom_call_target="tpu_custom_call" | custom-call | bytes 62914560 | tf_op jit(solution)/shard_map/pallas_call | solution.py:570
  247.8 15.4 %fusion.27 = f32[1280,2304]{0,1:T(8,128)} fusion(bf16[1280,1536]{1,0:T(8,128)(2,1)} %bitcast.124, bf16[1536,2304]{1,0:T(8,128)(2,1)} %all-gather.7.cloned.1.call-done), kind=kOutput, calls=%fused_computation.117 | convolution fusion | flops 9059696640 | bytes 22806528 | tf_op jit(solution)/shard_map/dot_general | solution.py:1091
  263.2 16.5 %all-gather.5.cloned.1.call-done = bf16[1280,1536]{1,0:T(8,128)(2,1)} async-done(((bf16[160,1536]{1,0:T(8,128)(2,1)}), bf16[1280,1536]{1,0:T(8,128)(2,1)}) %all-gather.5.cloned.1.call-update) | async-done | bytes 3932176 | tf_op jit(solution)/shard_map/all_gather | solution.py:1036
  279.6 11.5 %multiply_convert_fusion.2 = (bf16[1280,1152]{0,1:T(8,128)(2,1)S(1)}, bf16[1280,1152]{0,1:T(8,128)(2,1)S(1)}, bf16[1280,1152]{0,1:T(8,128)(2,1)S(1)}) fusion(f32[1280,2304]{0,1:T(8,128)} %fusion.27, bf16[1280,1536]{1,0:T(8,128)(2,1)} %all-gather.5.cloned.1.call-done, bf16[1120,1536]{1,0:T(8,128)(2,1)} %param.20), kind=kOutput, calls=%fused_computation.10 | convolution fusion | flops 4551966720 | bytes 28016640 | tf_op jit(solution)/shard_map/dot_general | solution.py:1096
  296.2 6.2 convolution_convert_fusion.3
  302.4 14.7 %convolution_convert_fusion = bf16[1536,2304]{1,0:T(8,128)(2,1)} fusion(bf16[1280,1536]{1,0:T(8,128)(2,1)} %bitcast.125, bf16[1280,2304]{0,1:T(8,128)(2,1)} %pad_maximum_fusion), kind=kOutput, calls=%fused_computation | convolution fusion | flops 9063235584 | bytes 16908288 | tf_op jit(solution)/shard_map/dot_general | solution.py:1108
  317.7 14.9 %convolution_convert_fusion.5 = bf16[1280,1536]{1,0:T(8,128)(2,1)} fusion(bf16[1280,2304]{0,1:T(8,128)(2,1)} %pad_maximum_fusion, bf16[1536,2304]{1,0:T(8,128)(2,1)} %all-gather.7.cloned.1.call-done), kind=kOutput, calls=%fused_computation.6 | convolution fusion | flops 9061662720 | bytes 16908288 | tf_op jit(solution)/shard_map/dot_general | solution.py:1115
  332.6 41.6 %shard_map.197 = f32[160,1536]{1,0:T(8,128)} custom-call(bf16[8,160,1536]{2,1,0:T(8,128)(2,1)} %bitcast.122), custom_call_target="tpu_custom_call" | custom-call | bytes 31457280 | tf_op jit(solution)/shard_map/pallas_call | solution.py:925
  381.2 4.4 convolution_convert_fusion.6
  387.3 29.3 %attend_backward.1 = (f32[2,2,2,240,128]{4,3,2,1,0:T(8,128)}, bf16[1280,2048]{1,0:T(8,128)(2,1)}) custom-call(s32[18]{0:T(128)} %pad_add_fusion.scalars, bf16[2,2,2,240,128]{4,3,2,1,0:T(8,128)(2,1)} %bitcast.119, bf16[2,2,2,240,128]{4,3,2,1,0:T(8,128)(2,1)} %bitcast.133, f32[2,2,2,240,128]{4,3,2,1,0:T(8,128)} %get-tuple-element.36.att_ref, ...), custom_call_target="tpu_custom_call" | custom-call | tf_op jit(solution)/shard_map/attend_backward/pallas_call | solution.py:252
  416.7 7.1 convolution_convert_fusion.1
  423.8 80.0 %shard_map.198 = (f32[40,2048]{1,0:T(8,128)}, f32[160,1536]{1,0:T(8,128)}) custom-call(bf16[32,40,2048]{2,1,0:T(8,128)(2,1)} %bitcast.117, bf16[8,160,1536]{2,1,0:T(8,128)(2,1)} %bitcast.126), custom_call_target="tpu_custom_call" | custom-call | bytes 83886080 | tf_op jit(solution)/shard_map/pallas_call | solution.py:877
  503.8 35.0 %shard_map.200 = bf16[8,48,2304]{2,1,0:T(8,128)(2,1)} custom-call(bf16[8,48,2304]{2,1,0:T(8,128)(2,1)} %bitcast.136), custom_call_target="tpu_custom_call" | custom-call | bytes 56623104 | tf_op jit(solution)/shard_map/pallas_call | solution.py:357
  546.7 4.8 convolution_convert_fusion.4
  552.3 6.3 slice_convert_fusion
  560.2 6.6 multiply_reduce_fusion.1
  567.7 4.9 convolution_convert_fusion.2
  572.6 182.6 %shard_map.199 = (f32[4,8,128]{2,1,0:T(8,128)}, f32[4,48,2048]{2,1,0:T(8,128)}, f32[4,48,1536]{2,1,0:T(8,128)}) custom-call(f32[32,8,128]{2,1,0:T(8,128)} %bitcast.143, bf16[8,4,48,2048]{3,2,1,0:T(8,128)(2,1)} %bitcast.105, bf16[8,4,48,1536]{3,2,1,0:T(8,128)(2,1)} %bitcast.106), custom_call_target="tpu_custom_call" | custom-call | bytes 2097152 | tf_op jit(solution)/shard_map/pallas_call | solution.py:877
  761.5 8.9 %unpack.1 = (f32[4,48,8960]{2,1,0:T(8,128)}, f32[4,48,8960]{2,1,0:T(8,128)}) custom-call(bf16[4,8,48,2304]{3,2,1,0:T(8,128)(2,1)} %bitcast.113), custom_call_target="tpu_custom_call" | custom-call | tf_op jit(solution)/shard_map/unpack/pallas_call | solution.py:973
  (209 shorter events, 72.2 us)
Async XLA Ops:
  7.2 240.6 %all-gather.7.cloned.1.call-start = ((), (), s32[]{:S(2)}) async-start(), calls=%async_computation.2 | async-start | bytes 8847360 | tf_op jit(solution)/shard_map/all_gather | solution.py:1073
  74.4 4.6 copy-start.28
  78.6 7.1 copy-start.26
  85.8 54.5 %copy-start.12 = (bf16[40,4,1536]{2,1,0:T(4,128)(2,1)S(1)}, bf16[40,4,1536]{2,1,0:T(4,128)(2,1)}, u32[]{:S(2)}) copy-start(bf16[40,4,1536]{2,1,0:T(4,128)(2,1)} %param.21) | copy-start | bytes 1474564
  140.2 139.4 %all-gather.5.cloned.1.call-start = ((), (), s32[]{:S(2)}) async-start(), calls=%async_computation.1 | async-start | bytes 4423680 | tf_op jit(solution)/shard_map/all_gather | solution.py:1036
  141.2 362.6 %reduce-scatter.2.cloned.1.call-start = ((), (), s32[]{:S(2)}) async-start(), calls=%async_computation.3 | async-start | bytes 8847360 | tf_op jit(solution)/shard_map/reduce_scatter | solution.py:1111
  143.2 41.5 %copy-start.2 = (f32[160,1536]{1,0:T(8,128)}, f32[160,1536]{1,0:T(8,128)S(1)}, u32[]{:S(2)}) copy-start(f32[160,1536]{1,0:T(8,128)S(1)} %reshape.515) | copy-start | bytes 2949124
  188.2 59.6 %copy-start.22 = (f32[160]{0:T(256)}, f32[160]{0:T(256)S(1)}, u32[]{:S(2)}) copy-start(f32[160]{0:T(256)S(1)} %add_rsqrt_fusion.1) | copy-start | bytes 1924
  291.2 5.1 copy-start.29
  317.1 235.2 %all-reduce.5.cloned.1.call-start = ((), (), s32[]{:S(2)}) async-start(), calls=%async_computation.4 | async-start | bytes 7077888 | tf_op jit(solution)/shard_map/psum | solution.py:1104
  317.7 443.8 %all-gather.9.cloned.1.call-start = ((), (), s32[]{:S(2)}) async-start(), calls=%async_computation.5 | async-start | bytes 8847360 | tf_op jit(solution)/shard_map/all_gather | solution.py:1150
  374.2 4.9 copy-start.20
  374.2 4.9 copy-start.23
  386.2 30.5 %copy-start.30 = (bf16[1120,1536]{1,0:T(8,128)(2,1)S(1)}, bf16[1120,1536]{1,0:T(8,128)(2,1)}, u32[]{:S(2)}) copy-start(bf16[1120,1536]{1,0:T(8,128)(2,1)} %param.20) | copy-start | bytes 10321924
  387.3 29.3 %copy-start.32 = (bf16[1280,1152]{0,1:T(8,128)(2,1)S(1)}, bf16[1280,1152]{0,1:T(8,128)(2,1)}, u32[]{:S(2)}) copy-start(bf16[1280,1152]{0,1:T(8,128)(2,1)} %copy-done.31) | copy-start | bytes 8847364
  503.7 35.1 %copy-start.18 = (f32[40,4]{1,0:T(8,128)S(1)}, f32[40,4]{1,0:T(8,128)}, u32[]{:S(2)}) copy-start(f32[40,4]{1,0:T(8,128)} %copy-done.17) | copy-start | bytes 1924
  503.7 35.2 %copy-start.25 = (f32[40,4]{0,1:T(4,128)S(1)}, f32[40,4]{0,1:T(4,128)}, u32[]{:S(2)}) copy-start(f32[40,4]{0,1:T(4,128)} %get-tuple-element.80) | copy-start | bytes 1924
  503.8 35.4 %copy-start.27 = (f32[64]{0:T(128)S(1)}, f32[64]{0:T(128)}, u32[]{:S(2)}) copy-start(f32[64]{0:T(128)} %copy-done.26) | copy-start | bytes 772
  503.8 36.6 %copy-start.11 = (f32[2,2,2,240,128]{4,3,2,1,0:T(8,128)S(1)}, f32[2,2,2,240,128]{4,3,2,1,0:T(8,128)}, u32[]{:S(2)}) copy-start(f32[2,2,2,240,128]{4,3,2,1,0:T(8,128)} %get-tuple-element.46) | copy-start | bytes 2949124
  538.9 28.7 %copy-start.24 = (f32[160]{0:T(256)}, f32[160]{0:T(256)S(1)}, u32[]{:S(2)}) copy-start(f32[160]{0:T(256)S(1)} %rsqrt.22) | copy-start | bytes 1924
  552.3 6.4 copy-start.13
  552.3 6.9 copy-start.14
  760.9 9.5 %copy-start.9 = (f32[4,48,2048]{2,1,0:T(8,128)S(1)}, f32[4,48,2048]{2,1,0:T(8,128)}, u32[]{:S(2)}) copy-start(f32[4,48,2048]{2,1,0:T(8,128)} %get-tuple-element.50) | copy-start | bytes 4718596
  761.5 11.7 %copy-start.1 = (bf16[192,2048]{1,0:T(8,128)(2,1)S(1)}, bf16[192,2048]{1,0:T(8,128)(2,1)}, u32[]{:S(2)}) copy-start(bf16[192,2048]{1,0:T(8,128)(2,1)} %param.14) | copy-start | bytes 2359300
  (14 other events, 36.0 us)
Sparse Core Ops, SparseCore 0:
  140.4 92.2 all-gather.6
  234.9 44.6 all-gather.4
  317.2 75.3 reduce-scatter.1
  395.7 104.8 all-reduce.4
  538.9 86.1 all-gather.8

commit v8 on v6

--- a/solution.py
+++ b/solution.py
@@ -1000,12 +1000,13 @@
     small = lax.dynamic_slice_in_dim(small, own_ctx, 1, 0)
     small = jnp.pad(small, ((0, 0), (0, 16 * HD - small_width))).reshape(16, HD)
     width = -(-columns // HD) * HD
-    w_qkv_all, w_o_all, small_all, gate_up_cut = gather(
-        [own_cut(w_qkv), own_cut(w_o), small],
-        [by_rows, by_rows, by_rows],
+    w_qkv_all, w_o_all, small_all, cotangent_all = gather(
+        [own_cut(w_qkv), own_cut(w_o), small, cotangent.reshape(-1, D)],
+        [by_rows, by_rows, by_rows, lambda ctx, shard: shard],
         1,
-        swaps=[pack(own_cut(w_gate), own_cut(w_up), shard_count, columns, width)],
-    )
+        wide=(0, 1, 2),
+    )
+    cotangent_all = cotangent_all.reshape(-1, D)
     w_qkv_all = w_qkv_all.reshape(D, QKV)
     w_o_all = w_o_all.reshape(D, D)
     small_all = small_all.reshape(shard_count, ctx_size, -1)[:, :, :small_width]
@@ -1016,9 +1017,6 @@
     gain_one = small_all[:, bias_width : bias_width + gain_width].reshape(-1)
     gain_two = small_all[:, bias_width + gain_width :].reshape(-1)
 
-    gate_up_cols = lax.all_gather(
-        gate_up_cut.reshape(shard_count * cut, 2 * width), "ctx", axis=0, tiled=True
-    )
     down_padded = jnp.pad(w_down, ((0, width - columns), (0, 0)))
 
     inputs = layer_input.reshape(-1, D).astype(jnp.float32)
@@ -1039,10 +1037,15 @@
     own_kv = jnp.stack([key_tokens, value_raw.astype(jnp.bfloat16)], 1)
     own_kv = own_kv.reshape(rows_here, 2, SEQS, 2, KVH, HD).transpose(0, 2, 4, 1, 3, 5)
     own_kv = own_kv.reshape(rows_here, SEQS * KVH * 4 * HD)
-    all_kv, cotangent_all = gather(
-        [own_kv, cotangent.reshape(-1, D)], [by_tokens, lambda ctx, shard: shard], 2, wide=(0,)
-    )
-    cotangent_all = cotangent_all.reshape(-1, D)
+    all_kv, gate_up_cut = gather(
+        [own_kv],
+        [by_tokens],
+        2,
+        swaps=[pack(own_cut(w_gate), own_cut(w_up), shard_count, columns, width)],
+    )
+    gate_up_cols = lax.all_gather(
+        gate_up_cut.reshape(shard_count * cut, 2 * width), "ctx", axis=0, tiled=True
+    )
     all_kv = all_kv.reshape(-1, SEQS * KVH * 4 * HD)
     queries = to_groups(query_tokens, rows_here)
     scalars = jnp.concatenate(
@@ -1070,23 +1073,26 @@
     grad_gate_up = jnp.concatenate([grad_gate, grad_hidden * activated], -1).astype(jnp.bfloat16)
     grad_tokens = lax.dot_general(
         grad_gate_up, gate_up_cols, CONTRACT_LAST, preferred_element_type=jnp.float32
-    )
+    ).astype(jnp.bfloat16)
     grad_normed_two = lax.psum_scatter(
-        grad_tokens.astype(jnp.bfloat16), "fsdp", scatter_dimension=0, tiled=True
-    )
+        grad_tokens, "fsdp", scatter_dimension=0, tiled=True
+    ).astype(jnp.float32)
+    grad_gate_up, hidden, grad_tokens = lax.optimization_barrier(
+        (grad_gate_up, hidden, grad_tokens)
+    )
+    gate_up_terms = lax.dot_general(
+        tokens_all, grad_gate_up, CONTRACT_FIRST, preferred_element_type=jnp.float32
+    ).astype(jnp.bfloat16)
+    gate_up_rows = lax.psum_scatter(gate_up_terms, "ctx", scatter_dimension=0, tiled=True)
     down_terms = lax.dot_general(
         hidden, cotangent_all, CONTRACT_FIRST, preferred_element_type=jnp.float32
     ).astype(jnp.bfloat16)
-    gate_up_terms = lax.dot_general(
-        tokens_all, grad_gate_up, CONTRACT_FIRST, preferred_element_type=jnp.float32
-    ).astype(jnp.bfloat16)
+    down_rows = lax.psum(down_terms, "ctx")
     mixed_terms = jnp.dot(hidden, down_padded, preferred_element_type=jnp.float32).astype(jnp.bfloat16)
-    down_rows = lax.psum(down_terms, "ctx")
-    gate_up_rows = lax.psum_scatter(gate_up_terms, "ctx", scatter_dimension=0, tiled=True)
     grad_normed_two, down_terms, gate_up_terms, mixed_terms = lax.optimization_barrier(
         (grad_normed_two, down_terms, gate_up_terms, mixed_terms)
     )
-    grad_normed_two = unmix_features(grad_normed_two.astype(jnp.float32))
+    grad_normed_two = unmix_features(grad_normed_two)
     grad_middle_norm, grad_gain_two = norm_back(grad_normed_two, unit_two, scale_two, gain_two)
     grad_middle = cotangent.reshape(-1, D).astype(jnp.float32) + grad_middle_norm
     grad_branch_one = grad_middle.astype(jnp.bfloat16)
@@ -1107,18 +1113,15 @@
         block_rows,
         rows_here,
     )
-    grad_kv, mixed_rows = scatter(
+    (grad_kv,) = scatter(
         [grad_kv_full.reshape(-1, rows_here, SEQS * KVH * 4 * HD)],
         by_tokens,
         3,
         out_dtype=jnp.float32,
-        lines=[mixed_terms.reshape(shard_count, -1, D)],
     )
     gate_up_rows, grad_kv = lax.optimization_barrier((gate_up_rows, grad_kv))
     gate_up_rows = exchange(gate_up_rows.reshape(shard_count, cut, 2 * width), 5)
     gate_up_rows = lax.all_gather(gate_up_rows, "ctx", axis=0, tiled=False)
-    mixed_out = middle + mixed_rows
-    output = mixed_out.astype(jnp.bfloat16).reshape(rows_here, slots, D)
     grad_kv_low = narrowed(grad_kv).reshape(rows_here, SEQS, KVH, 2, 2, HD)
     grad_kv_low = grad_kv_low.transpose(0, 3, 1, 4, 2, 5).reshape(-1, 2 * kv_width)
     grad_query_tokens = from_groups(narrowed(grad_queries), rows_here) * query_scale
@@ -1149,7 +1152,7 @@
     )
     small_terms = small_terms.reshape(ctx_size * shard_count, small_width)
     small_terms = jnp.pad(small_terms, ((0, 0), (0, 8 * HD - small_width)))
-    qkv_rows, small_rows, o_rows = scatter(
+    qkv_rows, small_rows, o_rows, mixed_rows = scatter(
         [
             qkv_terms.reshape(-1, cut, QKV),
             small_terms.reshape(-1, 8, HD),
@@ -1157,8 +1160,13 @@
         by_rows,
         4,
         spread_ctx=True,
-        lines=[o_terms.reshape(shard_count, ctx_size, cut, D)],
-    )
+        lines=[
+            o_terms.reshape(shard_count, ctx_size, cut, D),
+            mixed_terms.reshape(shard_count, -1, D),
+        ],
+    )
+    mixed_out = middle + mixed_rows
+    output = mixed_out.astype(jnp.bfloat16).reshape(rows_here, slots, D)
     small_rows = small_rows.reshape(ctx_size, -1)[:, :small_width].reshape(-1)
     bias_start = 2 * gain_width
     value_start = bias_start + QK // shard_count

time: 733 us -> 773 us (1.055)
  waiting for transfers between devices: 43.7 us -> 70.3 us
    pallas_call x2, Pallas kernels: 179 us -> 201 us  [scatter(): pl.pallas_call(functools.partial(scatter_kernel, arity, ctx_size, pair_co...]
    psum x1, waiting for transfers between devices: 30.9 us -> 51.5 us  [shards(): down_rows = lax.psum(down_terms, 'ctx')]
    pallas_call x3, Pallas kernels: 213 us -> 200 us  [gather(): pl.pallas_call(functools.partial(gather_kernel, arity, ctx_size, pair_cou...]
  transfers between devices with their start and end apart: 5 -> 5, of which waited for: 2 -> 3; matrix products, arithmetic and copies ran while one was open for 16% -> 14% of each run, Pallas kernels for 57% -> 46%
where the time goes in v8:
time: 773 us; the launch traced here: 763 us
  Pallas kernels  503 us (65%)
  matrix products  95.1 us (12%)
  waiting for transfers between devices  70.3 us (9%)
  local copies, waits for them, and re-layouts  45.7 us (6%)
  other arithmetic  33.4 us (4%)
  between operations  15.1 us (2%)
    pallas_call x2, Pallas kernels, scatter(): pl.pallas_call(functools.partial(scatter_kernel, arity, ctx_size, pair_co...  201 us
    pallas_call x3, Pallas kernels, gather(): pl.pallas_call(functools.partial(gather_kernel, arity, ctx_size, pair_cou...  200 us
    psum x1, waiting for transfers between devices, shards(): down_rows = lax.psum(down_terms, 'ctx')  51.5 us
    pallas_call x1, Pallas kernels, exchange(): pl.pallas_call(functools.partial(exchange_kernel, shard_count // 2), in_s...  32.8 us
    pallas_call x1, Pallas kernels, attend_backward(): pl.pallas_call(kernel, grid_spec=pltpu.PrefetchScalarGridSpec(num_scalar_...  29.1 us
    pallas_call x1, Pallas kernels, attend_forward(): pl.pallas_call(kernel, grid_spec=pltpu.PrefetchScalarGridSpec(num_scalar_...  27.9 us
    dot_general x1, matrix products, shards(): jnp.dot(tokens_all, gate_up_cols, preferred_element_type=jnp.float32)  15.5 us
  transfers between devices with their start and end apart: 5, of which 3 were waited for; matrix products, arithmetic and copies ran while one was open for 14% of the time, Pallas kernels for 46%

profile of v8, /device:TPU:0, one launch (start us, length us, event | category | flops | bytes accessed | tf_op | source)
XLA Modules:
  0.0 762.6 jit_solution(14043893047511927144)
XLA Ops:
  14.0 90.9 %shard_map.194 = (bf16[32,48,2048]{2,1,0:T(8,128)(2,1)}, bf16[32,48,1536]{2,1,0:T(8,128)(2,1)}, bf16[32,16,128]{2,1,0:T(8,128)(2,1)}, bf16[8,160,1536]{2,1,0:T(8,128)(2,1)}) custom-call(bf16[48,2048]{1,0:T(8,128)(2,1)} %constant_dynamic-slice_fusion.4.refs_0_, bf16[48,1536]{1,0:T(8,128)(2,1)} %constant_dynamic-slice_fusion.3.refs_1_, ...), custom_call_target="tpu_custom_call" | custom-call | bytes 107479040 | tf_op jit(solution)/shard_map/pallas_call | solution.py:570
  109.6 4.0 convolution_add_fusion.1
  124.1 51.2 %shard_map.195 = (bf16[32,40,2048]{2,1,0:T(8,128)(2,1)}, bf16[8,48,2304]{2,1,0:T(8,128)(2,1)}) custom-call(bf16[40,2048]{1,0:T(8,128)(2,1)} %reshape.479.refs_0_, bf16[8,48,2304]{2,1,0:T(8,128)(2,1)} %pack.1.refs_1_), custom_call_target="tpu_custom_call" | custom-call | bytes 20971520 | tf_op jit(solution)/shard_map/pallas_call | solution.py:570
  189.4 27.9 %attend_forward.1 = (f32[2,2,2,240,128]{4,3,2,1,0:T(8,128)}, f32[2,2,2,1,240]{4,3,2,1,0:T(1,128)}) custom-call(s32[18]{0:T(128)} %pad_add_fusion.scalars, bf16[2,2,2,240,128]{4,3,2,1,0:T(8,128)(2,1)} %bitcast.117, bf16[1280,2048]{1,0:T(8,128)(2,1)} %bitcast.108), custom_call_target="tpu_custom_call" | custom-call | tf_op jit(solution)/shard_map/attend_forward/pallas_call | solution.py:154
  224.4 57.9 %shard_map.196 = bf16[8,160,1536]{2,1,0:T(8,128)(2,1)} custom-call(bf16[160,1536]{1,0:T(8,128)(2,1)} %copy.128.refs_0_), custom_call_target="tpu_custom_call" | custom-call | bytes 62914560 | tf_op jit(solution)/shard_map/pallas_call | solution.py:570
  282.4 15.5 %fusion.28 = f32[1280,2304]{0,1:T(8,128)} fusion(bf16[1280,1536]{1,0:T(8,128)(2,1)} %bitcast.123, bf16[1536,2304]{1,0:T(8,128)(2,1)} %all-gather.4.cloned.1.call-done), kind=kOutput, calls=%fused_computation.118 | convolution fusion | flops 9059696640 | bytes 22806528 | tf_op jit(solution)/shard_map/dot_general | solution.py:1064
  297.9 12.9 %multiply_convert_fusion.2 = (bf16[1280,1152]{0,1:T(8,128)(2,1)S(1)}, bf16[1280,1152]{0,1:T(8,128)(2,1)S(1)}, bf16[1280,1152]{0,1:T(8,128)(2,1)}) fusion(f32[1280,2304]{0,1:T(8,128)} %fusion.28, bf16[1280,1536]{1,0:T(8,128)(2,1)} %bitcast.152, bf16[1120,1536]{1,0:T(8,128)(2,1)} %param.20), kind=kOutput, calls=%fused_computation.9 | convolution fusion | flops 4551966720 | bytes 28016640 | tf_op jit(solution)/shard_map/dot_general | solution.py:1069
  313.3 11.1 %convolution_convert_fusion.5 = bf16[1280,1536]{1,0:T(8,128)(2,1)} fusion(bf16[1536,2304]{1,0:T(8,128)(2,1)S(1)} %bitcast.149, bf16[1280,1152]{0,1:T(8,128)(2,1)S(1)} %get-tuple-element.60, bf16[1280,1152]{0,1:T(8,128)(2,1)S(1)} %get-tuple-element.59), kind=kOutput, calls=%fused_computation.5 | convolution fusion | flops 9073459200 | bytes 16908288 | tf_op jit(solution)/shard_map/dot_general | solution.py:1074
  328.6 11.3 %convolution_convert_fusion = bf16[1536,2304]{1,0:T(8,128)(2,1)} fusion(bf16[1280,1536]{1,0:T(8,128)(2,1)S(1)} %bitcast.124, bf16[1280,2304]{0,1:T(8,128)(2,1)S(1)} %pad_maximum_fusion), kind=kOutput, calls=%fused_computation | convolution fusion | flops 9063235584 | bytes 16908288 | tf_op jit(solution)/shard_map/dot_general | solution.py:1083
  340.1 9.6 %convolution_convert_fusion.1 = bf16[1280,1536]{1,0:T(8,128)(2,1)} fusion(bf16[1280,1152]{0,1:T(8,128)(2,1)} %get-tuple-element.40, bf16[1120,1536]{1,0:T(8,128)(2,1)} %param.20), kind=kOutput, calls=%fused_computation.1 | convolution fusion | flops 4531814400 | bytes 10321920 | tf_op jit(solution)/shard_map/dot_general | solution.py:1091
  349.7 6.2 convolution_convert_fusion.3
  355.9 13.1 %reduce-scatter.3.cloned.1.call-done = bf16[160,1536]{1,0:T(8,128)(2,1)} async-done(((bf16[1280,1536]{1,0:T(8,128)(2,1)}), bf16[160,1536]{1,0:T(8,128)(2,1)}) %reduce-scatter.3.cloned.1.call-update) | async-done | bytes 491536 | tf_op jit(solution)/shard_map/reduce_scatter | solution.py:1077
  375.9 5.1 convolution_convert_fusion.6
  382.7 29.1 %attend_backward.1 = (f32[2,2,2,240,128]{4,3,2,1,0:T(8,128)}, bf16[1280,2048]{1,0:T(8,128)(2,1)}) custom-call(s32[18]{0:T(128)} %pad_add_fusion.scalars, bf16[2,2,2,240,128]{4,3,2,1,0:T(8,128)(2,1)} %bitcast.118, bf16[2,2,2,240,128]{4,3,2,1,0:T(8,128)(2,1)} %bitcast.131, f32[2,2,2,240,128]{4,3,2,1,0:T(8,128)} %get-tuple-element.36.att_ref, ...), custom_call_target="tpu_custom_call" | custom-call | tf_op jit(solution)/shard_map/attend_backward/pallas_call | solution.py:252
  411.8 44.8 %shard_map.197 = f32[40,2048]{1,0:T(8,128)} custom-call(bf16[32,40,2048]{2,1,0:T(8,128)(2,1)} %bitcast.116), custom_call_target="tpu_custom_call" | custom-call | bytes 83886080 | tf_op jit(solution)/shard_map/pallas_call | solution.py:877
  456.6 5.7 reduce-scatter.5.cloned.1.call-done
  462.3 32.8 %shard_map.199 = bf16[8,48,2304]{2,1,0:T(8,128)(2,1)} custom-call(bf16[8,48,2304]{2,1,0:T(8,128)(2,1)} %bitcast.134), custom_call_target="tpu_custom_call" | custom-call | bytes 56623104 | tf_op jit(solution)/shard_map/pallas_call | solution.py:357
  502.5 3.6 convolution_convert_fusion.4
  506.8 51.5 %all-reduce.5.cloned.1.call-done = bf16[1152,1536]{1,0:T(8,128)(2,1)} async-done(((bf16[1152,1536]{1,0:T(8,128)(2,1)}), bf16[1152,1536]{1,0:T(8,128)(2,1)}) %all-reduce.5.cloned.1.call-update) | async-done | bytes 3538960 | tf_op jit(solution)/shard_map/psum | solution.py:1090
  558.3 5.8 slice_convert_fusion
  565.6 7.6 multiply_reduce_fusion
  574.1 4.9 convolution_convert_fusion.2
  579.0 155.8 %shard_map.198 = (bf16[4,48,2048]{2,1,0:T(8,128)(2,1)}, f32[4,8,128]{2,1,0:T(8,128)}, f32[4,48,1536]{2,1,0:T(8,128)}, f32[160,1536]{1,0:T(8,128)}) custom-call(bf16[32,48,2048]{2,1,0:T(8,128)(2,1)} %bitcast.104, f32[32,8,128]{2,1,0:T(8,128)} %bitcast.140, bf16[8,4,48,1536]{3,2,1,0:T(8,128)(2,1)} %bitcast.105, bf16[8,160,1536]{2,1,0:T(8,128)(2,1)} %bitcast.121), custom_call_target="tpu_custom_call" | custom-call | bytes 102760448 | tf_op jit(solution)/shard_map/pallas_call | solution.py:877
  745.7 8.9 %unpack.1 = (f32[4,48,8960]{2,1,0:T(8,128)}, f32[4,48,8960]{2,1,0:T(8,128)}) custom-call(bf16[4,8,48,2304]{3,2,1,0:T(8,128)(2,1)} %bitcast.112), custom_call_target="tpu_custom_call" | custom-call | tf_op jit(solution)/shard_map/unpack/pallas_call | solution.py:943
  (220 shorter events, 80.4 us)
Async XLA Ops:
  7.2 275.2 %all-gather.4.cloned.1.call-start = ((), (), s32[]{:S(2)}) async-start(), calls=%async_computation.2 | async-start | bytes 8847360 | tf_op jit(solution)/shard_map/all_gather | solution.py:1046
  106.0 8.7 %copy-start.31 = (f32[64]{0:T(128)}, f32[64]{0:T(128)S(1)}, u32[]{:S(2)}) copy-start(f32[64]{0:T(128)S(1)} %multiply_power_fusion) | copy-start | bytes 772
  120.9 54.7 %copy-start.11 = (bf16[40,4,1536]{2,1,0:T(4,128)(2,1)S(1)}, bf16[40,4,1536]{2,1,0:T(4,128)(2,1)}, u32[]{:S(2)}) copy-start(bf16[40,4,1536]{2,1,0:T(4,128)(2,1)} %param.11) | copy-start | bytes 1474564
  175.3 193.7 %reduce-scatter.3.cloned.1.call-start = ((), (), s32[]{:S(2)}) async-start(), calls=%async_computation.3 | async-start | bytes 4423680 | tf_op jit(solution)/shard_map/reduce_scatter | solution.py:1077
  175.7 43.7 %copy-start.2 = (f32[160,1536]{1,0:T(8,128)}, f32[160,1536]{1,0:T(8,128)S(1)}, u32[]{:S(2)}) copy-start(f32[160,1536]{1,0:T(8,128)S(1)} %reshape.514) | copy-start | bytes 2949124
  282.4 30.9 %slice-start = ((s8[7077888]{0:T(1024)(128)(4,1)}), s8[4194304]{0:T(1024)(128)(4,1)S(1)}, s32[]{:S(2)}) async-start(s8[7077888]{0:T(1024)(128)(4,1)} %bitcast.148), calls=%async_computation.7 | async-start | bytes 8388608
  297.9 15.4 %slice-start.1 = ((s8[7077888]{0:T(1024)(128)(4,1)}), s8[2883584]{0:T(1024)(128)(4,1)S(1)}, s32[]{:S(2)}) async-start(s8[7077888]{0:T(1024)(128)(4,1)} %bitcast.148), calls=%async_computation.8 | async-start | bytes 5767168
  324.4 137.9 %reduce-scatter.5.cloned.1.call-start = ((), (), s32[]{:S(2)}) async-start(), calls=%async_computation.4 | async-start | bytes 8847360 | tf_op jit(solution)/shard_map/reduce_scatter | solution.py:1086
  340.0 218.3 %all-reduce.5.cloned.1.call-start = ((), (), s32[]{:S(2)}) async-start(), calls=%async_computation.5 | async-start | bytes 7077888 | tf_op jit(solution)/shard_map/psum | solution.py:1090
  340.0 9.7 %copy-start.34 = (bf16[8,160,1536]{2,1,0:T(8,128)(2,1)S(1)}, bf16[8,160,1536]{2,1,0:T(8,128)(2,1)}, u32[]{:S(2)}) copy-start(bf16[8,160,1536]{2,1,0:T(8,128)(2,1)} %get-tuple-element.38) | copy-start | bytes 11796484
  340.0 9.6 %copy-start.35 = (bf16[1280,1152]{0,1:T(8,128)(2,1)S(1)}, bf16[1280,1152]{0,1:T(8,128)(2,1)}, u32[]{:S(2)}) copy-start(bf16[1280,1152]{0,1:T(8,128)(2,1)} %get-tuple-element.40) | copy-start | bytes 8847364
  370.1 375.6 %all-gather.6.cloned.1.call-start = ((), (), s32[]{:S(2)}) async-start(), calls=%async_computation.6 | async-start | bytes 8847360 | tf_op jit(solution)/shard_map/all_gather | solution.py:1124
  456.6 38.6 %copy-start.24 = (f32[40,4]{1,0:T(8,128)S(1)}, f32[40,4]{1,0:T(8,128)}, u32[]{:S(2)}) copy-start(f32[40,4]{1,0:T(8,128)} %copy-done.23) | copy-start | bytes 1924
  456.6 38.7 %copy-start.30 = (f32[40,4]{0,1:T(4,128)S(1)}, f32[40,4]{0,1:T(4,128)}, u32[]{:S(2)}) copy-start(f32[40,4]{0,1:T(4,128)} %get-tuple-element.80) | copy-start | bytes 1924
  456.6 38.9 %copy-start.32 = (f32[64]{0:T(128)S(1)}, f32[64]{0:T(128)}, u32[]{:S(2)}) copy-start(f32[64]{0:T(128)} %copy-done.31) | copy-start | bytes 772
  456.6 40.1 %copy-start.19 = (f32[2,2,2,240,128]{4,3,2,1,0:T(8,128)S(1)}, f32[2,2,2,240,128]{4,3,2,1,0:T(8,128)}, u32[]{:S(2)}) copy-start(f32[2,2,2,240,128]{4,3,2,1,0:T(8,128)} %get-tuple-element.44) | copy-start | bytes 2949124
  495.3 78.9 %copy-start.27 = (f32[160]{0:T(256)}, f32[160]{0:T(256)S(1)}, u32[]{:S(2)}) copy-start(f32[160]{0:T(256)S(1)} %rsqrt.21) | copy-start | bytes 1924
  506.8 57.3 %copy-start.17 = (f32[40,2048]{1,0:T(8,128)S(1)}, f32[40,2048]{1,0:T(8,128)}, u32[]{:S(2)}) copy-start(f32[40,2048]{1,0:T(8,128)} %shard_map.197) | copy-start | bytes 983044
  506.8 57.8 %copy-start.20 = (f32[160,128]{1,0:T(8,128)S(1)}, f32[160,128]{1,0:T(8,128)}, u32[]{:S(2)}) copy-start(f32[160,128]{1,0:T(8,128)} %get-tuple-element.73) | copy-start | bytes 245764
  565.6 7.6 %copy-start.26 = (f32[8,192]{1,0:T(8,128)S(1)}, f32[8,192]{1,0:T(8,128)}, u32[]{:S(2)}) copy-start(f32[8,192]{1,0:T(8,128)} %reshape.499) | copy-start | bytes 18436
  734.8 5.0 copy-start.4
  734.9 5.0 copy-start.7
  745.7 8.9 %copy-start.18 = (f32[4,48,1536]{2,1,0:T(8,128)S(1)}, f32[4,48,1536]{2,1,0:T(8,128)}, u32[]{:S(2)}) copy-start(f32[4,48,1536]{2,1,0:T(8,128)} %get-tuple-element.51) | copy-start | bytes 3538948
  745.7 10.0 %copy-start.1 = (bf16[192,2048]{1,0:T(8,128)(2,1)S(1)}, bf16[192,2048]{1,0:T(8,128)(2,1)}, u32[]{:S(2)}) copy-start(bf16[192,2048]{1,0:T(8,128)(2,1)} %param.14) | copy-start | bytes 2359300
  (19 other events, 53.0 us)
Sparse Core Ops, SparseCore 0:
  175.4 93.2 all-gather.3
  324.5 44.4 reduce-scatter.2
  372.0 90.2 reduce-scatter.4
  465.9 92.3 all-reduce.4
  560.0 97.0 all-gather.5

commit v9 on v8

--- a/solution.py
+++ b/solution.py
@@ -25,53 +25,38 @@
 CONTRACT_FIRST = (((0,), (0,)), ((), ()))
 
 
-def narrowed(values):
-    return lax.optimization_barrier(values.astype(jnp.bfloat16)).astype(jnp.float32)
-
-
-def block_positions(block_order, first_row, row_count, block_rows, ctx_size):
-    row_index = first_row + jnp.arange(row_count, dtype=jnp.int32)
-    slot_index = jnp.arange(2 * SEQS, dtype=jnp.int32)
-    entries = (slot_index // SEQS)[None, :] * ctx_size + (row_index // block_rows)[:, None]
-    tiled = jnp.tile(block_order, (2, 1))
-    entry_ids = jnp.arange(2 * ctx_size, dtype=jnp.int32)
-    picked = jnp.sum(
-        jnp.where(entries[:, :, None] == entry_ids[None, None, :], tiled[None, :, :], 0), -1
-    )
-    return picked * block_rows + (row_index % block_rows)[:, None]
+def by_slot(tokens):
+    return tokens.transpose(1, 0, 2).reshape(-1, tokens.shape[2])
+
+
+def from_slot(tokens, row_count):
+    return tokens.reshape(2 * SEQS, row_count, -1).transpose(1, 0, 2)
 
 
 def to_groups(tokens, row_count):
-    shaped = tokens.reshape(row_count, 2, SEQS, KVH, H // KVH, HD)
-    return shaped.transpose(2, 1, 3, 4, 0, 5).reshape(SEQS, 2, KVH, H // KVH * row_count, HD)
+    shaped = tokens.reshape(2, SEQS, row_count, KVH, H // KVH, HD)
+    return shaped.transpose(1, 0, 3, 4, 2, 5).reshape(SEQS, 2, KVH, H // KVH * row_count, HD)
 
 
 def from_groups(grouped, row_count):
-    shaped = grouped.reshape(SEQS, 2, KVH, H // KVH, row_count, HD).transpose(4, 1, 0, 2, 3, 5)
+    shaped = grouped.reshape(SEQS, 2, KVH, H // KVH, row_count, HD).transpose(1, 0, 4, 2, 3, 5)
     return shaped.reshape(row_count * 2 * SEQS, H * HD)
 
 
-def rope_tables(positions):
+def turn_tables(block_order, own_ctx, ctx_size, block_rows, first_row, row_count):
     half_width = HD // 2
     frequency = THETA ** (-jnp.arange(half_width, dtype=jnp.float32) * 2.0 / HD)
-    angles = positions.astype(jnp.float32)[:, None] * frequency[None, :]
-    cosine_table = jnp.concatenate([jnp.cos(angles), jnp.cos(angles)], -1)[:, None, :]
-    sine_table = jnp.concatenate([jnp.sin(angles), jnp.sin(angles)], -1)[:, None, :]
-    return (cosine_table, sine_table)
-
-
-def rotate(head_values, cosine_table, sine_table):
-    half_width = HD // 2
-    turned = jnp.concatenate([-head_values[..., half_width:], head_values[..., :half_width]], -1)
-    return head_values * cosine_table + turned * sine_table
-
-
-def rotate_back(grad_values, cosine_table, sine_table):
-    half_width = HD // 2
-    moved = grad_values * sine_table
-    return grad_values * cosine_table + jnp.concatenate(
-        [moved[..., half_width:], -moved[..., :half_width]], -1
-    )
+    frequency = jnp.tile(frequency, 2)[None, :]
+    order = lax.dynamic_index_in_dim(block_order.reshape(SEQS, 2, ctx_size), own_ctx, 2, False)
+    start = (order.T.reshape(-1) * block_rows + first_row).astype(jnp.float32)
+    far = start[:, None] * frequency
+    near = jnp.arange(row_count, dtype=jnp.float32)[:, None] * frequency
+    far_cos, far_sin = jnp.cos(far)[:, None, :], jnp.sin(far)[:, None, :]
+    near_cos, near_sin = jnp.cos(near)[None], jnp.sin(near)[None]
+    sign = jnp.where(jnp.arange(HD) < half_width, -1.0, 1.0).astype(jnp.float32)
+    cosine = far_cos * near_cos - far_sin * near_sin
+    sine = (far_sin * near_cos + far_cos * near_sin) * sign
+    return cosine.reshape(-1, HD), sine.reshape(-1, HD)
 
 
 def normalize(values, gain):
@@ -512,19 +497,31 @@
             arrive(item, place, ctx_sems, (2, step, item))
             to_core(item, outs[item].at[place], ctx ^ 3, 3, step)
 
+    def straight_core(item, source, place, step):
+        sibling = (ctx, pair * 2 + 1 - core)
+        send(item, source, place, sibling, core_sems, (0, step, item), lambda: None)
+
+    def go_straight(item):
+        for step in range(1, pair_count):
+            there = lax.rem(pair + step, pair_count) * 2 + core
+            at = (0, step - 1, item)
+            send(item, sources[item], homes[item], (ctx, there), pair_sems, at, lambda: None)
+        straight_core(item, sources[item], homes[item], 0)
+
     locals_ = []
     for item in range(arity):
         copy = pltpu.make_async_copy(sources[item], outs[item].at[homes[item]], local_sem.at[item])
         copy.start()
         locals_.append(copy)
-    spread(0, wide)
+    spread(0, wide or range(arity))
     flows = []
     count = len(steps)
     for turn in range(1, count + 4):
         if turn < count:
-            when(present(turn), functools.partial(spread, turn, wide))
+            when(present(turn), functools.partial(spread, turn, wide or range(arity)))
         if turn == count:
-            spread(0, narrow)
+            for item in narrow if wide else ():
+                go_straight(item)
             for item in range(swaps):
                 flow = Exchange(
                     swap_sources[item],
@@ -540,13 +537,21 @@
         if square and 0 <= turn - 4 < count:
             when(present(turn - 4), functools.partial(collect_far, turn - 4))
 
-    for turn in range(1, count):
-        when(present(turn), functools.partial(spread, turn, narrow))
+    for item in narrow if wide else ():
+        for step in range(1, pair_count):
+            come = lax.rem(pair + pair_count - step, pair_count)
+            place = slots[item](ctx, come * 2 + core)
+            arrive(item, place, pair_sems, (0, step - 1, item))
+            straight_core(item, outs[item].at[place], place, step)
+    for item in narrow if wide else ():
+        for step in range(pair_count):
+            come = lax.rem(pair + pair_count - step, pair_count)
+            arrive(item, slots[item](ctx, come * 2 + 1 - core), core_sems, (0, step, item))
 
     def from_core(step):
         for way in (0, *ways):
             come = ctx_source(ctx, way, square, ctx_size) if way else ctx
-            for item in wide if way else range(arity):
+            for item in wide or range(arity):
                 arrive(item, slots[item](come, origin(step) * 2 + 1 - core), core_sems, (way, step, item))
 
     for step in range(count):
@@ -909,6 +914,149 @@
     )(*terms, *lines)
 
 
+def turned(values, cosine, signed_sine):
+    return values * cosine + pltpu.roll(values, HD // 2, 1) * signed_sine
+
+
+def turned_back(grads, cosine, signed_sine):
+    return grads * cosine + pltpu.roll(grads * signed_sine, HD // 2, 1)
+
+
+def slot_of(index):
+    return index % SEQS, index // SEQS
+
+
+def key_column(index, group, part):
+    seq, half = slot_of(index)
+    return (((seq * KVH + group) * 2 + half) * 2 + part) * HD
+
+
+def project_kernel(rows, x_ref, gain_ref, w_hbm, bias_ref, cos_ref, sin_ref, normed_ref, q_ref, kv_ref, w_ref, q_acc, sems):
+    wide = w_ref.shape[2]
+    copies = []
+    for part in range(w_ref.shape[0]):
+        copy = pltpu.make_async_copy(
+            w_hbm.at[:, part * wide : (part + 1) * wide], w_ref.at[part], sems.at[part]
+        )
+        copy.start()
+        copies.append(copy)
+    values = x_ref[...].astype(jnp.float32)
+    scale = lax.rsqrt(jnp.mean(values * values, -1, keepdims=True) + EPS)
+    normed = (values * scale * gain_ref[...]).astype(jnp.bfloat16)
+    normed_ref[...] = normed
+    cosine, sine = cos_ref[...], sin_ref[...]
+    for part, copy in enumerate(copies):
+        copy.wait()
+        columns = jnp.dot(normed, w_ref[part], preferred_element_type=jnp.float32)
+        columns = columns + bias_ref[:, part * wide : (part + 1) * wide]
+        for index in range(wide // HD):
+            head = part * (wide // HD) + index
+            piece = columns[:, index * HD : (index + 1) * HD]
+            if head < H + KVH:
+                piece = turned(piece, cosine, sine)
+            if head < H:
+                piece = piece * (HD**-0.5)
+            for slot in range(2 * SEQS):
+                seq, half = slot_of(slot)
+                own = piece[slot * rows : (slot + 1) * rows]
+                if head < H:
+                    group, member = head // (H // KVH), head % (H // KVH)
+                    q_acc[seq, half, group, member * rows : (member + 1) * rows] = own
+                else:
+                    group, kind = (head - H) % KVH, (head - H) // KVH
+                    at = key_column(slot, group, kind)
+                    kv_ref[:, at : at + HD] = own.astype(jnp.bfloat16)
+    q_ref[...] = q_acc[...].astype(jnp.bfloat16)
+
+
+def project(tokens, gain, weight, bias, cosine, signed_sine, rows):
+    vmem = pl.BlockSpec(memory_space=pltpu.VMEM)
+    parts = 8
+    grouped = (SEQS, 2, KVH, H // KVH * rows, HD)
+    return pl.pallas_call(
+        functools.partial(project_kernel, rows),
+        in_specs=[vmem, vmem, pl.BlockSpec(memory_space=pl.ANY), vmem, vmem, vmem],
+        out_specs=[vmem, vmem, vmem],
+        out_shape=[
+            jax.ShapeDtypeStruct(tokens.shape, jnp.bfloat16),
+            jax.ShapeDtypeStruct(grouped, jnp.bfloat16),
+            jax.ShapeDtypeStruct((rows, SEQS * KVH * 4 * HD), jnp.bfloat16),
+        ],
+        scratch_shapes=[
+            pltpu.VMEM((parts, D, QKV // parts), jnp.bfloat16),
+            pltpu.VMEM(grouped, jnp.float32),
+            pltpu.SemaphoreType.DMA((parts,)),
+        ],
+        compiler_params=pltpu.CompilerParams(vmem_limit_bytes=40 * 2**20),
+        cost_estimate=pl.CostEstimate(
+            flops=2 * tokens.shape[0] * D * QKV, bytes_accessed=2 * D * QKV, transcendentals=0
+        ),
+        name="project",
+    )(tokens, gain.reshape(1, -1), weight, bias.reshape(1, -1), cosine, signed_sine)
+
+
+def unproject_kernel(rows, gq_ref, gkv_ref, cos_ref, sin_ref, w_hbm, x_ref, gain_ref, past_ref, gp_ref, gi_ref, gg_ref, gb_ref, w_ref, gp_acc, sem):
+    copy = pltpu.make_async_copy(w_hbm, w_ref, sem)
+    copy.start()
+    cosine, sine = cos_ref[...], sin_ref[...]
+
+    def rounded(values):
+        return values.astype(jnp.bfloat16).astype(jnp.float32)
+
+    for head in range(H + 2 * KVH):
+        for slot in range(2 * SEQS):
+            seq, half = slot_of(slot)
+            at = slice(slot * rows, (slot + 1) * rows)
+            if head < H:
+                group, member = head // (H // KVH), head % (H // KVH)
+                grad = gq_ref[seq, half, group, member * rows : (member + 1) * rows]
+                grad = rounded(grad) * (HD**-0.5)
+            else:
+                group, kind = (head - H) % KVH, (head - H) // KVH
+                column = key_column(slot, group, kind)
+                grad = rounded(gkv_ref[:, column : column + HD])
+            if head < H + KVH:
+                grad = turned_back(grad, cosine[at], sine[at])
+            gp_acc[at, head * HD : (head + 1) * HD] = grad
+    low = gp_acc[...].astype(jnp.bfloat16)
+    gp_ref[...] = low
+    gb_ref[...] = jnp.sum(low.astype(jnp.float32), 0, keepdims=True)
+    values = x_ref[...].astype(jnp.float32)
+    scale = lax.rsqrt(jnp.mean(values * values, -1, keepdims=True) + EPS)
+    unit = values * scale
+    copy.wait()
+    grad_normed = lax.dot_general(low, w_ref[...], CONTRACT_LAST, preferred_element_type=jnp.float32)
+    gg_ref[...] = jnp.sum(grad_normed * unit, 0, keepdims=True)
+    grad_unit = grad_normed * gain_ref[...]
+    inner = jnp.mean(grad_unit * unit, -1, keepdims=True)
+    gi_ref[...] = past_ref[...] + scale * (grad_unit - unit * inner)
+
+
+def unproject(grad_queries, grad_kv, cosine, signed_sine, weight, tokens, gain, past, rows):
+    vmem = pl.BlockSpec(memory_space=pltpu.VMEM)
+    return pl.pallas_call(
+        functools.partial(unproject_kernel, rows),
+        in_specs=[vmem, vmem, vmem, vmem, pl.BlockSpec(memory_space=pl.ANY), vmem, vmem, vmem],
+        out_specs=[vmem] * 4,
+        out_shape=[
+            jax.ShapeDtypeStruct((tokens.shape[0], QKV), jnp.bfloat16),
+            jax.ShapeDtypeStruct(tokens.shape, jnp.float32),
+            jax.ShapeDtypeStruct((1, D), jnp.float32),
+            jax.ShapeDtypeStruct((1, QKV), jnp.float32),
+        ],
+        scratch_shapes=[
+            pltpu.VMEM((D, QKV), jnp.bfloat16),
+            pltpu.VMEM((tokens.shape[0], QKV), jnp.float32),
+            pltpu.SemaphoreType.DMA,
+        ],
+        compiler_params=pltpu.CompilerParams(vmem_limit_bytes=40 * 2**20),
+        cost_estimate=pl.CostEstimate(
+            flops=2 * tokens.shape[0] * D * QKV, bytes_accessed=2 * D * QKV, transcendentals=0
+        ),
+        name="unproject",
+    )(grad_queries, grad_kv, cosine, signed_sine, weight, tokens, gain.reshape(1, -1), past)
+
+
 def pack_kernel(columns, gate_ref, up_ref, out_ref):
     width = out_ref.shape[2] // 2
     cut = out_ref.shape[1]
@@ -968,15 +1116,14 @@
     own_ctx = lax.axis_index("ctx")
     own_shard = lax.axis_index("fsdp")
     rows_here = layer_input.shape[0]
-    slots = layer_input.shape[1]
     block_rows = rows_here * shard_count
-    kv_width = KVH * HD
     cut = D // (ctx_size * shard_count)
     columns = FF // shard_count
-    first_row = (own_ctx * shard_count + own_shard) * rows_here
-    own_pos = block_positions(block_order, first_row, rows_here, block_rows, ctx_size)
-    cosine_table, sine_table = rope_tables(own_pos.reshape(-1))
-    query_scale = HD ** (-0.5)
+    cosine, signed_sine = turn_tables(
+        block_order, own_ctx, ctx_size, block_rows, own_shard * rows_here, rows_here
+    )
+    tokens = by_slot(layer_input)
+    grad_out = by_slot(cotangent)
 
     def by_rows(ctx, shard):
         return shard * ctx_size + ctx
@@ -1001,7 +1148,7 @@
     small = jnp.pad(small, ((0, 0), (0, 16 * HD - small_width))).reshape(16, HD)
     width = -(-columns // HD) * HD
     w_qkv_all, w_o_all, small_all, cotangent_all = gather(
-        [own_cut(w_qkv), own_cut(w_o), small, cotangent.reshape(-1, D)],
+        [own_cut(w_qkv), own_cut(w_o), small, grad_out],
         [by_rows, by_rows, by_rows, lambda ctx, shard: shard],
         1,
         wide=(0, 1, 2),
@@ -1019,24 +1166,9 @@
 
     down_padded = jnp.pad(w_down, ((0, width - columns), (0, 0)))
 
-    inputs = layer_input.reshape(-1, D).astype(jnp.float32)
-    unit_one, scale_one, normed = normalize(inputs, gain_one)
-    normed_one = normed.astype(jnp.bfloat16)
-    projected = jnp.dot(normed_one, w_qkv_all, preferred_element_type=jnp.float32) + bias_all
-    query_raw = projected[:, : H * HD].reshape(-1, H, HD)
-    key_raw = projected[:, H * HD : H * HD + kv_width].reshape(-1, KVH, HD)
-    value_raw = projected[:, H * HD + kv_width :]
-    query_tokens = (
-        (rotate(query_raw, cosine_table, sine_table) * query_scale)
-        .astype(jnp.bfloat16)
-        .reshape(-1, H * HD)
-    )
-    key_tokens = (
-        rotate(key_raw, cosine_table, sine_table).astype(jnp.bfloat16).reshape(-1, kv_width)
-    )
-    own_kv = jnp.stack([key_tokens, value_raw.astype(jnp.bfloat16)], 1)
-    own_kv = own_kv.reshape(rows_here, 2, SEQS, 2, KVH, HD).transpose(0, 2, 4, 1, 3, 5)
-    own_kv = own_kv.reshape(rows_here, SEQS * KVH * 4 * HD)
+    normed_one, queries, own_kv = project(
+        tokens, gain_one, w_qkv_all, bias_all, cosine, signed_sine, rows_here
+    )
     all_kv, gate_up_cut = gather(
         [own_kv],
         [by_tokens],
@@ -1047,7 +1179,6 @@
         gate_up_cut.reshape(shard_count * cut, 2 * width), "ctx", axis=0, tiled=True
     )
     all_kv = all_kv.reshape(-1, SEQS * KVH * 4 * HD)
-    queries = to_groups(query_tokens, rows_here)
     scalars = jnp.concatenate(
         [block_order.reshape(-1), jnp.stack([own_ctx, own_shard]).astype(jnp.int32)]
     )
@@ -1055,7 +1186,7 @@
         scalars, queries, all_kv, ctx_size, block_rows, rows_here
     )
     attended_low = from_groups(attended_grouped, rows_here).astype(jnp.bfloat16)
-    middle = inputs + jnp.dot(attended_low, w_o_all, preferred_element_type=jnp.float32)
+    middle = tokens.astype(jnp.float32) + jnp.dot(attended_low, w_o_all, preferred_element_type=jnp.float32)
     unit_two, scale_two, normed = normalize(middle, gain_two)
     normed_two = mix_features(normed.astype(jnp.bfloat16))
 
@@ -1094,7 +1225,7 @@
     )
     grad_normed_two = unmix_features(grad_normed_two)
     grad_middle_norm, grad_gain_two = norm_back(grad_normed_two, unit_two, scale_two, gain_two)
-    grad_middle = cotangent.reshape(-1, D).astype(jnp.float32) + grad_middle_norm
+    grad_middle = grad_out.astype(jnp.float32) + grad_middle_norm
     grad_branch_one = grad_middle.astype(jnp.bfloat16)
     grad_attended = lax.dot_general(
         grad_branch_one, w_o_all, CONTRACT_LAST, preferred_element_type=jnp.float32
@@ -1113,33 +1244,29 @@
         block_rows,
         rows_here,
     )
-    (grad_kv,) = scatter(
+    grad_kv, mixed_rows = scatter(
         [grad_kv_full.reshape(-1, rows_here, SEQS * KVH * 4 * HD)],
         by_tokens,
         3,
         out_dtype=jnp.float32,
+        lines=[mixed_terms.reshape(shard_count, -1, D)],
     )
     gate_up_rows, grad_kv = lax.optimization_barrier((gate_up_rows, grad_kv))
     gate_up_rows = exchange(gate_up_rows.reshape(shard_count, cut, 2 * width), 5)
     gate_up_rows = lax.all_gather(gate_up_rows, "ctx", axis=0, tiled=False)
-    grad_kv_low = narrowed(grad_kv).reshape(rows_here, SEQS, KVH, 2, 2, HD)
-    grad_kv_low = grad_kv_low.transpose(0, 3, 1, 4, 2, 5).reshape(-1, 2 * kv_width)
-    grad_query_tokens = from_groups(narrowed(grad_queries), rows_here) * query_scale
-    grad_query_raw = rotate_back(
-        grad_query_tokens.reshape(-1, H, HD), cosine_table, sine_table
-    ).reshape(-1, H * HD)
-    grad_key_raw = rotate_back(
-        grad_kv_low[:, :kv_width].reshape(-1, KVH, HD), cosine_table, sine_table
-    ).reshape(-1, kv_width)
-    grad_projected = jnp.concatenate(
-        [grad_query_raw, grad_key_raw, grad_kv_low[:, kv_width:]], -1
-    ).astype(jnp.bfloat16)
-    grad_bias = jnp.sum(grad_projected, 0, dtype=jnp.float32)
-    grad_normed_one = lax.dot_general(
-        grad_projected, w_qkv_all, CONTRACT_LAST, preferred_element_type=jnp.float32
-    )
-    grad_input_norm, grad_gain_one = norm_back(grad_normed_one, unit_one, scale_one, gain_one)
-    grad_input = (grad_middle + grad_input_norm).reshape(rows_here, slots, D)
+    grad_projected, grad_input, grad_gain_one, grad_bias = unproject(
+        grad_queries,
+        grad_kv,
+        cosine,
+        signed_sine,
+        w_qkv_all,
+        tokens,
+        gain_one,
+        grad_middle,
+        rows_here,
+    )
+    grad_input = from_slot(grad_input, rows_here)
+    grad_bias = grad_bias.reshape(-1)
     qkv_terms = lax.dot_general(
         normed_one, grad_projected, CONTRACT_FIRST, preferred_element_type=jnp.float32
     ).astype(jnp.bfloat16)
@@ -1152,21 +1279,18 @@
     )
     small_terms = small_terms.reshape(ctx_size * shard_count, small_width)
     small_terms = jnp.pad(small_terms, ((0, 0), (0, 8 * HD - small_width)))
-    qkv_rows, small_rows, o_rows, mixed_rows = scatter(
+    qkv_rows, o_rows, small_rows = scatter(
         [
             qkv_terms.reshape(-1, cut, QKV),
+            o_terms.reshape(-1, cut, D),
             small_terms.reshape(-1, 8, HD),
         ],
         by_rows,
         4,
         spread_ctx=True,
-        lines=[
-            o_terms.reshape(shard_count, ctx_size, cut, D),
-            mixed_terms.reshape(shard_count, -1, D),
-        ],
     )
     mixed_out = middle + mixed_rows
-    output = mixed_out.astype(jnp.bfloat16).reshape(rows_here, slots, D)
+    output = from_slot(mixed_out.astype(jnp.bfloat16), rows_here)
     small_rows = small_rows.reshape(ctx_size, -1)[:, :small_width].reshape(-1)
     bias_start = 2 * gain_width
     value_start = bias_start + QK // shard_count
@@ -1179,7 +1303,7 @@
         qkv_rows.reshape(-1, QKV).astype(jnp.float32),
         small_rows[bias_start:value_start],
         small_rows[value_start:],
-        o_rows.reshape(-1, D),
+        o_rows.reshape(-1, D).astype(jnp.float32),
         small_rows[gain_width:bias_start],
         gate_rows.reshape(-1, FF),
         up_rows.reshape(-1, FF),

time: 773 us -> 722 us (0.934)
  waiting for transfers between devices: 70.3 us -> 51.4 us
  matrix products: 95.1 us -> 83.4 us
  other arithmetic: 33.4 us -> 22.4 us
    pallas_call x2, Pallas kernels: 201 us -> 182 us  [scatter(): pl.pallas_call(functools.partial(scatter_kernel, arity, ctx_size, pair_co...]
    psum x1, waiting for transfers between devices: 51.5 us -> 37.3 us  [shards(): down_rows = lax.psum(down_terms, 'ctx')]
    dot_general x2 -> x0, matrix products: 11.5 us -> none  [the longest x1 7.56 us: shards(): lax.dot_general(grad_projected, w_qkv_all, CONTRACT_LAST, preferred_eleme...]
    pallas_call x0 -> x2, Pallas kernels: none -> 8.65 us  [the longest x1 5.01 us: project(): pl.pallas_call(functools.partial(project_kernel, rows), in_specs=[vmem, v...]
    pallas_call x3, Pallas kernels: 200 us -> 208 us  [gather(): pl.pallas_call(functools.partial(gather_kernel, arity, ctx_size, pair_cou...]
  transfers between devices with their start and end apart: 5 -> 5, of which waited for: 3 -> 2; matrix products, arithmetic and copies ran while one was open for 14% -> 11% of each run, Pallas kernels for 46% -> 47%
where the time goes in v9:
time: 722 us; the launch traced here: 714 us
  Pallas kernels  503 us (70%)
  matrix products  83.4 us (12%)
  waiting for transfers between devices  51.4 us (7%)
  local copies, waits for them, and re-layouts  39 us (5%)
  other arithmetic  22.4 us (3%)
  between operations  14.5 us (2%)
    pallas_call x3, Pallas kernels, gather(): pl.pallas_call(functools.partial(gather_kernel, arity, ctx_size, pair_cou...  208 us
    pallas_call x2, Pallas kernels, scatter(): pl.pallas_call(functools.partial(scatter_kernel, arity, ctx_size, pair_co...  182 us
    psum x1, waiting for transfers between devices, shards(): down_rows = lax.psum(down_terms, 'ctx')  37.3 us
    pallas_call x1, Pallas kernels, exchange(): pl.pallas_call(functools.partial(exchange_kernel, shard_count // 2), in_s...  35 us
    pallas_call x1, Pallas kernels, attend_backward(): pl.pallas_call(kernel, grid_spec=pltpu.PrefetchScalarGridSpec(num_scalar_...  29.3 us
    pallas_call x1, Pallas kernels, attend_forward(): pl.pallas_call(kernel, grid_spec=pltpu.PrefetchScalarGridSpec(num_scalar_...  27.9 us
    dot_general x1, matrix products, shards(): jnp.dot(tokens_all, gate_up_cols, preferred_element_type=jnp.float32)  15.5 us
    unnamed x79, local copies, waits for them, and re-layouts  14.6 us
  transfers between devices with their start and end apart: 5, of which 2 were waited for; matrix products, arithmetic and copies ran while one was open for 11% of the time, Pallas kernels for 47%

profile of v9, /device:TPU:0, one launch (start us, length us, event | category | flops | bytes accessed | tf_op | source)
XLA Modules:
  0.0 714.4 jit_solution(28466794807467128)
XLA Ops:
  13.0 80.3 %shard_map.194 = (bf16[32,48,2048]{2,1,0:T(8,128)(2,1)}, bf16[32,48,1536]{2,1,0:T(8,128)(2,1)}, bf16[32,16,128]{2,1,0:T(8,128)(2,1)}, bf16[8,160,1536]{2,1,0:T(8,128)(2,1)}) custom-call(bf16[48,2048]{1,0:T(8,128)(2,1)} %constant_dynamic-slice_fusion.4.refs_0_, bf16[48,1536]{1,0:T(8,128)(2,1)} %constant_dynamic-slice_fusion.3.refs_1_, ...), custom_call_target="tpu_custom_call" | custom-call | bytes 107479040 | tf_op jit(solution)/shard_map/pallas_call | solution.py:575
  105.8 5.0 project.1
  113.1 70.2 %shard_map.195 = (bf16[32,40,2048]{2,1,0:T(8,128)(2,1)}, bf16[8,48,2304]{2,1,0:T(8,128)(2,1)}) custom-call(bf16[40,2048]{1,0:T(8,128)(2,1)} %copy-done.18, bf16[8,48,2304]{2,1,0:T(8,128)(2,1)} %pack.1.refs_1_), custom_call_target="tpu_custom_call" | custom-call | bytes 20971520 | tf_op jit(solution)/shard_map/pallas_call | solution.py:575
  184.3 27.9 %attend_forward.1 = (f32[2,2,2,240,128]{4,3,2,1,0:T(8,128)}, f32[2,2,2,1,240]{4,3,2,1,0:T(1,128)}) custom-call(s32[18]{0:T(128)} %pad_add_fusion.scalars, bf16[2,2,2,240,128]{4,3,2,1,0:T(8,128)(2,1)} %copy-done.6, bf16[1280,2048]{1,0:T(8,128)(2,1)} %bitcast.91), custom_call_target="tpu_custom_call" | custom-call | tf_op jit(solution)/shard_map/attend_forward/pallas_call | solution.py:139
  214.1 3.6 multiply_reduce_fusion.2
  219.2 57.7 %shard_map.196 = bf16[8,160,1536]{2,1,0:T(8,128)(2,1)} custom-call(bf16[160,1536]{1,0:T(8,128)(2,1)} %copy.54.refs_0_), custom_call_target="tpu_custom_call" | custom-call | bytes 62914560 | tf_op jit(solution)/shard_map/pallas_call | solution.py:575
  277.0 15.5 %fusion.12 = f32[1280,2304]{0,1:T(8,128)} fusion(bf16[1280,1536]{1,0:T(8,128)(2,1)} %bitcast.101, bf16[1536,2304]{1,0:T(8,128)(2,1)} %all-gather.4.cloned.1.call-done), kind=kOutput, calls=%fused_computation.63 | convolution fusion | flops 9059696640 | bytes 22806528 | tf_op jit(solution)/shard_map/dot_general | solution.py:1195
  292.4 12.5 %multiply_convert_fusion.2 = (bf16[1280,1152]{0,1:T(8,128)(2,1)S(1)}, bf16[1280,1152]{0,1:T(8,128)(2,1)S(1)}, bf16[1280,1152]{0,1:T(8,128)(2,1)}) fusion(f32[1280,2304]{0,1:T(8,128)} %fusion.12, bf16[1280,1536]{1,0:T(8,128)(2,1)} %bitcast.125, bf16[1120,1536]{1,0:T(8,128)(2,1)} %param.20), kind=kOutput, calls=%fused_computation.9 | convolution fusion | flops 4551966720 | bytes 28016640 | tf_op jit(solution)/shard_map/dot_general | solution.py:1200
  307.5 11.0 %convolution_convert_fusion.5 = bf16[1280,1536]{1,0:T(8,128)(2,1)} fusion(bf16[1536,2304]{1,0:T(8,128)(2,1)S(1)} %bitcast.122, bf16[1280,1152]{0,1:T(8,128)(2,1)S(1)} %get-tuple-element.74, bf16[1280,1152]{0,1:T(8,128)(2,1)S(1)} %get-tuple-element.73), kind=kOutput, calls=%fused_computation.5 | convolution fusion | flops 9073459200 | bytes 16908288 | tf_op jit(solution)/shard_map/dot_general | solution.py:1205
  322.5 11.4 %convolution_convert_fusion = bf16[1536,2304]{1,0:T(8,128)(2,1)} fusion(bf16[1280,1536]{1,0:T(8,128)(2,1)S(1)} %bitcast.102, bf16[1280,2304]{0,1:T(8,128)(2,1)S(1)} %pad_maximum_fusion), kind=kOutput, calls=%fused_computation | convolution fusion | flops 9063235584 | bytes 16908288 | tf_op jit(solution)/shard_map/dot_general | solution.py:1214
  334.0 9.9 %convolution_convert_fusion.1 = bf16[1280,1536]{1,0:T(8,128)(2,1)} fusion(bf16[1280,1152]{0,1:T(8,128)(2,1)} %get-tuple-element.50, bf16[1120,1536]{1,0:T(8,128)(2,1)} %param.20), kind=kOutput, calls=%fused_computation.1 | convolution fusion | flops 4531814400 | bytes 10321920 | tf_op jit(solution)/shard_map/dot_general | solution.py:1222
  343.9 6.2 convolution_convert_fusion.3
  350.1 13.9 %reduce-scatter.3.cloned.1.call-done = bf16[160,1536]{1,0:T(8,128)(2,1)} async-done(((bf16[1280,1536]{1,0:T(8,128)(2,1)}), bf16[160,1536]{1,0:T(8,128)(2,1)}) %reduce-scatter.3.cloned.1.call-update) | async-done | bytes 491536 | tf_op jit(solution)/shard_map/reduce_scatter | solution.py:1208
  373.0 4.0 convolution_convert_fusion.6
  378.5 29.3 %attend_backward.1 = (f32[2,2,2,240,128]{4,3,2,1,0:T(8,128)}, bf16[1280,2048]{1,0:T(8,128)(2,1)}) custom-call(s32[18]{0:T(128)} %pad_add_fusion.scalars, bf16[2,2,2,240,128]{4,3,2,1,0:T(8,128)(2,1)} %copy-done.6, bf16[2,2,2,240,128]{4,3,2,1,0:T(8,128)(2,1)} %bitcast.108, f32[2,2,2,240,128]{4,3,2,1,0:T(8,128)} %get-tuple-element.46.att_ref, ...), custom_call_target="tpu_custom_call" | custom-call | tf_op jit(solution)/shard_map/attend_backward/pallas_call | solution.py:237
  407.8 69.0 %shard_map.197 = (f32[40,2048]{1,0:T(8,128)}, f32[160,1536]{1,0:T(8,128)}) custom-call(bf16[32,40,2048]{2,1,0:T(8,128)(2,1)} %bitcast.98, bf16[8,160,1536]{2,1,0:T(8,128)(2,1)} %bitcast.100), custom_call_target="tpu_custom_call" | custom-call | bytes 83886080 | tf_op jit(solution)/shard_map/pallas_call | solution.py:882
  476.9 35.0 %shard_map.199 = bf16[8,48,2304]{2,1,0:T(8,128)(2,1)} custom-call(bf16[8,48,2304]{2,1,0:T(8,128)(2,1)} %bitcast.110), custom_call_target="tpu_custom_call" | custom-call | bytes 56623104 | tf_op jit(solution)/shard_map/pallas_call | solution.py:342
  514.4 3.6 convolution_convert_fusion.4
  518.0 37.3 %all-reduce.5.cloned.1.call-done = bf16[1152,1536]{1,0:T(8,128)(2,1)} async-done(((bf16[1152,1536]{1,0:T(8,128)(2,1)}), bf16[1152,1536]{1,0:T(8,128)(2,1)}) %all-reduce.5.cloned.1.call-update) | async-done | bytes 3538960 | tf_op jit(solution)/shard_map/psum | solution.py:1221
  555.3 5.8 slice_convert_fusion
  564.3 3.6 unproject.1
  570.8 5.6 convolution_convert_fusion.2
  576.5 113.5 %shard_map.198 = (bf16[4,48,2048]{2,1,0:T(8,128)(2,1)}, bf16[4,48,1536]{2,1,0:T(8,128)(2,1)}, f32[4,8,128]{2,1,0:T(8,128)}) custom-call(bf16[32,48,2048]{2,1,0:T(8,128)(2,1)} %bitcast.89, bf16[32,48,1536]{2,1,0:T(8,128)(2,1)} %bitcast.90, f32[32,8,128]{2,1,0:T(8,128)} %bitcast.113), custom_call_target="tpu_custom_call" | custom-call | bytes 178257920 | tf_op jit(solution)/shard_map/pallas_call | solution.py:882
  698.9 8.8 %unpack.1 = (f32[4,48,8960]{2,1,0:T(8,128)}, f32[4,48,8960]{2,1,0:T(8,128)}) custom-call(bf16[4,8,48,2304]{3,2,1,0:T(8,128)(2,1)} %bitcast.95), custom_call_target="tpu_custom_call" | custom-call | tf_op jit(solution)/shard_map/unpack/pallas_call | solution.py:1091
  (160 shorter events, 59.2 us)
Async XLA Ops:
  7.2 269.8 %all-gather.4.cloned.1.call-start = ((), (), s32[]{:S(2)}) async-start(), calls=%async_computation.2 | async-start | bytes 8847360 | tf_op jit(solution)/shard_map/all_gather | solution.py:1178
  97.0 117.1 %copy-start.4 = (bf16[4,40,1536]{2,1,0:T(8,128)(2,1)}, bf16[4,40,1536]{2,1,0:T(8,128)(2,1)S(1)}, u32[]{:S(2)}) copy-start(bf16[4,40,1536]{2,1,0:T(8,128)(2,1)S(1)} %copy.48) | copy-start | bytes 1474564
  97.1 13.7 %copy-start.19 = (f32[1,1536]{1,0:T(1,128)}, f32[1,1536]{1,0:T(1,128)S(1)}, u32[]{:S(2)}) copy-start(f32[1,1536]{1,0:T(1,128)S(1)} %reshape_reshape.7.gain_ref) | copy-start | bytes 18436
  97.1 13.7 %copy-start.12 = (f32[4,40,128]{2,1,0:T(8,128)}, f32[4,40,128]{2,1,0:T(8,128)S(1)}, u32[]{:S(2)}) copy-start(f32[4,40,128]{2,1,0:T(8,128)S(1)} %get-tuple-element.77) | copy-start | bytes 245764
  105.8 77.7 %copy-start.32 = (s32[2,8]{1,0:T(2,128)S(1)}, s32[2,8]{1,0:T(2,128)}, u32[]{:S(2)}) copy-start(s32[2,8]{1,0:T(2,128)} %param.12) | copy-start | bytes 196
  183.3 180.8 %reduce-scatter.3.cloned.1.call-start = ((), (), s32[]{:S(2)}) async-start(), calls=%async_computation.3 | async-start | bytes 4423680 | tf_op jit(solution)/shard_map/reduce_scatter | solution.py:1208
  183.7 187.4 %copy-start.29 = (f32[1536]{0:T(1024)}, f32[1536]{0:T(1024)S(1)}, u32[]{:S(2)}) copy-start(f32[1536]{0:T(1024)S(1)} %mul.246) | copy-start | bytes 18436
  217.6 154.3 %copy-start.21 = (f32[160,1536]{1,0:T(8,128)}, f32[160,1536]{1,0:T(8,128)S(1)}, u32[]{:S(2)}) copy-start(f32[160,1536]{1,0:T(8,128)S(1)} %get-tuple-element.87) | copy-start | bytes 2949124
  217.7 153.4 %copy-start.31 = (f32[160]{0:T(256)}, f32[160]{0:T(256)S(1)}, u32[]{:S(2)}) copy-start(f32[160]{0:T(256)S(1)} %add_rsqrt_fusion) | copy-start | bytes 1924
  277.0 30.6 %slice-start = ((s8[7077888]{0:T(1024)(128)(4,1)}), s8[4194304]{0:T(1024)(128)(4,1)S(1)}, s32[]{:S(2)}) async-start(s8[7077888]{0:T(1024)(128)(4,1)} %bitcast.121), calls=%async_computation.7 | async-start | bytes 8388608
  292.4 15.1 %slice-start.1 = ((s8[7077888]{0:T(1024)(128)(4,1)}), s8[2883584]{0:T(1024)(128)(4,1)S(1)}, s32[]{:S(2)}) async-start(s8[7077888]{0:T(1024)(128)(4,1)} %bitcast.121), calls=%async_computation.8 | async-start | bytes 5767168
  318.6 158.3 %reduce-scatter.5.cloned.1.call-start = ((), (), s32[]{:S(2)}) async-start(), calls=%async_computation.4 | async-start | bytes 8847360 | tf_op jit(solution)/shard_map/reduce_scatter | solution.py:1217
  334.0 221.4 %all-reduce.5.cloned.1.call-start = ((), (), s32[]{:S(2)}) async-start(), calls=%async_computation.5 | async-start | bytes 7077888 | tf_op jit(solution)/shard_map/psum | solution.py:1221
  366.2 332.7 %all-gather.6.cloned.1.call-start = ((), (), s32[]{:S(2)}) async-start(), calls=%async_computation.6 | async-start | bytes 8847360 | tf_op jit(solution)/shard_map/all_gather | solution.py:1256
  476.8 35.1 %copy-start.30 = (f32[1536]{0:T(1024)S(1)}, f32[1536]{0:T(1024)}, u32[]{:S(2)}) copy-start(f32[1536]{0:T(1024)} %get-tuple-element.71) | copy-start | bytes 18436
  476.8 35.2 %copy-start.22 = (f32[160,1536]{1,0:T(8,128)S(1)}, f32[160,1536]{1,0:T(8,128)}, u32[]{:S(2)}) copy-start(f32[160,1536]{1,0:T(8,128)} %copy-done.21) | copy-start | bytes 2949124
  476.9 37.5 %copy-start.24 = (bf16[160,1536]{1,0:T(8,128)(2,1)S(1)}, bf16[160,1536]{1,0:T(8,128)(2,1)}, u32[]{:S(2)}) copy-start(bf16[160,1536]{1,0:T(8,128)(2,1)} %copy-done.23) | copy-start | bytes 1474564
  518.0 43.2 %copy-start.5 = (bf16[4,40,1536]{2,1,0:T(8,128)(2,1)S(1)}, bf16[4,40,1536]{2,1,0:T(8,128)(2,1)}, u32[]{:S(2)}) copy-start(bf16[4,40,1536]{2,1,0:T(8,128)(2,1)} %copy-done.4) | copy-start | bytes 1474564
  518.0 43.2 %copy-start.9 = (f32[2,2,2,240,128]{4,3,2,1,0:T(8,128)S(1)}, f32[2,2,2,240,128]{4,3,2,1,0:T(8,128)}, u32[]{:S(2)}) copy-start(f32[2,2,2,240,128]{4,3,2,1,0:T(8,128)} %get-tuple-element.57.gq_ref) | copy-start | bytes 2949124
  518.0 43.2 %copy-start.13 = (f32[4,40,128]{2,1,0:T(8,128)S(1)}, f32[4,40,128]{2,1,0:T(8,128)}, u32[]{:S(2)}) copy-start(f32[4,40,128]{2,1,0:T(8,128)} %copy-done.12) | copy-start | bytes 245764
  518.0 43.2 %copy-start.15 = (f32[160,128]{1,0:T(8,128)S(1)}, f32[160,128]{1,0:T(8,128)}, u32[]{:S(2)}) copy-start(f32[160,128]{1,0:T(8,128)} %copy-done.14) | copy-start | bytes 245764
  518.0 43.2 %copy-start.17 = (f32[40,2048]{1,0:T(8,128)S(1)}, f32[40,2048]{1,0:T(8,128)}, u32[]{:S(2)}) copy-start(f32[40,2048]{1,0:T(8,128)} %get-tuple-element.59.gkv_ref) | copy-start | bytes 983044
  518.0 43.2 %copy-start.20 = (f32[1,1536]{1,0:T(1,128)S(1)}, f32[1,1536]{1,0:T(1,128)}, u32[]{:S(2)}) copy-start(f32[1,1536]{1,0:T(1,128)} %copy-done.19) | copy-start | bytes 18436
  576.5 115.5 %copy-start.11 = (f32[160,1536]{1,0:T(8,128)S(1)}, f32[160,1536]{1,0:T(8,128)}, u32[]{:S(2)}) copy-start(f32[160,1536]{1,0:T(8,128)} %copy-done.10) | copy-start | bytes 2949124
  (18 other events, 82.4 us)
Sparse Core Ops, SparseCore 0:
  183.4 91.3 all-gather.3
  318.7 45.3 reduce-scatter.2
  367.1 92.2 reduce-scatter.4
  462.4 92.8 all-reduce.4
  557.0 116.2 all-gather.5

commit v10 on v9

--- a/solution.py
+++ b/solution.py
@@ -912,6 +912,36 @@
         ),
         cost_estimate=pl.CostEstimate(flops=0, bytes_accessed=moved * 16, transcendentals=0),
     )(*terms, *lines)
+
+
+def line_sum_kernel(pair_count, source, out, half, room, *sems):
+    where = greet(1, pair_count, False, False)
+    flow = LineScatter(source, out, half, room, sems, where, (pair_count, 1), ())
+    flow.start()
+    for step in flow.order:
+        flow.fold(step)
+    flow.finish()
+
+
+def line_sum(terms, collective_id):
+    pair_count = lax.axis_size("fsdp") // 2
+    extent = terms.shape[1:]
+    dma = pltpu.SemaphoreType.DMA((pair_count,))
+    return pl.pallas_call(
+        functools.partial(line_sum_kernel, pair_count),
+        in_specs=[pl.BlockSpec(memory_space=pltpu.VMEM)],
+        out_specs=pl.BlockSpec(memory_space=pltpu.VMEM),
+        out_shape=jax.ShapeDtypeStruct(extent, jnp.float32),
+        scratch_shapes=[
+            pltpu.VMEM((pair_count,) + extent, terms.dtype),
+            pltpu.VMEM((pair_count - 1,) + extent, terms.dtype),
+        ]
+        + [dma] * 4,
+        compiler_params=pltpu.CompilerParams(
+            collective_id=collective_id, has_side_effects=True, vmem_limit_bytes=63 * 2**20
+        ),
+        cost_estimate=pl.CostEstimate(flops=0, bytes_accessed=terms.size * 16, transcendentals=0),
+    )(terms)
 
 
 def turned(values, cosine, signed_sine):
@@ -1147,15 +1177,13 @@
     small = lax.dynamic_slice_in_dim(small, own_ctx, 1, 0)
     small = jnp.pad(small, ((0, 0), (0, 16 * HD - small_width))).reshape(16, HD)
     width = -(-columns // HD) * HD
-    w_qkv_all, w_o_all, small_all, cotangent_all = gather(
-        [own_cut(w_qkv), own_cut(w_o), small, grad_out],
-        [by_rows, by_rows, by_rows, lambda ctx, shard: shard],
+    w_qkv_all, small_all, gate_up_cut = gather(
+        [own_cut(w_qkv), small],
+        [by_rows, by_rows],
         1,
-        wide=(0, 1, 2),
-    )
-    cotangent_all = cotangent_all.reshape(-1, D)
+        swaps=[pack(own_cut(w_gate), own_cut(w_up), shard_count, columns, width)],
+    )
     w_qkv_all = w_qkv_all.reshape(D, QKV)
-    w_o_all = w_o_all.reshape(D, D)
     small_all = small_all.reshape(shard_count, ctx_size, -1)[:, :, :small_width]
     small_all = small_all.reshape(shard_count, -1).astype(jnp.float32)
     bias_width = QKV // shard_count
@@ -1169,12 +1197,15 @@
     normed_one, queries, own_kv = project(
         tokens, gain_one, w_qkv_all, bias_all, cosine, signed_sine, rows_here
     )
-    all_kv, gate_up_cut = gather(
-        [own_kv],
-        [by_tokens],
+    all_kv, w_o_all, cotangent_all = gather(
+        [own_kv, own_cut(w_o), grad_out],
+        [by_tokens, by_rows, lambda ctx, shard: shard],
         2,
-        swaps=[pack(own_cut(w_gate), own_cut(w_up), shard_count, columns, width)],
-    )
+        wide=(0, 1),
+    )
+    w_o_all = w_o_all.reshape(D, D)
+    cotangent_all = cotangent_all.reshape(-1, D)
+    gate_up_cut, all_kv = lax.optimization_barrier((gate_up_cut, all_kv))
     gate_up_cols = lax.all_gather(
         gate_up_cut.reshape(shard_count * cut, 2 * width), "ctx", axis=0, tiled=True
     )
@@ -1202,26 +1233,25 @@
     )
     grad_gate = grad_hidden * up_part * sigmoid_gate * (1.0 + gate_part * (1.0 - sigmoid_gate))
     grad_gate_up = jnp.concatenate([grad_gate, grad_hidden * activated], -1).astype(jnp.bfloat16)
-    grad_tokens = lax.dot_general(
-        grad_gate_up, gate_up_cols, CONTRACT_LAST, preferred_element_type=jnp.float32
-    ).astype(jnp.bfloat16)
-    grad_normed_two = lax.psum_scatter(
-        grad_tokens, "fsdp", scatter_dimension=0, tiled=True
-    ).astype(jnp.float32)
-    grad_gate_up, hidden, grad_tokens = lax.optimization_barrier(
-        (grad_gate_up, hidden, grad_tokens)
-    )
     gate_up_terms = lax.dot_general(
         tokens_all, grad_gate_up, CONTRACT_FIRST, preferred_element_type=jnp.float32
     ).astype(jnp.bfloat16)
     gate_up_rows = lax.psum_scatter(gate_up_terms, "ctx", scatter_dimension=0, tiled=True)
+    grad_gate_up, hidden, gate_up_terms = lax.optimization_barrier(
+        (grad_gate_up, hidden, gate_up_terms)
+    )
+    grad_tokens = lax.dot_general(
+        grad_gate_up, gate_up_cols, CONTRACT_LAST, preferred_element_type=jnp.float32
+    ).astype(jnp.bfloat16)
+    grad_normed_two = line_sum(grad_tokens.reshape(shard_count, -1, D), 7)
+    grad_normed_two, hidden = lax.optimization_barrier((grad_normed_two, hidden))
     down_terms = lax.dot_general(
         hidden, cotangent_all, CONTRACT_FIRST, preferred_element_type=jnp.float32
     ).astype(jnp.bfloat16)
     down_rows = lax.psum(down_terms, "ctx")
     mixed_terms = jnp.dot(hidden, down_padded, preferred_element_type=jnp.float32).astype(jnp.bfloat16)
-    grad_normed_two, down_terms, gate_up_terms, mixed_terms = lax.optimization_barrier(
-        (grad_normed_two, down_terms, gate_up_terms, mixed_terms)
+    grad_normed_two, down_terms, mixed_terms = lax.optimization_barrier(
+        (grad_normed_two, down_terms, mixed_terms)
     )
     grad_normed_two = unmix_features(grad_normed_two)
     grad_middle_norm, grad_gain_two = norm_back(grad_normed_two, unit_two, scale_two, gain_two)
@@ -1230,6 +1260,10 @@
     grad_attended = lax.dot_general(
         grad_branch_one, w_o_all, CONTRACT_LAST, preferred_element_type=jnp.float32
     ).astype(jnp.bfloat16)
+    gate_up_rows, grad_attended = lax.optimization_barrier((gate_up_rows, grad_attended))
+    gate_up_rows = exchange(gate_up_rows.reshape(shard_count, cut, 2 * width), 5)
+    gate_up_rows, grad_attended = lax.optimization_barrier((gate_up_rows, grad_attended))
+    gate_up_rows = lax.all_gather(gate_up_rows, "ctx", axis=0, tiled=False)
     o_terms = lax.dot_general(
         attended_low, grad_branch_one, CONTRACT_FIRST, preferred_element_type=jnp.float32
     ).astype(jnp.bfloat16)
@@ -1251,9 +1285,6 @@
         out_dtype=jnp.float32,
         lines=[mixed_terms.reshape(shard_count, -1, D)],
     )
-    gate_up_rows, grad_kv = lax.optimization_barrier((gate_up_rows, grad_kv))
-    gate_up_rows = exchange(gate_up_rows.reshape(shard_count, cut, 2 * width), 5)
-    gate_up_rows = lax.all_gather(gate_up_rows, "ctx", axis=0, tiled=False)
     grad_projected, grad_input, grad_gain_one, grad_bias = unproject(
         grad_queries,
         grad_kv,

time: 722 us -> 743 us (1.029)
  Pallas kernels: 503 us -> 531 us
  waiting for transfers between devices: 51.4 us -> 43.2 us
    pallas_call x0 -> x1, Pallas kernels: none -> 41.9 us  [line_sum(): pl.pallas_call(functools.partial(line_sum_kernel, pair_count), in_specs=[...]
    pallas_call x2, Pallas kernels: 182 us -> 160 us  [scatter(): pl.pallas_call(functools.partial(scatter_kernel, arity, ctx_size, pair_co...]
    reduce_scatter x1 -> x0, waiting for transfers between devices: 13.9 us -> none  [shards(): lax.psum_scatter(grad_tokens, 'fsdp', scatter_dimension=0, tiled=True)]
    unnamed x79 -> x85, local copies, waits for them, and re-layouts: 14.6 us -> 19.3 us
  transfers between devices with their start and end apart: 5 -> 4, of which waited for: 2 -> 1; matrix products, arithmetic and copies ran while one was open for 11% -> 11% of each run, Pallas kernels for 47% -> 50%
where the time goes in v10:
time: 743 us; the launch traced here: 736 us
  Pallas kernels  531 us (71%)
  matrix products  86.7 us (12%)
  waiting for transfers between devices  43.2 us (6%)
  local copies, waits for them, and re-layouts  41.5 us (6%)
  other arithmetic  18.5 us (2%)
  between operations  14.5 us (2%)
    pallas_call x3, Pallas kernels, gather(): pl.pallas_call(functools.partial(gather_kernel, arity, ctx_size, pair_cou...  210 us
    pallas_call x2, Pallas kernels, scatter(): pl.pallas_call(functools.partial(scatter_kernel, arity, ctx_size, pair_co...  160 us
    psum x1, waiting for transfers between devices, shards(): down_rows = lax.psum(down_terms, 'ctx')  43.1 us
    pallas_call x1, Pallas kernels, exchange(): pl.pallas_call(functools.partial(exchange_kernel, shard_count // 2), in_s...  42.1 us
    pallas_call x1, Pallas kernels, line_sum(): pl.pallas_call(functools.partial(line_sum_kernel, pair_count), in_specs=[...  41.9 us
    pallas_call x1, Pallas kernels, attend_backward(): pl.pallas_call(kernel, grid_spec=pltpu.PrefetchScalarGridSpec(num_scalar_...  29.3 us
    pallas_call x1, Pallas kernels, attend_forward(): pl.pallas_call(kernel, grid_spec=pltpu.PrefetchScalarGridSpec(num_scalar_...  27.9 us
    unnamed x85, local copies, waits for them, and re-layouts  19.3 us
  transfers between devices with their start and end apart: 4, of which 1 were waited for; matrix products, arithmetic and copies ran while one was open for 11% of the time, Pallas kernels for 50%

profile of v10, /device:TPU:0, one launch (start us, length us, event | category | flops | bytes accessed | tf_op | source)
XLA Modules:
  0.0 736.1 jit_solution(6810263707689239162)
XLA Ops:
  15.4 58.7 %shard_map.194 = (bf16[32,48,2048]{2,1,0:T(8,128)(2,1)}, bf16[32,16,128]{2,1,0:T(8,128)(2,1)}, bf16[8,48,2304]{2,1,0:T(8,128)(2,1)}) custom-call(bf16[48,2048]{1,0:T(8,128)(2,1)} %constant_dynamic-slice_fusion.4.refs_0_, bf16[16,128]{1,0:T(8,128)(2,1)} %bitcast.120, bf16[8,48,2304]{2,1,0:T(8,128)(2,1)} %pack.1.refs_2_), custom_call_target="tpu_custom_call" | custom-call | bytes 25690112 | tf_op jit(solution)/shard_map/pallas_call | solution.py:575
  81.5 5.0 project.1
  88.8 89.9 %shard_map.195 = (bf16[32,40,2048]{2,1,0:T(8,128)(2,1)}, bf16[32,48,1536]{2,1,0:T(8,128)(2,1)}, bf16[8,160,1536]{2,1,0:T(8,128)(2,1)}) custom-call(bf16[40,2048]{1,0:T(8,128)(2,1)} %copy-done.17, bf16[48,1536]{1,0:T(8,128)(2,1)} %constant_dynamic-slice_fusion.refs_1_, bf16[160,1536]{1,0:T(8,128)(2,1)} %bitcast.100), custom_call_target="tpu_custom_call" | custom-call | bytes 102760448 | tf_op jit(solution)/shard_map/pallas_call | solution.py:575
  179.7 27.9 %attend_forward.1 = (f32[2,2,2,240,128]{4,3,2,1,0:T(8,128)}, f32[2,2,2,1,240]{4,3,2,1,0:T(1,128)}) custom-call(s32[18]{0:T(128)} %pad_add_fusion.scalars, bf16[2,2,2,240,128]{4,3,2,1,0:T(8,128)(2,1)} %copy-done.6, bf16[1280,2048]{1,0:T(8,128)(2,1)} %bitcast.92), custom_call_target="tpu_custom_call" | custom-call | tf_op jit(solution)/shard_map/attend_forward/pallas_call | solution.py:139
  209.8 3.6 multiply_reduce_fusion.2
  215.5 60.9 %shard_map.196 = bf16[8,160,1536]{2,1,0:T(8,128)(2,1)} custom-call(bf16[160,1536]{1,0:T(8,128)(2,1)} %copy.54.refs_0_), custom_call_target="tpu_custom_call" | custom-call | bytes 62914560 | tf_op jit(solution)/shard_map/pallas_call | solution.py:575
  276.5 15.5 %fusion.12 = f32[1280,2304]{0,1:T(8,128)} fusion(bf16[1280,1536]{1,0:T(8,128)(2,1)} %bitcast.103, bf16[1536,2304]{1,0:T(8,128)(2,1)} %all-gather.4.cloned.1.call-done), kind=kOutput, calls=%fused_computation.63 | convolution fusion | flops 9059696640 | bytes 22806528 | tf_op jit(solution)/shard_map/dot_general | solution.py:1226
  291.9 12.7 %multiply_convert_fusion.2 = (bf16[1280,1152]{0,1:T(8,128)(2,1)S(1)}, bf16[1280,1152]{0,1:T(8,128)(2,1)S(1)}, bf16[1280,1152]{0,1:T(8,128)(2,1)}) fusion(f32[1280,2304]{0,1:T(8,128)} %fusion.12, bf16[1280,1536]{1,0:T(8,128)(2,1)S(1)} %bitcast.125, bf16[1120,1536]{1,0:T(8,128)(2,1)} %param.20), kind=kOutput, calls=%fused_computation.9 | convolution fusion | flops 4551966720 | bytes 28016640 | tf_op jit(solution)/shard_map/dot_general | solution.py:1231
  307.2 12.7 %convolution_convert_fusion = bf16[1536,2304]{1,0:T(8,128)(2,1)} fusion(bf16[1280,1536]{1,0:T(8,128)(2,1)S(1)} %bitcast.104, bf16[1280,1152]{0,1:T(8,128)(2,1)S(1)} %get-tuple-element.86, bf16[1280,1152]{0,1:T(8,128)(2,1)S(1)} %get-tuple-element.85), kind=kOutput, calls=%fused_computation | convolution fusion | flops 9075032064 | bytes 16908288 | tf_op jit(solution)/shard_map/dot_general | solution.py:1236
  323.1 14.1 %convolution_convert_fusion.5 = bf16[1280,1536]{1,0:T(8,128)(2,1)} fusion(bf16[1280,2304]{0,1:T(8,128)(2,1)S(1)} %pad_maximum_fusion, bf16[1536,2304]{1,0:T(8,128)(2,1)} %all-gather.4.cloned.1.call-done), kind=kOutput, calls=%fused_computation.5 | convolution fusion | flops 9061662720 | bytes 16908288 | tf_op jit(solution)/shard_map/dot_general | solution.py:1243
  337.3 41.9 %shard_map.197 = f32[160,1536]{1,0:T(8,128)} custom-call(bf16[8,160,1536]{2,1,0:T(8,128)(2,1)} %bitcast.101), custom_call_target="tpu_custom_call" | custom-call | bytes 31457280 | tf_op jit(solution)/shard_map/pallas_call | solution.py:930
  379.2 9.7 %convolution_convert_fusion.1 = bf16[1280,1536]{1,0:T(8,128)(2,1)} fusion(bf16[1280,1152]{0,1:T(8,128)(2,1)} %get-tuple-element.61, bf16[1120,1536]{1,0:T(8,128)(2,1)} %param.20), kind=kOutput, calls=%fused_computation.1 | convolution fusion | flops 4531814400 | bytes 10321920 | tf_op jit(solution)/shard_map/dot_general | solution.py:1252
  388.9 6.2 convolution_convert_fusion.3
  402.1 4.1 convolution_convert_fusion.6
  406.2 42.1 %shard_map.198 = bf16[8,48,2304]{2,1,0:T(8,128)(2,1)} custom-call(bf16[8,48,2304]{2,1,0:T(8,128)(2,1)} %bitcast.113), custom_call_target="tpu_custom_call" | custom-call | bytes 56623104 | tf_op jit(solution)/shard_map/pallas_call | solution.py:342
  449.0 3.6 convolution_convert_fusion.4
  452.6 43.1 %all-reduce.5.cloned.1.call-done = bf16[1152,1536]{1,0:T(8,128)(2,1)} async-done(((bf16[1152,1536]{1,0:T(8,128)(2,1)}), bf16[1152,1536]{1,0:T(8,128)(2,1)}) %all-reduce.5.cloned.1.call-update) | async-done | bytes 3538960 | tf_op jit(solution)/shard_map/psum | solution.py:1251
  495.7 5.8 slice_convert_fusion
  503.0 29.3 %attend_backward.1 = (f32[2,2,2,240,128]{4,3,2,1,0:T(8,128)}, bf16[1280,2048]{1,0:T(8,128)(2,1)}) custom-call(s32[18]{0:T(128)} %pad_add_fusion.scalars, bf16[2,2,2,240,128]{4,3,2,1,0:T(8,128)(2,1)} %copy-done.6, bf16[2,2,2,240,128]{4,3,2,1,0:T(8,128)(2,1)} %bitcast.110, f32[2,2,2,240,128]{4,3,2,1,0:T(8,128)} %get-tuple-element.54.att_ref, ...), custom_call_target="tpu_custom_call" | custom-call | tf_op jit(solution)/shard_map/attend_backward/pallas_call | solution.py:237
  532.3 75.6 %shard_map.199 = (f32[40,2048]{1,0:T(8,128)}, f32[160,1536]{1,0:T(8,128)}) custom-call(bf16[32,40,2048]{2,1,0:T(8,128)(2,1)} %bitcast.99, bf16[8,160,1536]{2,1,0:T(8,128)(2,1)} %bitcast.102), custom_call_target="tpu_custom_call" | custom-call | bytes 83886080 | tf_op jit(solution)/shard_map/pallas_call | solution.py:882
  616.4 3.7 unproject.1
  622.2 4.5 convolution_convert_fusion.2
  626.7 84.3 %shard_map.200 = (bf16[4,48,2048]{2,1,0:T(8,128)(2,1)}, bf16[4,48,1536]{2,1,0:T(8,128)(2,1)}, f32[4,8,128]{2,1,0:T(8,128)}) custom-call(bf16[32,48,2048]{2,1,0:T(8,128)(2,1)} %bitcast.90, bf16[32,48,1536]{2,1,0:T(8,128)(2,1)} %bitcast.91, f32[32,8,128]{2,1,0:T(8,128)} %bitcast.115), custom_call_target="tpu_custom_call" | custom-call | bytes 178257920 | tf_op jit(solution)/shard_map/pallas_call | solution.py:882
  720.5 8.8 %unpack.1 = (f32[4,48,8960]{2,1,0:T(8,128)}, f32[4,48,8960]{2,1,0:T(8,128)}) custom-call(bf16[4,8,48,2304]{3,2,1,0:T(8,128)(2,1)} %bitcast.96), custom_call_target="tpu_custom_call" | custom-call | tf_op jit(solution)/shard_map/unpack/pallas_call | solution.py:1121
  (162 shorter events, 57.9 us)
Async XLA Ops:
  7.2 269.3 %all-gather.4.cloned.1.call-start = ((), (), s32[]{:S(2)}) async-start(), calls=%async_computation.1 | async-start | bytes 8847360 | tf_op jit(solution)/shard_map/all_gather | solution.py:1209
  9.5 65.8 %copy-start.36 = (s32[2,8]{1,0:T(2,128)S(1)}, s32[2,8]{1,0:T(2,128)}, u32[]{:S(2)}) copy-start(s32[2,8]{1,0:T(2,128)} %param.12) | copy-start | bytes 196
  9.5 68.0 %copy-start.29 = (bf16[40,4,1536]{2,1,0:T(4,128)(2,1)S(1)}, bf16[40,4,1536]{2,1,0:T(4,128)(2,1)}, u32[]{:S(2)}) copy-start(bf16[40,4,1536]{2,1,0:T(4,128)(2,1)} %param.21) | copy-start | bytes 1474564
  9.5 68.9 %copy-start.30 = (bf16[40,4,1536]{2,1,0:T(4,128)(2,1)S(1)}, bf16[40,4,1536]{2,1,0:T(4,128)(2,1)}, u32[]{:S(2)}) copy-start(bf16[40,4,1536]{2,1,0:T(4,128)(2,1)} %param.11) | copy-start | bytes 1474564
  78.5 131.3 %copy-start.4 = (bf16[4,40,1536]{2,1,0:T(8,128)(2,1)}, bf16[4,40,1536]{2,1,0:T(8,128)(2,1)S(1)}, u32[]{:S(2)}) copy-start(bf16[4,40,1536]{2,1,0:T(8,128)(2,1)S(1)} %copy.48) | copy-start | bytes 1474564
  78.6 100.2 %copy-start.18 = (f32[1,1536]{1,0:T(1,128)}, f32[1,1536]{1,0:T(1,128)S(1)}, u32[]{:S(2)}) copy-start(f32[1,1536]{1,0:T(1,128)S(1)} %reshape_reshape.7.gain_ref) | copy-start | bytes 18436
  78.6 7.9 %copy-start.12 = (f32[4,40,128]{2,1,0:T(8,128)}, f32[4,40,128]{2,1,0:T(8,128)S(1)}, u32[]{:S(2)}) copy-start(f32[4,40,128]{2,1,0:T(8,128)S(1)} %get-tuple-element.89) | copy-start | bytes 245764
  78.6 10.2 %copy-start.14 = (f32[160,128]{1,0:T(8,128)}, f32[160,128]{1,0:T(8,128)S(1)}, u32[]{:S(2)}) copy-start(f32[160,128]{1,0:T(8,128)S(1)} %bitcast_multiply_fusion.sin_ref) | copy-start | bytes 245764
  178.7 227.4 %reduce-scatter.2.cloned.1.call-start = ((), (), s32[]{:S(2)}) async-start(), calls=%async_computation.2 | async-start | bytes 8847360 | tf_op jit(solution)/shard_map/reduce_scatter | solution.py:1239
  179.1 34.2 %copy-start.31 = (f32[1536]{0:T(1024)}, f32[1536]{0:T(1024)S(1)}, u32[]{:S(2)}) copy-start(f32[1536]{0:T(1024)S(1)} %mul.246) | copy-start | bytes 18436
  213.3 186.8 %copy-start.20 = (f32[160,1536]{1,0:T(8,128)}, f32[160,1536]{1,0:T(8,128)S(1)}, u32[]{:S(2)}) copy-start(f32[160,1536]{1,0:T(8,128)S(1)} %get-tuple-element.99) | copy-start | bytes 2949124
  276.5 15.5 %copy-start.37 = (bf16[8,160,1536]{2,1,0:T(8,128)(2,1)S(1)}, bf16[8,160,1536]{2,1,0:T(8,128)(2,1)}, u32[]{:S(2)}) copy-start(bf16[8,160,1536]{2,1,0:T(8,128)(2,1)} %get-tuple-element.56) | copy-start | bytes 11796484
  291.9 15.3 %copy-start.24 = (bf16[8,160,1536]{2,1,0:T(8,128)(2,1)S(1)}, bf16[8,160,1536]{2,1,0:T(8,128)(2,1)}, u32[]{:S(2)}) copy-start(bf16[8,160,1536]{2,1,0:T(8,128)(2,1)} %shard_map.196) | copy-start | bytes 11796484
  320.0 175.7 %all-reduce.5.cloned.1.call-start = ((), (), s32[]{:S(2)}) async-start(), calls=%async_computation.3 | async-start | bytes 7077888 | tf_op jit(solution)/shard_map/psum | solution.py:1251
  379.2 9.7 %copy-start.38 = (bf16[8,160,1536]{2,1,0:T(8,128)(2,1)S(1)}, bf16[8,160,1536]{2,1,0:T(8,128)(2,1)}, u32[]{:S(2)}) copy-start(bf16[8,160,1536]{2,1,0:T(8,128)(2,1)} %get-tuple-element.56) | copy-start | bytes 11796484
  379.2 9.7 %copy-start.39 = (bf16[1280,1152]{0,1:T(8,128)(2,1)S(1)}, bf16[1280,1152]{0,1:T(8,128)(2,1)}, u32[]{:S(2)}) copy-start(bf16[1280,1152]{0,1:T(8,128)(2,1)} %get-tuple-element.61) | copy-start | bytes 8847364
  395.1 5.4 copy-start.23
  395.1 325.4 %all-gather.6.cloned.1.call-start = ((), (), s32[]{:S(2)}) async-start(), calls=%async_computation.4 | async-start | bytes 8847360 | tf_op jit(solution)/shard_map/all_gather | solution.py:1266
  402.1 46.9 %copy-start.22 = (bf16[160,1536]{1,0:T(8,128)(2,1)S(1)}, bf16[160,1536]{1,0:T(8,128)(2,1)}, u32[]{:S(2)}) copy-start(bf16[160,1536]{1,0:T(8,128)(2,1)} %copy-done.21) | copy-start | bytes 1474564
  616.4 5.8 copy-start.8
  626.7 89.0 %copy-start.10 = (f32[160,1536]{1,0:T(8,128)S(1)}, f32[160,1536]{1,0:T(8,128)}, u32[]{:S(2)}) copy-start(f32[160,1536]{1,0:T(8,128)} %copy-done.9) | copy-start | bytes 2949124
  711.0 6.9 copy-start.28
  711.0 8.1 %copy-start.27 = (bf16[4,48,2048]{2,1,0:T(8,128)(2,1)S(1)}, bf16[4,48,2048]{2,1,0:T(8,128)(2,1)}, u32[]{:S(2)}) copy-start(bf16[4,48,2048]{2,1,0:T(8,128)(2,1)} %get-tuple-element.78) | copy-start | bytes 2359300
  719.1 10.2 %copy-start.1 = (bf16[192,2048]{1,0:T(8,128)(2,1)S(1)}, bf16[192,2048]{1,0:T(8,128)(2,1)}, u32[]{:S(2)}) copy-start(bf16[192,2048]{1,0:T(8,128)(2,1)} %param.14) | copy-start | bytes 2359300
  (20 other events, 40.7 us)
Sparse Core Ops, SparseCore 0:
  178.8 95.4 all-gather.3
  320.1 74.6 reduce-scatter.1
  398.6 97.0 all-reduce.4
  497.4 97.6 all-gather.5

commit v11 on v10

--- a/solution.py
+++ b/solution.py
@@ -71,12 +71,23 @@
     return (scale * (grad_unit - unit * inner), jnp.sum(grad_out * unit, 0))
 
 
+def hidden_rows(scores, own_shard, rows_here):
+    row = lax.broadcasted_iota(jnp.int32, scores.shape, 0)
+    lane = lax.broadcasted_iota(jnp.int32, scores.shape, 1)
+    return row > own_shard * rows_here + lax.rem(lane, rows_here)
+
+
+def key_part(group, half_key, part):
+    at = ((group * 2 + half_key) * 2 + part) * HD
+    return slice(at, at + HD)
+
+
 def attend_forward_kernel(ctx_size, block_rows, rows_here, scalars, q_ref, kv_ref, out_ref, stat_ref, best_ref, total_ref, accum_ref):
     seq = pl.program_id(0)
     blocks = 2 * ctx_size
     own_ctx = scalars[SEQS * blocks]
     own_shard = scalars[SEQS * blocks + 1]
-    lanes = q_ref.shape[3]
+    groups = range(KVH)
     best_ref[...] = jnp.full(best_ref.shape, NEG_FILL, jnp.float32)
     total_ref[...] = jnp.zeros(total_ref.shape, jnp.float32)
     accum_ref[...] = jnp.zeros(accum_ref.shape, jnp.float32)
@@ -87,29 +98,39 @@
 
         def work(masked):
             rows = pl.ds(pl.multiple_of(key_ctx * block_rows, block_rows), block_rows)
-            keys = kv_ref[rows, half_key * 2 * HD : half_key * 2 * HD + HD]
-            values = kv_ref[rows, half_key * 2 * HD + HD : half_key * 2 * HD + 2 * HD]
-            scores = lax.dot_general(
-                keys, q_ref[0, half, 0], CONTRACT_LAST, preferred_element_type=jnp.float32
-            )
+            scores = [
+                lax.dot_general(
+                    kv_ref[rows, key_part(group, half_key, 0)],
+                    q_ref[0, half, group],
+                    CONTRACT_LAST,
+                    preferred_element_type=jnp.float32,
+                )
+                for group in groups
+            ]
             if masked:
-                row = lax.broadcasted_iota(jnp.int32, (block_rows, lanes), 0)
-                lane = lax.broadcasted_iota(jnp.int32, (block_rows, lanes), 1)
-                scores = jnp.where(
-                    row <= own_shard * rows_here + lax.rem(lane, rows_here), scores, NEG_FILL
-                )
-            best = best_ref[half]
-            fresh = jnp.maximum(best, jnp.max(scores, 0, keepdims=True))
-            decay = jnp.exp(best - fresh)
-            weights = jnp.exp(scores - fresh)
-            total_ref[half] = total_ref[half] * decay + jnp.sum(weights, 0, keepdims=True)
-            accum_ref[half] = accum_ref[half] * decay + lax.dot_general(
-                values,
-                weights.astype(jnp.bfloat16),
-                CONTRACT_FIRST,
-                preferred_element_type=jnp.float32,
-            )
-            best_ref[half] = fresh
+                hidden = hidden_rows(scores[0], own_shard, rows_here)
+                scores = [jnp.where(hidden, NEG_FILL, score) for score in scores]
+            best = [best_ref[half, group] for group in groups]
+            fresh = [
+                jnp.maximum(best[group], jnp.max(scores[group], 0, keepdims=True)) for group in groups
+            ]
+            weights = [jnp.exp(scores[group] - fresh[group]) for group in groups]
+            decay = [jnp.exp(best[group] - fresh[group]) for group in groups]
+            added = [
+                lax.dot_general(
+                    kv_ref[rows, key_part(group, half_key, 1)],
+                    weights[group].astype(jnp.bfloat16),
+                    CONTRACT_FIRST,
+                    preferred_element_type=jnp.float32,
+                )
+                for group in groups
+            ]
+            for group in groups:
+                total_ref[half, group] = total_ref[half, group] * decay[group] + jnp.sum(
+                    weights[group], 0, keepdims=True
+                )
+                accum_ref[half, group] = accum_ref[half, group] * decay[group] + added[group]
+                best_ref[half, group] = fresh[group]
 
         @pl.when(order_key < order_query)
         def full():
@@ -126,37 +147,41 @@
                 step(key_ctx, half_key, half)
 
     for half in range(2):
-        totals = total_ref[half]
-        out_ref[0, half, 0] = (accum_ref[half] / totals).T
-        stat_ref[0, half, 0] = best_ref[half] + jnp.log(totals)
+        for group in groups:
+            totals = total_ref[half, group]
+            out_ref[0, half, group] = (accum_ref[half, group] / totals).T
+            stat_ref[0, half, group] = best_ref[half, group] + jnp.log(totals)
+
+
+def group_blocks(lanes, key_rows):
+    group = pl.BlockSpec((1, 2, KVH, lanes, HD), lambda s, _: (s, 0, 0, 0, 0))
+    stat = pl.BlockSpec((1, 2, KVH, 1, lanes), lambda s, _: (s, 0, 0, 0, 0))
+    keys = pl.BlockSpec((key_rows, KVH * 4 * HD), lambda s, _: (0, s))
+    return group, stat, keys
 
 
 def attend_forward(scalars, queries, all_kv, ctx_size, block_rows, rows_here):
     lanes = queries.shape[3]
     kernel = functools.partial(attend_forward_kernel, ctx_size, block_rows, rows_here)
-    group = pl.BlockSpec((1, 2, 1, lanes, HD), lambda s, n, _: (s, 0, n, 0, 0))
-    stat = pl.BlockSpec((1, 2, 1, 1, lanes), lambda s, n, _: (s, 0, n, 0, 0))
+    group, stat, keys = group_blocks(lanes, all_kv.shape[0])
     return pl.pallas_call(
         kernel,
         grid_spec=pltpu.PrefetchScalarGridSpec(
             num_scalar_prefetch=1,
-            grid=(SEQS, KVH),
-            in_specs=[
-                group,
-                pl.BlockSpec((all_kv.shape[0], 4 * HD), lambda s, n, _: (0, s * KVH + n)),
-            ],
+            grid=(SEQS,),
+            in_specs=[group, keys],
             out_specs=[group, stat],
             scratch_shapes=[
-                pltpu.VMEM((2, 1, lanes), jnp.float32),
-                pltpu.VMEM((2, 1, lanes), jnp.float32),
-                pltpu.VMEM((2, HD, lanes), jnp.float32),
+                pltpu.VMEM((2, KVH, 1, lanes), jnp.float32),
+                pltpu.VMEM((2, KVH, 1, lanes), jnp.float32),
+                pltpu.VMEM((2, KVH, HD, lanes), jnp.float32),
             ],
         ),
         out_shape=(
             jax.ShapeDtypeStruct(queries.shape, jnp.float32),
             jax.ShapeDtypeStruct((SEQS, 2, KVH, 1, lanes), jnp.float32),
         ),
-        compiler_params=pltpu.CompilerParams(vmem_limit_bytes=56 * 2**20),
+        compiler_params=pltpu.CompilerParams(vmem_limit_bytes=60 * 2**20),
         name="attend_forward",
     )(scalars, queries, all_kv)
 
@@ -166,11 +191,12 @@
     blocks = 2 * ctx_size
     own_ctx = scalars[SEQS * blocks]
     own_shard = scalars[SEQS * blocks + 1]
-    lanes = q_ref.shape[3]
+    groups = range(KVH)
     gq_acc[...] = jnp.zeros(gq_acc.shape, jnp.float32)
     for half in range(2):
-        product = go_ref[0, half, 0].astype(jnp.float32) * att_ref[0, half, 0]
-        delta_ref[half] = jnp.sum(product.T, 0, keepdims=True)
+        for group in groups:
+            product = go_ref[0, half, group].astype(jnp.float32) * att_ref[0, half, group]
+            delta_ref[half, group] = jnp.sum(product.T, 0, keepdims=True)
 
     def step(key_ctx, half_key, half):
         order_key = scalars[seq * blocks + half_key * ctx_size + key_ctx]
@@ -178,31 +204,44 @@
 
         def work(masked):
             rows = pl.ds(pl.multiple_of(key_ctx * block_rows, block_rows), block_rows)
-            keys = kv_ref[rows, half_key * 2 * HD : half_key * 2 * HD + HD]
-            values = kv_ref[rows, half_key * 2 * HD + HD : half_key * 2 * HD + 2 * HD]
-            queries = q_ref[0, half, 0]
-            grad_out = go_ref[0, half, 0]
-            scores = lax.dot_general(
-                keys, queries, CONTRACT_LAST, preferred_element_type=jnp.float32
-            )
-            probs = jnp.exp(scores - stat_ref[0, half, 0])
+            keys = [kv_ref[rows, key_part(group, half_key, 0)] for group in groups]
+            queries = [q_ref[0, half, group] for group in groups]
+            grad_out = [go_ref[0, half, group] for group in groups]
+            scores = [
+                lax.dot_general(
+                    keys[group], queries[group], CONTRACT_LAST, preferred_element_type=jnp.float32
+                )
+                for group in groups
+            ]
+            grad_probs = [
+                lax.dot_general(
+                    kv_ref[rows, key_part(group, half_key, 1)],
+                    grad_out[group],
+                    CONTRACT_LAST,
+                    preferred_element_type=jnp.float32,
+                )
+                for group in groups
+            ]
+            probs = [jnp.exp(scores[group] - stat_ref[0, half, group]) for group in groups]
             if masked:
-                row = lax.broadcasted_iota(jnp.int32, (block_rows, lanes), 0)
-                lane = lax.broadcasted_iota(jnp.int32, (block_rows, lanes), 1)
-                probs = jnp.where(
-                    row <= own_shard * rows_here + lax.rem(lane, rows_here), probs, 0.0
-                )
-            grad_probs = lax.dot_general(
-                values, grad_out, CONTRACT_LAST, preferred_element_type=jnp.float32
-            )
-            grad_scores = (probs * (grad_probs - delta_ref[half])).astype(jnp.bfloat16)
-            gv_acc[...] += jnp.dot(
-                probs.astype(jnp.bfloat16), grad_out, preferred_element_type=jnp.float32
-            )
-            gk_acc[...] += jnp.dot(grad_scores, queries, preferred_element_type=jnp.float32)
-            gq_acc[half] += lax.dot_general(
-                keys, grad_scores, CONTRACT_FIRST, preferred_element_type=jnp.float32
-            )
+                hidden = hidden_rows(scores[0], own_shard, rows_here)
+                probs = [jnp.where(hidden, 0.0, prob) for prob in probs]
+            grad_scores = [
+                (probs[group] * (grad_probs[group] - delta_ref[half, group])).astype(jnp.bfloat16)
+                for group in groups
+            ]
+            for group in groups:
+                gv_acc[group] += jnp.dot(
+                    probs[group].astype(jnp.bfloat16),
+                    grad_out[group],
+                    preferred_element_type=jnp.float32,
+                )
+                gk_acc[group] += jnp.dot(
+                    grad_scores[group], queries[group], preferred_element_type=jnp.float32
+                )
+                gq_acc[half, group] += lax.dot_general(
+                    keys[group], grad_scores[group], CONTRACT_FIRST, preferred_element_type=jnp.float32
+                )
 
         @pl.when(order_key < order_query)
         def full():
@@ -220,39 +259,38 @@
             gv_acc[...] = jnp.zeros(gv_acc.shape, jnp.float32)
             for half in range(2):
                 step(key_ctx, half_key, half)
-            at = half_key * 2 * HD
-            gkv_ref[rows, at : at + HD] = gk_acc[...].astype(jnp.bfloat16)
-            gkv_ref[rows, at + HD : at + 2 * HD] = gv_acc[...].astype(jnp.bfloat16)
+            for group in groups:
+                gkv_ref[rows, key_part(group, half_key, 0)] = gk_acc[group].astype(jnp.bfloat16)
+                gkv_ref[rows, key_part(group, half_key, 1)] = gv_acc[group].astype(jnp.bfloat16)
 
     for half in range(2):
-        gq_ref[0, half, 0] = gq_acc[half].T
+        for group in groups:
+            gq_ref[0, half, group] = gq_acc[half, group].T
 
 
 def attend_backward(scalars, queries, grad_out, attended, stats, all_kv, ctx_size, block_rows, rows_here):
     lanes = queries.shape[3]
     kernel = functools.partial(attend_backward_kernel, ctx_size, block_rows, rows_here)
-    group = pl.BlockSpec((1, 2, 1, lanes, HD), lambda s, n, _: (s, 0, n, 0, 0))
-    stat = pl.BlockSpec((1, 2, 1, 1, lanes), lambda s, n, _: (s, 0, n, 0, 0))
-    full = pl.BlockSpec((all_kv.shape[0], 4 * HD), lambda s, n, _: (0, s * KVH + n))
+    group, stat, keys = group_blocks(lanes, all_kv.shape[0])
     return pl.pallas_call(
         kernel,
         grid_spec=pltpu.PrefetchScalarGridSpec(
             num_scalar_prefetch=1,
-            grid=(SEQS, KVH),
-            in_specs=[group, group, group, stat, full],
-            out_specs=[group, full],
+            grid=(SEQS,),
+            in_specs=[group, group, group, stat, keys],
+            out_specs=[group, keys],
             scratch_shapes=[
-                pltpu.VMEM((2, 1, lanes), jnp.float32),
-                pltpu.VMEM((2, HD, lanes), jnp.float32),
-                pltpu.VMEM((block_rows, HD), jnp.float32),
-                pltpu.VMEM((block_rows, HD), jnp.float32),
+                pltpu.VMEM((2, KVH, 1, lanes), jnp.float32),
+                pltpu.VMEM((2, KVH, HD, lanes), jnp.float32),
+                pltpu.VMEM((KVH, block_rows, HD), jnp.float32),
+                pltpu.VMEM((KVH, block_rows, HD), jnp.float32),
             ],
         ),
         out_shape=(
             jax.ShapeDtypeStruct(queries.shape, jnp.float32),
             jax.ShapeDtypeStruct(all_kv.shape, jnp.bfloat16),
         ),
-        compiler_params=pltpu.CompilerParams(vmem_limit_bytes=56 * 2**20),
+        compiler_params=pltpu.CompilerParams(vmem_limit_bytes=60 * 2**20),
         name="attend_backward",
     )(scalars, queries, grad_out, attended, stats, all_kv)
 
@@ -1194,17 +1232,13 @@
 
     down_padded = jnp.pad(w_down, ((0, width - columns), (0, 0)))
 
+    late_grad_out, w_qkv_all = lax.optimization_barrier((grad_out, w_qkv_all))
+    cotangent_all = lax.all_gather(late_grad_out, "fsdp", axis=0, tiled=True)
     normed_one, queries, own_kv = project(
         tokens, gain_one, w_qkv_all, bias_all, cosine, signed_sine, rows_here
     )
-    all_kv, w_o_all, cotangent_all = gather(
-        [own_kv, own_cut(w_o), grad_out],
-        [by_tokens, by_rows, lambda ctx, shard: shard],
-        2,
-        wide=(0, 1),
-    )
+    all_kv, w_o_all = gather([own_kv, own_cut(w_o)], [by_tokens, by_rows], 2)
     w_o_all = w_o_all.reshape(D, D)
-    cotangent_all = cotangent_all.reshape(-1, D)
     gate_up_cut, all_kv = lax.optimization_barrier((gate_up_cut, all_kv))
     gate_up_cols = lax.all_gather(
         gate_up_cut.reshape(shard_count * cut, 2 * width), "ctx", axis=0, tiled=True
@@ -1278,13 +1312,14 @@
         block_rows,
         rows_here,
     )
-    grad_kv, mixed_rows = scatter(
+    (grad_kv,) = scatter(
         [grad_kv_full.reshape(-1, rows_here, SEQS * KVH * 4 * HD)],
         by_tokens,
         3,
         out_dtype=jnp.float32,
-        lines=[mixed_terms.reshape(shard_count, -1, D)],
-    )
+    )
+    mixed_terms, grad_kv = lax.optimization_barrier((mixed_terms, grad_kv))
+    mixed_rows = lax.psum_scatter(mixed_terms, "fsdp", scatter_dimension=0, tiled=True)
     grad_projected, grad_input, grad_gain_one, grad_bias = unproject(
         grad_queries,
         grad_kv,
@@ -1320,7 +1355,7 @@
         4,
         spread_ctx=True,
     )
-    mixed_out = middle + mixed_rows
+    mixed_out = middle + mixed_rows.astype(jnp.float32)
     output = from_slot(mixed_out.astype(jnp.bfloat16), rows_here)
     small_rows = small_rows.reshape(ctx_size, -1)[:, :small_width].reshape(-1)
     bias_start = 2 * gain_width

time: 743 us -> 693 us (0.933)
  Pallas kernels: 531 us -> 476 us
    psum x1, waiting for transfers between devices: 43.1 us -> 0.02 us  [shards(): down_rows = lax.psum(down_terms, 'ctx')]
    pallas_call x3, Pallas kernels: 210 us -> 168 us  [gather(): pl.pallas_call(functools.partial(gather_kernel, arity, ctx_size, pair_cou...]
    all_gather x0 -> x1, waiting for transfers between devices: none -> 31 us  [shards(): cotangent_all = lax.all_gather(late_grad_out, 'fsdp', axis=0, tiled=True)]
    all_gather x1, waiting for transfers between devices: 0.01 us -> 9.92 us  [shards(): gate_up_rows = lax.all_gather(gate_up_rows, 'ctx', axis=0, tiled=False)]
    pallas_call x1, Pallas kernels: 27.9 us -> 19 us  [attend_forward(): pl.pallas_call(kernel, grid_spec=pltpu.PrefetchScalarGridSpec(num_scalar_...]
    unnamed x85 -> x79, local copies, waits for them, and re-layouts: 19.3 us -> 14.8 us
  transfers between devices with their start and end apart: 4 -> 6, of which waited for: 1 -> 3; matrix products, arithmetic and copies ran while one was open for 11% -> 14% of each run, Pallas kernels for 50% -> 49%
where the time goes in v11:
time: 693 us; the launch traced here: 686 us
  Pallas kernels  476 us (69%)
  matrix products  89.7 us (13%)
  waiting for transfers between devices  47 us (7%)
  local copies, waits for them, and re-layouts  36.4 us (5%)
  other arithmetic  20.9 us (3%)
  between operations  15.1 us (2%)
    pallas_call x3, Pallas kernels, gather(): pl.pallas_call(functools.partial(gather_kernel, arity, ctx_size, pair_cou...  168 us
    pallas_call x2, Pallas kernels, scatter(): pl.pallas_call(functools.partial(scatter_kernel, arity, ctx_size, pair_co...  163 us
    pallas_call x1, Pallas kernels, exchange(): pl.pallas_call(functools.partial(exchange_kernel, shard_count // 2), in_s...  42.1 us
    pallas_call x1, Pallas kernels, line_sum(): pl.pallas_call(functools.partial(line_sum_kernel, pair_count), in_specs=[...  41.8 us
    all_gather x1, waiting for transfers between devices, shards(): cotangent_all = lax.all_gather(late_grad_out, 'fsdp', axis=0, tiled=True)  31 us
    pallas_call x1, Pallas kernels, attend_backward(): pl.pallas_call(kernel, grid_spec=pltpu.PrefetchScalarGridSpec(num_scalar_...  22.2 us
    pallas_call x1, Pallas kernels, attend_forward(): pl.pallas_call(kernel, grid_spec=pltpu.PrefetchScalarGridSpec(num_scalar_...  19 us
    dot_general x1, matrix products, shards(): jnp.dot(tokens_all, gate_up_cols, preferred_element_type=jnp.float32)  15.3 us
  transfers between devices with their start and end apart: 6, of which 3 were waited for; matrix products, arithmetic and copies ran while one was open for 14% of the time, Pallas kernels for 49%

profile of v11, /device:TPU:0, one launch (start us, length us, event | category | flops | bytes accessed | tf_op | source)
XLA Modules:
  0.0 686.2 jit_solution(3105428510081858595)
XLA Ops:
  15.4 58.7 %shard_map.194 = (bf16[32,48,2048]{2,1,0:T(8,128)(2,1)}, bf16[32,16,128]{2,1,0:T(8,128)(2,1)}, bf16[8,48,2304]{2,1,0:T(8,128)(2,1)}) custom-call(bf16[48,2048]{1,0:T(8,128)(2,1)} %constant_dynamic-slice_fusion.4.refs_0_, bf16[16,128]{1,0:T(8,128)(2,1)} %bitcast.117, bf16[8,48,2304]{2,1,0:T(8,128)(2,1)} %pack.1.refs_2_), custom_call_target="tpu_custom_call" | custom-call | bytes 25690112 | tf_op jit(solution)/shard_map/pallas_call | solution.py:613
  81.5 5.0 project.1
  88.8 66.5 %shard_map.195 = (bf16[32,40,2048]{2,1,0:T(8,128)(2,1)}, bf16[32,48,1536]{2,1,0:T(8,128)(2,1)}) custom-call(bf16[40,2048]{1,0:T(8,128)(2,1)} %copy-done.18, bf16[48,1536]{1,0:T(8,128)(2,1)} %constant_dynamic-slice_fusion.refs_1_), custom_call_target="tpu_custom_call" | custom-call | bytes 39845888 | tf_op jit(solution)/shard_map/pallas_call | solution.py:613
  157.0 19.0 %attend_forward.1 = (f32[2,2,2,240,128]{4,3,2,1,0:T(8,128)}, f32[2,2,2,1,240]{4,3,2,1,0:T(1,128)}) custom-call(s32[18]{0:T(128)} %pad_add_fusion.scalars, bf16[2,2,2,240,128]{4,3,2,1,0:T(8,128)(2,1)} %copy-done.6, bf16[1280,2048]{1,0:T(8,128)(2,1)} %bitcast.90), custom_call_target="tpu_custom_call" | custom-call | tf_op jit(solution)/shard_map/attend_forward/pallas_call | solution.py:167
  183.8 43.0 %shard_map.196 = bf16[8,160,1536]{2,1,0:T(8,128)(2,1)} custom-call(bf16[160,1536]{1,0:T(8,128)(2,1)} %copy.54.refs_0_), custom_call_target="tpu_custom_call" | custom-call | bytes 62914560 | tf_op jit(solution)/shard_map/pallas_call | solution.py:613
  226.8 5.0 all-gather.7.cloned.1.call-done
  231.8 15.3 %fusion.12 = f32[1280,2304]{0,1:T(8,128)} fusion(bf16[1280,1536]{1,0:T(8,128)(2,1)} %bitcast.100, bf16[1536,2304]{1,0:T(8,128)(2,1)} %all-gather.7.cloned.1.call-done), kind=kOutput, calls=%fused_computation.63 | convolution fusion | flops 9059696640 | bytes 22806528 | tf_op jit(solution)/shard_map/dot_general | solution.py:1260
  247.1 31.0 %all-gather.5.cloned.1.call-done = bf16[1280,1536]{1,0:T(8,128)(2,1)} async-done(((bf16[160,1536]{1,0:T(8,128)(2,1)}), bf16[1280,1536]{1,0:T(8,128)(2,1)}) %all-gather.5.cloned.1.call-update) | async-done | bytes 3932176 | tf_op jit(solution)/shard_map/all_gather | solution.py:1236
  278.2 12.8 %multiply_convert_fusion.2 = (bf16[1280,1152]{0,1:T(8,128)(2,1)S(1)}, bf16[1280,1152]{0,1:T(8,128)(2,1)S(1)}, bf16[1280,1152]{0,1:T(8,128)(2,1)}) fusion(f32[1280,2304]{0,1:T(8,128)} %fusion.12, bf16[1280,1536]{1,0:T(8,128)(2,1)} %all-gather.5.cloned.1.call-done, bf16[1120,1536]{1,0:T(8,128)(2,1)} %param.20), kind=kOutput, calls=%fused_computation.9 | convolution fusion | flops 4551966720 | bytes 28016640 | tf_op jit(solution)/shard_map/dot_general | solution.py:1265
  293.5 12.8 %convolution_convert_fusion = bf16[1536,2304]{1,0:T(8,128)(2,1)} fusion(bf16[1280,1536]{1,0:T(8,128)(2,1)S(1)} %bitcast.101, bf16[1280,1152]{0,1:T(8,128)(2,1)S(1)} %get-tuple-element.88, bf16[1280,1152]{0,1:T(8,128)(2,1)S(1)} %get-tuple-element.87), kind=kOutput, calls=%fused_computation | convolution fusion | flops 9075032064 | bytes 16908288 | tf_op jit(solution)/shard_map/dot_general | solution.py:1270
  309.5 13.1 %convolution_convert_fusion.5 = bf16[1280,1536]{1,0:T(8,128)(2,1)} fusion(bf16[1280,2304]{0,1:T(8,128)(2,1)S(1)} %pad_maximum_fusion, bf16[1536,2304]{1,0:T(8,128)(2,1)} %all-gather.7.cloned.1.call-done), kind=kOutput, calls=%fused_computation.5 | convolution fusion | flops 9061662720 | bytes 16908288 | tf_op jit(solution)/shard_map/dot_general | solution.py:1277
  322.6 41.8 %shard_map.197 = f32[160,1536]{1,0:T(8,128)} custom-call(bf16[8,160,1536]{2,1,0:T(8,128)(2,1)} %bitcast.99), custom_call_target="tpu_custom_call" | custom-call | bytes 31457280 | tf_op jit(solution)/shard_map/pallas_call | solution.py:968
  364.4 9.3 %convolution_convert_fusion.1 = bf16[1280,1536]{1,0:T(8,128)(2,1)} fusion(bf16[1280,1152]{0,1:T(8,128)(2,1)} %get-tuple-element.63, bf16[1120,1536]{1,0:T(8,128)(2,1)} %param.20), kind=kOutput, calls=%fused_computation.1 | convolution fusion | flops 4531814400 | bytes 10321920 | tf_op jit(solution)/shard_map/dot_general | solution.py:1286
  373.7 9.6 %convolution_convert_fusion.3 = bf16[1152,1536]{1,0:T(8,128)(2,1)} fusion(bf16[1280,1152]{0,1:T(8,128)(2,1)} %get-tuple-element.63, bf16[1280,1536]{1,0:T(8,128)(2,1)} %all-gather.5.cloned.1.call-done), kind=kOutput, calls=%fused_computation.3 | convolution fusion | flops 4531617792 | bytes 10420224 | tf_op jit(solution)/shard_map/dot_general | solution.py:1282
  390.7 4.0 convolution_convert_fusion.6
  394.8 42.1 %shard_map.198 = bf16[8,48,2304]{2,1,0:T(8,128)(2,1)} custom-call(bf16[8,48,2304]{2,1,0:T(8,128)(2,1)} %bitcast.110), custom_call_target="tpu_custom_call" | custom-call | bytes 56623104 | tf_op jit(solution)/shard_map/pallas_call | solution.py:380
  438.4 22.2 %attend_backward.1 = (f32[2,2,2,240,128]{4,3,2,1,0:T(8,128)}, bf16[1280,2048]{1,0:T(8,128)(2,1)}) custom-call(s32[18]{0:T(128)} %pad_add_fusion.scalars, bf16[2,2,2,240,128]{4,3,2,1,0:T(8,128)(2,1)} %copy-done.6, bf16[2,2,2,240,128]{4,3,2,1,0:T(8,128)(2,1)} %bitcast.106, f32[2,2,2,240,128]{4,3,2,1,0:T(8,128)} %get-tuple-element.56.att_ref, ...), custom_call_target="tpu_custom_call" | custom-call | tf_op jit(solution)/shard_map/attend_backward/pallas_call | solution.py:275
  460.6 51.4 %shard_map.199.gkv_ref = f32[40,2048]{1,0:T(8,128)} custom-call(bf16[32,40,2048]{2,1,0:T(8,128)(2,1)} %bitcast.97), custom_call_target="tpu_custom_call" | custom-call | bytes 83886080 | tf_op jit(solution)/shard_map/pallas_call | solution.py:920
  513.1 3.6 convolution_convert_fusion.4
  516.8 6.2 slice_convert_fusion
  532.2 5.6 convolution_convert_fusion.2
  537.9 111.2 %shard_map.200 = (bf16[4,48,2048]{2,1,0:T(8,128)(2,1)}, bf16[4,48,1536]{2,1,0:T(8,128)(2,1)}, f32[4,8,128]{2,1,0:T(8,128)}) custom-call(bf16[32,48,2048]{2,1,0:T(8,128)(2,1)} %bitcast.88, bf16[32,48,1536]{2,1,0:T(8,128)(2,1)} %bitcast.89, f32[32,8,128]{2,1,0:T(8,128)} %bitcast.112), custom_call_target="tpu_custom_call" | custom-call | bytes 178257920 | tf_op jit(solution)/shard_map/pallas_call | solution.py:920
  660.2 9.9 %all-gather.9.cloned.1.call-done = bf16[32,48,2304]{2,1,0:T(8,128)(2,1)} async-done(((bf16[8,48,2304]{2,1,0:T(8,128)(2,1)}), bf16[32,48,2304]{2,1,0:T(8,128)(2,1)}) %all-gather.9.cloned.1.call-update) | async-done | bytes 7077904 | tf_op jit(solution)/shard_map/all_gather | solution.py:1300
  670.2 8.8 %unpack.1 = (f32[4,48,8960]{2,1,0:T(8,128)}, f32[4,48,8960]{2,1,0:T(8,128)}) custom-call(bf16[4,8,48,2304]{3,2,1,0:T(8,128)(2,1)} %bitcast.94), custom_call_target="tpu_custom_call" | custom-call | tf_op jit(solution)/shard_map/unpack/pallas_call | solution.py:1159
  (162 shorter events, 63.1 us)
Async XLA Ops:
  7.2 224.6 %all-gather.7.cloned.1.call-start = ((), (), s32[]{:S(2)}) async-start(), calls=%async_computation.3 | async-start | bytes 8847360 | tf_op jit(solution)/shard_map/all_gather | solution.py:1243
  9.5 65.8 %copy-start.36 = (s32[2,8]{1,0:T(2,128)S(1)}, s32[2,8]{1,0:T(2,128)}, u32[]{:S(2)}) copy-start(s32[2,8]{1,0:T(2,128)} %param.12) | copy-start | bytes 196
  9.5 68.0 %copy-start.29 = (bf16[40,4,1536]{2,1,0:T(4,128)(2,1)S(1)}, bf16[40,4,1536]{2,1,0:T(4,128)(2,1)}, u32[]{:S(2)}) copy-start(bf16[40,4,1536]{2,1,0:T(4,128)(2,1)} %param.21) | copy-start | bytes 1474564
  9.5 68.9 %copy-start.30 = (bf16[40,4,1536]{2,1,0:T(4,128)(2,1)S(1)}, bf16[40,4,1536]{2,1,0:T(4,128)(2,1)}, u32[]{:S(2)}) copy-start(bf16[40,4,1536]{2,1,0:T(4,128)(2,1)} %param.11) | copy-start | bytes 1474564
  78.5 99.6 %copy-start.4 = (bf16[4,40,1536]{2,1,0:T(8,128)(2,1)}, bf16[4,40,1536]{2,1,0:T(8,128)(2,1)S(1)}, u32[]{:S(2)}) copy-start(bf16[4,40,1536]{2,1,0:T(8,128)(2,1)S(1)} %copy.48) | copy-start | bytes 1474564
  78.6 76.7 %copy-start.19 = (f32[1,1536]{1,0:T(1,128)}, f32[1,1536]{1,0:T(1,128)S(1)}, u32[]{:S(2)}) copy-start(f32[1,1536]{1,0:T(1,128)S(1)} %reshape_reshape.7.gain_ref) | copy-start | bytes 18436
  78.6 7.9 %copy-start.13 = (f32[4,40,128]{2,1,0:T(8,128)}, f32[4,40,128]{2,1,0:T(8,128)S(1)}, u32[]{:S(2)}) copy-start(f32[4,40,128]{2,1,0:T(8,128)S(1)} %get-tuple-element.91) | copy-start | bytes 245764
  78.6 7.9 %copy-start.15 = (f32[160,128]{1,0:T(8,128)}, f32[160,128]{1,0:T(8,128)S(1)}, u32[]{:S(2)}) copy-start(f32[160,128]{1,0:T(8,128)S(1)} %bitcast_multiply_fusion.sin_ref) | copy-start | bytes 245764
  155.3 122.9 %all-gather.5.cloned.1.call-start = ((), (), s32[]{:S(2)}) async-start(), calls=%async_computation.2 | async-start | bytes 4423680 | tf_op jit(solution)/shard_map/all_gather | solution.py:1236
  156.0 238.8 %reduce-scatter.3.cloned.1.call-start = ((), (), s32[]{:S(2)}) async-start(), calls=%async_computation.4 | async-start | bytes 8847360 | tf_op jit(solution)/shard_map/reduce_scatter | solution.py:1273
  156.4 25.2 %copy-start.31 = (f32[1536]{0:T(1024)}, f32[1536]{0:T(1024)S(1)}, u32[]{:S(2)}) copy-start(f32[1536]{0:T(1024)S(1)} %mul.246) | copy-start | bytes 18436
  181.6 206.8 %copy-start.21 = (f32[160,1536]{1,0:T(8,128)}, f32[160,1536]{1,0:T(8,128)S(1)}, u32[]{:S(2)}) copy-start(f32[160,1536]{1,0:T(8,128)S(1)} %get-tuple-element.101) | copy-start | bytes 2949124
  278.2 15.3 %copy-start.26 = (bf16[8,160,1536]{2,1,0:T(8,128)(2,1)S(1)}, bf16[8,160,1536]{2,1,0:T(8,128)(2,1)}, u32[]{:S(2)}) copy-start(bf16[8,160,1536]{2,1,0:T(8,128)(2,1)} %shard_map.196) | copy-start | bytes 11796484
  306.4 210.4 %all-reduce.5.cloned.1.call-start = ((), (), s32[]{:S(2)}) async-start(), calls=%async_computation.6 | async-start | bytes 7077888 | tf_op jit(solution)/shard_map/psum | solution.py:1285
  383.3 274.8 %reduce-scatter.5.cloned.1.call-start = ((), (), s32[]{:S(2)}) async-start(), calls=%async_computation.5 | async-start | bytes 4423680 | tf_op jit(solution)/shard_map/reduce_scatter | solution.py:1322
  512.1 158.1 %all-gather.9.cloned.1.call-start = ((), (), s32[]{:S(2)}) async-start(), calls=%async_computation.7 | async-start | bytes 8847360 | tf_op jit(solution)/shard_map/all_gather | solution.py:1300
  516.7 6.3 copy-start.12
  516.7 6.3 copy-start.14
  516.7 6.3 copy-start.16
  516.7 6.3 copy-start.20
  525.9 6.4 copy-start.9
  537.9 113.3 %copy-start.11 = (f32[160,1536]{1,0:T(8,128)S(1)}, f32[160,1536]{1,0:T(8,128)}, u32[]{:S(2)}) copy-start(f32[160,1536]{1,0:T(8,128)} %copy-done.10) | copy-start | bytes 2949124
  649.1 9.0 %copy-start.22 = (f32[160,1536]{1,0:T(8,128)S(1)}, f32[160,1536]{1,0:T(8,128)}, u32[]{:S(2)}) copy-start(f32[160,1536]{1,0:T(8,128)} %copy-done.21) | copy-start | bytes 2949124
  655.6 23.4 %copy-start.1 = (bf16[192,2048]{1,0:T(8,128)(2,1)S(1)}, bf16[192,2048]{1,0:T(8,128)(2,1)}, u32[]{:S(2)}) copy-start(bf16[192,2048]{1,0:T(8,128)(2,1)} %param.14) | copy-start | bytes 2359300
  (19 other events, 51.2 us)
Sparse Core Ops, SparseCore 0:
  155.4 76.3 all-gather.6
  233.4 44.6 all-gather.4
  306.5 75.3 reduce-scatter.2
  385.5 106.8 all-reduce.4
  512.2 47.8 reduce-scatter.4
  561.8 108.2 all-gather.8

commit v12 on v11

--- a/solution.py
+++ b/solution.py
@@ -365,29 +365,6 @@
         self.own.wait()
         for copy in self.copies:
             copy.wait_send()
-
-
-def exchange_kernel(pair_count, source, out, send_sem, recv_sem, own_sem):
-    greet(1, pair_count, False, True)
-    flow = Exchange(source, out, (send_sem, recv_sem), own_sem, pair_count)
-    flow.start()
-    flow.finish()
-
-
-def exchange(pieces, collective_id):
-    shard_count = lax.axis_size("fsdp")
-    dma = pltpu.SemaphoreType.DMA
-    return pl.pallas_call(
-        functools.partial(exchange_kernel, shard_count // 2),
-        in_specs=[pl.BlockSpec(memory_space=pltpu.VMEM)],
-        out_specs=pl.BlockSpec(memory_space=pl.ANY),
-        out_shape=jax.ShapeDtypeStruct(pieces.shape, pieces.dtype),
-        scratch_shapes=[dma((shard_count - 1,))] * 2 + [dma],
-        compiler_params=pltpu.CompilerParams(collective_id=collective_id, has_side_effects=True),
-        cost_estimate=pl.CostEstimate(
-            flops=0, bytes_accessed=pieces.size * 64, transcendentals=0
-        ),
-    )(pieces)
 
 
 def gather_kernel(arity, ctx_size, pair_count, slots, swaps, wide, *refs):
@@ -1145,25 +1122,30 @@
     )(gate, up)
 
 
-def unpack_kernel(columns, in_ref, gate_ref, up_ref):
+def unpack_kernel(columns, own_shard, in_ref, gate_ref, up_ref):
     width = in_ref.shape[3] // 2
-    for there in range(in_ref.shape[1]):
+    shard_count = in_ref.shape[1]
+    for there in range(shard_count):
+        step = lax.rem(own_shard[0] + shard_count - there, shard_count)
         for side, ref in enumerate((gate_ref, up_ref)):
-            part = in_ref[0, there, :, side * width : side * width + columns]
+            part = in_ref[0, step, :, side * width : side * width + columns]
             ref[0, :, there * columns : (there + 1) * columns] = part.astype(jnp.float32)
 
 
-def unpack(rows, columns):
+def unpack(own_shard, rows, columns):
     ctx_size, shard_count, cut, _ = rows.shape
     out = jax.ShapeDtypeStruct((ctx_size, cut, shard_count * columns), jnp.float32)
     return pl.pallas_call(
         functools.partial(unpack_kernel, columns),
-        grid=(ctx_size,),
-        in_specs=[pl.BlockSpec((1,) + rows.shape[1:], lambda c: (c, 0, 0, 0))],
-        out_specs=[pl.BlockSpec((1, cut, shard_count * columns), lambda c: (c, 0, 0))] * 2,
+        grid_spec=pltpu.PrefetchScalarGridSpec(
+            num_scalar_prefetch=1,
+            grid=(ctx_size,),
+            in_specs=[pl.BlockSpec((1,) + rows.shape[1:], lambda c, _: (c, 0, 0, 0))],
+            out_specs=[pl.BlockSpec((1, cut, shard_count * columns), lambda c, _: (c, 0, 0))] * 2,
+        ),
         out_shape=[out, out],
         name="unpack",
-    )(rows)
+    )(own_shard, rows)
 
 
 def shards(
@@ -1232,13 +1214,12 @@
 
     down_padded = jnp.pad(w_down, ((0, width - columns), (0, 0)))
 
-    late_grad_out, w_qkv_all = lax.optimization_barrier((grad_out, w_qkv_all))
-    cotangent_all = lax.all_gather(late_grad_out, "fsdp", axis=0, tiled=True)
+    late_w_o, w_qkv_all = lax.optimization_barrier((w_o, w_qkv_all))
+    w_o_all = lax.all_gather(late_w_o, "fsdp", axis=0, tiled=True)
     normed_one, queries, own_kv = project(
         tokens, gain_one, w_qkv_all, bias_all, cosine, signed_sine, rows_here
     )
-    all_kv, w_o_all = gather([own_kv, own_cut(w_o)], [by_tokens, by_rows], 2)
-    w_o_all = w_o_all.reshape(D, D)
+    (all_kv,) = gather([own_kv], [by_tokens], 2)
     gate_up_cut, all_kv = lax.optimization_barrier((gate_up_cut, all_kv))
     gate_up_cols = lax.all_gather(
         gate_up_cut.reshape(shard_count * cut, 2 * width), "ctx", axis=0, tiled=True
@@ -1255,8 +1236,11 @@
     unit_two, scale_two, normed = normalize(middle, gain_two)
     normed_two = mix_features(normed.astype(jnp.bfloat16))
 
-    (tokens_all,) = gather([normed_two], [lambda ctx, shard: shard], 6, wide=())
+    tokens_all, cotangent_all = gather(
+        [normed_two, grad_out], [lambda ctx, shard: shard] * 2, 6, wide=()
+    )
     tokens_all = tokens_all.reshape(-1, D)
+    cotangent_all = cotangent_all.reshape(-1, D)
     gate_up_part = jnp.dot(tokens_all, gate_up_cols, preferred_element_type=jnp.float32)
     gate_part, up_part = gate_up_part[:, :width], gate_up_part[:, width:]
     sigmoid_gate = jax.nn.sigmoid(gate_part)
@@ -1294,10 +1278,17 @@
     grad_attended = lax.dot_general(
         grad_branch_one, w_o_all, CONTRACT_LAST, preferred_element_type=jnp.float32
     ).astype(jnp.bfloat16)
-    gate_up_rows, grad_attended = lax.optimization_barrier((gate_up_rows, grad_attended))
-    gate_up_rows = exchange(gate_up_rows.reshape(shard_count, cut, 2 * width), 5)
-    gate_up_rows, grad_attended = lax.optimization_barrier((gate_up_rows, grad_attended))
-    gate_up_rows = lax.all_gather(gate_up_rows, "ctx", axis=0, tiled=False)
+    own_rows = gate_up_rows.reshape(shard_count, cut, 2 * width)
+    swapped = [lax.dynamic_index_in_dim(own_rows, own_shard, 0, False)]
+    for step in range(1, shard_count):
+        there = lax.rem(own_shard + step, shard_count)
+        swapped.append(
+            lax.ppermute(
+                lax.dynamic_index_in_dim(own_rows, there, 0, False),
+                "fsdp",
+                [(shard, (shard + step) % shard_count) for shard in range(shard_count)],
+            )
+        )
     o_terms = lax.dot_general(
         attended_low, grad_branch_one, CONTRACT_FIRST, preferred_element_type=jnp.float32
     ).astype(jnp.bfloat16)
@@ -1318,7 +1309,8 @@
         3,
         out_dtype=jnp.float32,
     )
-    mixed_terms, grad_kv = lax.optimization_barrier((mixed_terms, grad_kv))
+    *swapped, mixed_terms, grad_kv = lax.optimization_barrier((*swapped, mixed_terms, grad_kv))
+    gate_up_rows = lax.all_gather(jnp.stack(swapped), "ctx", axis=0, tiled=False)
     mixed_rows = lax.psum_scatter(mixed_terms, "fsdp", scatter_dimension=0, tiled=True)
     grad_projected, grad_input, grad_gain_one, grad_bias = unproject(
         grad_queries,
@@ -1361,7 +1353,7 @@
     bias_start = 2 * gain_width
     value_start = bias_start + QK // shard_count
 
-    gate_rows, up_rows = unpack(gate_up_rows, columns)
+    gate_rows, up_rows = unpack(own_shard.reshape(1).astype(jnp.int32), gate_up_rows, columns)
     return (
         output,
         grad_input,

time: 693 us -> 675 us (0.974)
  waiting for transfers between devices: 47 us -> 13.3 us
  starting transfers between devices: 0.92 us -> 22.5 us
  Pallas kernels: 476 us -> 465 us
  local copies, waits for them, and re-layouts: 36.4 us -> 45 us
    pallas_call x3, Pallas kernels: 168 us -> 210 us  [gather(): pl.pallas_call(functools.partial(gather_kernel, arity, ctx_size, pair_cou...]
    pallas_call x2 -> x1, Pallas kernels: 50.9 us -> 8.8 us  [unpack(): pl.pallas_call(functools.partial(unpack_kernel, columns), grid_spec=pltpu...]
    all_gather x2, waiting for transfers between devices: 41 us -> 12.6 us  [the longest x1 12.6 us: shards(): lax.all_gather(jnp.stack(swapped), 'ctx', axis=0, tiled=False)]
    ppermute x0 -> x7, starting transfers between devices: none -> 21.7 us  [shards(): lax.ppermute(lax.dynamic_index_in_dim(own_rows, there, 0, False), 'fsdp',...]
    pallas_call x2, Pallas kernels: 163 us -> 151 us  [scatter(): pl.pallas_call(functools.partial(scatter_kernel, arity, ctx_size, pair_co...]
    unnamed x79 -> x102, local copies, waits for them, and re-layouts: 14.8 us -> 22.3 us
  transfers between devices with their start and end apart: 6 -> 13, of which waited for: 3 -> 2; matrix products, arithmetic and copies ran while one was open for 14% -> 14% of each run, Pallas kernels for 49% -> 59%
where the time goes in v12:
time: 675 us; the launch traced here: 669 us
  Pallas kernels  465 us (69%)
  matrix products  89.1 us (13%)
  local copies, waits for them, and re-layouts  45 us (7%)
  starting transfers between devices  22.5 us (3%)
  other arithmetic  18.4 us (3%)
  between operations  15 us (2%)
  waiting for transfers between devices  13.3 us (2%)
    pallas_call x3, Pallas kernels, gather(): pl.pallas_call(functools.partial(gather_kernel, arity, ctx_size, pair_cou...  210 us
    pallas_call x2, Pallas kernels, scatter(): pl.pallas_call(functools.partial(scatter_kernel, arity, ctx_size, pair_co...  151 us
    pallas_call x1, Pallas kernels, line_sum(): pl.pallas_call(functools.partial(line_sum_kernel, pair_count), in_specs=[...  41.8 us
    unnamed x102, local copies, waits for them, and re-layouts  22.3 us
    pallas_call x1, Pallas kernels, attend_backward(): pl.pallas_call(kernel, grid_spec=pltpu.PrefetchScalarGridSpec(num_scalar_...  22.2 us
    ppermute x7, starting transfers between devices, shards(): lax.ppermute(lax.dynamic_index_in_dim(own_rows, there, 0, False), 'fsdp',...  21.7 us
    pallas_call x1, Pallas kernels, attend_forward(): pl.pallas_call(kernel, grid_spec=pltpu.PrefetchScalarGridSpec(num_scalar_...  19.2 us
    dot_general x1, matrix products, shards(): jnp.dot(tokens_all, gate_up_cols, preferred_element_type=jnp.float32)  15.4 us
  transfers between devices with their start and end apart: 13, of which 2 were waited for; matrix products, arithmetic and copies ran while one was open for 14% of the time, Pallas kernels for 59%

profile of v12, /device:TPU:0, one launch (start us, length us, event | category | flops | bytes accessed | tf_op | source)
XLA Modules:
  0.0 668.6 jit_solution(6123437431788109382)
XLA Ops:
  15.3 58.7 %shard_map.194 = (bf16[32,48,2048]{2,1,0:T(8,128)(2,1)}, bf16[32,16,128]{2,1,0:T(8,128)(2,1)}, bf16[8,48,2304]{2,1,0:T(8,128)(2,1)}) custom-call(bf16[48,2048]{1,0:T(8,128)(2,1)} %constant_dynamic-slice_fusion.4.refs_0_, bf16[16,128]{1,0:T(8,128)(2,1)} %bitcast.145, bf16[8,48,2304]{2,1,0:T(8,128)(2,1)} %pack.1.refs_2_), custom_call_target="tpu_custom_call" | custom-call | bytes 25690112 | tf_op jit(solution)/shard_map/pallas_call | solution.py:590
  79.2 5.0 project.1
  86.5 77.6 %shard_map.195 = bf16[32,40,2048]{2,1,0:T(8,128)(2,1)} custom-call(bf16[40,2048]{1,0:T(8,128)(2,1)} %copy-done.18), custom_call_target="tpu_custom_call" | custom-call | bytes 20971520 | tf_op jit(solution)/shard_map/pallas_call | solution.py:590
  165.1 19.2 %attend_forward.1 = (f32[2,2,2,240,128]{4,3,2,1,0:T(8,128)}, f32[2,2,2,1,240]{4,3,2,1,0:T(1,128)}) custom-call(s32[18]{0:T(128)} %pad_add_fusion.scalars, bf16[2,2,2,240,128]{4,3,2,1,0:T(8,128)(2,1)} %copy-done.6, bf16[1280,2048]{1,0:T(8,128)(2,1)} %bitcast.120), custom_call_target="tpu_custom_call" | custom-call | tf_op jit(solution)/shard_map/attend_forward/pallas_call | solution.py:167
  192.4 74.2 %shard_map.196 = (bf16[8,160,1536]{2,1,0:T(8,128)(2,1)}, bf16[8,160,1536]{2,1,0:T(8,128)(2,1)}) custom-call(bf16[160,1536]{1,0:T(8,128)(2,1)} %copy.54.refs_0_, bf16[160,1536]{1,0:T(8,128)(2,1)} %bitcast.128), custom_call_target="tpu_custom_call" | custom-call | bytes 125829120 | tf_op jit(solution)/shard_map/pallas_call | solution.py:590
  266.7 15.4 %fusion.16 = f32[1280,2304]{0,1:T(8,128)} fusion(bf16[1280,1536]{1,0:T(8,128)(2,1)} %bitcast.152, bf16[1536,2304]{1,0:T(8,128)(2,1)} %all-gather.7.cloned.1.call-done), kind=kOutput, calls=%fused_computation.82 | convolution fusion | flops 9059696640 | bytes 22806528 | tf_op jit(solution)/shard_map/dot_general | solution.py:1244
  282.1 11.8 %multiply_convert_fusion.2 = (bf16[1280,1152]{0,1:T(8,128)(2,1)}, bf16[1280,1152]{0,1:T(8,128)(2,1)S(1)}, bf16[1280,1152]{0,1:T(8,128)(2,1)}) fusion(f32[1280,2304]{0,1:T(8,128)} %fusion.16, bf16[1280,1536]{1,0:T(8,128)(2,1)S(1)} %bitcast.151, bf16[1120,1536]{1,0:T(8,128)(2,1)S(1)} %copy-done.44), kind=kOutput, calls=%fused_computation.9 | convolution fusion | flops 4551966720 | bytes 28016640 | tf_op jit(solution)/shard_map/dot_general | solution.py:1249
  295.5 13.0 %convolution_convert_fusion = bf16[1536,2304]{1,0:T(8,128)(2,1)} fusion(bf16[1280,1536]{1,0:T(8,128)(2,1)S(1)} %bitcast.153, bf16[1280,1152]{0,1:T(8,128)(2,1)S(1)} %get-tuple-element.96, bf16[1280,1152]{0,1:T(8,128)(2,1)} %get-tuple-element.95), kind=kOutput, calls=%fused_computation | convolution fusion | flops 9075032064 | bytes 16908288 | tf_op jit(solution)/shard_map/dot_general | solution.py:1254
  311.7 13.1 %convolution_convert_fusion.5 = bf16[1280,1536]{1,0:T(8,128)(2,1)} fusion(bf16[1280,2304]{0,1:T(8,128)(2,1)S(1)} %pad_maximum_fusion, bf16[1536,2304]{1,0:T(8,128)(2,1)} %all-gather.7.cloned.1.call-done), kind=kOutput, calls=%fused_computation.5 | convolution fusion | flops 9061662720 | bytes 16908288 | tf_op jit(solution)/shard_map/dot_general | solution.py:1261
  324.8 41.8 %shard_map.197 = f32[160,1536]{1,0:T(8,128)} custom-call(bf16[8,160,1536]{2,1,0:T(8,128)(2,1)} %bitcast.129), custom_call_target="tpu_custom_call" | custom-call | bytes 31457280 | tf_op jit(solution)/shard_map/pallas_call | solution.py:945
  366.6 9.5 %convolution_convert_fusion.1 = bf16[1280,1536]{1,0:T(8,128)(2,1)} fusion(bf16[1280,1152]{0,1:T(8,128)(2,1)} %get-tuple-element.67, bf16[1120,1536]{1,0:T(8,128)(2,1)} %param.20), kind=kOutput, calls=%fused_computation.1 | convolution fusion | flops 4531814400 | bytes 10321920 | tf_op jit(solution)/shard_map/dot_general | solution.py:1270
  376.0 9.7 %convolution_convert_fusion.3 = bf16[1152,1536]{1,0:T(8,128)(2,1)} fusion(bf16[1280,1152]{0,1:T(8,128)(2,1)} %get-tuple-element.67, bf16[1280,1536]{1,0:T(8,128)(2,1)} %bitcast.150), kind=kOutput, calls=%fused_computation.3 | convolution fusion | flops 4531617792 | bytes 10420224 | tf_op jit(solution)/shard_map/dot_general | solution.py:1266
  394.1 11.3 %collective-permute-start.1 = (bf16[48,2304]{1,0:T(8,128)(2,1)S(1)}, bf16[48,2304]{1,0:T(8,128)(2,1)S(1)}, u32[]{:S(2)}, u32[]{:S(2)}) collective-permute-start(bf16[48,2304]{1,0:T(8,128)(2,1)S(1)} %get-tuple-element.103), channel_id=1, source_target_pairs={{0,2},{1,3},{2,4},{3,5},{4,6},{5,7},{6,0},{7,1},{8,10},{9,11},{10,... | collective-permute-start | bytes 663560 | tf_op jit(solution)/shard_map/ppermute | solution.py:1286
  406.0 3.6 collective-permute-start.3
  412.8 4.6 collective-permute-start.6
  417.4 4.0 convolution_convert_fusion.6
  422.9 22.2 %attend_backward.1 = (f32[2,2,2,240,128]{4,3,2,1,0:T(8,128)}, bf16[1280,2048]{1,0:T(8,128)(2,1)}) custom-call(s32[18]{0:T(128)} %pad_add_fusion.scalars, bf16[2,2,2,240,128]{4,3,2,1,0:T(8,128)(2,1)} %copy-done.6, bf16[2,2,2,240,128]{4,3,2,1,0:T(8,128)(2,1)} %bitcast.134, f32[2,2,2,240,128]{4,3,2,1,0:T(8,128)} %get-tuple-element.59.att_ref, ...), custom_call_target="tpu_custom_call" | custom-call | tf_op jit(solution)/shard_map/attend_backward/pallas_call | solution.py:275
  445.1 42.9 %shard_map.198.gkv_ref = f32[40,2048]{1,0:T(8,128)} custom-call(bf16[32,40,2048]{2,1,0:T(8,128)(2,1)} %bitcast.127), custom_call_target="tpu_custom_call" | custom-call | bytes 83886080 | tf_op jit(solution)/shard_map/pallas_call | solution.py:897
  497.1 3.6 convolution_convert_fusion.4
  500.7 6.0 slice_convert_fusion
  515.9 5.6 convolution_convert_fusion.2
  521.5 108.5 %shard_map.199 = (bf16[4,48,2048]{2,1,0:T(8,128)(2,1)}, bf16[4,48,1536]{2,1,0:T(8,128)(2,1)}, f32[4,8,128]{2,1,0:T(8,128)}) custom-call(bf16[32,48,2048]{2,1,0:T(8,128)(2,1)} %bitcast.122, bf16[32,48,1536]{2,1,0:T(8,128)(2,1)} %bitcast.123, f32[32,8,128]{2,1,0:T(8,128)} %bitcast.140), custom_call_target="tpu_custom_call" | custom-call | bytes 178257920 | tf_op jit(solution)/shard_map/pallas_call | solution.py:897
  640.1 12.6 %all-gather.9.cloned.1.call-done = bf16[32,48,2304]{2,1,0:T(8,128)(2,1)} async-done(((bf16[8,48,2304]{2,1,0:T(8,128)(2,1)}), bf16[32,48,2304]{2,1,0:T(8,128)(2,1)}) %all-gather.9.cloned.1.call-update) | async-done | bytes 7077904 | tf_op jit(solution)/shard_map/all_gather | solution.py:1313
  652.8 8.8 %unpack.1 = (f32[4,48,8960]{2,1,0:T(8,128)}, f32[4,48,8960]{2,1,0:T(8,128)}) custom-call(s32[1]{0:T(128)} %bitcast.3.own_shard, bf16[4,8,48,2304]{3,2,1,0:T(8,128)(2,1)} %bitcast.124), custom_call_target="tpu_custom_call" | custom-call | tf_op jit(solution)/shard_map/unpack/pallas_call | solution.py:1138
  (199 shorter events, 71.1 us)
Async XLA Ops:
  7.2 179.9 %all-gather.5.cloned.1.call-start = ((), (), s32[]{:S(2)}) async-start(), calls=%async_computation.2 | async-start | bytes 5308416 | tf_op jit(solution)/shard_map/all_gather | solution.py:1218
  9.5 64.6 %copy-start.32 = (bf16[40,4,1536]{2,1,0:T(4,128)(2,1)S(1)}, bf16[40,4,1536]{2,1,0:T(4,128)(2,1)}, u32[]{:S(2)}) copy-start(bf16[40,4,1536]{2,1,0:T(4,128)(2,1)} %param.11) | copy-start | bytes 1474564
  12.3 63.4 %copy-start.41 = (s32[2,8]{1,0:T(2,128)S(1)}, s32[2,8]{1,0:T(2,128)}, u32[]{:S(2)}) copy-start(s32[2,8]{1,0:T(2,128)} %param.12) | copy-start | bytes 196
  74.1 192.6 %all-gather.7.cloned.1.call-start = ((), (), s32[]{:S(2)}) async-start(), calls=%async_computation.3 | async-start | bytes 8847360 | tf_op jit(solution)/shard_map/all_gather | solution.py:1224
  74.2 112.9 %copy-start.4 = (bf16[4,40,1536]{2,1,0:T(8,128)(2,1)}, bf16[4,40,1536]{2,1,0:T(8,128)(2,1)S(1)}, u32[]{:S(2)}) copy-start(bf16[4,40,1536]{2,1,0:T(8,128)(2,1)S(1)} %copy.48) | copy-start | bytes 1474564
  75.6 88.6 %copy-start.19 = (f32[1,1536]{1,0:T(1,128)}, f32[1,1536]{1,0:T(1,128)S(1)}, u32[]{:S(2)}) copy-start(f32[1,1536]{1,0:T(1,128)S(1)} %reshape_reshape.7.gain_ref) | copy-start | bytes 18436
  164.2 227.3 %reduce-scatter.3.cloned.1.call-start = ((), (), s32[]{:S(2)}) async-start(), calls=%async_computation.4 | async-start | bytes 8847360 | tf_op jit(solution)/shard_map/reduce_scatter | solution.py:1257
  165.0 21.2 %copy-start.33 = (bf16[40,4,1536]{2,1,0:T(4,128)(2,1)S(1)}, bf16[40,4,1536]{2,1,0:T(4,128)(2,1)}, u32[]{:S(2)}) copy-start(bf16[40,4,1536]{2,1,0:T(4,128)(2,1)} %param.21) | copy-start | bytes 1474564
  190.5 200.0 %copy-start.21 = (f32[160,1536]{1,0:T(8,128)}, f32[160,1536]{1,0:T(8,128)S(1)}, u32[]{:S(2)}) copy-start(f32[160,1536]{1,0:T(8,128)S(1)} %get-tuple-element.117) | copy-start | bytes 2949124
  266.6 15.4 %copy-start.42 = (bf16[8,160,1536]{2,1,0:T(8,128)(2,1)S(1)}, bf16[8,160,1536]{2,1,0:T(8,128)(2,1)}, u32[]{:S(2)}) copy-start(bf16[8,160,1536]{2,1,0:T(8,128)(2,1)} %get-tuple-element.62) | copy-start | bytes 11796484
  266.6 15.4 %copy-start.44 = (bf16[1120,1536]{1,0:T(8,128)(2,1)S(1)}, bf16[1120,1536]{1,0:T(8,128)(2,1)}, u32[]{:S(2)}) copy-start(bf16[1120,1536]{1,0:T(8,128)(2,1)} %param.20) | copy-start | bytes 10321924
  308.5 192.2 %all-reduce.5.cloned.1.call-start = ((), (), s32[]{:S(2)}) async-start(), calls=%async_computation.6 | async-start | bytes 7077888 | tf_op jit(solution)/shard_map/psum | solution.py:1269
  385.7 252.2 %reduce-scatter.5.cloned.1.call-start = ((), (), s32[]{:S(2)}) async-start(), calls=%async_computation.5 | async-start | bytes 4423680 | tf_op jit(solution)/shard_map/reduce_scatter | solution.py:1314
  388.7 16.8 %copy-start.26 = (bf16[4,40,1536]{2,1,0:T(8,128)(2,1)S(1)}, bf16[4,40,1536]{2,1,0:T(8,128)(2,1)}, u32[]{:S(2)}) copy-start(bf16[4,40,1536]{2,1,0:T(8,128)(2,1)} %copy.53) | copy-start | bytes 1474564
  394.1 16.0 %collective-permute-start = (bf16[48,2304]{1,0:T(8,128)(2,1)S(1)}, bf16[48,2304]{1,0:T(8,128)(2,1)S(1)}, u32[]{:S(2)}, u32[]{:S(2)}) collective-permute-start(bf16[48,2304]{1,0:T(8,128)(2,1)S(1)} %get-tuple-element.104), channel_id=1, source_target_pairs={{0,1},{1,2},{2,3},{3,4},{4,5},{5,6},{6,7},{7,0},{8,9},{9,10},{10,1... | collective-permute-start | bytes 663560 | tf_op jit(solution)/shard_map/ppermute | solution.py:1286
  394.1 18.0 %collective-permute-start.1 = (bf16[48,2304]{1,0:T(8,128)(2,1)S(1)}, bf16[48,2304]{1,0:T(8,128)(2,1)S(1)}, u32[]{:S(2)}, u32[]{:S(2)}) collective-permute-start(bf16[48,2304]{1,0:T(8,128)(2,1)S(1)} %get-tuple-element.103), channel_id=1, source_target_pairs={{0,2},{1,3},{2,4},{3,5},{4,6},{5,7},{6,0},{7,1},{8,10},{9,11},{10,... | collective-permute-start | bytes 663560 | tf_op jit(solution)/shard_map/ppermute | solution.py:1286
  405.7 82.4 %collective-permute-start.2 = (bf16[48,2304]{1,0:T(8,128)(2,1)}, bf16[48,2304]{1,0:T(8,128)(2,1)}, u32[]{:S(2)}, u32[]{:S(2)}) collective-permute-start(bf16[48,2304]{1,0:T(8,128)(2,1)} %get-tuple-element.102), channel_id=1, source_target_pairs={{0,3},{1,4},{2,5},{3,6},{4,7},{5,0},{6,1},{7,2},{8,11},{9,12},{10,... | collective-permute-start | bytes 663560 | tf_op jit(solution)/shard_map/ppermute | solution.py:1286
  406.0 82.1 %collective-permute-start.3 = (bf16[48,2304]{1,0:T(8,128)(2,1)}, bf16[48,2304]{1,0:T(8,128)(2,1)}, u32[]{:S(2)}, u32[]{:S(2)}) collective-permute-start(bf16[48,2304]{1,0:T(8,128)(2,1)} %get-tuple-element.101), channel_id=1, source_target_pairs={{0,4},{1,5},{2,6},{3,7},{4,0},{5,1},{6,2},{7,3},{8,12},{9,13},{10,... | collective-permute-start | bytes 663560 | tf_op jit(solution)/shard_map/ppermute | solution.py:1286
  409.6 78.5 %collective-permute-start.4 = (bf16[48,2304]{1,0:T(8,128)(2,1)}, bf16[48,2304]{1,0:T(8,128)(2,1)}, u32[]{:S(2)}, u32[]{:S(2)}) collective-permute-start(bf16[48,2304]{1,0:T(8,128)(2,1)} %get-tuple-element.100), channel_id=1, source_target_pairs={{0,5},{1,6},{2,7},{3,0},{4,1},{5,2},{6,3},{7,4},{8,13},{9,14},{10,... | collective-permute-start | bytes 663560 | tf_op jit(solution)/shard_map/ppermute | solution.py:1286
  410.1 78.0 %collective-permute-start.5 = (bf16[48,2304]{1,0:T(8,128)(2,1)}, bf16[48,2304]{1,0:T(8,128)(2,1)}, u32[]{:S(2)}, u32[]{:S(2)}) collective-permute-start(bf16[48,2304]{1,0:T(8,128)(2,1)} %get-tuple-element.99), channel_id=1, source_target_pairs={{0,6},{1,7},{2,0},{3,1},{4,2},{5,3},{6,4},{7,5},{8,14},{9,15},{10,... | collective-permute-start | bytes 663560 | tf_op jit(solution)/shard_map/ppermute | solution.py:1286
  412.8 75.3 %collective-permute-start.6 = (bf16[48,2304]{1,0:T(8,128)(2,1)}, bf16[48,2304]{1,0:T(8,128)(2,1)}, u32[]{:S(2)}, u32[]{:S(2)}) collective-permute-start(bf16[48,2304]{1,0:T(8,128)(2,1)} %get-tuple-element.98), channel_id=1, source_target_pairs={{0,7},{1,0},{2,1},{3,2},{4,3},{5,4},{6,5},{7,6},{8,15},{9,8},{10,9... | collective-permute-start | bytes 663560 | tf_op jit(solution)/shard_map/ppermute | solution.py:1286
  488.2 164.6 %all-gather.9.cloned.1.call-start = ((), (), s32[]{:S(2)}) async-start(), calls=%async_computation.7 | async-start | bytes 8847360 | tf_op jit(solution)/shard_map/all_gather | solution.py:1313
  521.5 110.6 %copy-start.12 = (f32[160,1536]{1,0:T(8,128)S(1)}, f32[160,1536]{1,0:T(8,128)}, u32[]{:S(2)}) copy-start(f32[160,1536]{1,0:T(8,128)} %copy-done.11) | copy-start | bytes 2949124
  639.1 22.5 %copy-start.1 = (bf16[192,2048]{1,0:T(8,128)(2,1)S(1)}, bf16[192,2048]{1,0:T(8,128)(2,1)}, u32[]{:S(2)}) copy-start(bf16[192,2048]{1,0:T(8,128)(2,1)} %param.14) | copy-start | bytes 2359300
  (34 other events, 154.2 us)
Sparse Core Ops, SparseCore 0:
  74.2 75.2 all-gather.4
  164.3 75.1 all-gather.6
  308.6 72.6 reduce-scatter.2
  385.8 112.9 all-reduce.4
  501.0 46.4 reduce-scatter.4
  549.2 103.5 all-gather.8

commit v13 on v11

--- a/solution.py
+++ b/solution.py
@@ -952,34 +952,112 @@
     )(*terms, *lines)
 
 
-def line_sum_kernel(pair_count, source, out, half, room, *sems):
-    where = greet(1, pair_count, False, False)
-    flow = LineScatter(source, out, half, room, sems, where, (pair_count, 1), ())
-    flow.start()
-    for step in flow.order:
-        flow.fold(step)
-    flow.finish()
-
-
-def line_sum(terms, collective_id):
-    pair_count = lax.axis_size("fsdp") // 2
-    extent = terms.shape[1:]
-    dma = pltpu.SemaphoreType.DMA((pair_count,))
+class CtxScatter:
+    def __init__(self, source, out, relay, sums, asides, sems, where, ctx_size):
+        self.source, self.out, self.relay, self.sums, self.asides = source, out, relay, sums, asides
+        self.relay_sems, self.aside_sems = sems[0:2], sems[2:4]
+        self.ctx, self.pair, self.core = where
+        self.ctx_size = ctx_size
+        self.square, ways = peers_of(ctx_size)
+        self.near = [way for way in ways if not (self.square and way == 3)]
+        self.parts = range(source.shape[1])
+        self.copies = []
+
+    def copy(self, source, target, ctx, sems, at):
+        return pltpu.make_async_remote_copy(
+            src_ref=source,
+            dst_ref=target,
+            send_sem=sems[0].at[at],
+            recv_sem=sems[1].at[at],
+            device_id=(ctx, self.pair * 2 + self.core),
+            device_id_type=MESH_ID,
+        )
+
+    def send(self, *what):
+        self.copies.append(self.copy(*what))
+        self.copies[-1].start()
+
+    def arrive(self, target, sems, at):
+        self.copy(target, target, self.ctx, sems, at).wait_recv()
+
+    def start(self):
+        for part in self.parts if self.square else ():
+            there = self.ctx ^ (1 if part % 2 == 0 else 2)
+            self.send(
+                self.source.at[self.ctx ^ 3, part], self.relay.at[part], there, self.relay_sems, part
+            )
+
+    def advance(self, part):
+        for way in self.near:
+            there = ctx_target(self.ctx, way, self.square, self.ctx_size)
+            source = self.source.at[there, part]
+            if self.square and (part % 2 == 0) == (way == 2):
+                self.arrive(self.relay.at[part], self.relay_sems, part)
+                total = source[...].astype(jnp.float32) + self.relay[part].astype(jnp.float32)
+                self.sums[part] = total.astype(self.sums.dtype)
+                source = self.sums.at[part]
+            self.send(source, self.asides.at[way - 1, part], there, self.aside_sems, (way - 1, part))
+
+    def close(self, part):
+        total = self.source[self.ctx, part].astype(jnp.float32)
+        for way in self.near:
+            aside = self.asides.at[way - 1, part]
+            self.arrive(aside, self.aside_sems, (way - 1, part))
+            total = total + aside[...].astype(jnp.float32)
+        self.out[part] = total.astype(self.out.dtype)
+
+    def finish(self):
+        for copy in self.copies:
+            copy.wait_send()
+
+
+def sum_tokens_kernel(pair_count, ctx_size, tokens, rows, tokens_out, rows_out, half, room, relay, sums, asides, *sems):
+    where = greet(ctx_size, pair_count, True, False)
+    line = LineScatter(tokens, tokens_out, half, room, sems[:4], where, (pair_count, 1), ())
+    square = CtxScatter(rows, rows_out, relay, sums, asides, sems[4:], where, ctx_size)
+    line.start()
+    square.start()
+    for step in line.order:
+        line.fold(step)
+    late = 2
+    for part in range(rows.shape[1] + late):
+        if part < rows.shape[1]:
+            square.advance(part)
+        if part >= late:
+            square.close(part - late)
+    line.finish()
+    square.finish()
+
+
+def sum_tokens(tokens, rows, collective_id):
+    ctx_size, pair_count = lax.axis_size("ctx"), lax.axis_size("fsdp") // 2
+    vmem = pl.BlockSpec(memory_space=pltpu.VMEM)
+    extent, piece, parts = tokens.shape[1:], rows.shape[2:], rows.shape[1]
+    asides = 2 if ctx_size == 4 else ctx_size - 1
+    dma = pltpu.SemaphoreType.DMA
     return pl.pallas_call(
-        functools.partial(line_sum_kernel, pair_count),
-        in_specs=[pl.BlockSpec(memory_space=pltpu.VMEM)],
-        out_specs=pl.BlockSpec(memory_space=pltpu.VMEM),
-        out_shape=jax.ShapeDtypeStruct(extent, jnp.float32),
+        functools.partial(sum_tokens_kernel, pair_count, ctx_size),
+        in_specs=[vmem, vmem],
+        out_specs=[vmem, vmem],
+        out_shape=[
+            jax.ShapeDtypeStruct(extent, jnp.float32),
+            jax.ShapeDtypeStruct((parts,) + piece, rows.dtype),
+        ],
         scratch_shapes=[
-            pltpu.VMEM((pair_count,) + extent, terms.dtype),
-            pltpu.VMEM((pair_count - 1,) + extent, terms.dtype),
+            pltpu.VMEM((pair_count,) + extent, tokens.dtype),
+            pltpu.VMEM((pair_count - 1,) + extent, tokens.dtype),
+            pltpu.VMEM((parts,) + piece, rows.dtype),
+            pltpu.VMEM((parts,) + piece, rows.dtype),
+            pltpu.VMEM((asides, parts) + piece, rows.dtype),
         ]
-        + [dma] * 4,
+        + [dma((pair_count,))] * 4
+        + [dma((parts,))] * 2
+        + [dma((asides, parts))] * 2,
         compiler_params=pltpu.CompilerParams(
             collective_id=collective_id, has_side_effects=True, vmem_limit_bytes=63 * 2**20
         ),
-        cost_estimate=pl.CostEstimate(flops=0, bytes_accessed=terms.size * 16, transcendentals=0),
-    )(terms)
+        cost_estimate=pl.CostEstimate(flops=0, bytes_accessed=tokens.size * 32, transcendentals=0),
+    )(tokens, rows)
 
 
 def turned(values, cosine, signed_sine):
@@ -1267,26 +1345,27 @@
     )
     grad_gate = grad_hidden * up_part * sigmoid_gate * (1.0 + gate_part * (1.0 - sigmoid_gate))
     grad_gate_up = jnp.concatenate([grad_gate, grad_hidden * activated], -1).astype(jnp.bfloat16)
-    gate_up_terms = lax.dot_general(
-        tokens_all, grad_gate_up, CONTRACT_FIRST, preferred_element_type=jnp.float32
-    ).astype(jnp.bfloat16)
-    gate_up_rows = lax.psum_scatter(gate_up_terms, "ctx", scatter_dimension=0, tiled=True)
-    grad_gate_up, hidden, gate_up_terms = lax.optimization_barrier(
-        (grad_gate_up, hidden, gate_up_terms)
-    )
-    grad_tokens = lax.dot_general(
-        grad_gate_up, gate_up_cols, CONTRACT_LAST, preferred_element_type=jnp.float32
-    ).astype(jnp.bfloat16)
-    grad_normed_two = line_sum(grad_tokens.reshape(shard_count, -1, D), 7)
-    grad_normed_two, hidden = lax.optimization_barrier((grad_normed_two, hidden))
     down_terms = lax.dot_general(
         hidden, cotangent_all, CONTRACT_FIRST, preferred_element_type=jnp.float32
     ).astype(jnp.bfloat16)
     down_rows = lax.psum(down_terms, "ctx")
+    grad_gate_up, hidden, down_terms = lax.optimization_barrier(
+        (grad_gate_up, hidden, down_terms)
+    )
+    gate_up_terms = lax.dot_general(
+        tokens_all, grad_gate_up, CONTRACT_FIRST, preferred_element_type=jnp.float32
+    ).astype(jnp.bfloat16)
+    grad_tokens = lax.dot_general(
+        grad_gate_up, gate_up_cols, CONTRACT_LAST, preferred_element_type=jnp.float32
+    ).astype(jnp.bfloat16)
+    grad_normed_two, gate_up_rows = sum_tokens(
+        grad_tokens.reshape(shard_count, -1, D),
+        gate_up_terms.reshape(ctx_size, shard_count, cut, 2 * width),
+        7,
+    )
+    grad_normed_two, hidden = lax.optimization_barrier((grad_normed_two, hidden))
     mixed_terms = jnp.dot(hidden, down_padded, preferred_element_type=jnp.float32).astype(jnp.bfloat16)
-    grad_normed_two, down_terms, mixed_terms = lax.optimization_barrier(
-        (grad_normed_two, down_terms, mixed_terms)
-    )
+    grad_normed_two, mixed_terms = lax.optimization_barrier((grad_normed_two, mixed_terms))
     grad_normed_two = unmix_features(grad_normed_two)
     grad_middle_norm, grad_gain_two = norm_back(grad_normed_two, unit_two, scale_two, gain_two)
     grad_middle = grad_out.astype(jnp.float32) + grad_middle_norm
@@ -1295,7 +1374,7 @@
         grad_branch_one, w_o_all, CONTRACT_LAST, preferred_element_type=jnp.float32
     ).astype(jnp.bfloat16)
     gate_up_rows, grad_attended = lax.optimization_barrier((gate_up_rows, grad_attended))
-    gate_up_rows = exchange(gate_up_rows.reshape(shard_count, cut, 2 * width), 5)
+    gate_up_rows = exchange(gate_up_rows, 5)
     gate_up_rows, grad_attended = lax.optimization_barrier((gate_up_rows, grad_attended))
     gate_up_rows = lax.all_gather(gate_up_rows, "ctx", axis=0, tiled=False)
     o_terms = lax.dot_general(

time: 693 us -> 723 us (1.043)
  Pallas kernels: 476 us -> 503 us
  waiting for transfers between devices: 47 us -> 54.4 us
    pallas_call x1, Pallas kernels: 41.8 us -> 103 us  [sum_tokens(): pl.pallas_call(functools.partial(sum_tokens_kernel, pair_count, ctx_size)...]
    pallas_call x2, Pallas kernels: 163 us -> 136 us  [scatter(): pl.pallas_call(functools.partial(scatter_kernel, arity, ctx_size, pair_co...]
    pallas_call x1, Pallas kernels: 42.1 us -> 33.9 us  [exchange(): pl.pallas_call(functools.partial(exchange_kernel, shard_count // 2), in_s...]
    unnamed x79 -> x81, local copies, waits for them, and re-layouts: 14.8 us -> 14.2 us
  transfers between devices with their start and end apart: 6 -> 5, of which waited for: 3 -> 3; matrix products, arithmetic and copies ran while one was open for 14% -> 14% of each run, Pallas kernels for 49% -> 50%
where the time goes in v13:
time: 723 us; the launch traced here: 716 us
  Pallas kernels  503 us (70%)
  matrix products  86.9 us (12%)
  waiting for transfers between devices  54.4 us (8%)
  local copies, waits for them, and re-layouts  35.8 us (5%)
  other arithmetic  20.8 us (3%)
  between operations  14.5 us (2%)
    pallas_call x3, Pallas kernels, gather(): pl.pallas_call(functools.partial(gather_kernel, arity, ctx_size, pair_cou...  168 us
    pallas_call x2, Pallas kernels, scatter(): pl.pallas_call(functools.partial(scatter_kernel, arity, ctx_size, pair_co...  136 us
    pallas_call x1, Pallas kernels, sum_tokens(): pl.pallas_call(functools.partial(sum_tokens_kernel, pair_count, ctx_size)...  103 us
    pallas_call x1, Pallas kernels, exchange(): pl.pallas_call(functools.partial(exchange_kernel, shard_count // 2), in_s...  33.9 us
    all_gather x1, waiting for transfers between devices, shards(): cotangent_all = lax.all_gather(late_grad_out, 'fsdp', axis=0, tiled=True)  31.1 us
    pallas_call x1, Pallas kernels, attend_backward(): pl.pallas_call(kernel, grid_spec=pltpu.PrefetchScalarGridSpec(num_scalar_...  22.3 us
    pallas_call x1, Pallas kernels, attend_forward(): pl.pallas_call(kernel, grid_spec=pltpu.PrefetchScalarGridSpec(num_scalar_...  19 us
    all_gather x1, waiting for transfers between devices, shards(): gate_up_rows = lax.all_gather(gate_up_rows, 'ctx', axis=0, tiled=False)  17.1 us
  transfers between devices with their start and end apart: 5, of which 3 were waited for; matrix products, arithmetic and copies ran while one was open for 14% of the time, Pallas kernels for 50%

profile of v13, /device:TPU:0, one launch (start us, length us, event | category | flops | bytes accessed | tf_op | source)
XLA Modules:
  0.0 716.0 jit_solution(5796987053288476782)
XLA Ops:
  15.4 58.7 %shard_map.194 = (bf16[32,48,2048]{2,1,0:T(8,128)(2,1)}, bf16[32,16,128]{2,1,0:T(8,128)(2,1)}, bf16[8,48,2304]{2,1,0:T(8,128)(2,1)}) custom-call(bf16[48,2048]{1,0:T(8,128)(2,1)} %constant_dynamic-slice_fusion.4.refs_0_, bf16[16,128]{1,0:T(8,128)(2,1)} %bitcast.118, bf16[8,48,2304]{2,1,0:T(8,128)(2,1)} %pack.1.refs_2_), custom_call_target="tpu_custom_call" | custom-call | bytes 25690112 | tf_op jit(solution)/shard_map/pallas_call | solution.py:613
  81.5 5.0 project.1
  88.8 66.5 %shard_map.195 = (bf16[32,40,2048]{2,1,0:T(8,128)(2,1)}, bf16[32,48,1536]{2,1,0:T(8,128)(2,1)}) custom-call(bf16[40,2048]{1,0:T(8,128)(2,1)} %copy-done.19, bf16[48,1536]{1,0:T(8,128)(2,1)} %constant_dynamic-slice_fusion.refs_1_), custom_call_target="tpu_custom_call" | custom-call | bytes 39845888 | tf_op jit(solution)/shard_map/pallas_call | solution.py:613
  157.0 19.0 %attend_forward.1 = (f32[2,2,2,240,128]{4,3,2,1,0:T(8,128)}, f32[2,2,2,1,240]{4,3,2,1,0:T(1,128)}) custom-call(s32[18]{0:T(128)} %pad_add_fusion.scalars, bf16[2,2,2,240,128]{4,3,2,1,0:T(8,128)(2,1)} %copy-done.6, bf16[1280,2048]{1,0:T(8,128)(2,1)} %bitcast.91), custom_call_target="tpu_custom_call" | custom-call | tf_op jit(solution)/shard_map/attend_forward/pallas_call | solution.py:167
  183.7 43.1 %shard_map.196 = bf16[8,160,1536]{2,1,0:T(8,128)(2,1)} custom-call(bf16[160,1536]{1,0:T(8,128)(2,1)} %copy.54.refs_0_), custom_call_target="tpu_custom_call" | custom-call | bytes 62914560 | tf_op jit(solution)/shard_map/pallas_call | solution.py:613
  226.8 5.0 all-gather.7.cloned.1.call-done
  231.8 15.3 %fusion.12 = f32[1280,2304]{0,1:T(8,128)} fusion(bf16[1280,1536]{1,0:T(8,128)(2,1)} %bitcast.101, bf16[1536,2304]{1,0:T(8,128)(2,1)} %all-gather.7.cloned.1.call-done), kind=kOutput, calls=%fused_computation.63 | convolution fusion | flops 9059696640 | bytes 22806528 | tf_op jit(solution)/shard_map/dot_general | solution.py:1338
  247.1 31.1 %all-gather.5.cloned.1.call-done = bf16[1280,1536]{1,0:T(8,128)(2,1)} async-done(((bf16[160,1536]{1,0:T(8,128)(2,1)}), bf16[1280,1536]{1,0:T(8,128)(2,1)}) %all-gather.5.cloned.1.call-update) | async-done | bytes 3932176 | tf_op jit(solution)/shard_map/all_gather | solution.py:1314
  278.2 11.5 %multiply_convert_fusion.2 = (bf16[1280,1152]{0,1:T(8,128)(2,1)S(1)}, bf16[1280,1152]{0,1:T(8,128)(2,1)S(1)}, bf16[1280,1152]{0,1:T(8,128)(2,1)S(1)}) fusion(f32[1280,2304]{0,1:T(8,128)} %fusion.12, bf16[1280,1536]{1,0:T(8,128)(2,1)} %all-gather.5.cloned.1.call-done, bf16[1120,1536]{1,0:T(8,128)(2,1)} %param.20), kind=kOutput, calls=%fused_computation.9 | convolution fusion | flops 4551966720 | bytes 28016640 | tf_op jit(solution)/shard_map/dot_general | solution.py:1343
  294.7 6.3 convolution_convert_fusion.3
  301.1 14.8 %convolution_convert_fusion.5 = bf16[1280,1536]{1,0:T(8,128)(2,1)} fusion(bf16[1280,2304]{0,1:T(8,128)(2,1)} %pad_maximum_fusion, bf16[1536,2304]{1,0:T(8,128)(2,1)} %all-gather.7.cloned.1.call-done), kind=kOutput, calls=%fused_computation.5 | convolution fusion | flops 9061662720 | bytes 16908288 | tf_op jit(solution)/shard_map/dot_general | solution.py:1358
  315.9 13.9 %convolution_convert_fusion = bf16[1536,2304]{1,0:T(8,128)(2,1)} fusion(bf16[1280,1536]{1,0:T(8,128)(2,1)S(1)} %bitcast.102, bf16[1280,2304]{0,1:T(8,128)(2,1)} %pad_maximum_fusion), kind=kOutput, calls=%fused_computation | convolution fusion | flops 9063235584 | bytes 16908288 | tf_op jit(solution)/shard_map/dot_general | solution.py:1355
  329.8 103.0 %shard_map.197 = (f32[160,1536]{1,0:T(8,128)}, bf16[8,48,2304]{2,1,0:T(8,128)(2,1)}) custom-call(bf16[8,160,1536]{2,1,0:T(8,128)(2,1)} %bitcast.103, bf16[4,8,48,2304]{3,2,1,0:T(8,128)(2,1)} %bitcast.96), custom_call_target="tpu_custom_call" | custom-call | bytes 62914560 | tf_op jit(solution)/shard_map/pallas_call | solution.py:1038
  432.8 9.4 %convolution_convert_fusion.1 = bf16[1280,1536]{1,0:T(8,128)(2,1)} fusion(bf16[1280,1152]{0,1:T(8,128)(2,1)} %copy-done.37, bf16[1120,1536]{1,0:T(8,128)(2,1)} %param.20), kind=kOutput, calls=%fused_computation.1 | convolution fusion | flops 4531814400 | bytes 10321920 | tf_op jit(solution)/shard_map/dot_general | solution.py:1367
  449.5 4.0 convolution_convert_fusion.6
  453.5 33.9 %shard_map.198 = bf16[8,48,2304]{2,1,0:T(8,128)(2,1)} custom-call(bf16[8,48,2304]{2,1,0:T(8,128)(2,1)} %get-tuple-element.70.source), custom_call_target="tpu_custom_call" | custom-call | bytes 56623104 | tf_op jit(solution)/shard_map/pallas_call | solution.py:380
  488.9 22.3 %attend_backward.1 = (f32[2,2,2,240,128]{4,3,2,1,0:T(8,128)}, bf16[1280,2048]{1,0:T(8,128)(2,1)}) custom-call(s32[18]{0:T(128)} %pad_add_fusion.scalars, bf16[2,2,2,240,128]{4,3,2,1,0:T(8,128)(2,1)} %copy-done.6, bf16[2,2,2,240,128]{4,3,2,1,0:T(8,128)(2,1)} %bitcast.108, f32[2,2,2,240,128]{4,3,2,1,0:T(8,128)} %get-tuple-element.58.att_ref, ...), custom_call_target="tpu_custom_call" | custom-call | tf_op jit(solution)/shard_map/attend_backward/pallas_call | solution.py:275
  511.2 42.2 %shard_map.199.gkv_ref = f32[40,2048]{1,0:T(8,128)} custom-call(bf16[32,40,2048]{2,1,0:T(8,128)(2,1)} %bitcast.99), custom_call_target="tpu_custom_call" | custom-call | bytes 83886080 | tf_op jit(solution)/shard_map/pallas_call | solution.py:920
  564.2 3.6 convolution_convert_fusion.4
  567.9 4.5 convolution_convert_fusion.2
  572.4 94.0 %shard_map.200 = (bf16[4,48,2048]{2,1,0:T(8,128)(2,1)}, bf16[4,48,1536]{2,1,0:T(8,128)(2,1)}, f32[4,8,128]{2,1,0:T(8,128)}) custom-call(bf16[32,48,2048]{2,1,0:T(8,128)(2,1)} %bitcast.89, bf16[32,48,1536]{2,1,0:T(8,128)(2,1)} %bitcast.90, f32[32,8,128]{2,1,0:T(8,128)} %bitcast.113), custom_call_target="tpu_custom_call" | custom-call | bytes 178257920 | tf_op jit(solution)/shard_map/pallas_call | solution.py:920
  675.3 6.0 slice_convert_fusion
  683.4 17.1 %all-gather.9.cloned.1.call-done = bf16[32,48,2304]{2,1,0:T(8,128)(2,1)} async-done(((bf16[8,48,2304]{2,1,0:T(8,128)(2,1)}), bf16[32,48,2304]{2,1,0:T(8,128)(2,1)}) %all-gather.9.cloned.1.call-update) | async-done | bytes 7077904 | tf_op jit(solution)/shard_map/all_gather | solution.py:1379
  700.5 8.8 %unpack.1 = (f32[4,48,8960]{2,1,0:T(8,128)}, f32[4,48,8960]{2,1,0:T(8,128)}) custom-call(bf16[4,8,48,2304]{3,2,1,0:T(8,128)(2,1)} %bitcast.95), custom_call_target="tpu_custom_call" | custom-call | tf_op jit(solution)/shard_map/unpack/pallas_call | solution.py:1237
  (161 shorter events, 62.6 us)
Async XLA Ops:
  7.2 224.6 %all-gather.7.cloned.1.call-start = ((), (), s32[]{:S(2)}) async-start(), calls=%async_computation.2 | async-start | bytes 8847360 | tf_op jit(solution)/shard_map/all_gather | solution.py:1321
  9.5 65.8 %copy-start.35 = (s32[2,8]{1,0:T(2,128)S(1)}, s32[2,8]{1,0:T(2,128)}, u32[]{:S(2)}) copy-start(s32[2,8]{1,0:T(2,128)} %param.12) | copy-start | bytes 196
  9.5 68.0 %copy-start.28 = (bf16[40,4,1536]{2,1,0:T(4,128)(2,1)S(1)}, bf16[40,4,1536]{2,1,0:T(4,128)(2,1)}, u32[]{:S(2)}) copy-start(bf16[40,4,1536]{2,1,0:T(4,128)(2,1)} %param.21) | copy-start | bytes 1474564
  9.5 68.9 %copy-start.29 = (bf16[40,4,1536]{2,1,0:T(4,128)(2,1)S(1)}, bf16[40,4,1536]{2,1,0:T(4,128)(2,1)}, u32[]{:S(2)}) copy-start(bf16[40,4,1536]{2,1,0:T(4,128)(2,1)} %param.11) | copy-start | bytes 1474564
  78.5 99.5 %copy-start.4 = (bf16[4,40,1536]{2,1,0:T(8,128)(2,1)}, bf16[4,40,1536]{2,1,0:T(8,128)(2,1)S(1)}, u32[]{:S(2)}) copy-start(bf16[4,40,1536]{2,1,0:T(8,128)(2,1)S(1)} %copy.48) | copy-start | bytes 1474564
  78.6 76.7 %copy-start.20 = (f32[1,1536]{1,0:T(1,128)}, f32[1,1536]{1,0:T(1,128)S(1)}, u32[]{:S(2)}) copy-start(f32[1,1536]{1,0:T(1,128)S(1)} %reshape_reshape.7.gain_ref) | copy-start | bytes 18436
  78.6 7.9 %copy-start.13 = (f32[4,40,128]{2,1,0:T(8,128)}, f32[4,40,128]{2,1,0:T(8,128)S(1)}, u32[]{:S(2)}) copy-start(f32[4,40,128]{2,1,0:T(8,128)S(1)} %get-tuple-element.95) | copy-start | bytes 245764
  78.6 7.9 %copy-start.15 = (f32[160,128]{1,0:T(8,128)}, f32[160,128]{1,0:T(8,128)S(1)}, u32[]{:S(2)}) copy-start(f32[160,128]{1,0:T(8,128)S(1)} %bitcast_multiply_fusion.sin_ref) | copy-start | bytes 245764
  155.3 122.9 %all-gather.5.cloned.1.call-start = ((), (), s32[]{:S(2)}) async-start(), calls=%async_computation.1 | async-start | bytes 4423680 | tf_op jit(solution)/shard_map/all_gather | solution.py:1314
  156.0 519.2 %all-reduce.5.cloned.1.call-start = ((), (), s32[]{:S(2)}) async-start(), calls=%async_computation.4 | async-start | bytes 7077888 | tf_op jit(solution)/shard_map/psum | solution.py:1351
  156.4 25.2 %copy-start.30 = (f32[1536]{0:T(1024)}, f32[1536]{0:T(1024)S(1)}, u32[]{:S(2)}) copy-start(f32[1536]{0:T(1024)S(1)} %mul.246) | copy-start | bytes 18436
  178.0 4.6 copy-start.24
  181.6 265.5 %copy-start.22 = (f32[160,1536]{1,0:T(8,128)}, f32[160,1536]{1,0:T(8,128)S(1)}, u32[]{:S(2)}) copy-start(f32[160,1536]{1,0:T(8,128)S(1)} %get-tuple-element.105) | copy-start | bytes 2949124
  289.7 5.1 copy-start.36
  301.0 380.2 %reduce-scatter.2.cloned.1.call-start = ((), (), s32[]{:S(2)}) async-start(), calls=%async_computation.3 | async-start | bytes 4423680 | tf_op jit(solution)/shard_map/reduce_scatter | solution.py:1401
  301.1 14.8 %copy-start.27 = (bf16[8,160,1536]{2,1,0:T(8,128)(2,1)S(1)}, bf16[8,160,1536]{2,1,0:T(8,128)(2,1)}, u32[]{:S(2)}) copy-start(bf16[8,160,1536]{2,1,0:T(8,128)(2,1)} %shard_map.196) | copy-start | bytes 11796484
  442.2 4.9 copy-start.31
  442.2 4.9 copy-start.34
  442.2 5.8 copy-start.26
  553.5 147.0 %all-gather.9.cloned.1.call-start = ((), (), s32[]{:S(2)}) async-start(), calls=%async_computation.5 | async-start | bytes 8847360 | tf_op jit(solution)/shard_map/all_gather | solution.py:1379
  557.7 6.6 copy-start.25
  572.4 96.0 %copy-start.11 = (f32[160,1536]{1,0:T(8,128)S(1)}, f32[160,1536]{1,0:T(8,128)}, u32[]{:S(2)}) copy-start(f32[160,1536]{1,0:T(8,128)} %copy-done.10) | copy-start | bytes 2949124
  675.3 6.0 copy-start.23
  675.3 34.0 %copy-start.1 = (bf16[192,2048]{1,0:T(8,128)(2,1)S(1)}, bf16[192,2048]{1,0:T(8,128)(2,1)}, u32[]{:S(2)}) copy-start(bf16[192,2048]{1,0:T(8,128)(2,1)} %param.14) | copy-start | bytes 2359300
  (19 other events, 32.1 us)
Sparse Core Ops, SparseCore 0:
  155.4 76.3 all-gather.6
  233.4 44.6 all-gather.4
  301.1 128.9 all-reduce.4
  553.6 49.8 reduce-scatter.1
  605.3 95.1 all-gather.8

commit v14 on v11

--- a/solution.py
+++ b/solution.py
@@ -365,29 +365,6 @@
         self.own.wait()
         for copy in self.copies:
             copy.wait_send()
-
-
-def exchange_kernel(pair_count, source, out, send_sem, recv_sem, own_sem):
-    greet(1, pair_count, False, True)
-    flow = Exchange(source, out, (send_sem, recv_sem), own_sem, pair_count)
-    flow.start()
-    flow.finish()
-
-
-def exchange(pieces, collective_id):
-    shard_count = lax.axis_size("fsdp")
-    dma = pltpu.SemaphoreType.DMA
-    return pl.pallas_call(
-        functools.partial(exchange_kernel, shard_count // 2),
-        in_specs=[pl.BlockSpec(memory_space=pltpu.VMEM)],
-        out_specs=pl.BlockSpec(memory_space=pl.ANY),
-        out_shape=jax.ShapeDtypeStruct(pieces.shape, pieces.dtype),
-        scratch_shapes=[dma((shard_count - 1,))] * 2 + [dma],
-        compiler_params=pltpu.CompilerParams(collective_id=collective_id, has_side_effects=True),
-        cost_estimate=pl.CostEstimate(
-            flops=0, bytes_accessed=pieces.size * 64, transcendentals=0
-        ),
-    )(pieces)
 
 
 def gather_kernel(arity, ctx_size, pair_count, slots, swaps, wide, *refs):
@@ -732,16 +709,18 @@
             copy.wait_send()
 
 
-def scatter_kernel(arity, ctx_size, pair_count, slot, spread_ctx, lines, *refs):
+def scatter_kernel(arity, ctx_size, pair_count, slot, spread_ctx, lines, swaps, *refs):
     sources, refs = refs[:arity], refs[arity:]
     line_sources, refs = refs[:lines], refs[lines:]
+    swap_sources, refs = refs[:swaps], refs[swaps:]
     outs, refs = refs[:arity], refs[arity:]
     line_outs, refs = refs[:lines], refs[lines:]
+    swap_outs, refs = refs[:swaps], refs[swaps:]
     halves, relays, asides, ends, finals = (refs[i * arity : (i + 1) * arity] for i in range(5))
     sems = refs[5 * arity : 5 * arity + 10]
     core_sems, relay_sems, ctx_sems, pair_sems, last_sems = (sems[2 * i : 2 * i + 2] for i in range(5))
     square, ways = peers_of(ctx_size)
-    ctx, pair, core = greet(ctx_size, pair_count, True, False)
+    ctx, pair, core = greet(ctx_size, pair_count, True, swaps > 0)
     order = list(range(1, pair_count)) + [0]
     started = []
     flows = []
@@ -869,6 +848,14 @@
 
     for flow in flows:
         flow.start()
+    exchanges = []
+    for item in range(swaps):
+        at = 5 * arity + 10 + 13 * lines + 3 * item
+        flow = Exchange(
+            swap_sources[item], swap_outs[item], refs[at : at + 2], refs[at + 2], pair_count
+        )
+        flow.start()
+        exchanges.append(flow)
     for turn in range(pair_count + 2):
         if turn < pair_count:
             fold_core(order[turn])
@@ -892,13 +879,13 @@
         for item in range(arity):
             for way in ways:
                 arrive(outs[item].at[ctx_source(ctx, way, square, ctx_size)], last_sems, (way - 1, item))
-    for flow in flows:
+    for flow in (*flows, *exchanges):
         flow.finish()
     for copy in started:
         copy.wait_send()
 
 
-def scatter(terms, slot, collective_id, spread_ctx=False, out_dtype=None, lines=()):
+def scatter(terms, slot, collective_id, spread_ctx=False, out_dtype=None, lines=(), swaps=()):
     ctx_size, shard_count = lax.axis_size("ctx"), lax.axis_size("fsdp")
     pair_count = shard_count // 2
     arity = len(terms)
@@ -918,13 +905,15 @@
 
     moved = sum(term.size * term.dtype.itemsize for term in terms)
     return pl.pallas_call(
-        functools.partial(scatter_kernel, arity, ctx_size, pair_count, slot, spread_ctx, len(lines)),
-        in_specs=[pl.BlockSpec(memory_space=pltpu.VMEM)] * (arity + len(lines)),
-        out_specs=[pl.BlockSpec(memory_space=pltpu.VMEM)] * (arity + len(lines)),
+        functools.partial(scatter_kernel, arity, ctx_size, pair_count, slot, spread_ctx, len(lines), len(swaps)),
+        in_specs=[pl.BlockSpec(memory_space=pltpu.VMEM)] * (arity + len(lines) + len(swaps)),
+        out_specs=[pl.BlockSpec(memory_space=pltpu.VMEM)] * (arity + len(lines))
+        + [pl.BlockSpec(memory_space=pl.ANY)] * len(swaps),
         out_shape=[
             jax.ShapeDtypeStruct(lead + term.shape[1:], out_dtype or term.dtype) for term in terms
         ]
-        + [jax.ShapeDtypeStruct(line.shape[1:], jnp.float32) for line in lines],
+        + [jax.ShapeDtypeStruct(line.shape[1:], jnp.float32) for line in lines]
+        + [jax.ShapeDtypeStruct(swap.shape, swap.dtype) for swap in swaps],
         scratch_shapes=room(ctx_size, pair_count)
         + room(pair_count)
         + room(asides, pair_count)
@@ -944,12 +933,13 @@
             ]
             + [dma((pair_count,))] * 4
             + line_room(line)
-        ],
+        ]
+        + [dma((shard_count - 1,)), dma((shard_count - 1,)), dma] * len(swaps),
         compiler_params=pltpu.CompilerParams(
             collective_id=collective_id, has_side_effects=True, vmem_limit_bytes=63 * 2**20
         ),
         cost_estimate=pl.CostEstimate(flops=0, bytes_accessed=moved * 16, transcendentals=0),
-    )(*terms, *lines)
+    )(*terms, *lines, *swaps)
 
 
 def line_sum_kernel(pair_count, source, out, half, room, *sems):
@@ -1055,7 +1045,7 @@
             pltpu.VMEM(grouped, jnp.float32),
             pltpu.SemaphoreType.DMA((parts,)),
         ],
-        compiler_params=pltpu.CompilerParams(vmem_limit_bytes=40 * 2**20),
+        compiler_params=pltpu.CompilerParams(vmem_limit_bytes=62 * 2**20),
         cost_estimate=pl.CostEstimate(
             flops=2 * tokens.shape[0] * D * QKV, bytes_accessed=2 * D * QKV, transcendentals=0
         ),
@@ -1117,7 +1107,7 @@
             pltpu.VMEM((tokens.shape[0], QKV), jnp.float32),
             pltpu.SemaphoreType.DMA,
         ],
-        compiler_params=pltpu.CompilerParams(vmem_limit_bytes=40 * 2**20),
+        compiler_params=pltpu.CompilerParams(vmem_limit_bytes=62 * 2**20),
         cost_estimate=pl.CostEstimate(
             flops=2 * tokens.shape[0] * D * QKV, bytes_accessed=2 * D * QKV, transcendentals=0
         ),
@@ -1215,13 +1205,14 @@
     small = lax.dynamic_slice_in_dim(small, own_ctx, 1, 0)
     small = jnp.pad(small, ((0, 0), (0, 16 * HD - small_width))).reshape(16, HD)
     width = -(-columns // HD) * HD
-    w_qkv_all, small_all, gate_up_cut = gather(
-        [own_cut(w_qkv), small],
-        [by_rows, by_rows],
+    w_qkv_all, w_o_all, small_all, gate_up_cut = gather(
+        [own_cut(w_qkv), own_cut(w_o), small],
+        [by_rows, by_rows, by_rows],
         1,
         swaps=[pack(own_cut(w_gate), own_cut(w_up), shard_count, columns, width)],
     )
     w_qkv_all = w_qkv_all.reshape(D, QKV)
+    w_o_all = w_o_all.reshape(D, D)
     small_all = small_all.reshape(shard_count, ctx_size, -1)[:, :, :small_width]
     small_all = small_all.reshape(shard_count, -1).astype(jnp.float32)
     bias_width = QKV // shard_count
@@ -1237,8 +1228,7 @@
     normed_one, queries, own_kv = project(
         tokens, gain_one, w_qkv_all, bias_all, cosine, signed_sine, rows_here
     )
-    all_kv, w_o_all = gather([own_kv, own_cut(w_o)], [by_tokens, by_rows], 2)
-    w_o_all = w_o_all.reshape(D, D)
+    (all_kv,) = gather([own_kv], [by_tokens], 2)
     gate_up_cut, all_kv = lax.optimization_barrier((gate_up_cut, all_kv))
     gate_up_cols = lax.all_gather(
         gate_up_cut.reshape(shard_count * cut, 2 * width), "ctx", axis=0, tiled=True
@@ -1294,10 +1284,6 @@
     grad_attended = lax.dot_general(
         grad_branch_one, w_o_all, CONTRACT_LAST, preferred_element_type=jnp.float32
     ).astype(jnp.bfloat16)
-    gate_up_rows, grad_attended = lax.optimization_barrier((gate_up_rows, grad_attended))
-    gate_up_rows = exchange(gate_up_rows.reshape(shard_count, cut, 2 * width), 5)
-    gate_up_rows, grad_attended = lax.optimization_barrier((gate_up_rows, grad_attended))
-    gate_up_rows = lax.all_gather(gate_up_rows, "ctx", axis=0, tiled=False)
     o_terms = lax.dot_general(
         attended_low, grad_branch_one, CONTRACT_FIRST, preferred_element_type=jnp.float32
     ).astype(jnp.bfloat16)
@@ -1312,12 +1298,14 @@
         block_rows,
         rows_here,
     )
-    (grad_kv,) = scatter(
+    grad_kv, gate_up_rows = scatter(
         [grad_kv_full.reshape(-1, rows_here, SEQS * KVH * 4 * HD)],
         by_tokens,
         3,
         out_dtype=jnp.float32,
-    )
+        swaps=[gate_up_rows.reshape(shard_count, cut, 2 * width)],
+    )
+    gate_up_rows = lax.all_gather(gate_up_rows, "ctx", axis=0, tiled=False)
     mixed_terms, grad_kv = lax.optimization_barrier((mixed_terms, grad_kv))
     mixed_rows = lax.psum_scatter(mixed_terms, "fsdp", scatter_dimension=0, tiled=True)
     grad_projected, grad_input, grad_gain_one, grad_bias = unproject(

time: 693 us -> 674 us (0.973)
  Pallas kernels: 476 us -> 452 us
  waiting for transfers between devices: 47 us -> 57.8 us
    pallas_call x1 -> x0, Pallas kernels: 42.1 us -> none  [exchange(): pl.pallas_call(functools.partial(exchange_kernel, shard_count // 2), in_s...]
    pallas_call x2, Pallas kernels: 163 us -> 174 us  [scatter(): pl.pallas_call(functools.partial(scatter_kernel, arity, ctx_size, pair_co...]
    psum x1, waiting for transfers between devices: 0.02 us -> 8.49 us  [shards(): down_rows = lax.psum(down_terms, 'ctx')]
    unnamed x79 -> x51, local copies, waits for them, and re-layouts: 14.8 us -> 6.64 us
  transfers between devices with their start and end apart: 6 -> 6, of which waited for: 3 -> 4; matrix products, arithmetic and copies ran while one was open for 14% -> 15% of each run, Pallas kernels for 49% -> 46%
where the time goes in v14:
time: 674 us; the launch traced here: 668 us
  Pallas kernels  452 us (67%)
  matrix products  89.7 us (13%)
  waiting for transfers between devices  57.8 us (9%)
  local copies, waits for them, and re-layouts  31 us (5%)
  other arithmetic  21.2 us (3%)
  between operations  14.9 us (2%)
    pallas_call x2, Pallas kernels, scatter(): pl.pallas_call(functools.partial(scatter_kernel, arity, ctx_size, pair_co...  174 us
    pallas_call x3, Pallas kernels, gather(): pl.pallas_call(functools.partial(gather_kernel, arity, ctx_size, pair_cou...  167 us
    pallas_call x1, Pallas kernels, line_sum(): pl.pallas_call(functools.partial(line_sum_kernel, pair_count), in_specs=[...  41.8 us
    all_gather x1, waiting for transfers between devices, shards(): cotangent_all = lax.all_gather(late_grad_out, 'fsdp', axis=0, tiled=True)  31 us
    pallas_call x1, Pallas kernels, attend_backward(): pl.pallas_call(kernel, grid_spec=pltpu.PrefetchScalarGridSpec(num_scalar_...  23.3 us
    pallas_call x1, Pallas kernels, attend_forward(): pl.pallas_call(kernel, grid_spec=pltpu.PrefetchScalarGridSpec(num_scalar_...  19.2 us
    dot_general x1, matrix products, shards(): jnp.dot(tokens_all, gate_up_cols, preferred_element_type=jnp.float32)  15.3 us
  transfers between devices with their start and end apart: 6, of which 4 were waited for; matrix products, arithmetic and copies ran while one was open for 15% of the time, Pallas kernels for 46%

profile of v14, /device:TPU:0, one launch (start us, length us, event | category | flops | bytes accessed | tf_op | source)
XLA Modules:
  0.0 667.7 jit_solution(2633537034928468748)
XLA Ops:
  17.0 73.7 %shard_map.194 = (bf16[32,48,2048]{2,1,0:T(8,128)(2,1)}, bf16[32,48,1536]{2,1,0:T(8,128)(2,1)}, bf16[32,16,128]{2,1,0:T(8,128)(2,1)}, bf16[8,48,2304]{2,1,0:T(8,128)(2,1)}) custom-call(bf16[48,2048]{1,0:T(8,128)(2,1)} %constant_dynamic-slice_fusion.4.refs_0_, bf16[48,1536]{1,0:T(8,128)(2,1)} %constant_dynamic-slice_fusion.3.refs_1_, ...), custom_call_target="tpu_custom_call" | custom-call | bytes 44564480 | tf_op jit(solution)/shard_map/pallas_call | solution.py:590
  96.9 6.8 %project.1 = (bf16[160,1536]{1,0:T(8,128)(2,1)}, bf16[2,2,2,240,128]{4,3,2,1,0:T(8,128)(2,1)}, bf16[40,2048]{1,0:T(8,128)(2,1)}) custom-call(bf16[160,1536]{1,0:T(8,128)(2,1)} %bitcast.87, f32[1,1536]{1,0:T(1,128)} %reshape_reshape.7.gain_ref, bf16[1536,2048]{1,0:T(8,128)(2,1)} %bitcast.83, f32[1,2048]{1,0:T(1,128)} %bitcast.115, f32[160,128]{1,0:T(8,128)} %bitcast.109, ...), custom_call_target="tpu_custom_call" | custom-call | flops 1006632960 | bytes 6291456 | tf_op jit(solution)/shard_map/project/pallas_call | solution.py:1034
  103.7 50.9 %shard_map.195 = bf16[32,40,2048]{2,1,0:T(8,128)(2,1)} custom-call(bf16[40,2048]{1,0:T(8,128)(2,1)} %get-tuple-element.50.refs_0_), custom_call_target="tpu_custom_call" | custom-call | bytes 20971520 | tf_op jit(solution)/shard_map/pallas_call | solution.py:590
  156.4 19.2 %attend_forward.1 = (f32[2,2,2,240,128]{4,3,2,1,0:T(8,128)}, f32[2,2,2,1,240]{4,3,2,1,0:T(1,128)}) custom-call(s32[18]{0:T(128)} %pad_add_fusion.scalars, bf16[2,2,2,240,128]{4,3,2,1,0:T(8,128)(2,1)} %get-tuple-element.48.q_ref, bf16[1280,2048]{1,0:T(8,128)(2,1)} %bitcast.79), custom_call_target="tpu_custom_call" | custom-call | tf_op jit(solution)/shard_map/attend_forward/pallas_call | solution.py:167
  183.2 42.4 %shard_map.196 = bf16[8,160,1536]{2,1,0:T(8,128)(2,1)} custom-call(bf16[160,1536]{1,0:T(8,128)(2,1)} %copy.54.refs_0_), custom_call_target="tpu_custom_call" | custom-call | bytes 62914560 | tf_op jit(solution)/shard_map/pallas_call | solution.py:590
  225.6 4.6 all-gather.7.cloned.1.call-done
  230.2 15.3 %fusion.12 = f32[1280,2304]{0,1:T(8,128)} fusion(bf16[1280,1536]{1,0:T(8,128)(2,1)} %bitcast.96, bf16[1536,2304]{1,0:T(8,128)(2,1)} %all-gather.7.cloned.1.call-done), kind=kOutput, calls=%fused_computation.63 | convolution fusion | flops 9059696640 | bytes 22806528 | tf_op jit(solution)/shard_map/dot_general | solution.py:1250
  245.5 31.0 %all-gather.5.cloned.1.call-done = bf16[1280,1536]{1,0:T(8,128)(2,1)} async-done(((bf16[160,1536]{1,0:T(8,128)(2,1)}), bf16[1280,1536]{1,0:T(8,128)(2,1)}) %all-gather.5.cloned.1.call-update) | async-done | bytes 3932176 | tf_op jit(solution)/shard_map/all_gather | solution.py:1227
  276.5 12.7 %multiply_convert_fusion.2 = (bf16[1280,1152]{0,1:T(8,128)(2,1)S(1)}, bf16[1280,1152]{0,1:T(8,128)(2,1)S(1)}, bf16[1280,1152]{0,1:T(8,128)(2,1)}) fusion(f32[1280,2304]{0,1:T(8,128)} %fusion.12, bf16[1280,1536]{1,0:T(8,128)(2,1)} %all-gather.5.cloned.1.call-done, bf16[1120,1536]{1,0:T(8,128)(2,1)} %param.20), kind=kOutput, calls=%fused_computation.9 | convolution fusion | flops 4551966720 | bytes 28016640 | tf_op jit(solution)/shard_map/dot_general | solution.py:1255
  291.9 12.7 %convolution_convert_fusion = bf16[1536,2304]{1,0:T(8,128)(2,1)} fusion(bf16[1280,1536]{1,0:T(8,128)(2,1)S(1)} %bitcast.97, bf16[1280,1152]{0,1:T(8,128)(2,1)S(1)} %get-tuple-element.82, bf16[1280,1152]{0,1:T(8,128)(2,1)S(1)} %get-tuple-element.81), kind=kOutput, calls=%fused_computation | convolution fusion | flops 9075032064 | bytes 16908288 | tf_op jit(solution)/shard_map/dot_general | solution.py:1260
  307.8 13.1 %convolution_convert_fusion.5 = bf16[1280,1536]{1,0:T(8,128)(2,1)} fusion(bf16[1280,2304]{0,1:T(8,128)(2,1)S(1)} %pad_maximum_fusion, bf16[1536,2304]{1,0:T(8,128)(2,1)} %all-gather.7.cloned.1.call-done), kind=kOutput, calls=%fused_computation.5 | convolution fusion | flops 9061662720 | bytes 16908288 | tf_op jit(solution)/shard_map/dot_general | solution.py:1267
  320.9 41.8 %shard_map.197 = f32[160,1536]{1,0:T(8,128)} custom-call(bf16[8,160,1536]{2,1,0:T(8,128)(2,1)} %bitcast.95), custom_call_target="tpu_custom_call" | custom-call | bytes 31457280 | tf_op jit(solution)/shard_map/pallas_call | solution.py:958
  362.6 9.4 %convolution_convert_fusion.1 = bf16[1280,1536]{1,0:T(8,128)(2,1)} fusion(bf16[1280,1152]{0,1:T(8,128)(2,1)} %get-tuple-element.59, bf16[1120,1536]{1,0:T(8,128)(2,1)} %param.20), kind=kOutput, calls=%fused_computation.1 | convolution fusion | flops 4531814400 | bytes 10321920 | tf_op jit(solution)/shard_map/dot_general | solution.py:1276
  372.1 9.6 %convolution_convert_fusion.3 = bf16[1152,1536]{1,0:T(8,128)(2,1)} fusion(bf16[1280,1152]{0,1:T(8,128)(2,1)} %get-tuple-element.59, bf16[1280,1536]{1,0:T(8,128)(2,1)} %all-gather.5.cloned.1.call-done), kind=kOutput, calls=%fused_computation.3 | convolution fusion | flops 4531617792 | bytes 10420224 | tf_op jit(solution)/shard_map/dot_general | solution.py:1272
  388.9 4.0 convolution_convert_fusion.6
  394.4 23.3 %attend_backward.1 = (f32[2,2,2,240,128]{4,3,2,1,0:T(8,128)}, bf16[1280,2048]{1,0:T(8,128)(2,1)}) custom-call(s32[18]{0:T(128)} %pad_add_fusion.scalars, bf16[2,2,2,240,128]{4,3,2,1,0:T(8,128)(2,1)} %get-tuple-element.48.q_ref, bf16[2,2,2,240,128]{4,3,2,1,0:T(8,128)(2,1)} %bitcast.102, f32[2,2,2,240,128]{4,3,2,1,0:T(8,128)} %get-tuple-element.52.att_ref, ...), custom_call_target="tpu_custom_call" | custom-call | tf_op jit(solution)/shard_map/attend_backward/pallas_call | solution.py:275
  417.7 66.1 %shard_map.198 = (f32[40,2048]{1,0:T(8,128)}, bf16[8,48,2304]{2,1,0:T(8,128)(2,1)}) custom-call(bf16[32,40,2048]{2,1,0:T(8,128)(2,1)} %bitcast.93, bf16[8,48,2304]{2,1,0:T(8,128)(2,1)} %bitcast.106), custom_call_target="tpu_custom_call" | custom-call | bytes 83886080 | tf_op jit(solution)/shard_map/pallas_call | solution.py:907
  488.4 8.5 %all-reduce.5.cloned.1.call-done = bf16[1152,1536]{1,0:T(8,128)(2,1)} async-done(((bf16[1152,1536]{1,0:T(8,128)(2,1)}), bf16[1152,1536]{1,0:T(8,128)(2,1)}) %all-reduce.5.cloned.1.call-update) | async-done | bytes 3538960 | tf_op jit(solution)/shard_map/psum | solution.py:1275
  496.9 5.8 slice_convert_fusion
  502.7 8.2 %unproject.1 = (bf16[160,2048]{1,0:T(8,128)(2,1)}, f32[160,1536]{1,0:T(8,128)}, f32[1,1536]{1,0:T(1,128)}, f32[1,2048]{1,0:T(1,128)}) custom-call(f32[2,2,2,240,128]{4,3,2,1,0:T(8,128)} %get-tuple-element.66.gq_ref, f32[40,2048]{1,0:T(8,128)} %get-tuple-element.67.gkv_ref, f32[160,128]{1,0:T(8,128)} %bitcast.110, f32[160,128]{1,0:T(8,128)} %bitcast_multiply_fusion.sin_ref, ...), custom_call_target="tpu_custom_call" | custom-call | flops 1006632960 | bytes 6291456 | tf_op jit(solution)/shard_map/unproject/pallas_call | solution.py:1095
  514.1 5.6 convolution_convert_fusion.2
  519.8 108.0 %shard_map.199 = (bf16[4,48,2048]{2,1,0:T(8,128)(2,1)}, bf16[4,48,1536]{2,1,0:T(8,128)(2,1)}, f32[4,8,128]{2,1,0:T(8,128)}) custom-call(bf16[32,48,2048]{2,1,0:T(8,128)(2,1)} %bitcast.81, bf16[32,48,1536]{2,1,0:T(8,128)(2,1)} %bitcast.82, f32[32,8,128]{2,1,0:T(8,128)} %bitcast.111), custom_call_target="tpu_custom_call" | custom-call | bytes 178257920 | tf_op jit(solution)/shard_map/pallas_call | solution.py:907
  639.0 12.6 %all-gather.9.cloned.1.call-done = bf16[32,48,2304]{2,1,0:T(8,128)(2,1)} async-done(((bf16[8,48,2304]{2,1,0:T(8,128)(2,1)}), bf16[32,48,2304]{2,1,0:T(8,128)(2,1)}) %all-gather.9.cloned.1.call-update) | async-done | bytes 7077904 | tf_op jit(solution)/shard_map/all_gather | solution.py:1308
  651.6 8.8 %unpack.1 = (f32[4,48,8960]{2,1,0:T(8,128)}, f32[4,48,8960]{2,1,0:T(8,128)}) custom-call(bf16[4,8,48,2304]{3,2,1,0:T(8,128)(2,1)} %bitcast.90), custom_call_target="tpu_custom_call" | custom-call | tf_op jit(solution)/shard_map/unpack/pallas_call | solution.py:1149
  (133 shorter events, 58.6 us)
Async XLA Ops:
  7.2 3.2 copy-start
  7.2 223.0 %all-gather.7.cloned.1.call-start = ((), (), s32[]{:S(2)}) async-start(), calls=%async_computation.3 | async-start | bytes 8847360 | tf_op jit(solution)/shard_map/all_gather | solution.py:1233
  11.1 80.8 %copy-start.22 = (s32[2,8]{1,0:T(2,128)S(1)}, s32[2,8]{1,0:T(2,128)}, u32[]{:S(2)}) copy-start(s32[2,8]{1,0:T(2,128)} %param.12) | copy-start | bytes 196
  11.1 81.5 %copy-start.15 = (bf16[40,4,1536]{2,1,0:T(4,128)(2,1)S(1)}, bf16[40,4,1536]{2,1,0:T(4,128)(2,1)}, u32[]{:S(2)}) copy-start(bf16[40,4,1536]{2,1,0:T(4,128)(2,1)} %param.21) | copy-start | bytes 1474564
  11.1 82.4 %copy-start.16 = (bf16[40,4,1536]{2,1,0:T(4,128)(2,1)S(1)}, bf16[40,4,1536]{2,1,0:T(4,128)(2,1)}, u32[]{:S(2)}) copy-start(bf16[40,4,1536]{2,1,0:T(4,128)(2,1)} %param.11) | copy-start | bytes 1474564
  154.6 121.9 %all-gather.5.cloned.1.call-start = ((), (), s32[]{:S(2)}) async-start(), calls=%async_computation.2 | async-start | bytes 4423680 | tf_op jit(solution)/shard_map/all_gather | solution.py:1227
  155.4 262.3 %reduce-scatter.3.cloned.1.call-start = ((), (), s32[]{:S(2)}) async-start(), calls=%async_computation.4 | async-start | bytes 8847360 | tf_op jit(solution)/shard_map/reduce_scatter | solution.py:1263
  155.8 25.3 %copy-start.17 = (f32[1536]{0:T(1024)}, f32[1536]{0:T(1024)S(1)}, u32[]{:S(2)}) copy-start(f32[1536]{0:T(1024)S(1)} %mul.246) | copy-start | bytes 18436
  156.4 21.1 %copy-start.6 = (bf16[4,40,1536]{2,1,0:T(8,128)(2,1)S(1)}, bf16[4,40,1536]{2,1,0:T(8,128)(2,1)}, u32[]{:S(2)}) copy-start(bf16[4,40,1536]{2,1,0:T(8,128)(2,1)} %copy.48) | copy-start | bytes 1474564
  177.5 4.6 copy-start.7
  181.1 206.6 %copy-start.2 = (f32[160,1536]{1,0:T(8,128)}, f32[160,1536]{1,0:T(8,128)S(1)}, u32[]{:S(2)}) copy-start(f32[160,1536]{1,0:T(8,128)S(1)} %get-tuple-element.95) | copy-start | bytes 2949124
  276.5 15.3 %copy-start.10 = (bf16[8,160,1536]{2,1,0:T(8,128)(2,1)S(1)}, bf16[8,160,1536]{2,1,0:T(8,128)(2,1)}, u32[]{:S(2)}) copy-start(bf16[8,160,1536]{2,1,0:T(8,128)(2,1)} %shard_map.196) | copy-start | bytes 11796484
  289.3 2.6 copy-start.12
  304.6 192.3 %all-reduce.5.cloned.1.call-start = ((), (), s32[]{:S(2)}) async-start(), calls=%async_computation.6 | async-start | bytes 7077888 | tf_op jit(solution)/shard_map/psum | solution.py:1275
  381.6 5.1 copy-start.18
  381.6 5.1 copy-start.21
  381.7 6.0 copy-start.9
  381.7 255.2 %reduce-scatter.5.cloned.1.call-start = ((), (), s32[]{:S(2)}) async-start(), calls=%async_computation.5 | async-start | bytes 4423680 | tf_op jit(solution)/shard_map/reduce_scatter | solution.py:1310
  417.7 66.9 %copy-start.5 = (f32[160,1536]{1,0:T(8,128)S(1)}, f32[160,1536]{1,0:T(8,128)}, u32[]{:S(2)}) copy-start(f32[160,1536]{1,0:T(8,128)} %copy-done.4) | copy-start | bytes 2949124
  483.8 167.8 %all-gather.9.cloned.1.call-start = ((), (), s32[]{:S(2)}) async-start(), calls=%async_computation.7 | async-start | bytes 8847360 | tf_op jit(solution)/shard_map/all_gather | solution.py:1308
  502.7 11.4 %copy-start.13 = (bf16[160,1536]{1,0:T(8,128)(2,1)S(1)}, bf16[160,1536]{1,0:T(8,128)(2,1)}, u32[]{:S(2)}) copy-start(bf16[160,1536]{1,0:T(8,128)(2,1)} %get-tuple-element.69) | copy-start | bytes 1474564
  519.8 110.1 %copy-start.14 = (f32[160,1536]{1,0:T(8,128)S(1)}, f32[160,1536]{1,0:T(8,128)}, u32[]{:S(2)}) copy-start(f32[160,1536]{1,0:T(8,128)} %get-tuple-element.68) | copy-start | bytes 2949124
  627.8 9.0 %copy-start.3 = (f32[160,1536]{1,0:T(8,128)S(1)}, f32[160,1536]{1,0:T(8,128)}, u32[]{:S(2)}) copy-start(f32[160,1536]{1,0:T(8,128)} %copy-done.2) | copy-start | bytes 2949124
  634.3 26.1 %copy-start.1 = (bf16[192,2048]{1,0:T(8,128)(2,1)S(1)}, bf16[192,2048]{1,0:T(8,128)(2,1)}, u32[]{:S(2)}) copy-start(bf16[192,2048]{1,0:T(8,128)(2,1)} %param.14) | copy-start | bytes 2359300
  (5 other events, 4.9 us)
Sparse Core Ops, SparseCore 0:
  154.7 75.3 all-gather.6
  231.8 44.6 all-gather.4
  304.7 75.3 reduce-scatter.2
  383.8 113.0 all-reduce.4
  499.1 47.4 reduce-scatter.4
  548.3 103.3 all-gather.8
